TPU v7x, 128 devices: a whole 4x4x4 slice. The times are simulated.
128 devices in a mesh: rep: 4 (over x), fsdp: 32 (over z, y, core).
Axes of the slice: x: 4, y: 4, z: 4, core: 2. Of those that a mesh axis runs over, the one named last changes fastest.
Arguments:
- x_tokens: bfloat16 [256, 257, 1408], P(('rep', 'fsdp'))
- grad_z: bfloat16 [256, 257, 1408], P(('rep', 'fsdp'))
- w_qkv: float32 [1408, 4224], P('fsdp')
- b_qkv: float32 [4224], P('fsdp')
- w_out: float32 [1408, 1408], P('fsdp')
- w_up: float32 [1408, 6144], P('fsdp')
- b_up: float32 [6144], P('fsdp')
- w_down: float32 [6144, 1408], P('fsdp')
- vec_params: float32 [8, 1408], P(None, 'fsdp')
Outputs:
- output 1: bfloat16 [256, 257, 1408], P(('rep', 'fsdp'))
- output 2: bfloat16 [256, 257, 1408], P(('rep', 'fsdp'))
- output 3: float32 [1408, 4224], P('fsdp')
- output 4: float32 [4224], P('fsdp')
- output 5: float32 [1408, 1408], P('fsdp')
- output 6: float32 [1408, 6144], P('fsdp')
- output 7: float32 [6144], P('fsdp')
- output 8: float32 [6144, 1408], P('fsdp')
- output 9: float32 [8, 1408], P(None, 'fsdp')
All inputs are finite; a program needn't handle non-finite values.
Results may differ from a plain program's by a relative error of at most 0.02.
Values are sent between devices in bfloat16 or wider.
A program may use at most 1 GiB of HBM per device.

v0:
```python
import jax
import jax.numpy as jnp
from jax import lax
from jax.sharding import PartitionSpec as P

HEADS = 16
LN_EPS = 1e-5


def normalize(t):
    mean = jnp.mean(t, axis=-1, keepdims=True)
    centered = t - mean
    variance = jnp.mean(centered * centered, axis=-1, keepdims=True)
    return centered * lax.rsqrt(variance + LN_EPS)


def gelu_exact(t):
    return jax.nn.gelu(t, approximate=False)


def layer_forward(x_loc, weights):
    w_qkv, b_qkv, w_out, w_up, b_up, w_down, vec_rows = weights
    ln1_gain, ln1_bias, out_bias, scale_attn, ln2_gain, ln2_bias, down_bias, scale_mlp = vec_rows
    num_seqs, tokens, width = x_loc.shape
    head_dim = width // HEADS
    score_scale = head_dim ** -0.5
    x_float = x_loc.astype(jnp.float32)
    h_one = (normalize(x_float) * ln1_gain + ln1_bias).astype(jnp.bfloat16)
    qkv_proj = jnp.einsum("std,de->ste", h_one, w_qkv, preferred_element_type=jnp.float32) + b_qkv
    qkv_heads = qkv_proj.astype(jnp.bfloat16).reshape(num_seqs, tokens, 3, HEADS, head_dim)
    q_heads = qkv_heads[:, :, 0]
    k_heads = qkv_heads[:, :, 1]
    v_heads = qkv_heads[:, :, 2]
    scores = jnp.einsum("sqhe,skhe->shqk", q_heads, k_heads, preferred_element_type=jnp.float32) * score_scale
    attn_probs = jax.nn.softmax(scores, axis=-1)
    probs_bf = attn_probs.astype(jnp.bfloat16)
    head_out = jnp.einsum("shqk,skhe->sqhe", probs_bf, v_heads, preferred_element_type=jnp.float32)
    head_out = head_out.astype(jnp.bfloat16).reshape(num_seqs, tokens, width)
    att_out = jnp.einsum("std,de->ste", head_out, w_out, preferred_element_type=jnp.float32) + out_bias
    resid_mid = x_float + scale_attn * att_out
    h_two = (normalize(resid_mid) * ln2_gain + ln2_bias).astype(jnp.bfloat16)
    pre_act = jnp.einsum("std,df->stf", h_two, w_up, preferred_element_type=jnp.float32) + b_up
    mlp_act = gelu_exact(pre_act).astype(jnp.bfloat16)
    mlp_out = jnp.einsum("stf,fd->std", mlp_act, w_down, preferred_element_type=jnp.float32) + down_bias
    z_loc = (resid_mid + scale_mlp * mlp_out).astype(jnp.bfloat16)
    saved = (h_one, qkv_heads, attn_probs, probs_bf, head_out, att_out, resid_mid, h_two, pre_act, mlp_act, mlp_out)
    return z_loc, saved


def layer_backward(x_loc, dz_loc, saved, weights):
    w_qkv, b_qkv, w_out, w_up, b_up, w_down, vec_rows = weights
    ln1_gain, ln1_bias, out_bias, scale_attn, ln2_gain, ln2_bias, down_bias, scale_mlp = vec_rows
    h_one, qkv_heads, attn_probs, probs_bf, head_out, att_out, resid_mid, h_two, pre_act, mlp_act, mlp_out = saved
    num_seqs, tokens, width = x_loc.shape
    head_dim = width // HEADS
    score_scale = head_dim ** -0.5
    g_out = dz_loc.astype(jnp.float32)
    grad_scale_mlp = jnp.sum(g_out * mlp_out, axis=(0, 1))
    d_mlp = g_out * scale_mlp
    grad_down_bias = jnp.sum(d_mlp, axis=(0, 1))
    d_mlp_bf = d_mlp.astype(jnp.bfloat16)
    grad_w_down = jnp.einsum("stf,std->fd", mlp_act, d_mlp_bf, preferred_element_type=jnp.float32)
    d_act = jnp.einsum("std,fd->stf", d_mlp_bf, w_down, preferred_element_type=jnp.float32)
    d_pre = jax.vjp(gelu_exact, pre_act)[1](d_act)[0]
    grad_b_up = jnp.sum(d_pre, axis=(0, 1))
    d_pre_bf = d_pre.astype(jnp.bfloat16)
    grad_w_up = jnp.einsum("std,stf->df", h_two, d_pre_bf, preferred_element_type=jnp.float32)
    d_h_two = jnp.einsum("stf,df->std", d_pre_bf, w_up, preferred_element_type=jnp.float32)
    array_b8, norm_two_back = jax.vjp(normalize, resid_mid)
    grad_ln2_gain = jnp.sum(d_h_two * array_b8, axis=(0, 1))
    grad_ln2_bias = jnp.sum(d_h_two, axis=(0, 1))
    g_resid = g_out + norm_two_back(d_h_two * ln2_gain)[0]
    grad_scale_attn = jnp.sum(g_resid * att_out, axis=(0, 1))
    d_att = g_resid * scale_attn
    grad_out_bias = jnp.sum(d_att, axis=(0, 1))
    d_att_bf = d_att.astype(jnp.bfloat16)
    grad_w_out = jnp.einsum("std,ste->de", head_out, d_att_bf, preferred_element_type=jnp.float32)
    d_heads = jnp.einsum("ste,de->std", d_att_bf, w_out, preferred_element_type=jnp.float32)
    d_heads = d_heads.astype(jnp.bfloat16).reshape(num_seqs, tokens, HEADS, head_dim)
    q_heads = qkv_heads[:, :, 0]
    k_heads = qkv_heads[:, :, 1]
    v_heads = qkv_heads[:, :, 2]
    d_probs = jnp.einsum("sqhe,skhe->shqk", d_heads, v_heads, preferred_element_type=jnp.float32)
    grad_v = jnp.einsum("shqk,sqhe->skhe", probs_bf, d_heads, preferred_element_type=jnp.float32)
    d_scores = attn_probs * (d_probs - jnp.sum(d_probs * attn_probs, axis=-1, keepdims=True))
    d_scores_bf = (d_scores * score_scale).astype(jnp.bfloat16)
    grad_q = jnp.einsum("shqk,skhe->sqhe", d_scores_bf, k_heads, preferred_element_type=jnp.float32)
    grad_k = jnp.einsum("shqk,sqhe->skhe", d_scores_bf, q_heads, preferred_element_type=jnp.float32)
    d_qkv = jnp.stack([grad_q, grad_k, grad_v], axis=2).reshape(num_seqs, tokens, 3 * width)
    grad_b_qkv = jnp.sum(d_qkv, axis=(0, 1))
    d_qkv_bf = d_qkv.astype(jnp.bfloat16)
    grad_w_qkv = jnp.einsum("std,ste->de", h_one, d_qkv_bf, preferred_element_type=jnp.float32)
    d_h_one = jnp.einsum("ste,de->std", d_qkv_bf, w_qkv, preferred_element_type=jnp.float32)
    value_a8, norm_one_back = jax.vjp(normalize, x_loc.astype(jnp.float32))
    grad_ln1_gain = jnp.sum(d_h_one * value_a8, axis=(0, 1))
    grad_ln1_bias = jnp.sum(d_h_one, axis=(0, 1))
    dx_loc = (g_resid + norm_one_back(d_h_one * ln1_gain)[0]).astype(jnp.bfloat16)
    grad_vec = jnp.stack([grad_ln1_gain, grad_ln1_bias, grad_out_bias, grad_scale_attn,
                          grad_ln2_gain, grad_ln2_bias, grad_down_bias, grad_scale_mlp])
    return dx_loc, (grad_w_qkv, grad_b_qkv, grad_w_out, grad_w_up, grad_b_up, grad_w_down, grad_vec)


def gather_weights(shards):
    w_qkv, b_qkv, w_out, w_up, b_up, w_down, vec_params = shards

    def full_rows(shard):
        return lax.all_gather(shard.astype(jnp.bfloat16), "fsdp", axis=0, tiled=True)

    vec_full = lax.all_gather(vec_params.astype(jnp.bfloat16), "fsdp", axis=1, tiled=True)
    return (full_rows(w_qkv), full_rows(b_qkv).astype(jnp.float32), full_rows(w_out), full_rows(w_up),
            full_rows(b_up).astype(jnp.float32), full_rows(w_down), vec_full.astype(jnp.float32))


def reduce_grads(local_grads):
    grad_w_qkv, grad_b_qkv, grad_w_out, grad_w_up, grad_b_up, grad_w_down, grad_vec = local_grads

    def total_rows(full):
        return lax.psum(lax.psum_scatter(full, "fsdp", scatter_dimension=0, tiled=True), "rep")

    vec_total = lax.psum(lax.psum_scatter(grad_vec, "fsdp", scatter_dimension=1, tiled=True), "rep")
    return (total_rows(grad_w_qkv), total_rows(grad_b_qkv), total_rows(grad_w_out), total_rows(grad_w_up),
            total_rows(grad_b_up), total_rows(grad_w_down), vec_total)


def solution(mesh):
    batch_spec = P(("rep", "fsdp"), None, None)
    row_spec = P("fsdp", None)
    flat_spec = P("fsdp")
    col_spec = P(None, "fsdp")
    param_specs = (row_spec, flat_spec, row_spec, row_spec, flat_spec, row_spec, col_spec)

    def device_step(x_loc, dz_loc, w_qkv, b_qkv, w_out, w_up, b_up, w_down, vec_params):
        shards = (w_qkv, b_qkv, w_out, w_up, b_up, w_down, vec_params)
        weights_fwd = gather_weights(shards)
        z_loc, saved = layer_forward(x_loc, weights_fwd)
        shards_bwd = lax.optimization_barrier((shards, z_loc))[0]
        weights_bwd = gather_weights(shards_bwd)
        dx_loc, local_grads = layer_backward(x_loc, dz_loc, saved, weights_bwd)
        return (z_loc, dx_loc) + reduce_grads(local_grads)

    return jax.shard_map(device_step, mesh=mesh, in_specs=(batch_spec, batch_spec) + param_specs,
                         out_specs=(batch_spec, batch_spec) + param_specs, check_vma=False)
```

profile of v0, /device:TPU:1, one launch (start us, length us, event | category | flops | bytes accessed | tf_op | source)
XLA Modules:
  0.0 1508.8 jit_solution(2639057263500645084)
XLA Ops:
  16.8 126.3 %all-reduce.14 = (bf16[4224]{0:T(1024)(128)(2,1)S(1)}, bf16[6144]{0:T(1024)(128)(2,1)S(1)}) all-reduce(bf16[4224]{0:T(1024)(128)(2,1)S(1)} %dynamic-update-slice, bf16[6144]{0:T(1024)(128)(2,1)S(1)} %dynamic-update-slice.1), channel_id=1, replica_groups=mesh['rep'=4,'fsdp'=32] {'fsdp'}, use_global_device_ids=true, to_apply=%add | all-reduce | flops 10368 | bytes 41472
  143.1 27.0 %all-gather = bf16[32,44,8]{1,2,0:T(8,128)(2,1)S(1)} all-gather(bf16[1,44,8]{1,2,0:T(8,128)(2,1)S(1)} %convert_bitcast_fusion.7), channel_id=1, replica_groups=mesh['rep'=4,'fsdp'=32] {'fsdp'}, dimensions={0}, use_global_device_ids=true | all-gather | bytes 23232 | tf_op jit(solution)/shard_map/all_gather | solution.py:109
  242.2 16.7 %fusion.92 = (f32[2,16,257]{2,1,0:T(8,128)S(1)}, f32[2,16,257,257]{2,3,1,0:T(8,128)}) fusion(f32[2,16,257,257]{2,3,1,0:T(8,128)} %fusion.61), kind=kOutput, calls=%fused_computation.146 | output fusion | flops 8454528 | bytes 16941440 | tf_op jit(solution)/shard_map/sub | solution.py:35
  271.3 19.5 %reshape.128 = bf16[1408,6144,1]{1,0,2:T(8,128)(2,1)} reshape(bf16[32,44,6144]{2,1,0:T(8,128)(2,1)} %all-gather.25.cloned.1.call-done) | data formatting | bytes 34603008
  290.9 23.8 %fusion.51 = (u8[257,6144]{1,0:T(8,128)(4,1)}, u8[257,6144]{1,0:T(8,128)(4,1)}, f32[2,257,6144]{2,1,0:T(8,128)}) fusion(f32[6144]{0:T(1024)S(1)} %convert_element_type.118, bf16[1408,6144,1]{1,0,2:T(8,128)(2,1)} %reshape.128, f32[2,257,1408]{2,1,0:T(8,128)S(1)} %get-tuple-element.101, f32[1408]{0:T(1024)S(1)} %get-tuple-element.75, ...), kind=kOutput, calls=%fused_computation.71 | convolution fusion | flops 8937646080 | bytes 36026384 | tf_op jit(solution)/shard_map/std,df->stf/dot_general | solution.py:42
  314.8 33.0 %multiply_convert_fusion.1 = (bf16[2,257,6144]{2,1,0:T(8,128)(2,1)}, f32[2,257,6144]{2,1,0:T(8,128)}) fusion(f32[2,257,6144]{2,1,0:T(8,128)} %get-tuple-element.114, f32[6144]{0:T(1024)S(1)} %convert_element_type.118, u8[257,6144]{1,0:T(8,128)(4,1)} %get-tuple-element.56, u8[257,6144]{1,0:T(8,128)(4,1)} %get-tuple-element.55), kind=kLoop, calls=%fused_computation.20 | loop fusion | flops 224219136 | bytes 34762752 | tf_op jit(solution)/shard_map/convert_element_type | solution.py:43
  347.8 17.6 %add_convert_fusion.2 = (bf16[2,257,1408]{2,1,0:T(8,128)(2,1)}, f32[2,257,1408]{2,1,0:T(8,128)}) fusion(f32[2,257,1408]{2,1,0:T(8,128)S(1)} %get-tuple-element.101, f32[1408]{0:T(1024)S(1)} %get-tuple-element.73, f32[1408]{0:T(1024)S(1)} %get-tuple-element.74, bf16[2,257,6144]{2,1,0:T(8,128)(2,1)} %get-tuple-element.98, ...), kind=kOutput, calls=%fused_computation.83 | convolution fusion | flops 8895868928 | bytes 30865920 | tf_op jit(solution)/shard_map/stf,fd->std/dot_general | solution.py:44
  373.3 24.4 %all-gather.4 = bf16[32,44,8]{1,2,0:T(8,128)(2,1)S(1)} all-gather(bf16[1,44,8]{1,2,0:T(8,128)(2,1)S(1)} %convert_bitcast_fusion.6), channel_id=1, replica_groups=mesh['rep'=4,'fsdp'=32] {'fsdp'}, dimensions={0}, use_global_device_ids=true | all-gather | bytes 23232 | tf_op jit(solution)/shard_map/all_gather | solution.py:109
  398.4 21.3 %convolution_bitcast_fusion = f32[6144,1408]{1,0:T(8,128)} fusion(bf16[2,257,6144]{2,1,0:T(8,128)(2,1)} %get-tuple-element.98, f32[1408]{0:T(1024)S(1)} %get-tuple-element.72, bf16[2,257,1408]{2,0,1:T(2,128)(2,1)} %param.10), kind=kOutput, calls=%fused_computation.2 | convolution fusion | flops 8895143936 | bytes 42372096 | tf_op jit(solution)/shard_map/stf,std->fd/dot_general | solution.py:62
  426.0 52.0 %all-gather.31.cloned.1.call-done = bf16[32,44,4224]{2,1,0:T(8,128)(2,1)} async-done(((bf16[1,44,4224]{2,1,0:T(8,128)(2,1)}), bf16[32,44,4224]{2,1,0:T(8,128)(2,1)}) %all-gather.31.cloned.1.call-update) | async-done | bytes 11894800 | tf_op jit(solution)/shard_map/all_gather | solution.py:107
  493.7 64.1 %all-gather.27.cloned.1.call-done = bf16[32,44,6144]{2,1,0:T(8,128)(2,1)} async-done(((bf16[1,44,6144]{2,1,0:T(8,128)(2,1)}), bf16[32,44,6144]{2,1,0:T(8,128)(2,1)}) %all-gather.27.cloned.1.call-update) | async-done | bytes 17301520 | tf_op jit(solution)/shard_map/all_gather | solution.py:107
  557.8 19.1 %reshape.131 = bf16[1408,6144,1]{1,0,2:T(8,128)(2,1)} reshape(bf16[32,44,6144]{2,1,0:T(8,128)(2,1)} %all-gather.27.cloned.1.call-done) | data formatting | bytes 34603008
  576.9 56.8 %all-gather.19.cloned.1.call-done = bf16[6144,1408]{1,0:T(8,128)(2,1)} async-done(((bf16[192,1408]{1,0:T(8,128)(2,1)}), bf16[6144,1408]{1,0:T(8,128)(2,1)}) %all-gather.19.cloned.1.call-update) | async-done | bytes 17301520 | tf_op jit(solution)/shard_map/all_gather | solution.py:107
  633.7 24.7 %fusion.93 = (f32[6144]{0:T(1024)}, bf16[2,257,6144]{2,1,0:T(8,128)(2,1)}) fusion(f32[2,257,6144]{2,1,0:T(8,128)} %get-tuple-element.99, bf16[6144,1408]{1,0:T(8,128)(2,1)} %all-gather.19.cloned.1.call-done, f32[1408]{0:T(1024)S(1)} %get-tuple-element.72, bf16[2,257,1408]{2,0,1:T(2,128)(2,1)} %param.10, f32[2,257,6144]{2,1,0:T(8,128)} %get-tuple-element.114, ...), kind=kOutput, calls=%fused_computation.147 | convolution fusion | flops 8945666048 | bytes 50383872 | tf_op jit(solution)/shard_map/std,fd->stf/dot_general | solution.py:63
  658.3 18.1 %fusion.85 = (f32[1408]{0:T(1024)}, f32[2,257]{1,0:T(2,128)S(1)}, f32[2,257,1408]{2,1,0:T(8,128)}) fusion(f32[1408]{0:T(1024)S(1)} %get-tuple-element.71, f32[2,257,1408]{2,1,0:T(8,128)S(1)} %get-tuple-element.101, f32[2,257]{1,0:T(2,128)S(1)} %broadcast_multiply_fusion, bf16[1408,6144,1]{1,0,2:T(8,128)(2,1)} %reshape.131, ...), kind=kOutput, calls=%fused_computation.141 | convolution fusion | flops 8896589824 | bytes 29422608 | tf_op jit(solution)/shard_map/stf,df->std/dot_general | solution.py:68
  704.7 21.8 %fusion.30 = f32[2,16,88,257]{3,2,1,0:T(8,128)} fusion(f32[2,16,257,257]{2,3,1,0:T(8,128)} %fusion.58, bf16[2,257,1,16,88]{4,3,2,1,0:T(8,128)(2,1)} %get-tuple-element.102, f32[2,16,257,257]{2,3,1,0:T(8,128)} %get-tuple-element.112, f32[2,16,257]{2,1,0:T(8,128)S(1)} %copy-done.20), kind=kOutput, calls=%fused_computation.44 | convolution fusion | flops 386791424 | bytes 21283712 | tf_op jit(solution)/shard_map/shqk,skhe->sqhe/dot_general | solution.py:87
  732.3 21.0 %fusion.27 = f32[2,16,88,257]{3,2,1,0:T(8,128)} fusion(f32[2,16,257,257]{2,3,1,0:T(8,128)} %fusion.58, bf16[2,257,1,16,88]{4,3,2,1,0:T(8,128)(2,1)} %copy-done.8, f32[2,16,257,257]{2,3,1,0:T(8,128)} %get-tuple-element.112, f32[2,16,257]{2,1,0:T(8,128)S(1)} %copy-done.20), kind=kOutput, calls=%fused_computation.43 | convolution fusion | flops 386791424 | bytes 21283712 | tf_op jit(solution)/shard_map/shqk,sqhe->skhe/dot_general | solution.py:88
  821.6 191.2 %fusion.87 = (f32[48,4224]{1,0:T(8,128)}, f32[48,1408]{1,0:T(8,128)}) fusion(f32[1408,4224]{1,0:T(8,128)} %convolution_bitcast_fusion.2, f32[1408,1408]{1,0:T(8,128)} %convolution_bitcast_fusion.3), kind=kCustom, calls=%all-reduce-scatter.3 | all-reduce-scatter fusion | flops 8650753 | bytes 32801280
  1047.3 22.2 %convolution_bitcast_fusion.1 = f32[1408,6144]{1,0:T(8,128)} fusion(bf16[2,257,6144]{2,1,0:T(8,128)(2,1)} %get-tuple-element.120, f32[2,257,1408]{2,1,0:T(8,128)S(1)} %get-tuple-element.101, f32[1408]{0:T(1024)S(1)} %copy-done.38, f32[1408]{0:T(1024)S(1)} %copy-done.40, f32[2,257]{1,0:T(2,128)S(1)} %copy-done.29, f32[2,257]{1,0:T(2,128)S(1)} %broadcast_multiply_fusion), kind=kOutput, calls=%fused_computation.3 | convolution fusion | flops 8896591872 | bytes 43829264 | tf_op jit(solution)/shard_map/std,stf->df/dot_general | solution.py:67
  1069.5 206.2 %fusion.2 = f32[48,6144]{1,0:T(8,128)S(1)} fusion(f32[1408,6144]{1,0:T(8,128)} %convolution_bitcast_fusion.1), kind=kCustom, calls=%all-reduce-scatter.2 | all-reduce-scatter fusion | flops 9437185 | bytes 35783168
  1331.3 16.6 %collective-permute-done.8 = f32[28,6144]{1,0:T(8,128)} collective-permute-done((f32[28,6144]{1,0:T(8,128)}, f32[28,6144]{1,0:T(8,128)}, u32[]{:S(2)}, u32[]{:S(2)}) %collective-permute-start.8) | collective-permute-done | bytes 688160
  1347.9 19.1 %concatenate.2 = f32[172,6144]{1,0:T(8,128)} concatenate(f32[28,6144]{1,0:T(8,128)} %collective-permute-done.8, f32[48,6144]{1,0:T(8,128)} %collective-permute-done.7, f32[48,6144]{1,0:T(8,128)} %collective-permute-done.6, f32[48,6144]{1,0:T(8,128)S(1)} %fusion.2), dimensions={0} | concatenate | bytes 8454144
  1379.4 34.1 %all-reduce.19.cloned.1.call-done = (f32[4224]{0:T(1024)}, f32[6144]{0:T(1024)}, f32[8,1408]{1,0:T(8,128)}) async-done(((f32[4224]{0:T(1024)}, f32[6144]{0:T(1024)}, f32[8,1408]{1,0:T(8,128)}), (f32[4224]{0:T(1024)}, f32[6144]{0:T(1024)}, f32[8,1408]{1,0:T(8,128)})) %all-reduce.19.cloned.1.call-update) | async-done | bytes 86544
  1424.8 69.8 %all-reduce.21.cloned.1.call-done = (f32[44,4224]{1,0:T(8,128)}, f32[44,1408]{1,0:T(8,128)}, f32[44,6144]{1,0:T(8,128)}, f32[192,1408]{1,0:T(8,128)}) async-done(((f32[44,4224]{1,0:T(8,128)}, f32[44,1408]{1,0:T(8,128)}, f32[44,6144]{1,0:T(8,128)}, f32[192,1408]{1,0:T(8,128)}), (f32[44,4224]{1,0:T(8,128)}, f32[44,1408]{1,0:T(8,128)}, f32[44,6144]{1,0:T(8,128)}, ...) | async-done | bytes 3153936 | tf_op jit(solution)/shard_map/psum | solution.py:118
  (235 shorter events, 343.3 us)
Async XLA Ops:
  7.2 163.2 %copy-start = (bf16[2,257,1408]{2,0,1:T(2,128)(2,1)S(1)}, bf16[2,257,1408]{2,0,1:T(2,128)(2,1)}, u32[]{:S(2)}) copy-start(bf16[2,257,1408]{2,0,1:T(2,128)(2,1)} %param.9) | copy-start | bytes 4342276
  7.2 164.1 %all-gather.23.cloned.1.call-start = ((), (), s32[]{:S(2)}) async-start(), calls=%async_computation.5 | async-start | bytes 4460544 | tf_op jit(solution)/shard_map/all_gather | solution.py:107
  9.1 168.3 %all-gather.21.cloned.1.call-start = ((), (), s32[]{:S(2)}) async-start(), calls=%async_computation.4 | async-start | bytes 13381632 | tf_op jit(solution)/shard_map/all_gather | solution.py:107
  11.1 260.2 %all-gather.25.cloned.1.call-start = ((), (), s32[]{:S(2)}) async-start(), calls=%async_computation.6 | async-start | bytes 19464192 | tf_op jit(solution)/shard_map/all_gather | solution.py:107
  13.3 334.5 %all-gather.17.cloned.1.call-start = ((), (), s32[]{:S(2)}) async-start(), calls=%async_computation.1 | async-start | bytes 17842176 | tf_op jit(solution)/shard_map/all_gather | solution.py:107
  14.3 405.5 %all-gather.29.cloned.1.call-start = ((), (), s32[]{:S(2)}) async-start(), calls=%async_computation.8 | async-start | bytes 4460544 | tf_op jit(solution)/shard_map/all_gather | solution.py:107
  366.1 111.9 %all-gather.31.cloned.1.call-start = ((), (), s32[]{:S(2)}) async-start(), calls=%async_computation.9 | async-start | bytes 13381632 | tf_op jit(solution)/shard_map/all_gather | solution.py:107
  368.2 189.6 %all-gather.27.cloned.1.call-start = ((), (), s32[]{:S(2)}) async-start(), calls=%async_computation.7 | async-start | bytes 19464192 | tf_op jit(solution)/shard_map/all_gather | solution.py:107
  370.4 263.3 %all-gather.19.cloned.1.call-start = ((), (), s32[]{:S(2)}) async-start(), calls=%async_computation.2 | async-start | bytes 17842176 | tf_op jit(solution)/shard_map/all_gather | solution.py:107
  372.5 997.1 %reduce-scatter.9.cloned.1.call-start = ((), (), s32[]{:S(2)}) async-start(), calls=%async_computation.3 | async-start | bytes 35684352 | tf_op jit(solution)/shard_map/reduce_scatter | solution.py:118
  419.7 993.8 %all-reduce.19.cloned.1.call-start = ((), (), s32[]{:S(2)}) async-start(), calls=%async_computation.10 | async-start | bytes 180224
  821.6 212.0 %copy-start.18 = (f32[1408]{0:T(1024)S(1)}, f32[1408]{0:T(1024)}, u32[]{:S(2)}) copy-start(f32[1408]{0:T(1024)} %get-tuple-element.69) | copy-start | bytes 16900
  1013.7 271.8 %collective-permute-start.3 = (f32[48,1408]{1,0:T(8,128)}, f32[48,1408]{1,0:T(8,128)}, u32[]{:S(2)}, u32[]{:S(2)}) collective-permute-start(f32[48,1408]{1,0:T(8,128)} %get-tuple-element.96), channel_id=1, source_target_pairs={{0,1},{1,2},{2,3},{3,4},{4,5},{5,6},{6,7},{7,8},{8,9},{9,10},{10,1... | collective-permute-start | bytes 811016
  1018.2 269.4 %collective-permute-start.4 = (f32[48,1408]{1,0:T(8,128)}, f32[48,1408]{1,0:T(8,128)}, u32[]{:S(2)}, u32[]{:S(2)}) collective-permute-start(f32[48,1408]{1,0:T(8,128)} %get-tuple-element.96), channel_id=1, source_target_pairs={{0,2},{1,3},{2,4},{3,5},{4,6},{5,7},{6,8},{7,9},{8,10},{9,11},{10,... | collective-permute-start | bytes 811016
  1023.9 289.4 %collective-permute-start = (f32[48,4224]{1,0:T(8,128)}, f32[48,4224]{1,0:T(8,128)}, u32[]{:S(2)}, u32[]{:S(2)}) collective-permute-start(f32[48,4224]{1,0:T(8,128)} %get-tuple-element.95), channel_id=1, source_target_pairs={{0,1},{1,2},{2,3},{3,4},{4,5},{5,6},{6,7},{7,8},{8,9},{9,10},{10,1... | collective-permute-start | bytes 2433032
  1025.8 287.5 %collective-permute-start.1 = (f32[48,4224]{1,0:T(8,128)}, f32[48,4224]{1,0:T(8,128)}, u32[]{:S(2)}, u32[]{:S(2)}) collective-permute-start(f32[48,4224]{1,0:T(8,128)} %get-tuple-element.95), channel_id=1, source_target_pairs={{0,2},{1,3},{2,4},{3,5},{4,6},{5,7},{6,8},{7,9},{8,10},{9,11},{10,... | collective-permute-start | bytes 2433032
  1029.1 246.7 %collective-permute-start.5 = (f32[28,1408]{1,0:T(8,128)S(1)}, f32[28,1408]{1,0:T(8,128)S(1)}, u32[]{:S(2)}, u32[]{:S(2)}) collective-permute-start(f32[28,1408]{1,0:T(8,128)S(1)} %slice.19), channel_id=1, source_target_pairs={{0,3},{1,4},{2,5},{3,6},{4,7},{5,8},{6,9},{7,10},{8,11},{9,12},{10... | collective-permute-start | bytes 473096
  1069.5 206.3 %copy-start.31 = (f32[2,257]{1,0:T(2,128)S(1)}, f32[2,257]{1,0:T(2,128)}, u32[]{:S(2)}) copy-start(f32[2,257]{1,0:T(2,128)} %copy-done.30) | copy-start | bytes 6172
  1069.5 212.0 %copy-start.3 = (bf16[2,257,1408]{2,0,1:T(2,128)(2,1)S(1)}, bf16[2,257,1408]{2,0,1:T(2,128)(2,1)}, u32[]{:S(2)}) copy-start(bf16[2,257,1408]{2,0,1:T(2,128)(2,1)} %param.9) | copy-start | bytes 4342276
  1275.8 29.5 %collective-permute-start.2 = (f32[28,4224]{1,0:T(8,128)}, f32[28,4224]{1,0:T(8,128)}, u32[]{:S(2)}, u32[]{:S(2)}) collective-permute-start(f32[28,4224]{1,0:T(8,128)} %slice.18), channel_id=1, source_target_pairs={{0,3},{1,4},{2,5},{3,6},{4,7},{5,8},{6,9},{7,10},{8,11},{9,12},{10... | collective-permute-start | bytes 1419272
  1285.5 62.4 %collective-permute-start.6 = (f32[48,6144]{1,0:T(8,128)S(1)}, f32[48,6144]{1,0:T(8,128)}, u32[]{:S(2)}, u32[]{:S(2)}) collective-permute-start(f32[48,6144]{1,0:T(8,128)S(1)} %fusion.2), channel_id=1, source_target_pairs={{0,1},{1,2},{2,3},{3,4},{4,5},{5,6},{6,7},{7,8},{8,9},{9,10},{10,1... | collective-permute-start | bytes 3538952
  1287.6 60.4 %collective-permute-start.7 = (f32[48,6144]{1,0:T(8,128)S(1)}, f32[48,6144]{1,0:T(8,128)}, u32[]{:S(2)}, u32[]{:S(2)}) collective-permute-start(f32[48,6144]{1,0:T(8,128)S(1)} %fusion.2), channel_id=1, source_target_pairs={{0,2},{1,3},{2,4},{3,5},{4,6},{5,7},{6,8},{7,9},{8,10},{9,11},{10,... | collective-permute-start | bytes 3538952
  1298.5 196.1 %all-reduce.21.cloned.1.call-start = ((), (), s32[]{:S(2)}) async-start(), calls=%async_computation.11 | async-start | bytes 6684672 | tf_op jit(solution)/shard_map/psum | solution.py:118
  1305.4 42.5 %collective-permute-start.8 = (f32[28,6144]{1,0:T(8,128)}, f32[28,6144]{1,0:T(8,128)}, u32[]{:S(2)}, u32[]{:S(2)}) collective-permute-start(f32[28,6144]{1,0:T(8,128)} %slice.20), channel_id=1, source_target_pairs={{0,3},{1,4},{2,5},{3,6},{4,7},{5,8},{6,9},{7,10},{8,11},{9,12},{10... | collective-permute-start | bytes 2064392
  (45 other events, 859.9 us)
Sparse Core Ops, SparseCore 0:
  10.9 49.9 all-gather.22
  63.9 63.1 all-gather.20
  129.9 76.7 all-gather.24
  209.3 73.0 all-gather.16
  366.3 46.0 all-gather.28
  415.2 62.8 all-gather.30
  480.8 76.8 all-gather.26
  560.6 73.0 all-gather.18
  637.7 166.4 reduce-scatter.8
  1298.6 114.7 all-reduce.18
  1416.7 77.9 all-reduce.20
where the time goes:
time: 1520 us; the launch traced here: 1510 us
  blocking collectives  584 us (38%)
  waiting for transfers between devices  294 us (19%)
  matrix products  266 us (18%)
  local copies, waits for them, and re-layouts  216 us (14%)
  other arithmetic  93.6 us (6%)
  starting transfers between devices  36.3 us (2%)
  between operations  19 us (1%)
    unnamed x3, blocking collectives  524 us
    all_gather x8, waiting for transfers between devices, full_rows(): lax.all_gather(shard.astype(jnp.bfloat16), 'fsdp', axis=0, tiled=True)  173 us
    unnamed x128, local copies, waits for them, and re-layouts  156 us
    psum x1, waiting for transfers between devices, total_rows(): lax.psum(lax.psum_scatter(full, 'fsdp', scatter_dimension=0, tiled=True),...  69.8 us
    all_gather x2, blocking collectives, gather_weights(): lax.all_gather(vec_params.astype(jnp.bfloat16), 'fsdp', axis=1, tiled=True)  51.4 us
    unnamed x21, waiting for transfers between devices  50.9 us
    unnamed x10, starting transfers between devices  35.8 us
    convert_element_type x1, other arithmetic, layer_forward(): mlp_act = gelu_exact(pre_act).astype(jnp.bfloat16)  33 us
  transfers between devices with their start and end apart: 20, of which 6 were waited for; matrix products, arithmetic and copies ran while one was open for 63% of the time, Pallas kernels for 0%

commit v1 on v0

v1 whole, which is shorter than its diff:
```python
import functools
import math

import jax
import jax.numpy as jnp
from jax import lax
from jax.experimental import pallas as pl
from jax.experimental.pallas import tpu as pltpu
from jax.sharding import PartitionSpec as P

HEADS = 16
LN_EPS = 1e-5
D = 1408
FF = 6144
SEQ = 257
HEAD = D // HEADS
SCALE = HEAD ** -0.5
QCOLS = 1536
HALF = 768
LANES = 128
F32 = jnp.float32
BF16 = jnp.bfloat16
VMEM_LIMIT = 62 * 1000 * 1000
G1, C1, BO, S1, G2, C2, B2, S2 = range(8)
Q, K, V, O = range(4)
SEQS = (2, SEQ, D)


def sds(dtype, *shape):
    return jax.ShapeDtypeStruct(shape, dtype)


MESH_ID = pl.DeviceIdType.MESH
SIDE = 4
PAIR = 2
COLOURS = range(3)
COLOUR_DIMS = ("xyz", "yzx", "zxy")
FIRST, SECOND, THIRD, LAST = range(4)
WAYS = range(PAIR)
NEAR, FAR, ADDED = 0, 2, 4
WIDE, DOWN = "wide", "down"
ANY = pl.BlockSpec(memory_space=pl.ANY)
ALL = slice(None)


def duo(m):
    return pl.ds(PAIR * m, PAIR)


def toward(m):
    return 1 - PAIR * (m % PAIR)


class Torus:
    def __init__(self):
        f = lax.axis_index("fsdp")
        self.at = {"x": lax.axis_index("rep"), "z": lax.div(f, SIDE * PAIR), "y": lax.rem(lax.div(f, PAIR), SIDE),
                   "c": lax.rem(f, PAIR)}

    def shift(self, dim, by):
        return lax.rem(self.at[dim] + (SIDE + by), SIDE)

    def device(self, **moved):
        p = {**self.at, **moved}
        return (p["x"], (p["z"] * SIDE + p["y"]) * PAIR + p["c"])

    def neighbour(self, dim, by):
        return self.device(**{dim: self.shift(dim, by)})

    def partner(self):
        return self.device(c=1 - self.at["c"])


def enter():
    me = Torus()
    barrier = pltpu.get_barrier_semaphore()
    others = [me.neighbour(d, toward(m)) for d in COLOUR_DIMS[0] for m in WAYS] + [me.partner()]
    for other in others:
        pl.semaphore_signal(barrier, device_id=other, device_id_type=MESH_ID)
    pl.semaphore_wait(barrier, len(others))


def remote(src, dst, sems, slot, device):
    return pltpu.make_async_remote_copy(src_ref=src, dst_ref=dst, send_sem=sems[0].at[slot], recv_sem=sems[1].at[slot],
                                        device_id=device, device_id_type=MESH_ID)


class Gather:
    def __init__(self, kind, src, dst, hop_send, hop_recv, push_send, push_recv, local):
        self.kind, self.src, self.dst, self.local = kind, src, dst, local
        self.hops, self.pushes = (hop_send, hop_recv), (push_send, push_recv)
        self.cols, self.cut = (256, 128) if kind == WIDE else (D, HALF)

    @staticmethod
    def semaphores():
        dma = pltpu.SemaphoreType.DMA
        return [dma((3, 3, 4))] * PAIR + [dma((3, 5))] * PAIR + [dma((3,))]

    @staticmethod
    def shape(kind):
        return (4, 4, 4, 88, QCOLS) if kind == WIDE else (4, 4, 2, 4, 3, 16, D)

    def source(self, k):
        return self.src.at[:, pl.ds(self.cols * k, self.cols)] if self.kind == WIDE else self.src.at[k]

    def piece(self, me, k, s, v, half=None):
        dims = COLOUR_DIMS[k]
        at = {**me.at, **{d: ALL for d in dims[:s]}, dims[s]: v}
        off, width = 0, self.cols
        if half is not None and s == FIRST:
            off, width = self.cut * half, (self.cut, self.cols - self.cut)[half]
        elif half is not None:
            at[dims[0]] = duo(half)
        if self.kind == WIDE:
            cols = pl.ds(pl.multiple_of(at["c"] * HALF + self.cols * k + off, 128), width)
            return self.dst.at[at["x"], at["z"], at["y"], :, cols]
        return self.dst.at[at["z"], at["y"], at["c"], at["x"], k, :, pl.ds(off, width)]

    def hop(self, k, s, m):
        me = Torus()
        dim = COLOUR_DIMS[k][s]
        by = toward(m)
        if m < FAR:
            ref = self.piece(me, k, s, me.at[dim])
        else:
            ref = self.piece(me, k, s, me.shift(dim, -by), m - FAR)
        src = self.source(k) if s == FIRST and m < FAR else ref
        return remote(src, ref, self.hops, (k, s, m), me.neighbour(dim, by))

    def push(self, k, n):
        me = Torus()
        dim = COLOUR_DIMS[k][THIRD]
        if n < FAR:
            ref = self.piece(me, k, THIRD, me.shift(dim, -toward(n)))
        elif n < ADDED:
            ref = self.piece(me, k, THIRD, me.shift(dim, FAR), n - FAR)
        else:
            ref = self.piece(me, k, THIRD, me.at[dim])
        return remote(ref, ref, self.pushes, (k, n), me.partner())

    def own(self, k):
        me = Torus()
        return pltpu.make_async_copy(self.source(k), self.piece(me, k, FIRST, me.at[COLOUR_DIMS[k][FIRST]]), self.local.at[k])

    def launch(self, s):
        for k in COLOURS:
            for m in WAYS:
                self.hop(k, s, m).start()
            if s == THIRD:
                self.push(k, ADDED).start()

    def relay(self, k, s):
        for m in WAYS:
            self.hop(k, s, m).wait_recv()
            self.hop(k, s, FAR + m).start()
            if s == THIRD:
                self.push(k, m).start()

    def settle(self, s):
        for k in COLOURS:
            for m in WAYS:
                self.hop(k, s, FAR + m).wait_recv()
                if s == THIRD:
                    self.push(k, FAR + m).start()
            if s == FIRST:
                self.own(k).wait()
        if s < THIRD:
            self.launch(s + 1)

    def begin(self):
        for k in COLOURS:
            self.own(k).start()
        self.launch(FIRST)

    def finish(self):
        for k in COLOURS:
            for s in COLOURS:
                for m in range(ADDED):
                    self.hop(k, s, m).wait_send()
            for n in range(ADDED + 1):
                self.push(k, n).wait()

    def steps(self):
        out = [self.begin]
        for s in COLOURS:
            out += [functools.partial(self.relay, k, s) for k in COLOURS] + [functools.partial(self.settle, s)]
        return out + [self.finish]


def add_into(total, *others):
    lead = total.shape[:-2]

    def body(i, carry):
        idx = []
        for n in reversed(lead):
            idx.insert(0, lax.rem(i, n))
            i = lax.div(i, n)
        value = total[tuple(idx)]
        for other in others:
            value = value + other[tuple(idx)]
        total[tuple(idx)] = value
        return carry

    lax.fori_loop(0, math.prod(lead), body, 0)


class Scatter:
    def __init__(self, kind, part, out, own, passed, relay1, in1, relay2, in2, relay3, in3, result, send, recv, load, store):
        self.kind, self.part, self.out, self.own, self.passed, self.result = kind, part, out, own, passed, result
        self.relays, self.ins = (relay1, relay2, relay3), (in1, in2, in3)
        self.sems, self.load_sem, self.store_sem = (send, recv), load, store
        self.order = "xzy" if kind == WIDE else "zyx"
        self.half = result.shape[-1] // PAIR

    @staticmethod
    def scratch(kind):
        rows, cols = Scatter.unit(kind)
        vm = lambda *shape: pltpu.VMEM(shape + (rows, cols), F32)
        dma = pltpu.SemaphoreType.DMA
        return [vm(3, 4, 4), vm(3, 2, 2, 4), vm(3, 2, 2, 4), vm(3, 2, 4, 4), vm(3, 2, 2), vm(3, 2, 4),
                pltpu.VMEM((3, 2, rows, cols // PAIR), F32), vm(3, 2), vm(4, 3),
                dma((3, 4, 6)), dma((3, 4, 6)), dma((3, 3)), dma]

    @staticmethod
    def unit(kind):
        return (88, 256) if kind == WIDE else (32, HALF)

    def rest(self, k):
        return [d for d in self.order if d != COLOUR_DIMS[k][FIRST]]

    def terms(self, k, s, v, half=None):
        if s == FIRST:
            at = {d: ALL for d in self.order}
            at[COLOUR_DIMS[k][FIRST]] = v
            if half is not None:
                at[self.rest(k)[0]] = duo(half)
            lead = tuple(at[d] for d in self.order)
            return self.part.at[lead + ((ALL, pl.ds(256 * k, 256)) if self.kind == WIDE else (k,))]
        if s == SECOND:
            other = ALL if half is None else duo(half)
            return self.own.at[(k, v, other) if self.rest(k)[0] == COLOUR_DIMS[k][SECOND] else (k, other, v)]
        return self.ins[SECOND].at[(k, 0, v) + (() if half is None else (ALL, self.cols(half)))]

    def cols(self, m):
        return pl.ds(self.half * m, self.half)

    def landing(self, k, s, m, half):
        return self.ins[s].at[(k, m) + ((ALL, self.cols(half)) if s == THIRD else (duo(half),))]

    def hop(self, k, s, m):
        me = Torus()
        way, by = m % PAIR, toward(m)
        dim = "x" if s == LAST else COLOUR_DIMS[k][s]
        if s == LAST:
            src = self.result.at[me.at["x"], k] if m < FAR else self.result.at[me.shift("x", -by), k, :, self.cols(way)]
            dst = src
        elif m < FAR:
            src, dst = self.terms(k, s, me.shift(dim, FAR), way), self.relays[s].at[k, way]
        elif m < ADDED:
            src, dst = self.terms(k, s, me.shift(dim, by), 1 - way), self.landing(k, s, way, 1 - way)
        else:
            src, dst = (self.passed if s == FIRST else self.relays[s]).at[k, way], self.landing(k, s, way, way)
        return remote(src, dst, self.sems, (k, s, m), me.neighbour(dim, by))

    def load(self, k, m):
        me = Torus()
        dim = COLOUR_DIMS[k][FIRST]
        if m in WAYS:
            src, dst = self.terms(k, FIRST, me.shift(dim, toward(m)), m), self.passed.at[k, m]
        else:
            src, dst = self.terms(k, FIRST, me.at[dim]), self.own.at[k]
        return pltpu.make_async_copy(src, dst, self.load_sem.at[k, m])

    def begin(self):
        for base in (NEAR, FAR):
            for k in COLOURS:
                for m in WAYS:
                    self.hop(k, FIRST, base + m).start()
        for m in COLOURS:
            for k in COLOURS:
                self.load(k, m).start()

    def relay(self, k, s):
        me = Torus()
        for m in WAYS:
            self.hop(k, s, m).wait_recv()
            mine = self.relays[s].at[k, m]
            if s == FIRST:
                self.load(k, m).wait()
                add_into(self.passed.at[k, m], mine)
            else:
                terms = self.terms(k, s, me.shift(COLOUR_DIMS[k][s], toward(m)), m)
                if s == SECOND:
                    add_into(mine, terms)
                else:
                    mine[...] += terms[...]
            self.hop(k, s, ADDED + m).start()

    def settle(self, k, s):
        me = Torus()
        if s == FIRST:
            self.load(k, FAR).wait()
        for m in WAYS:
            self.hop(k, s, FAR + m).wait_recv()
            self.hop(k, s, ADDED + m).wait_recv()
        plus, minus = (self.ins[s].at[k, m] for m in WAYS)
        if s == FIRST:
            add_into(self.own.at[k], plus, minus)
        elif s == SECOND:
            add_into(plus, minus, self.terms(k, s, me.at[COLOUR_DIMS[k][s]]))
        else:
            mine = self.terms(k, s, me.at[COLOUR_DIMS[k][s]])
            self.result[me.at["x"], k] = mine[...] + plus[...] + minus[...]
        for base in (NEAR,) if s == THIRD else (NEAR, FAR):
            for m in WAYS:
                self.hop(k, s + 1, base + m).start()

    def spread(self, k):
        for m in WAYS:
            self.hop(k, LAST, m).wait_recv()
            self.hop(k, LAST, FAR + m).start()

    def finish(self):
        for k in COLOURS:
            for m in WAYS:
                self.hop(k, LAST, FAR + m).wait_recv()
        store = pltpu.make_async_copy(self.result, self.out, self.store_sem)
        store.start()
        for k in COLOURS:
            for s in range(SIDE):
                for m in range(ADDED if s == LAST else ADDED + PAIR):
                    self.hop(k, s, m).wait_send()
        store.wait()

    def steps(self):
        out = [self.begin]
        for s in COLOURS:
            for what in (self.relay, self.settle):
                out += [functools.partial(what, k, s) for k in COLOURS]
        return out + [functools.partial(self.spread, k) for k in COLOURS] + [self.finish]


def comm_params(collective_id):
    return pltpu.CompilerParams(collective_id=collective_id, has_side_effects=True, vmem_limit_bytes=VMEM_LIMIT)


def torus_gather(kind, piece, collective_id):
    def kernel(*refs):
        enter()
        for step in Gather(kind, *refs).steps():
            step()

    return pl.pallas_call(
        kernel, out_shape=sds(BF16, *Gather.shape(kind)), in_specs=[ANY], out_specs=ANY,
        scratch_shapes=Gather.semaphores(), compiler_params=comm_params(collective_id), name="gather_" + kind)(piece)


def torus_scatter(kind, part, collective_id):
    def kernel(*refs):
        enter()
        for step in Scatter(kind, *refs).steps():
            step()

    return pl.pallas_call(
        kernel, out_shape=sds(F32, 4, 3, *Scatter.unit(kind)), in_specs=[ANY], out_specs=ANY,
        scratch_shapes=Scatter.scratch(kind), compiler_params=comm_params(collective_id), name="scatter_" + kind)(part)


SEQ_PAIR = range(SEQS[0])
NT = (((1,), (1,)), ((), ()))
TN = (((0,), (0,)), ((), ()))


def dot(a, b):
    return jnp.dot(a, b, preferred_element_type=F32)


def dot_nt(a, b):
    return lax.dot_general(a, b, NT, preferred_element_type=F32)


def dot_tn(a, b):
    return lax.dot_general(a, b, TN, preferred_element_type=F32)


def zeros_but(n, axis, value):
    return tuple(value if i == axis else 0 for i in range(n))


def whole(*shape):
    return pl.BlockSpec(shape, lambda *_: (0,) * len(shape))


def along(axis, *block, index=lambda j: j):
    return pl.BlockSpec(block, lambda j: zeros_but(len(block), axis, index(j)))


def compute_params():
    return pltpu.CompilerParams(dimension_semantics=("arbitrary",), vmem_limit_bytes=VMEM_LIMIT)


def work(flops):
    return pl.CostEstimate(flops=flops, bytes_accessed=D * FF, transcendentals=0)


def row(vec, i):
    return vec[i:i + 1]


def row_mean(t):
    return jnp.mean(t, axis=-1, keepdims=True)


def norm_stats(t):
    centered = t - row_mean(t)
    rstd = lax.rsqrt(row_mean(centered * centered) + LN_EPS)
    return centered * rstd, rstd


def norm_back(xhat, rstd, g):
    return rstd * (g - row_mean(g) - xhat * row_mean(g * xhat))


def col_sum(t):
    return jnp.sum(t, axis=0, keepdims=True)


def at_step(j):
    return pl.when(pl.program_id(0) == j)


def accumulate(ref, value):
    @at_step(0)
    def _():
        ref[...] = value

    @pl.when(pl.program_id(0) > 0)
    def _():
        ref[...] += value


def qkv_kernel(x, w, b, vec, qkv, h1):
    @at_step(0)
    def _():
        for s in SEQ_PAIR:
            xhat, _ = norm_stats(x[s].astype(F32))
            h1[s] = (xhat * row(vec, G1) + row(vec, C1)).astype(BF16)

    for s in SEQ_PAIR:
        qkv[0, s] = (dot(h1[s], w[0]) + b[0]).astype(BF16)


def qkv_call(x, w_attn, b_qkv, vec):
    return pl.pallas_call(
        qkv_kernel, grid=(O,), out_shape=(sds(BF16, O, *SEQS), sds(BF16, *SEQS)),
        in_specs=[whole(*SEQS), along(0, 1, D, D), along(0, 1, 1, D), whole(8, D)],
        out_specs=(along(0, 1, *SEQS), whole(*SEQS)),
        compiler_params=compute_params(), cost_estimate=work(SEQ * D * D), name="ln1_qkv",
    )(x, w_attn, b_qkv, vec)


def window(h):
    start = h * HEAD // LANES * LANES
    stop = min(D, -(-(h + 1) * HEAD // LANES) * LANES)
    lane = lax.broadcasted_iota(jnp.int32, (1, stop - start), 1) + (start - h * HEAD)
    return slice(start, stop), (lane >= 0) & (lane < HEAD)


def only(mask, t):
    return jnp.where(mask, t, jnp.zeros_like(t))


def softmax(scores):
    e = jnp.exp(scores - jnp.max(scores, axis=-1, keepdims=True))
    return e * (1.0 / jnp.sum(e, axis=-1, keepdims=True))


def attn_kernel(qkv, x, w_out, vec, o, att, h2, acc):
    acc[...] = jnp.zeros_like(acc)
    for h in range(HEADS):
        lanes, mask = window(h)
        k = only(mask, qkv[K, 0, :, lanes])
        v = only(mask, qkv[V, 0, :, lanes])
        probs = softmax(dot_nt(qkv[Q, 0, :, lanes], k) * SCALE).astype(BF16)
        acc[:, lanes] += dot(probs, v)
    heads = acc[...].astype(BF16)
    o[0] = heads
    a = dot(heads, w_out[0]) + row(vec, BO)
    att[0] = a
    xhat, _ = norm_stats(x[0].astype(F32) + row(vec, S1) * a)
    h2[0] = (xhat * row(vec, G2) + row(vec, C2)).astype(BF16)


def one_seq():
    return along(0, 1, SEQ, D)


def w_out_block():
    return along(0, 1, D, D, index=lambda j: O)


def attn_call(qkv, x, w_attn, vec):
    return pl.pallas_call(
        attn_kernel, grid=SEQS[:1], out_shape=(sds(BF16, *SEQS), sds(F32, *SEQS), sds(BF16, *SEQS)),
        in_specs=[along(1, O, 1, SEQ, D), one_seq(), w_out_block(), whole(8, D)],
        out_specs=(one_seq(),) * O, scratch_shapes=[pltpu.VMEM((SEQ, D), F32)],
        compiler_params=compute_params(), cost_estimate=work(SEQ * D * D), name="attn_wo_ln2",
    )(qkv, x, w_attn, vec)


def mlp_kernel(h2, gz, w_up, b_up, w_down, vec, act, d_pre, db_up, mlp, d_h2, dm_halves, dm):
    @at_step(0)
    def _():
        mlp[...] = jnp.zeros_like(mlp)
        d_h2[...] = jnp.zeros_like(d_h2)
        for s in SEQ_PAIR:
            d = (gz[s].astype(F32) * row(vec, S2)).astype(BF16)
            dm[s] = d
            dm_halves[0, s] = d[:, :HALF]
            dm_halves[1, s] = d[:, D - HALF:]

    db = jnp.zeros((1, HALF), F32)
    for s in SEQ_PAIR:
        u = dot(h2[s], w_up[0]) + b_up[0]
        phi = 0.5 * (1.0 + lax.erf(u * math.sqrt(0.5)))
        a = (u * phi).astype(BF16)
        act[s] = a
        slope = phi + u * (jnp.exp(-0.5 * u * u) * (math.sqrt(0.5 / math.pi)))
        mlp[s] += dot(a, w_down[...])
        d = dot_nt(dm[s], w_down[...]) * slope
        db = db + col_sum(d)
        d = d.astype(BF16)
        d_pre[0, 0, s] = d
        d_h2[s] += dot_nt(d, w_up[0])
    db_up[0] = db


def mlp_call(h2, gz, w_up, b_up, w_down, vec):
    n = FF // HALF
    tiled = along(2, 2, SEQ, HALF)
    bias = along(0, 1, 1, HALF)
    halved = pl.BlockSpec((1, 1, 2, SEQ, HALF), lambda j: (j % PAIR, j // PAIR, 0, 0, 0))
    return pl.pallas_call(
        mlp_kernel, grid=(n,),
        out_shape=(sds(BF16, 2, SEQ, FF), sds(BF16, 2, 4, 2, SEQ, HALF), sds(F32, n, 1, HALF), sds(F32, *SEQS),
                   sds(F32, *SEQS), sds(BF16, 2, 2, SEQ, HALF)),
        in_specs=[whole(*SEQS), whole(*SEQS), pl.BlockSpec((1, D, HALF), lambda j: (j // PAIR, 0, j % PAIR)), bias,
                  along(0, HALF, D), whole(8, D)],
        out_specs=(tiled, halved, bias, whole(*SEQS), whole(*SEQS), whole(2, 2, SEQ, HALF)),
        scratch_shapes=[pltpu.VMEM(SEQS, BF16)],
        compiler_params=compute_params(), cost_estimate=work(SEQ * D * FF), name="mlp",
    )(h2, gz, w_up, b_up.reshape(n, 1, HALF), w_down, vec)


def halves_of(t):
    return t[:, :HALF], jnp.concatenate([t[:, HALF:], jnp.zeros((SEQ, QCOLS - D), t.dtype)], axis=1)


def mid_kernel(mlp, d_h2, att, x, gz, vec, w_out, z, g_res, d_att, d_o, sums):
    a = att[0]
    y = x[0].astype(F32) + row(vec, S1) * a
    m = mlp[0] + row(vec, B2)
    g = gz[0].astype(F32)
    z[0] = (y + row(vec, S2) * m).astype(BF16)
    xhat, rstd = norm_stats(y)
    dh = d_h2[0]
    gr = g + norm_back(xhat, rstd, dh * row(vec, G2))
    g_res[0] = gr
    da = gr * row(vec, S1)
    terms = (da, gr * a, dh * xhat, dh, g * row(vec, S2), g * m)
    accumulate(sums, jnp.concatenate([jnp.zeros((BO, D), F32)] + [col_sum(t) for t in terms], axis=0))
    da = da.astype(BF16)
    for i, t in enumerate(halves_of(da)):
        d_att[i, 0] = t
    d_o[0] = dot_nt(da, w_out[0]).astype(BF16)


def mid_call(mlp, d_h2, att, x, gz, vec, w_attn):
    return pl.pallas_call(
        mid_kernel, grid=SEQS[:1],
        out_shape=(sds(BF16, *SEQS), sds(F32, *SEQS), sds(BF16, 2, 2, SEQ, HALF), sds(BF16, *SEQS), sds(F32, 8, D)),
        in_specs=[one_seq()] * len("mdaxg") + [whole(8, D), w_out_block()],
        out_specs=(one_seq(), one_seq(), along(1, 2, 1, SEQ, HALF), one_seq(), whole(8, D)),
        compiler_params=compute_params(), cost_estimate=work(SEQ * D * D), name="ln2_back_wo",
    )(mlp, d_h2, att, x, gz, vec, w_attn)


def attn_back_kernel(qkv, d_o, d_qkv, db, acc):
    acc[...] = jnp.zeros_like(acc)
    for h in range(HEADS):
        lanes, mask = window(h)
        q, k, v = (only(mask, qkv[i, 0, :, lanes]) for i in (Q, K, V))
        do = only(mask, d_o[0, :, lanes])
        probs = softmax(dot_nt(q, k) * SCALE)
        acc[V, :, lanes] += dot_tn(probs.astype(BF16), do)
        dp = dot_nt(do, v)
        ds = probs * (dp - jnp.sum(dp * probs, axis=-1, keepdims=True))
        ds = (ds * SCALE).astype(BF16)
        acc[Q, :, lanes] += dot(ds, k)
        acc[K, :, lanes] += dot_tn(ds, q)
    accumulate(db, jnp.concatenate([col_sum(acc[i]) for i in (Q, K, V)], axis=0))
    for n in (Q, K, V):
        for i, t in enumerate(halves_of(acc[n].astype(BF16))):
            d_qkv[i, n, 0] = t


def attn_back_call(qkv, d_o):
    return pl.pallas_call(
        attn_back_kernel, grid=SEQS[:1], out_shape=(sds(BF16, 2, O, 2, SEQ, HALF), sds(F32, O, D)),
        in_specs=[along(1, O, 1, SEQ, D), one_seq()], out_specs=(along(2, 2, O, 1, SEQ, HALF), whole(O, D)),
        scratch_shapes=[pltpu.VMEM((O, SEQ, D), F32)],
        compiler_params=compute_params(), cost_estimate=work(SEQ * D * D), name="attn_back",
    )(qkv, d_o)


def in_back_kernel(d_qkv, w, x, g_res, vec, dx, sums, acc):
    rest = D - HALF
    for s in SEQ_PAIR:
        part = dot_nt(d_qkv[0, 0, s], w[0, :, :HALF]) + dot_nt(d_qkv[1, 0, s, :, :rest], w[0, :, HALF:])
        accumulate(acc.at[s], part)

    @at_step(V)
    def _():
        total = jnp.zeros((BO, D), F32)
        for s in SEQ_PAIR:
            xhat, rstd = norm_stats(x[s].astype(F32))
            dh = acc[s]
            total = total + jnp.concatenate([col_sum(dh * xhat), col_sum(dh)], axis=0)
            dx[s] = (g_res[s] + norm_back(xhat, rstd, dh * row(vec, G1))).astype(BF16)
        sums[...] = total


def in_back_call(d_qkv, w_attn, x, g_res, vec):
    return pl.pallas_call(
        in_back_kernel, grid=(O,), out_shape=(sds(BF16, *SEQS), sds(F32, BO, D)),
        in_specs=[along(1, 2, 1, 2, SEQ, HALF), along(0, 1, D, D), whole(*SEQS), whole(*SEQS), whole(8, D)],
        out_specs=(whole(*SEQS), whole(BO, D)), scratch_shapes=[pltpu.VMEM(SEQS, F32)],
        compiler_params=compute_params(), cost_estimate=work(SEQ * D * D), name="ln1_back",
    )(d_qkv, w_attn, x, g_res, vec)


BODY = SEQ - 1
ROWS = 4 * SEQ + 12


def stack_tokens(dst, seqs):
    for i, seq in enumerate(seqs):
        dst[pl.ds(BODY * i, BODY)] = seq[:BODY]
    last = [seq[BODY:].astype(F32) for seq in seqs]
    tail = jnp.concatenate(last + [jnp.zeros((ROWS - len(seqs) * SEQ, dst.shape[1]), F32)], axis=0)
    dst[pl.ds(len(seqs) * BODY, ROWS - len(seqs) * BODY)] = tail.astype(BF16)


def grad_kernel(new_a, new_b, a_own, a_pair, b_own, b_pair, *rest):
    extra, (out, a_rows, b_rows) = rest[:-3], rest[-3:]
    j = pl.program_id(0)

    def fill(dst, own, pair):
        lead = (0,) * (len(own.shape) - len(SEQS))
        stack_tokens(dst, [ref[lead + (s,)] for ref in (own, pair) for s in SEQ_PAIR])

    pl.when(new_a(j))(lambda: fill(a_rows, a_own, a_pair))
    pl.when(new_b(j))(lambda: fill(b_rows, b_own, b_pair))
    value = dot_tn(a_rows[...], b_rows[...])
    out[...] = value.reshape(out.shape)
    if extra:
        @at_step(0)
        def _():
            out[0, :, HALF - LANES:] += extra[0][...]


def grad_call(name, grid, a, a_spec, b, b_spec, new_a, new_b, out_shape, out_spec, extra=()):
    return pl.pallas_call(
        functools.partial(grad_kernel, new_a, new_b), grid=(grid,), out_shape=out_shape,
        in_specs=[a_spec] * PAIR + [b_spec] * PAIR + [whole(*e.shape) for e in extra], out_specs=out_spec,
        scratch_shapes=[pltpu.VMEM((ROWS, a_spec.block_shape[-1]), BF16), pltpu.VMEM((ROWS, HALF), BF16)],
        compiler_params=compute_params(), cost_estimate=work(SEQ * D * FF), name=name,
    )(*a, *b, *extra)


def wide_grads(name, a, b, new_a, a_index, extra=()):
    return grad_call(name, SIDE, a, along(0, 1, *SEQS, index=a_index), b, along(0, 1, 2, SEQ, HALF), new_a,
                     lambda j: j >= 0, sds(F32, SIDE, D, HALF), along(0, 1, D, HALF), extra)


def down_grads(a, b):
    return grad_call("dw_down", FF // HALF, a, along(2, 2, SEQ, HALF), b, whole(2, SEQ, HALF), lambda j: j >= 0,
                     lambda j: j == 0, sds(F32, FF, HALF), along(0, HALF, HALF))


OWN = 44
CHIP = OWN * PAIR
BQ, BU, VEC = 3 * D // 32, 3 * D // 32 + FF // 32, 3 * D // 32 + FF // 32 + 8 * OWN
DEVICES = 32


def pair_swap(a):
    return lax.ppermute(a, "fsdp", [(i, i ^ 1) for i in range(DEVICES)])


def by_core(first, a, b):
    return jnp.where(first, a, b), jnp.where(first, b, a)


def my_pieces(shards, first):
    w_qkv, b_qkv, w_out, w_up, b_up, w_down, vec_params = shards
    x = lax.axis_index("rep")
    small = jnp.concatenate([b_qkv, b_up, vec_params.reshape(-1)])
    small = jnp.pad(small, (0, OWN * LANES - VEC)).reshape(OWN, LANES)
    attn = lax.dynamic_slice_in_dim(jnp.concatenate([w_qkv, w_out], axis=1), x * D, D, 1)
    attn = jnp.concatenate([attn, small], axis=1)
    up = lax.dynamic_slice_in_dim(w_up, x * QCOLS, QCOLS, 1)
    wide = jnp.stack([attn, up]).astype(BF16)
    mine, theirs = by_core(first, wide[..., :HALF], wide[..., HALF:])
    theirs = pair_swap(theirs)
    piece = jnp.concatenate(by_core(first, mine, theirs), axis=1)
    down = lax.dynamic_slice_in_dim(w_down, x * 48, 48, 0).astype(BF16).reshape(3, 16, D)
    return piece[0], piece[1], down


def small_params(w_attn):
    small = w_attn[0, :, D:].astype(F32).reshape(DEVICES, OWN * LANES)
    vec = small[:, BU:VEC].reshape(DEVICES, 8, OWN).transpose(1, 0, 2).reshape(8, D)
    return small[:, :BQ].reshape(O, 1, D), small[:, BQ:BU].reshape(FF), vec


def small_grads(db_qkv, db_up, sums, core):
    vec = sums.reshape(8, DEVICES, OWN).transpose(1, 0, 2).reshape(DEVICES, VEC - BU)
    small = jnp.concatenate([db_qkv.reshape(DEVICES, BQ), db_up.reshape(DEVICES, BU - BQ), vec], axis=1)
    small = (small + pair_swap(small)) * core.astype(F32)
    return jnp.pad(small, ((0, 0), (0, OWN * LANES - VEC))).reshape(D, LANES)


def final_rows(total, first):
    keep, give = by_core(first, total[:, :, :OWN], total[:, :, OWN:])
    pair = jnp.stack(by_core(first, keep, pair_swap(give)), axis=1)
    return pair.transpose(3, 0, 1, 2, 4).reshape(OWN, SIDE, QCOLS)


def final_down(down, first):
    keep, give = by_core(first, down[:FF // DEVICES], down[FF // DEVICES:])
    left, right = by_core(first, keep, pair_swap(give))
    return jnp.concatenate([left, right[:, 2 * HALF - D:]], axis=1)


def device_step(x, gz, *shards):
    core = lax.rem(lax.axis_index("fsdp"), PAIR)
    first = core == 0
    attn, up, down = my_pieces(shards, first)
    w_attn = torus_gather(WIDE, attn, 0).reshape(SIDE, D, QCOLS)
    w_up = torus_gather(WIDE, up, 1).reshape(SIDE, D, QCOLS)
    w_down = torus_gather(DOWN, down, 2).reshape(FF, D)
    b_qkv, b_up, vec = small_params(w_attn)
    pick = lambda a, i: lax.dynamic_index_in_dim(a, i, 0, keepdims=False)
    both = lambda a: (a, pair_swap(a))
    halves = lambda a: (pick(a, core), pair_swap(pick(a, 1 - core)))

    qkv, h1 = qkv_call(x, w_attn, b_qkv, vec)
    o, att, h2 = attn_call(qkv, x, w_attn, vec)
    act, d_pre, db_up, mlp, d_h2, d_mlp = mlp_call(h2, gz, w_up, b_up, w_down, vec)
    part_down = down_grads(both(act), halves(d_mlp))
    z, g_res, d_att, d_o, sums = mid_call(mlp, d_h2, att, x, gz, vec, w_attn)
    part_up = wide_grads("dw_up", both(h2[None]), halves(d_pre), lambda j: j == 0, lambda j: 0)
    d_qkv, db_qkv = attn_back_call(qkv, d_o)
    dx, in_sums = in_back_call(d_qkv, w_attn, x, g_res, vec)
    small = small_grads(db_qkv, db_up, jnp.concatenate([in_sums, sums[BO:]], axis=0), core)
    d_cols = jnp.concatenate([d_qkv, d_att[:, None]], axis=1)
    part_attn = wide_grads("dw_attn", both(jnp.stack([h1, o])), halves(d_cols), lambda j: (j == Q) | (j == O),
                           lambda j: j // O, (small,))

    down = torus_scatter(DOWN, part_down.reshape(4, 4, 4, 3, 32, HALF), 3).reshape(FF // 16, HALF)
    up = torus_scatter(WIDE, part_up.reshape(4, 4, 4, CHIP, HALF), 4)
    attn = torus_scatter(WIDE, part_attn.reshape(4, 4, 4, CHIP, HALF), 5)
    g_up = final_rows(up, first).reshape(OWN, FF)
    attn = final_rows(attn, first)
    small = attn[:, 0, D:].reshape(OWN * LANES)
    return (z, dx, attn[:, :O, :D].reshape(OWN, O * D), small[:BQ], attn[:, O, :D], g_up, small[BQ:BU],
            final_down(down, first), small[BU:VEC].reshape(8, OWN))


def solution(mesh):
    batch = P(("rep", "fsdp"), None, None)
    rows, flat, cols = P("fsdp", None), P("fsdp"), P(None, "fsdp")
    shards = (rows, flat, rows, rows, flat, rows, cols)
    return jax.shard_map(device_step, mesh=mesh, in_specs=(batch, batch) + shards,
                         out_specs=(batch, batch) + shards, check_vma=False)
```

time: 1520 us -> 721 us (0.47)
  Pallas kernels: 0 us -> 597 us
  blocking collectives: 584 us -> 0 us
  waiting for transfers between devices: 294 us -> 0.03 us
  matrix products: 266 us -> 0 us
  local copies, waits for them, and re-layouts: 216 us -> 80.3 us
  other arithmetic: 93.6 us -> 22.7 us
  starting transfers between devices: 36.3 us -> 15.1 us
  between operations: 19 us -> 1.59 us
    pallas_call x0 -> x15, Pallas kernels: none -> 597 us  [the longest x3 251 us: torus_scatter(): pl.pallas_call(kernel, out_shape=sds(F32, 4, 3, *Scatter.unit(kind)), in_...]
    unnamed x3 -> x0, blocking collectives: 524 us -> none
    dot_general x18 -> x0, matrix products: 266 us -> none  [the longest x1 24.7 us: layer_backward(): jnp.einsum('std,fd->stf', d_mlp_bf, w_down, preferred_element_type=jnp.fl...]
    all_gather x8 -> x0, waiting for transfers between devices: 173 us -> none  [full_rows(): lax.all_gather(shard.astype(jnp.bfloat16), 'fsdp', axis=0, tiled=True)]
    unnamed x128 -> x43, local copies, waits for them, and re-layouts: 156 us -> 10.9 us
    psum x1 -> x0, waiting for transfers between devices: 69.8 us -> none  [total_rows(): lax.psum(lax.psum_scatter(full, 'fsdp', scatter_dimension=0, tiled=True),...]
    all_gather x2 -> x0, blocking collectives: 51.4 us -> none  [gather_weights(): lax.all_gather(vec_params.astype(jnp.bfloat16), 'fsdp', axis=1, tiled=True)]
    unnamed x21 -> x0, waiting for transfers between devices: 50.9 us -> none
  transfers between devices with their start and end apart: 20 -> 11, of which waited for: 6 -> 0; matrix products, arithmetic and copies ran while one was open for 63% -> 11% of each run, Pallas kernels for 0% -> 58%
where the time goes in v1:
time: 721 us; the launch traced here: 717 us
  Pallas kernels  597 us (83%)
  local copies, waits for them, and re-layouts  80.3 us (11%)
  other arithmetic  22.7 us (3%)
  starting transfers between devices  15.1 us (2%)
    pallas_call x3, Pallas kernels, torus_scatter(): pl.pallas_call(kernel, out_shape=sds(F32, 4, 3, *Scatter.unit(kind)), in_...  251 us
    pallas_call x3, Pallas kernels, torus_gather(): pl.pallas_call(kernel, out_shape=sds(BF16, *Gather.shape(kind)), in_specs...  146 us
    pallas_call x3, Pallas kernels, grad_call(): pl.pallas_call(functools.partial(grad_kernel, new_a, new_b), grid=(grid,)...  55.7 us
    pallas_call x1, Pallas kernels, mlp_call(): pl.pallas_call(mlp_kernel, grid=(n,), out_shape=(sds(BF16, 2, SEQ, FF), s...  54 us
    pallas_call x1, Pallas kernels, attn_back_call(): pl.pallas_call(attn_back_kernel, grid=SEQS[:1], out_shape=(sds(BF16, 2, O...  29.9 us
    ppermute x6, local copies, waits for them, and re-layouts, pair_swap(): return lax.ppermute(a, 'fsdp', [(i, i ^ 1) for i in range(DEVICES)])  23.3 us
    pallas_call x1, Pallas kernels, in_back_call(): pl.pallas_call(in_back_kernel, grid=(O,), out_shape=(sds(BF16, *SEQS), sd...  17.4 us
    pallas_call x1, Pallas kernels, attn_call(): pl.pallas_call(attn_kernel, grid=SEQS[:1], out_shape=(sds(BF16, *SEQS), s...  16.4 us
  transfers between devices with their start and end apart: 11, of which 0 were waited for; matrix products, arithmetic and copies ran while one was open for 11% of the time, Pallas kernels for 58%

profile of v1, /device:TPU:1, one launch (start us, length us, event | category | flops | bytes accessed | tf_op | source)
XLA Modules:
  0.0 717.2 jit_solution(16652551688771352400)
XLA Ops:
  8.5 51.4 %gather_down.1 = bf16[4,4,2,4,3,16,1408]{6,5,4,3,2,1,0:T(8,128)(2,1)} custom-call(bf16[3,16,1408]{2,1,0:T(8,128)(2,1)} %bitcast.77), custom_call_target="tpu_custom_call" | custom-call | tf_op jit(solution)/shard_map/gather_down/pallas_call | solution.py:353
  62.0 47.0 %gather_wide.2 = bf16[4,4,4,88,1536]{4,3,2,1,0:T(8,128)(2,1)} custom-call(bf16[88,768]{1,0:T(8,128)(2,1)} %get-tuple-element.100.refs_0_), custom_call_target="tpu_custom_call" | custom-call | tf_op jit(solution)/shard_map/gather_wide/pallas_call | solution.py:353
  112.1 13.7 %ln1_qkv.1 = (bf16[3,2,257,1408]{3,2,1,0:T(8,128)(2,1)}, bf16[2,257,1408]{2,1,0:T(8,128)(2,1)}) custom-call(bf16[2,257,1408]{2,1,0:T(8,128)(2,1)} %copy.67.x, bf16[4,1408,1536]{2,1,0:T(8,128)(2,1)} %bitcast.58, f32[3,1,1408]{2,1,0:T(1,128)} %reshape.94.b, f32[8,1408]{1,0:T(8,128)} %reshape.96.vec), custom_call_target="tpu_custom_call" | custom-call | flops 509493248 | bytes 8650752 | tf_op jit(solution)/shard_map/ln1_qkv/pallas_call | solution.py:454
  125.7 16.4 %attn_wo_ln2.1 = (bf16[2,257,1408]{2,1,0:T(8,128)(2,1)}, f32[2,257,1408]{2,1,0:T(8,128)}, bf16[2,257,1408]{2,1,0:T(8,128)(2,1)}) custom-call(bf16[3,2,257,1408]{3,2,1,0:T(8,128)(2,1)} %get-tuple-element.29.qkv, bf16[2,257,1408]{2,1,0:T(8,128)(2,1)} %copy.67.x, bf16[4,1408,1536]{2,1,0:T(8,128)(2,1)} %bitcast.59, f32[8,1408]{1,0:T(8,128)} %reshape.96.vec), custom_call_target="tpu_custom_call" | custom-call | flops 509493248 | bytes 8650752 | tf_op jit(solution)/shard_map/attn_wo_ln2/pallas_call | solution.py:503
  142.9 48.0 %gather_wide.3 = bf16[4,4,4,88,1536]{4,3,2,1,0:T(8,128)(2,1)} custom-call(bf16[88,768]{1,0:T(8,128)(2,1)} %get-tuple-element.99.refs_0_), custom_call_target="tpu_custom_call" | custom-call | tf_op jit(solution)/shard_map/gather_wide/pallas_call | solution.py:353
  190.9 54.0 %mlp.1 = (bf16[2,257,6144]{2,1,0:T(8,128)(2,1)}, bf16[2,4,2,257,768]{4,3,2,1,0:T(8,128)(2,1)}, f32[8,1,768]{2,1,0:T(1,128)}, f32[2,257,1408]{2,1,0:T(8,128)}, f3...) custom-call(bf16[2,257,1408]{2,1,0:T(8,128)(2,1)} %get-tuple-element.30.h2, bf16[2,257,1408]{2,1,0:T(8,128)(2,1)} %copy.69.gz, ...), custom_call_target="tpu_custom_call" | custom-call | flops 2223243264 | bytes 8650752 | tf_op jit(solution)/shard_map/mlp/pallas_call | solution.py:543
  245.0 10.3 %copy.90 = bf16[2,257,6144]{2,0,1:T(2,128)(2,1)} copy(bf16[2,257,6144]{2,1,0:T(8,128)(2,1)} %get-tuple-element.47.a_own) | data formatting | bytes 12632064 | tf_op jit(solution)/shard_map/mlp/pallas_call | solution.py:543
  255.4 12.9 %ln2_back_wo.1 = (bf16[2,257,1408]{2,1,0:T(8,128)(2,1)}, f32[2,257,1408]{2,1,0:T(8,128)}, bf16[2,2,257,768]{3,2,1,0:T(8,128)(2,1)}, bf16[2,257,1408]{2,1,0:T(8,128)(2,1)}, f32[8,1408]{1,0:T(8,128)}) custom-call(f32[2,257,1408]{2,1,0:T(8,128)} %get-tuple-element.31.mlp, f32[2,257,1408]{2,1,0:T(8,128)} %get-tuple-element.32.d_h2, ...), custom_call_target="tpu_custom_call" | custom-call | flops 509493248 | bytes 8650752 | tf_op jit(solution)/shard_map/ln2_back_wo/pallas_call | solution.py:579
  268.4 29.9 %attn_back.1 = (bf16[2,3,2,257,768]{4,3,2,1,0:T(8,128)(2,1)}, f32[3,1408]{1,0:T(4,128)}) custom-call(bf16[3,2,257,1408]{3,2,1,0:T(8,128)(2,1)} %get-tuple-element.29.qkv, bf16[2,257,1408]{2,1,0:T(8,128)(2,1)} %get-tuple-element.35.d_o), custom_call_target="tpu_custom_call" | custom-call | flops 509493248 | bytes 8650752 | tf_op jit(solution)/shard_map/attn_back/pallas_call | solution.py:608
  298.3 4.3 fusion.1
  306.6 3.8 copy.73
  316.8 17.4 %ln1_back.1 = (bf16[2,257,1408]{2,1,0:T(8,128)(2,1)}, f32[2,1408]{1,0:T(2,128)}) custom-call(bf16[2,3,2,257,768]{4,3,2,1,0:T(8,128)(2,1)} %get-tuple-element.36.d_qkv, bf16[4,1408,1536]{2,1,0:T(8,128)(2,1)} %bitcast.61, bf16[2,257,1408]{2,1,0:T(8,128)(2,1)} %copy.67.x, f32[2,257,1408]{2,1,0:T(8,128)} %get-tuple-element.37.g_res, f32[8,1408]{1,0:T(8,128)} %reshape.96.vec), custom_call_target="tpu_custom_call" | custom-call | flops 509493248 | bytes 8650752 | tf_op jit(solution)/shard_map/ln1_back/pallas_call | solution.py:634
  343.0 3.8 copy.76.a_pair
  346.8 4.0 copy.77.b_pair
  350.8 18.5 %dw_attn.1 = f32[4,1408,768]{2,1,0:T(8,128)} custom-call(bf16[2,2,257,1408]{3,2,1,0:T(8,128)(2,1)} %copy-done.2, bf16[2,2,257,1408]{3,2,1,0:T(8,128)(2,1)} %copy.76.a_pair, bf16[4,2,257,768]{3,2,1,0:T(8,128)(2,1)} %get-tuple-element.88.b_own, bf16[4,2,257,768]{3,2,1,0:T(8,128)(2,1)} %copy.77.b_pair, f32[1408,128]{1,0:T(8,128)} %reshape.104.rest_0_), custom_call_target="tpu_custom_call" | custom-call | flops 2223243264 | bytes 8650752 | tf_op jit(solution)/shard_map/dw_attn/pallas_call | solution.py:673
  369.3 80.8 %scatter_wide.2 = f32[4,3,88,256]{3,2,1,0:T(8,128)} custom-call(f32[4,4,4,88,768]{4,3,2,1,0:T(8,128)} %bitcast.66), custom_call_target="tpu_custom_call" | custom-call | tf_op jit(solution)/shard_map/scatter_wide/pallas_call | solution.py:364
  451.9 4.7 collective-permute-start.4
  464.5 4.0 copy.85.b_pair
  468.5 17.4 %dw_up.1 = f32[4,1408,768]{2,1,0:T(8,128)} custom-call(bf16[1,2,257,1408]{3,2,1,0:T(8,128)(2,1)} %bitcast.67, bf16[1,2,257,1408]{3,2,1,0:T(8,128)(2,1)} %copy.84.a_pair, bf16[4,2,257,768]{3,2,1,0:T(8,128)(2,1)} %get-tuple-element.86.b_own, bf16[4,2,257,768]{3,2,1,0:T(8,128)(2,1)} %copy.85.b_pair), custom_call_target="tpu_custom_call" | custom-call | flops 2223243264 | bytes 8650752 | tf_op jit(solution)/shard_map/dw_up/pallas_call | solution.py:673
  485.8 81.7 %scatter_wide.3 = f32[4,3,88,256]{3,2,1,0:T(8,128)} custom-call(f32[4,4,4,88,768]{4,3,2,1,0:T(8,128)} %bitcast.65), custom_call_target="tpu_custom_call" | custom-call | tf_op jit(solution)/shard_map/scatter_wide/pallas_call | solution.py:364
  570.1 3.8 collective-permute-start.7
  575.1 8.1 %copy.92.a_pair = bf16[2,257,6144]{2,1,0:T(8,128)(2,1)} copy(bf16[2,257,6144]{2,0,1:T(2,128)(2,1)} %collective-permute-done.8) | data formatting | bytes 12632064 | tf_op jit(solution)/shard_map/ppermute | solution.py:698
  583.2 19.8 %dw_down.1 = f32[6144,768]{1,0:T(8,128)} custom-call(bf16[2,257,6144]{2,1,0:T(8,128)(2,1)} %get-tuple-element.47.a_own, bf16[2,257,6144]{2,1,0:T(8,128)(2,1)} %copy.92.a_pair, bf16[2,257,768]{2,1,0:T(8,128)(2,1)} %get-tuple-element.90.b_own, bf16[2,257,768]{2,1,0:T(8,128)(2,1)} %copy.93.b_pair), custom_call_target="tpu_custom_call" | custom-call | flops 2223243264 | bytes 8650752 | tf_op jit(solution)/shard_map/dw_down/pallas_call | solution.py:673
  603.0 88.5 %scatter_down.1 = f32[4,3,32,768]{3,2,1,0:T(8,128)} custom-call(f32[4,4,4,3,32,768]{5,4,3,2,1,0:T(8,128)} %bitcast.62), custom_call_target="tpu_custom_call" | custom-call | tf_op jit(solution)/shard_map/scatter_down/pallas_call | solution.py:364
  (129 shorter events, 71.4 us)
Async XLA Ops:
  0.6 7.2 %copy-start = (f32[192,1408]{1,0:T(8,128)S(1)}, f32[192,1408]{1,0:T(8,128)}, u32[]{:S(2)}) copy-start(f32[192,1408]{1,0:T(8,128)} %param.16) | copy-start | bytes 3244036
  0.7 5.9 copy-start.11
  5.1 56.1 %collective-permute-start = (bf16[2,44,768]{2,1,0:T(8,128)(2,1)S(1)}, bf16[2,44,768]{2,1,0:T(8,128)(2,1)S(1)}, u32[]{:S(2)}, u32[]{:S(2)}) collective-permute-start(bf16[2,44,768]{2,1,0:T(8,128)(2,1)S(1)} %broadcast_select_fusion.3), channel_id=1, source_target_pairs={{0,1},{1,0},{2,3},{3,2},{4,5},{5,4},{6,7},{7,6},{8,9},{9,8},{10,11... | collective-permute-start | bytes 405512 | tf_op jit(solution)/shard_map/ppermute | solution.py:698
  8.5 51.4 %copy-start.12 = (bf16[2,257,1408]{2,0,1:T(2,128)(2,1)S(1)}, bf16[2,257,1408]{2,0,1:T(2,128)(2,1)}, u32[]{:S(2)}) copy-start(bf16[2,257,1408]{2,0,1:T(2,128)(2,1)} %param.10) | copy-start | bytes 4342276
  255.2 319.8 %collective-permute-start.8 = (bf16[2,257,6144]{2,0,1:T(2,128)(2,1)}, bf16[2,257,6144]{2,0,1:T(2,128)(2,1)}, u32[]{:S(2)}, u32[]{:S(2)}) collective-permute-start(bf16[2,257,6144]{2,0,1:T(2,128)(2,1)} %copy.90), channel_id=1, source_target_pairs={{0,1},{1,0},{2,3},{3,2},{4,5},{5,4},{6,7},{7,6},{8,9},{9,8},{10,11... | collective-permute-start | bytes 18948104 | tf_op jit(solution)/shard_map/ppermute | solution.py:698
  268.4 29.9 %copy-start.6 = (bf16[2,2,257,768]{3,2,1,0:T(8,128)(2,1)S(1)}, bf16[2,2,257,768]{3,2,1,0:T(8,128)(2,1)}, u32[]{:S(2)}) copy-start(bf16[2,2,257,768]{3,2,1,0:T(8,128)(2,1)} %get-tuple-element.41) | copy-start | bytes 4737028
  305.9 40.9 %collective-permute-start.2 = (bf16[4,2,257,768]{3,0,2,1:T(4,128)(2,1)}, bf16[4,2,257,768]{3,0,2,1:T(4,128)(2,1)}, u32[]{:S(2)}, u32[]{:S(2)}) collective-permute-start(bf16[4,2,257,768]{3,0,2,1:T(4,128)(2,1)} %copy.74), channel_id=1, source_target_pairs={{0,1},{1,0},{2,3},{3,2},{4,5},{5,4},{6,7},{7,6},{8,9},{9,8},{10,11... | collective-permute-start | bytes 9474056 | tf_op jit(solution)/shard_map/ppermute | solution.py:698
  306.2 4.3 slice-start
  306.2 5.0 slice-start.1
  310.3 31.2 %collective-permute-start.1 = (bf16[2,2,257,1408]{3,1,2,0:T(2,128)(2,1)}, bf16[2,2,257,1408]{3,1,2,0:T(2,128)(2,1)}, u32[]{:S(2)}, u32[]{:S(2)}) collective-permute-start(bf16[2,2,257,1408]{3,1,2,0:T(2,128)(2,1)} %copy.73), channel_id=1, source_target_pairs={{0,1},{1,0},{2,3},{3,2},{4,5},{5,4},{6,7},{7,6},{8,9},{9,8},{10,11... | collective-permute-start | bytes 8684552 | tf_op jit(solution)/shard_map/ppermute | solution.py:698
  316.6 147.9 %collective-permute-start.6 = (bf16[4,2,257,768]{3,0,2,1:T(4,128)(2,1)}, bf16[4,2,257,768]{3,0,2,1:T(4,128)(2,1)}, u32[]{:S(2)}, u32[]{:S(2)}) collective-permute-start(bf16[4,2,257,768]{3,0,2,1:T(4,128)(2,1)} %copy.83), channel_id=1, source_target_pairs={{0,1},{1,0},{2,3},{3,2},{4,5},{5,4},{6,7},{7,6},{8,9},{9,8},{10,11... | collective-permute-start | bytes 9474056 | tf_op jit(solution)/shard_map/ppermute | solution.py:698
  316.8 18.5 %copy-start.15 = (f32[3,1408]{1,0:T(4,128)S(1)}, f32[3,1408]{1,0:T(4,128)}, u32[]{:S(2)}) copy-start(f32[3,1408]{1,0:T(4,128)} %get-tuple-element.42) | copy-start | bytes 50692
  316.8 18.7 %copy-start.14 = (f32[8,1,768]{2,1,0:T(1,128)S(1)}, f32[8,1,768]{2,1,0:T(1,128)}, u32[]{:S(2)}) copy-start(f32[8,1,768]{2,1,0:T(1,128)} %get-tuple-element.43) | copy-start | bytes 73732
  316.8 19.3 %copy-start.3 = (bf16[2,257,1408]{2,1,0:T(8,128)(2,1)S(1)}, bf16[2,257,1408]{2,1,0:T(8,128)(2,1)}, u32[]{:S(2)}) copy-start(bf16[2,257,1408]{2,1,0:T(8,128)(2,1)} %get-tuple-element.30.h2) | copy-start | bytes 4342276
  335.8 2.6 collective-permute-start.3
  338.4 124.8 %collective-permute-start.5 = (bf16[1,2,257,1408]{3,1,2,0:T(2,128)(2,1)}, bf16[1,2,257,1408]{3,1,2,0:T(2,128)(2,1)S(1)}, u32[]{:S(2)}, u32[]{:S(2)}) collective-permute-start(bf16[1,2,257,1408]{3,1,2,0:T(2,128)(2,1)} %copy.82), channel_id=1, source_target_pairs={{0,1},{1,0},{2,3},{3,2},{4,5},{5,4},{6,7},{7,6},{8,9},{9,8},{10,11... | collective-permute-start | bytes 4342280 | tf_op jit(solution)/shard_map/ppermute | solution.py:698
  341.6 119.5 %collective-permute-start.9 = (bf16[2,257,768]{2,0,1:T(2,128)(2,1)S(1)}, bf16[2,257,768]{2,0,1:T(2,128)(2,1)}, u32[]{:S(2)}, u32[]{:S(2)}) collective-permute-start(bf16[2,257,768]{2,0,1:T(2,128)(2,1)S(1)} %copy.91), channel_id=1, source_target_pairs={{0,1},{1,0},{2,3},{3,2},{4,5},{5,4},{6,7},{7,6},{8,9},{9,8},{10,11... | collective-permute-start | bytes 2368520 | tf_op jit(solution)/shard_map/ppermute | solution.py:698
  450.1 6.6 copy-start.8
  451.9 7.0 copy-start.7
  451.9 122.0 %collective-permute-start.4 = (f32[4,3,44,256]{3,0,2,1:T(4,128)S(1)}, f32[4,3,44,256]{3,0,2,1:T(4,128)}, u32[]{:S(2)}, u32[]{:S(2)}) collective-permute-start(f32[4,3,44,256]{3,0,2,1:T(4,128)S(1)} %copy.78), channel_id=1, source_target_pairs={{0,1},{1,0},{2,3},{3,2},{4,5},{5,4},{6,7},{7,6},{8,9},{9,8},{10,11... | collective-permute-start | bytes 1622024 | tf_op jit(solution)/shard_map/ppermute | solution.py:698
  567.5 6.3 copy-start.5
  570.1 135.6 %collective-permute-start.7 = (f32[4,3,44,256]{3,0,2,1:T(4,128)}, f32[4,3,44,256]{3,0,2,1:T(4,128)}, u32[]{:S(2)}, u32[]{:S(2)}) collective-permute-start(f32[4,3,44,256]{3,0,2,1:T(4,128)} %copy.86), channel_id=1, source_target_pairs={{0,1},{1,0},{2,3},{3,2},{4,5},{5,4},{6,7},{7,6},{8,9},{9,8},{10,11... | collective-permute-start | bytes 1622024 | tf_op jit(solution)/shard_map/ppermute | solution.py:698
  693.7 19.6 %collective-permute-start.10 = (f32[192,768]{1,0:T(8,128)}, f32[192,768]{1,0:T(8,128)}, u32[]{:S(2)}, u32[]{:S(2)}) collective-permute-start(f32[192,768]{1,0:T(8,128)} %bitcast.31), channel_id=1, source_target_pairs={{0,1},{1,0},{2,3},{3,2},{4,5},{5,4},{6,7},{7,6},{8,9},{9,8},{10,11... | collective-permute-start | bytes 1769480 | tf_op jit(solution)/shard_map/ppermute | solution.py:698
  699.7 6.0 copy-start.4
  (5 other events, 16.8 us)

commit v2 on v1

--- a/solution.py
+++ b/solution.py
@@ -20,10 +20,16 @@
 LANES = 128
 F32 = jnp.float32
 BF16 = jnp.bfloat16
-VMEM_LIMIT = 62 * 1000 * 1000
+VMEM_LIMIT = 66 * 1000 * 1000
 G1, C1, BO, S1, G2, C2, B2, S2 = range(8)
 Q, K, V, O = range(4)
 SEQS = (2, SEQ, D)
+SEQ_PAIR = range(SEQS[0])
+TAIL = 8
+BODY = SEQ - 1
+TOK = BODY + TAIL
+TOKS = (2, TOK, D)
+ROWS = 4 * TOK
 
 
 def sds(dtype, *shape):
@@ -220,6 +226,10 @@
         return [vm(3, 4, 4), vm(3, 2, 2, 4), vm(3, 2, 2, 4), vm(3, 2, 4, 4), vm(3, 2, 2), vm(3, 2, 4),
                 pltpu.VMEM((3, 2, rows, cols // PAIR), F32), vm(3, 2), vm(4, 3),
                 dma((3, 4, 6)), dma((3, 4, 6)), dma((3, 3)), dma]
+
+    @staticmethod
+    def total(kind):
+        return sds(F32, 4, 3, *Scatter.unit(kind))
 
     @staticmethod
     def unit(kind):
@@ -362,11 +372,53 @@
             step()
 
     return pl.pallas_call(
-        kernel, out_shape=sds(F32, 4, 3, *Scatter.unit(kind)), in_specs=[ANY], out_specs=ANY,
+        kernel, out_shape=Scatter.total(kind), in_specs=[ANY], out_specs=ANY,
         scratch_shapes=Scatter.scratch(kind), compiler_params=comm_params(collective_id), name="scatter_" + kind)(part)
 
 
-SEQ_PAIR = range(SEQS[0])
+class Background:
+    def __init__(self, steps, plan):
+        self.steps, self.plan = steps, plan
+
+    def visit(self, place):
+        for j, first, end in self.plan.get(place, ()):
+            @at_step(j)
+            def _():
+                for step in self.steps[first:end]:
+                    step()
+
+
+class Exchange:
+    def __init__(self, mine, theirs, rows, sems, slot):
+        self.moves = []
+        for s in SEQ_PAIR:
+            for i, (start, size) in enumerate(((0, BODY), (BODY, TAIL))):
+                place = lambda n: rows.at[pl.ds(start * len(SEQ_PAIR) * PAIR + size * n, size)]
+                n = len(SEQ_PAIR) + s
+                at = slot + (PAIR * s + i,)
+                local = pltpu.make_async_copy(mine.at[s, pl.ds(start, size)], place(s), sems[2].at[at])
+                far = remote(theirs.at[s, pl.ds(start, size)], place(n), sems, at, Torus().partner())
+                self.moves.append((local, far))
+
+    @staticmethod
+    def semaphores(*lead):
+        return [pltpu.SemaphoreType.DMA(lead + (2 * PAIR,))] * 3
+
+    def start(self):
+        for local, far in self.moves:
+            far.start()
+            local.start()
+
+    def wait(self):
+        for local, far in self.moves:
+            local.wait()
+            far.wait_recv()
+
+    def finish(self):
+        for _, far in self.moves:
+            far.wait_send()
+
+
 NT = (((1,), (1,)), ((), ()))
 TN = (((0,), (0,)), ((), ()))
 
@@ -439,24 +491,8 @@
         ref[...] += value
 
 
-def qkv_kernel(x, w, b, vec, qkv, h1):
-    @at_step(0)
-    def _():
-        for s in SEQ_PAIR:
-            xhat, _ = norm_stats(x[s].astype(F32))
-            h1[s] = (xhat * row(vec, G1) + row(vec, C1)).astype(BF16)
-
-    for s in SEQ_PAIR:
-        qkv[0, s] = (dot(h1[s], w[0]) + b[0]).astype(BF16)
-
-
-def qkv_call(x, w_attn, b_qkv, vec):
-    return pl.pallas_call(
-        qkv_kernel, grid=(O,), out_shape=(sds(BF16, O, *SEQS), sds(BF16, *SEQS)),
-        in_specs=[whole(*SEQS), along(0, 1, D, D), along(0, 1, 1, D), whole(8, D)],
-        out_specs=(along(0, 1, *SEQS), whole(*SEQS)),
-        compiler_params=compute_params(), cost_estimate=work(SEQ * D * D), name="ln1_qkv",
-    )(x, w_attn, b_qkv, vec)
+def pad(t):
+    return jnp.concatenate([t.astype(F32), jnp.zeros((TOK - SEQ, t.shape[1]), F32)], axis=0).astype(BF16)
 
 
 def window(h):
@@ -475,20 +511,67 @@
     return e * (1.0 / jnp.sum(e, axis=-1, keepdims=True))
 
 
-def attn_kernel(qkv, x, w_out, vec, o, att, h2, acc):
+def attention(s, rows, x, w_out, vec, o, att, h2, acc, visit):
     acc[...] = jnp.zeros_like(acc)
     for h in range(HEADS):
         lanes, mask = window(h)
-        k = only(mask, qkv[K, 0, :, lanes])
-        v = only(mask, qkv[V, 0, :, lanes])
-        probs = softmax(dot_nt(qkv[Q, 0, :, lanes], k) * SCALE).astype(BF16)
+        k = only(mask, rows[K, s, :, lanes])
+        v = only(mask, rows[V, s, :, lanes])
+        probs = softmax(dot_nt(rows[Q, s, :, lanes], k) * SCALE).astype(BF16)
         acc[:, lanes] += dot(probs, v)
-    heads = acc[...].astype(BF16)
-    o[0] = heads
-    a = dot(heads, w_out[0]) + row(vec, BO)
+        visit(h)
+    heads = acc[...]
+    o[0] = pad(heads)
+    a = dot(heads.astype(BF16), w_out[0]) + row(vec, BO)
     att[0] = a
-    xhat, _ = norm_stats(x[0].astype(F32) + row(vec, S1) * a)
-    h2[0] = (xhat * row(vec, G2) + row(vec, C2)).astype(BF16)
+    xhat, _ = norm_stats(x[s].astype(F32) + row(vec, S1) * a)
+    h2[0] = pad(xhat * row(vec, G2) + row(vec, C2))
+
+
+FRONT_PLAN = {"qkv": ((0, 0, 1), (1, 1, 5), (2, 5, 8)), HEADS - 2: ((O, 8, 9),), "end": ((O + 1, 9, None),)}
+
+
+def front_kernel(x, w, b, vec, up_src, down_src, qkv, h1, o, att, h2, up, down, rows, acc, *sems):
+    n = len(sems) // 2
+    gathers = Gather(WIDE, up_src, up, *sems[:n]), Gather(DOWN, down_src, down, *sems[n:])
+    steps = [lambda pair=pair: [step() for step in pair] for pair in zip(*(g.steps() for g in gathers))]
+    hosted = Background(steps, FRONT_PLAN)
+    j = pl.program_id(0)
+    at_step(0)(enter)
+    hosted.visit("qkv")
+
+    @at_step(0)
+    def _():
+        for s in SEQ_PAIR:
+            xhat, _ = norm_stats(x[s].astype(F32))
+            h1[s] = pad(xhat * row(vec, G1) + row(vec, C1))
+
+    @pl.when(j < O)
+    def _():
+        for s in SEQ_PAIR:
+            t = (dot(h1[s, :SEQ], w[0]) + b[0]).astype(BF16)
+            qkv[0, s] = t
+            rows[j, s] = t
+
+    @pl.when(j >= O)
+    def _():
+        attention(j - O, rows, x, w, vec, o, att, h2, acc, hosted.visit)
+
+    hosted.visit("end")
+
+
+def front_call(x, w_attn, b_qkv, vec, up, down, collective_id):
+    upto = lambda n: lambda j: jnp.minimum(j, n)
+    seq = lambda tokens: along(0, 1, tokens, D, index=lambda j: jnp.maximum(j - O, 0))
+    return pl.pallas_call(
+        front_kernel, grid=(O + PAIR,),
+        out_shape=(sds(BF16, O, *SEQS), sds(BF16, *TOKS), sds(BF16, *TOKS), sds(F32, *SEQS), sds(BF16, *TOKS),
+                   sds(BF16, *Gather.shape(WIDE)), sds(BF16, *Gather.shape(DOWN))),
+        in_specs=[whole(*SEQS), along(0, 1, D, D, index=upto(O)), along(0, 1, 1, D, index=upto(V)), whole(8, D), ANY, ANY],
+        out_specs=(along(0, 1, *SEQS, index=upto(V)), whole(*TOKS), seq(TOK), seq(SEQ), seq(TOK), ANY, ANY),
+        scratch_shapes=[pltpu.VMEM((O, *SEQS), BF16), pltpu.VMEM((SEQ, D), F32)] + Gather.semaphores() * PAIR,
+        compiler_params=comm_params(collective_id), name="front",
+    )(x, w_attn, b_qkv, vec, up, down)
 
 
 def one_seq():
@@ -497,15 +580,6 @@
 
 def w_out_block():
     return along(0, 1, D, D, index=lambda j: O)
-
-
-def attn_call(qkv, x, w_attn, vec):
-    return pl.pallas_call(
-        attn_kernel, grid=SEQS[:1], out_shape=(sds(BF16, *SEQS), sds(F32, *SEQS), sds(BF16, *SEQS)),
-        in_specs=[along(1, O, 1, SEQ, D), one_seq(), w_out_block(), whole(8, D)],
-        out_specs=(one_seq(),) * O, scratch_shapes=[pltpu.VMEM((SEQ, D), F32)],
-        compiler_params=compute_params(), cost_estimate=work(SEQ * D * D), name="attn_wo_ln2",
-    )(qkv, x, w_attn, vec)
 
 
 def mlp_kernel(h2, gz, w_up, b_up, w_down, vec, act, d_pre, db_up, mlp, d_h2, dm_halves, dm):
@@ -516,44 +590,47 @@
         for s in SEQ_PAIR:
             d = (gz[s].astype(F32) * row(vec, S2)).astype(BF16)
             dm[s] = d
+            d = pad(d)
             dm_halves[0, s] = d[:, :HALF]
             dm_halves[1, s] = d[:, D - HALF:]
 
     db = jnp.zeros((1, HALF), F32)
     for s in SEQ_PAIR:
-        u = dot(h2[s], w_up[0]) + b_up[0]
+        h = h2[s, :SEQ]
+        u = dot(h, w_up[0]) + b_up[0]
         phi = 0.5 * (1.0 + lax.erf(u * math.sqrt(0.5)))
         a = (u * phi).astype(BF16)
-        act[s] = a
+        act[s] = pad(a)
         slope = phi + u * (jnp.exp(-0.5 * u * u) * (math.sqrt(0.5 / math.pi)))
         mlp[s] += dot(a, w_down[...])
         d = dot_nt(dm[s], w_down[...]) * slope
         db = db + col_sum(d)
         d = d.astype(BF16)
-        d_pre[0, 0, s] = d
+        d_pre[0, 0, s] = pad(d)
         d_h2[s] += dot_nt(d, w_up[0])
     db_up[0] = db
 
 
 def mlp_call(h2, gz, w_up, b_up, w_down, vec):
     n = FF // HALF
-    tiled = along(2, 2, SEQ, HALF)
+    tiled = along(2, 2, TOK, HALF)
     bias = along(0, 1, 1, HALF)
-    halved = pl.BlockSpec((1, 1, 2, SEQ, HALF), lambda j: (j % PAIR, j // PAIR, 0, 0, 0))
+    halved = pl.BlockSpec((1, 1, 2, TOK, HALF), lambda j: (j % PAIR, j // PAIR, 0, 0, 0))
     return pl.pallas_call(
         mlp_kernel, grid=(n,),
-        out_shape=(sds(BF16, 2, SEQ, FF), sds(BF16, 2, 4, 2, SEQ, HALF), sds(F32, n, 1, HALF), sds(F32, *SEQS),
-                   sds(F32, *SEQS), sds(BF16, 2, 2, SEQ, HALF)),
-        in_specs=[whole(*SEQS), whole(*SEQS), pl.BlockSpec((1, D, HALF), lambda j: (j // PAIR, 0, j % PAIR)), bias,
+        out_shape=(sds(BF16, 2, TOK, FF), sds(BF16, 2, 4, 2, TOK, HALF), sds(F32, n, 1, HALF), sds(F32, *SEQS),
+                   sds(F32, *SEQS), sds(BF16, 2, 2, TOK, HALF)),
+        in_specs=[whole(*TOKS), whole(*SEQS), pl.BlockSpec((1, D, HALF), lambda j: (j // PAIR, 0, j % PAIR)), bias,
                   along(0, HALF, D), whole(8, D)],
-        out_specs=(tiled, halved, bias, whole(*SEQS), whole(*SEQS), whole(2, 2, SEQ, HALF)),
+        out_specs=(tiled, halved, bias, whole(*SEQS), whole(*SEQS), whole(2, 2, TOK, HALF)),
         scratch_shapes=[pltpu.VMEM(SEQS, BF16)],
         compiler_params=compute_params(), cost_estimate=work(SEQ * D * FF), name="mlp",
     )(h2, gz, w_up, b_up.reshape(n, 1, HALF), w_down, vec)
 
 
 def halves_of(t):
-    return t[:, :HALF], jnp.concatenate([t[:, HALF:], jnp.zeros((SEQ, QCOLS - D), t.dtype)], axis=1)
+    t = pad(t)
+    return t[:, :HALF], jnp.concatenate([t[:, HALF:], jnp.zeros((TOK, QCOLS - D), BF16)], axis=1)
 
 
 def mid_kernel(mlp, d_h2, att, x, gz, vec, w_out, z, g_res, d_att, d_o, sums):
@@ -569,23 +646,22 @@
     da = gr * row(vec, S1)
     terms = (da, gr * a, dh * xhat, dh, g * row(vec, S2), g * m)
     accumulate(sums, jnp.concatenate([jnp.zeros((BO, D), F32)] + [col_sum(t) for t in terms], axis=0))
-    da = da.astype(BF16)
     for i, t in enumerate(halves_of(da)):
         d_att[i, 0] = t
-    d_o[0] = dot_nt(da, w_out[0]).astype(BF16)
+    d_o[0] = dot_nt(da.astype(BF16), w_out[0]).astype(BF16)
 
 
 def mid_call(mlp, d_h2, att, x, gz, vec, w_attn):
     return pl.pallas_call(
         mid_kernel, grid=SEQS[:1],
-        out_shape=(sds(BF16, *SEQS), sds(F32, *SEQS), sds(BF16, 2, 2, SEQ, HALF), sds(BF16, *SEQS), sds(F32, 8, D)),
+        out_shape=(sds(BF16, *SEQS), sds(F32, *SEQS), sds(BF16, 2, 2, TOK, HALF), sds(BF16, *SEQS), sds(F32, 8, D)),
         in_specs=[one_seq()] * len("mdaxg") + [whole(8, D), w_out_block()],
-        out_specs=(one_seq(), one_seq(), along(1, 2, 1, SEQ, HALF), one_seq(), whole(8, D)),
+        out_specs=(one_seq(), one_seq(), along(1, 2, 1, TOK, HALF), one_seq(), whole(8, D)),
         compiler_params=compute_params(), cost_estimate=work(SEQ * D * D), name="ln2_back_wo",
     )(mlp, d_h2, att, x, gz, vec, w_attn)
 
 
-def attn_back_kernel(qkv, d_o, d_qkv, db, acc):
+def attention_back(qkv, d_o, d_qkv, db, acc, visit):
     acc[...] = jnp.zeros_like(acc)
     for h in range(HEADS):
         lanes, mask = window(h)
@@ -598,94 +674,193 @@
         ds = (ds * SCALE).astype(BF16)
         acc[Q, :, lanes] += dot(ds, k)
         acc[K, :, lanes] += dot_tn(ds, q)
+        visit(h)
     accumulate(db, jnp.concatenate([col_sum(acc[i]) for i in (Q, K, V)], axis=0))
     for n in (Q, K, V):
-        for i, t in enumerate(halves_of(acc[n].astype(BF16))):
+        for i, t in enumerate(halves_of(acc[n])):
             d_qkv[i, n, 0] = t
 
 
-def attn_back_call(qkv, d_o):
+THIN = HALF // PAIR
+
+
+class WideGrads:
+    def __init__(self, a, a_of, b, out, base, a_rows, b_rows, *sems):
+        self.a, self.a_of, self.b, self.out, self.base, self.a_rows, self.b_rows = a, a_of, b, out, base, a_rows, b_rows
+        self.a_sems, self.b_sems = sems[:3], sems[3:]
+
+    @staticmethod
+    def scratch(inputs):
+        return ([pltpu.VMEM((inputs, ROWS, D), BF16), pltpu.VMEM((SIDE, ROWS, HALF), BF16)] +
+                Exchange.semaphores(inputs) + Exchange.semaphores(SIDE))
+
+    def input(self, i):
+        return Exchange(self.a[i], self.a[i], self.a_rows.at[i], self.a_sems, (i,))
+
+    def cotangent(self, n):
+        c = Torus().at["c"]
+        b = self.b[n]
+        return Exchange(b(c), b(1 - c), self.b_rows.at[n], self.b_sems, (n,))
+
+    def begin(self):
+        for n in range(SIDE):
+            if n == 0 or self.a_of[n] != self.a_of[n - 1]:
+                self.input(self.a_of[n]).start()
+            self.cotangent(n).start()
+
+    def step(self):
+        j = pl.program_id(0)
+        for n in range(SIDE):
+            @at_step(self.base + PAIR * n)
+            def _():
+                if n == 0 or self.a_of[n] != self.a_of[n - 1]:
+                    self.input(self.a_of[n]).wait()
+                self.cotangent(n).wait()
+
+        @pl.when(j >= self.base)
+        def _():
+            n = lax.div(j - self.base, PAIR)
+            cols = pl.ds(pl.multiple_of(lax.rem(j - self.base, PAIR) * THIN, LANES), THIN)
+            a = self.a_rows[0 if len(self.a) == 1 else lax.div(n, O)]
+            self.out[0] = dot_tn(a, self.b_rows[n, :, cols])
+
+    def finish(self):
+        for i in range(len(self.a)):
+            self.input(i).finish()
+        for n in range(SIDE):
+            self.cotangent(n).finish()
+
+
+def grads_block(base):
+    def index(j):
+        n = jnp.maximum(j - base, 0)
+        return n // PAIR, 0, n % PAIR
+
+    return pl.BlockSpec((1, D, THIN), index)
+
+
+LAST_SEQ = SEQS[0] - 1
+ATTN_PLAN = {"start": ((0, 0, 1),), SIDE: ((LAST_SEQ, 1, 4),), "end": ((LAST_SEQ + PAIR * SIDE, 4, None),)}
+
+
+def attn_back_kernel(qkv, d_o, h2, d_pre, part, d_qkv, db, d_up, total, acc, *scratch):
+    n = len(WideGrads.scratch(1))
+    grads = WideGrads((h2,), (0,) * SIDE, [lambda c, i=i: d_pre.at[c, i] for i in range(SIDE)], d_up, SEQS[0], *scratch[:n])
+    hosted = Background(Scatter(DOWN, part, total, *scratch[n:]).steps(), ATTN_PLAN)
+    at_step(0)(enter)
+    hosted.visit("start")
+    at_step(0)(grads.begin)
+
+    @pl.when(pl.program_id(0) < SEQS[0])
+    def _():
+        attention_back(qkv, d_o, d_qkv, db, acc, hosted.visit)
+
+    grads.step()
+    hosted.visit("end")
+    at_step(LAST_SEQ + PAIR * SIDE)(grads.finish)
+
+
+def attn_back_call(qkv, d_o, h2, d_pre, part, collective_id):
+    upto = lambda j: jnp.minimum(j, LAST_SEQ)
     return pl.pallas_call(
-        attn_back_kernel, grid=SEQS[:1], out_shape=(sds(BF16, 2, O, 2, SEQ, HALF), sds(F32, O, D)),
-        in_specs=[along(1, O, 1, SEQ, D), one_seq()], out_specs=(along(2, 2, O, 1, SEQ, HALF), whole(O, D)),
-        scratch_shapes=[pltpu.VMEM((O, SEQ, D), F32)],
-        compiler_params=compute_params(), cost_estimate=work(SEQ * D * D), name="attn_back",
-    )(qkv, d_o)
-
-
-def in_back_kernel(d_qkv, w, x, g_res, vec, dx, sums, acc):
-    rest = D - HALF
-    for s in SEQ_PAIR:
-        part = dot_nt(d_qkv[0, 0, s], w[0, :, :HALF]) + dot_nt(d_qkv[1, 0, s, :, :rest], w[0, :, HALF:])
-        accumulate(acc.at[s], part)
-
-    @at_step(V)
-    def _():
-        total = jnp.zeros((BO, D), F32)
+        attn_back_kernel, grid=(SEQS[0] + PAIR * SIDE,),
+        out_shape=(sds(BF16, 2, O, 2, TOK, HALF), sds(F32, O, D), sds(F32, SIDE, D, HALF), Scatter.total(DOWN)),
+        in_specs=[along(1, O, 1, SEQ, D, index=upto), along(0, 1, SEQ, D, index=upto), ANY, ANY, ANY],
+        out_specs=(along(2, 2, O, 1, TOK, HALF, index=upto), whole(O, D), grads_block(SEQS[0]), ANY),
+        scratch_shapes=[pltpu.VMEM((O, SEQ, D), F32)] + WideGrads.scratch(1) + Scatter.scratch(DOWN),
+        compiler_params=comm_params(collective_id), name="attn_back",
+    )(qkv, d_o, h2, d_pre, part)
+
+
+IN_STEPS = PAIR * O
+IN_PLAN = {"start": ((0, 0, 1), (IN_STEPS, 1, 4)), "end": ((IN_STEPS + PAIR * SIDE - 1, 4, None),)}
+
+
+def in_back_kernel(d_half, w, x, g_res, vec, h1, o, d_qkv, d_att, part, dx, sums, d_attn, total, acc, *scratch):
+    n = len(WideGrads.scratch(2))
+    b = [lambda c, i=i: d_qkv.at[c, i] for i in range(O)] + [lambda c: d_att.at[c]]
+    grads = WideGrads((h1, o), (0,) * O + (1,), b, d_attn, IN_STEPS, *scratch[:n])
+    hosted = Background(Scatter(WIDE, part, total, *scratch[n:]).steps(), IN_PLAN)
+    at_step(0)(enter)
+    hosted.visit("start")
+    at_step(0)(grads.begin)
+
+    @pl.when(pl.program_id(0) < IN_STEPS)
+    def _():
+        for s in SEQ_PAIR:
+            accumulate(acc.at[s], dot_nt(d_half[0, 0, s, :SEQ], w[0]))
+
+    @at_step(IN_STEPS - 1)
+    def _():
+        rows = jnp.zeros((BO, D), F32)
         for s in SEQ_PAIR:
             xhat, rstd = norm_stats(x[s].astype(F32))
             dh = acc[s]
-            total = total + jnp.concatenate([col_sum(dh * xhat), col_sum(dh)], axis=0)
+            rows = rows + jnp.concatenate([col_sum(dh * xhat), col_sum(dh)], axis=0)
             dx[s] = (g_res[s] + norm_back(xhat, rstd, dh * row(vec, G1))).astype(BF16)
-        sums[...] = total
-
-
-def in_back_call(d_qkv, w_attn, x, g_res, vec):
+        sums[...] = rows
+
+    grads.step()
+    hosted.visit("end")
+    at_step(IN_STEPS + PAIR * SIDE - 1)(grads.finish)
+
+
+def in_back_call(d_qkv, w_attn, x, g_res, vec, h1, o, d_att, part, collective_id):
+    def at(j):
+        n = jnp.minimum(j, IN_STEPS - 1)
+        return n // PAIR, n % PAIR
+
+    once = lambda *shape: pl.BlockSpec(shape, lambda j: (0,) * len(shape), pipeline_mode=pl.Buffered(1))
     return pl.pallas_call(
-        in_back_kernel, grid=(O,), out_shape=(sds(BF16, *SEQS), sds(F32, BO, D)),
-        in_specs=[along(1, 2, 1, 2, SEQ, HALF), along(0, 1, D, D), whole(*SEQS), whole(*SEQS), whole(8, D)],
-        out_specs=(whole(*SEQS), whole(BO, D)), scratch_shapes=[pltpu.VMEM(SEQS, F32)],
-        compiler_params=compute_params(), cost_estimate=work(SEQ * D * D), name="ln1_back",
-    )(d_qkv, w_attn, x, g_res, vec)
-
-
-BODY = SEQ - 1
-ROWS = 4 * SEQ + 12
-
-
-def stack_tokens(dst, seqs):
-    for i, seq in enumerate(seqs):
-        dst[pl.ds(BODY * i, BODY)] = seq[:BODY]
-    last = [seq[BODY:].astype(F32) for seq in seqs]
-    tail = jnp.concatenate(last + [jnp.zeros((ROWS - len(seqs) * SEQ, dst.shape[1]), F32)], axis=0)
-    dst[pl.ds(len(seqs) * BODY, ROWS - len(seqs) * BODY)] = tail.astype(BF16)
-
-
-def grad_kernel(new_a, new_b, a_own, a_pair, b_own, b_pair, *rest):
-    extra, (out, a_rows, b_rows) = rest[:-3], rest[-3:]
-    j = pl.program_id(0)
-
-    def fill(dst, own, pair):
-        lead = (0,) * (len(own.shape) - len(SEQS))
-        stack_tokens(dst, [ref[lead + (s,)] for ref in (own, pair) for s in SEQ_PAIR])
-
-    pl.when(new_a(j))(lambda: fill(a_rows, a_own, a_pair))
-    pl.when(new_b(j))(lambda: fill(b_rows, b_own, b_pair))
-    value = dot_tn(a_rows[...], b_rows[...])
-    out[...] = value.reshape(out.shape)
-    if extra:
-        @at_step(0)
-        def _():
-            out[0, :, HALF - LANES:] += extra[0][...]
-
-
-def grad_call(name, grid, a, a_spec, b, b_spec, new_a, new_b, out_shape, out_spec, extra=()):
+        in_back_kernel, grid=(IN_STEPS + PAIR * SIDE,),
+        out_shape=(sds(BF16, *SEQS), sds(F32, BO, D), sds(F32, SIDE, D, HALF), Scatter.total(WIDE)),
+        in_specs=[pl.BlockSpec((1, 1, 2, TOK, HALF), lambda j: (at(j)[1], at(j)[0], 0, 0, 0)),
+                  pl.BlockSpec((1, D, HALF), lambda j: (at(j)[0], 0, at(j)[1])), once(*SEQS), once(*SEQS), whole(8, D),
+                  ANY, ANY, ANY, ANY, ANY],
+        out_specs=(whole(*SEQS), whole(BO, D), grads_block(IN_STEPS), ANY),
+        scratch_shapes=[pltpu.VMEM(SEQS, F32)] + WideGrads.scratch(2) + Scatter.scratch(WIDE),
+        compiler_params=comm_params(collective_id), name="in_back",
+    )(d_qkv, w_attn, x, g_res, vec, h1, o, d_qkv, d_att, part)
+
+
+DOWN_TILES = FF // HALF
+
+
+def down_kernel(act, d_mlp, out, a_rows, b_rows, *sems):
+    c = Torus().at["c"]
+    both = Exchange(d_mlp.at[c], d_mlp.at[1 - c], b_rows, sems[3:], ())
+
+    def tile(j):
+        mine = act.at[:, :, pl.ds(HALF * j, HALF)]
+        return Exchange(mine, mine, a_rows.at[j], sems[:3], (j,))
+
+    @at_step(0)
+    def _():
+        enter()
+        both.start()
+        for j in range(DOWN_TILES):
+            tile(j).start()
+        both.wait()
+
+    for j in range(DOWN_TILES):
+        at_step(j)(tile(j).wait)
+    out[...] = dot_tn(a_rows[pl.program_id(0)], b_rows[...])
+
+    @at_step(DOWN_TILES - 1)
+    def _():
+        both.finish()
+        for j in range(DOWN_TILES):
+            tile(j).finish()
+
+
+def down_grads(act, d_mlp, collective_id):
     return pl.pallas_call(
-        functools.partial(grad_kernel, new_a, new_b), grid=(grid,), out_shape=out_shape,
-        in_specs=[a_spec] * PAIR + [b_spec] * PAIR + [whole(*e.shape) for e in extra], out_specs=out_spec,
-        scratch_shapes=[pltpu.VMEM((ROWS, a_spec.block_shape[-1]), BF16), pltpu.VMEM((ROWS, HALF), BF16)],
-        compiler_params=compute_params(), cost_estimate=work(SEQ * D * FF), name=name,
-    )(*a, *b, *extra)
-
-
-def wide_grads(name, a, b, new_a, a_index, extra=()):
-    return grad_call(name, SIDE, a, along(0, 1, *SEQS, index=a_index), b, along(0, 1, 2, SEQ, HALF), new_a,
-                     lambda j: j >= 0, sds(F32, SIDE, D, HALF), along(0, 1, D, HALF), extra)
-
-
-def down_grads(a, b):
-    return grad_call("dw_down", FF // HALF, a, along(2, 2, SEQ, HALF), b, whole(2, SEQ, HALF), lambda j: j >= 0,
-                     lambda j: j == 0, sds(F32, FF, HALF), along(0, HALF, HALF))
+        down_kernel, grid=(DOWN_TILES,), out_shape=sds(F32, FF, HALF), in_specs=[ANY, ANY],
+        out_specs=along(0, HALF, HALF),
+        scratch_shapes=[pltpu.VMEM((DOWN_TILES, ROWS, HALF), BF16), pltpu.VMEM((ROWS, HALF), BF16)] +
+        Exchange.semaphores(DOWN_TILES) + Exchange.semaphores(),
+        compiler_params=comm_params(collective_id), name="dw_down",
+    )(act, d_mlp)
 
 
 OWN = 44
@@ -748,34 +923,22 @@
     first = core == 0
     attn, up, down = my_pieces(shards, first)
     w_attn = torus_gather(WIDE, attn, 0).reshape(SIDE, D, QCOLS)
-    w_up = torus_gather(WIDE, up, 1).reshape(SIDE, D, QCOLS)
-    w_down = torus_gather(DOWN, down, 2).reshape(FF, D)
     b_qkv, b_up, vec = small_params(w_attn)
-    pick = lambda a, i: lax.dynamic_index_in_dim(a, i, 0, keepdims=False)
-    both = lambda a: (a, pair_swap(a))
-    halves = lambda a: (pick(a, core), pair_swap(pick(a, 1 - core)))
-
-    qkv, h1 = qkv_call(x, w_attn, b_qkv, vec)
-    o, att, h2 = attn_call(qkv, x, w_attn, vec)
-    act, d_pre, db_up, mlp, d_h2, d_mlp = mlp_call(h2, gz, w_up, b_up, w_down, vec)
-    part_down = down_grads(both(act), halves(d_mlp))
+    qkv, h1, o, att, h2, w_up, w_down = front_call(x, w_attn, b_qkv, vec, up, down, 1)
+    act, d_pre, db_up, mlp, d_h2, d_mlp = mlp_call(h2, gz, w_up.reshape(SIDE, D, QCOLS), b_up, w_down.reshape(FF, D), vec)
     z, g_res, d_att, d_o, sums = mid_call(mlp, d_h2, att, x, gz, vec, w_attn)
-    part_up = wide_grads("dw_up", both(h2[None]), halves(d_pre), lambda j: j == 0, lambda j: 0)
-    d_qkv, db_qkv = attn_back_call(qkv, d_o)
-    dx, in_sums = in_back_call(d_qkv, w_attn, x, g_res, vec)
+    part = down_grads(act, d_mlp, 2).reshape(4, 4, 4, 3, 32, HALF)
+    d_qkv, db_qkv, part, down = attn_back_call(qkv, d_o, h2, d_pre, part, 3)
+    part = part.reshape(4, 4, 4, CHIP, HALF)
+    dx, in_sums, part, up = in_back_call(d_qkv, w_attn, x, g_res, vec, h1, o, d_att, part, 4)
     small = small_grads(db_qkv, db_up, jnp.concatenate([in_sums, sums[BO:]], axis=0), core)
-    d_cols = jnp.concatenate([d_qkv, d_att[:, None]], axis=1)
-    part_attn = wide_grads("dw_attn", both(jnp.stack([h1, o])), halves(d_cols), lambda j: (j == Q) | (j == O),
-                           lambda j: j // O, (small,))
-
-    down = torus_scatter(DOWN, part_down.reshape(4, 4, 4, 3, 32, HALF), 3).reshape(FF // 16, HALF)
-    up = torus_scatter(WIDE, part_up.reshape(4, 4, 4, CHIP, HALF), 4)
-    attn = torus_scatter(WIDE, part_attn.reshape(4, 4, 4, CHIP, HALF), 5)
+    part = part.at[0, :, HALF - LANES:].add(small).reshape(4, 4, 4, CHIP, HALF)
+    attn = torus_scatter(WIDE, part, 5)
     g_up = final_rows(up, first).reshape(OWN, FF)
     attn = final_rows(attn, first)
     small = attn[:, 0, D:].reshape(OWN * LANES)
     return (z, dx, attn[:, :O, :D].reshape(OWN, O * D), small[:BQ], attn[:, O, :D], g_up, small[BQ:BU],
-            final_down(down, first), small[BU:VEC].reshape(8, OWN))
+            final_down(down.reshape(FF // 16, HALF), first), small[BU:VEC].reshape(8, OWN))
 
 
 def solution(mesh):

time: 721 us -> 556 us (0.77)
  Pallas kernels: 597 us -> 487 us
  local copies, waits for them, and re-layouts: 80.3 us -> 28.9 us
    pallas_call x3 -> x1, Pallas kernels: 146 us -> 51.8 us  [torus_gather(): pl.pallas_call(kernel, out_shape=sds(BF16, *Gather.shape(kind)), in_specs...]
    ppermute x6 -> x0, local copies, waits for them, and re-layouts: 23.3 us -> none  [pair_swap(): return lax.ppermute(a, 'fsdp', [(i, i ^ 1) for i in range(DEVICES)])]
    pallas_call x11 -> x6, Pallas kernels: 438 us -> 423 us  [the longest x1 92.5 us: attn_back_call(): pl.pallas_call(attn_back_kernel, grid=(SEQS[0] + PAIR * SIDE,), out_shape...]
    squeeze x5 -> x0, local copies, waits for them, and re-layouts: 11.6 us -> none  [device_step(): pick = lambda a, i: lax.dynamic_index_in_dim(a, i, 0, keepdims=False)]
    pallas_call x1 -> x0, local copies, waits for them, and re-layouts: 10.3 us -> none  [mlp_call(): pl.pallas_call(mlp_kernel, grid=(n,), out_shape=(sds(BF16, 2, SEQ, FF), s...]
    ppermute x11 -> x5, starting transfers between devices: 15.1 us -> 13.3 us  [pair_swap(): return lax.ppermute(a, 'fsdp', [(i, i ^ 1) for i in range(DEVICES)])]
  transfers between devices with their start and end apart: 11 -> 5, of which waited for: 0 -> 0; matrix products, arithmetic and copies ran while one was open for 11% -> 6% of each run, Pallas kernels for 58% -> 30%
where the time goes in v2:
time: 556 us; the launch traced here: 553 us
  Pallas kernels  487 us (88%)
  local copies, waits for them, and re-layouts  28.9 us (5%)
  other arithmetic  22.1 us (4%)
  starting transfers between devices  13.3 us (2%)
    pallas_call x1, Pallas kernels, attn_back_call(): pl.pallas_call(attn_back_kernel, grid=(SEQS[0] + PAIR * SIDE,), out_shape...  92.5 us
    pallas_call x1, Pallas kernels, in_back_call(): pl.pallas_call(in_back_kernel, grid=(IN_STEPS + PAIR * SIDE,), out_shape=...  87.9 us
    pallas_call x1, Pallas kernels, front_call(): pl.pallas_call(front_kernel, grid=(O + PAIR,), out_shape=(sds(BF16, O, *S...  85.8 us
    pallas_call x1, Pallas kernels, torus_scatter(): pl.pallas_call(kernel, out_shape=Scatter.total(kind), in_specs=[ANY], out...  79.9 us
    pallas_call x1, Pallas kernels, mlp_call(): pl.pallas_call(mlp_kernel, grid=(n,), out_shape=(sds(BF16, 2, TOK, FF), s...  54.3 us
    pallas_call x1, Pallas kernels, torus_gather(): pl.pallas_call(kernel, out_shape=sds(BF16, *Gather.shape(kind)), in_specs...  51.8 us
    pallas_call x1, Pallas kernels, down_grads(): pl.pallas_call(down_kernel, grid=(DOWN_TILES,), out_shape=sds(F32, FF, HA...  22.3 us
    ppermute x5, starting transfers between devices, pair_swap(): return lax.ppermute(a, 'fsdp', [(i, i ^ 1) for i in range(DEVICES)])  13.3 us
  transfers between devices with their start and end apart: 5, of which 0 were waited for; matrix products, arithmetic and copies ran while one was open for 6% of the time, Pallas kernels for 30%

profile of v2, /device:TPU:1, one launch (start us, length us, event | category | flops | bytes accessed | tf_op | source)
XLA Modules:
  0.0 552.9 jit_solution(16007620396208156123)
XLA Ops:
  5.0 1.4 collective-permute-start
  6.5 1.6 dynamic-slice_convert_fusion.1
  8.7 1.3 copy.38.x
  10.6 1.3 copy.39.gz
  11.9 2.0 and_reduce_fusion
  14.7 51.8 %gather_wide.1 = bf16[4,4,4,88,1536]{4,3,2,1,0:T(8,128)(2,1)} custom-call(bf16[88,768]{1,0:T(8,128)(2,1)} %get-tuple-element.109.refs_0_), custom_call_target="tpu_custom_call" | custom-call | tf_op jit(solution)/shard_map/gather_wide/pallas_call | solution.py:363
  70.1 85.8 %front.1 = (bf16[3,2,257,1408]{3,2,1,0:T(8,128)(2,1)}, bf16[2,264,1408]{2,1,0:T(8,128)(2,1)}, bf16[2,264,1408]{2,1,0:T(8,128)(2,1)}, f32[2,257,1408]{2,1,0:T(8,1...) custom-call(bf16[2,257,1408]{2,1,0:T(8,128)(2,1)} %copy.38.x, ...), custom_call_target="tpu_custom_call" | custom-call | tf_op jit(solution)/shard_map/front/pallas_call | solution.py:566
  155.9 54.3 %mlp.1 = (bf16[2,264,6144]{2,1,0:T(8,128)(2,1)}, bf16[2,4,2,264,768]{4,3,2,1,0:T(8,128)(2,1)}, f32[8,1,768]{2,1,0:T(1,128)}, f32[2,257,1408]{2,1,0:T(8,128)}, f3...) custom-call(bf16[2,264,1408]{2,1,0:T(8,128)(2,1)} %get-tuple-element.47.h2, bf16[2,257,1408]{2,1,0:T(8,128)(2,1)} %copy.39.gz, ...), custom_call_target="tpu_custom_call" | custom-call | flops 2223243264 | bytes 8650752 | tf_op jit(solution)/shard_map/mlp/pallas_call | solution.py:619
  210.2 22.3 %dw_down.1 = f32[6144,768]{1,0:T(8,128)} custom-call(bf16[2,264,6144]{2,1,0:T(8,128)(2,1)} %get-tuple-element.57.act, bf16[2,2,264,768]{3,2,1,0:T(8,128)(2,1)} %get-tuple-element.58.d_mlp), custom_call_target="tpu_custom_call" | custom-call | tf_op jit(solution)/shard_map/dw_down/pallas_call | solution.py:857
  232.5 12.9 %ln2_back_wo.1 = (bf16[2,257,1408]{2,1,0:T(8,128)(2,1)}, f32[2,257,1408]{2,1,0:T(8,128)}, bf16[2,2,264,768]{3,2,1,0:T(8,128)(2,1)}, bf16[2,257,1408]{2,1,0:T(8,128)(2,1)}, f32[8,1408]{1,0:T(8,128)}) custom-call(f32[2,257,1408]{2,1,0:T(8,128)} %get-tuple-element.50.mlp, f32[2,257,1408]{2,1,0:T(8,128)} %get-tuple-element.51.d_h2, ...), custom_call_target="tpu_custom_call" | custom-call | flops 509493248 | bytes 8650752 | tf_op jit(solution)/shard_map/ln2_back_wo/pallas_call | solution.py:655
  245.4 92.5 %attn_back.1 = (bf16[2,3,2,264,768]{4,3,2,1,0:T(8,128)(2,1)}, f32[3,1408]{1,0:T(4,128)}, f32[4,1408,768]{2,1,0:T(8,128)}, f32[4,3,32,768]{3,2,1,0:T(8,128)}) custom-call(bf16[3,2,257,1408]{3,2,1,0:T(8,128)(2,1)} %get-tuple-element.54.qkv, bf16[2,257,1408]{2,1,0:T(8,128)(2,1)} %get-tuple-element.55.d_o, bf16[2,264,1408]{2,1,0:T(8,128)(2,1)} %get-tuple-element.47.h2, ...), custom_call_target="tpu_custom_call" | custom-call | tf_op jit(solution)/shard_map/attn_back/pallas_call | solution.py:765
  337.9 2.2 slice_select_fusion
  340.1 3.3 collective-permute-start.4
  343.4 87.9 %in_back.1 = (bf16[2,257,1408]{2,1,0:T(8,128)(2,1)}, f32[2,1408]{1,0:T(2,128)}, f32[4,1408,768]{2,1,0:T(8,128)}, f32[4,3,88,256]{3,2,1,0:T(8,128)}) custom-call(bf16[2,3,2,264,768]{4,3,2,1,0:T(8,128)(2,1)} %get-tuple-element.59.d_half.d_qkv, bf16[4,1408,1536]{2,1,0:T(8,128)(2,1)} %bitcast.46, bf16[2,257,1408]{2,1,0:T(8,128)(2,1)} %copy.38.x, ...), custom_call_target="tpu_custom_call" | custom-call | tf_op jit(solution)/shard_map/in_back/pallas_call | solution.py:814
  432.9 3.6 collective-permute-start.1
  437.9 2.2 copy.53
  440.1 2.2 copy.52
  442.6 3.3 add_select_fusion
  445.9 5.3 scatter-add.4
  451.1 79.9 %scatter_wide.1 = f32[4,3,88,256]{3,2,1,0:T(8,128)} custom-call(f32[4,4,4,88,768]{4,3,2,1,0:T(8,128)} %bitcast.48), custom_call_target="tpu_custom_call" | custom-call | tf_op jit(solution)/shard_map/scatter_wide/pallas_call | solution.py:374
  531.0 1.4 slice_select_fusion.4
  532.8 4.7 collective-permute-start.2
  537.6 1.2 select_bitcast_fusion.1
  539.6 1.8 reshape_reshape.7
  (84 shorter events, 25.5 us)
Async XLA Ops:
  0.6 8.1 %copy-start.5 = (bf16[2,257,1408]{2,0,1:T(2,128)(2,1)S(1)}, bf16[2,257,1408]{2,0,1:T(2,128)(2,1)}, u32[]{:S(2)}) copy-start(bf16[2,257,1408]{2,0,1:T(2,128)(2,1)} %param.11) | copy-start | bytes 4342276
  5.0 8.8 %collective-permute-start = (bf16[2,44,768]{2,1,0:T(8,128)(2,1)S(1)}, bf16[2,44,768]{2,1,0:T(8,128)(2,1)S(1)}, u32[]{:S(2)}, u32[]{:S(2)}) collective-permute-start(bf16[2,44,768]{2,1,0:T(8,128)(2,1)S(1)} %broadcast_select_fusion.3), channel_id=1, source_target_pairs={{0,1},{1,0},{2,3},{3,2},{4,5},{5,4},{6,7},{7,6},{8,9},{9,8},{10,11... | collective-permute-start | bytes 405512 | tf_op jit(solution)/shard_map/ppermute | solution.py:873
  8.7 1.9 copy-start.6
  10.6 1.3 copy-start.10
  337.9 5.5 copy-start.7
  340.1 201.3 %collective-permute-start.4 = (f32[192,768]{1,0:T(8,128)}, f32[192,768]{1,0:T(8,128)}, u32[]{:S(2)}, u32[]{:S(2)}) collective-permute-start(f32[192,768]{1,0:T(8,128)} %bitcast.23), channel_id=1, source_target_pairs={{0,1},{1,0},{2,3},{3,2},{4,5},{5,4},{6,7},{7,6},{8,9},{9,8},{10,11... | collective-permute-start | bytes 1769480 | tf_op jit(solution)/shard_map/ppermute | solution.py:873
  343.4 89.1 %copy-start.9 = (f32[3,1408]{1,0:T(4,128)S(1)}, f32[3,1408]{1,0:T(4,128)}, u32[]{:S(2)}) copy-start(f32[3,1408]{1,0:T(4,128)} %get-tuple-element.67) | copy-start | bytes 50692
  343.4 89.2 %copy-start.8 = (f32[8,1,768]{2,1,0:T(1,128)S(1)}, f32[8,1,768]{2,1,0:T(1,128)}, u32[]{:S(2)}) copy-start(f32[8,1,768]{2,1,0:T(1,128)} %get-tuple-element.68) | copy-start | bytes 73732
  431.3 5.2 copy-start.1
  432.9 9.5 %collective-permute-start.1 = (f32[32,676]{1,0:T(8,128)S(1)}, f32[32,676]{1,0:T(8,128)S(1)}, u32[]{:S(2)}, u32[]{:S(2)}) collective-permute-start(f32[32,676]{1,0:T(8,128)S(1)} %pad_maximum_fusion.3), channel_id=1, source_target_pairs={{0,1},{1,0},{2,3},{3,2},{4,5},{5,4},{6,7},{7,6},{8,9},{9,8},{10,11... | collective-permute-start | bytes 259592 | tf_op jit(solution)/shard_map/ppermute | solution.py:873
  436.4 1.5 copy-start.4
  437.7 99.9 %collective-permute-start.3 = (f32[4,3,44,256]{3,0,2,1:T(4,128)}, f32[4,3,44,256]{3,0,2,1:T(4,128)}, u32[]{:S(2)}, u32[]{:S(2)}) collective-permute-start(f32[4,3,44,256]{3,0,2,1:T(4,128)} %copy.48), channel_id=1, source_target_pairs={{0,1},{1,0},{2,3},{3,2},{4,5},{5,4},{6,7},{7,6},{8,9},{9,8},{10,11... | collective-permute-start | bytes 1622024 | tf_op jit(solution)/shard_map/ppermute | solution.py:873
  437.9 2.2 copy-start.3
  531.0 6.5 %copy-start.2 = (f32[4,3,88,256]{3,2,1,0:T(8,128)S(1)}, f32[4,3,88,256]{3,2,1,0:T(8,128)}, u32[]{:S(2)}) copy-start(f32[4,3,88,256]{3,2,1,0:T(8,128)} %get-tuple-element.71) | copy-start | bytes 3244036
  532.8 11.9 %collective-permute-start.2 = (f32[4,3,44,256]{3,0,2,1:T(4,128)S(1)}, f32[4,3,44,256]{3,0,2,1:T(4,128)}, u32[]{:S(2)}, u32[]{:S(2)}) collective-permute-start(f32[4,3,44,256]{3,0,2,1:T(4,128)S(1)} %copy.44), channel_id=1, source_target_pairs={{0,1},{1,0},{2,3},{3,2},{4,5},{5,4},{6,7},{7,6},{8,9},{9,8},{10,11... | collective-permute-start | bytes 1622024 | tf_op jit(solution)/shard_map/ppermute | solution.py:873
  543.6 1.6 copy-start

commit v3 on v2

v3 whole, which is shorter than its diff:
```python
import functools
import math

import jax
import jax.numpy as jnp
from jax import lax
from jax.experimental import pallas as pl
from jax.experimental.pallas import tpu as pltpu
from jax.sharding import PartitionSpec as P

HEADS = 16
LN_EPS = 1e-5
D = 1408
FF = 6144
SEQ = 257
HEAD = D // HEADS
SCALE = HEAD ** -0.5
QCOLS = 1536
HALF = 768
OWN = 44
CHIP = 2 * OWN
LANES = 128
F32 = jnp.float32
BF16 = jnp.bfloat16
VMEM_LIMIT = 66 * 1000 * 1000
G1, C1, BO, S1, G2, C2, B2, S2 = range(8)
Q, K, V, O = range(4)
SEQS = (2, SEQ, D)
SEQ_PAIR = range(SEQS[0])
TAIL = 8
BODY = SEQ - 1
TOK = BODY + TAIL
TOKS = (2, TOK, D)
ROWS = 4 * TOK


def sds(dtype, *shape):
    return jax.ShapeDtypeStruct(shape, dtype)


MESH_ID = pl.DeviceIdType.MESH
SIDE = 4
PAIR = 2
C = 3
COLOURS = range(C)
COLOUR_DIMS = ("xyz", "yzx", "zxy")
FIRST, SECOND, THIRD, LAST = range(4)
WAYS = range(PAIR)
NEAR, FAR, ADDED = 0, 2, 4
WIDE, DOWN = "wide", "down"
ANY = pl.BlockSpec(memory_space=pl.ANY)
ALL = slice(None)


def duo(m):
    return pl.ds(PAIR * m, PAIR)


def toward(m):
    return 1 - PAIR * (m % PAIR)


class Torus:
    def __init__(self):
        f = lax.axis_index("fsdp")
        self.at = {"x": lax.axis_index("rep"), "z": lax.div(f, SIDE * PAIR), "y": lax.rem(lax.div(f, PAIR), SIDE),
                   "c": lax.rem(f, PAIR)}

    def shift(self, dim, by):
        return lax.rem(self.at[dim] + (SIDE + by), SIDE)

    def device(self, **moved):
        p = {**self.at, **moved}
        return (p["x"], (p["z"] * SIDE + p["y"]) * PAIR + p["c"])

    def neighbour(self, dim, by):
        return self.device(**{dim: self.shift(dim, by)})

    def partner(self):
        return self.device(c=1 - self.at["c"])


def enter():
    me = Torus()
    barrier = pltpu.get_barrier_semaphore()
    others = [me.neighbour(d, toward(m)) for d in COLOUR_DIMS[0] for m in WAYS] + [me.partner()]
    for other in others:
        pl.semaphore_signal(barrier, device_id=other, device_id_type=MESH_ID)
    pl.semaphore_wait(barrier, len(others))


def remote(src, dst, sems, slot, device):
    return pltpu.make_async_remote_copy(src_ref=src, dst_ref=dst, send_sem=sems[0].at[slot], recv_sem=sems[1].at[slot],
                                        device_id=device, device_id_type=MESH_ID)


class Gather:
    def __init__(self, kind, src, dst, hop_send, hop_recv, push_send, push_recv, local):
        self.kind, self.src, self.dst, self.local = kind, src, dst, local
        self.hops, self.pushes = (hop_send, hop_recv), (push_send, push_recv)
        self.cols, self.cut = (256, 128) if kind == WIDE else (D, HALF)

    @staticmethod
    def semaphores():
        dma = pltpu.SemaphoreType.DMA
        return [dma((C, C, ADDED))] * PAIR + [dma((C, ADDED + 1))] * PAIR + [dma((C,))]

    @staticmethod
    def shape(kind):
        return (SIDE,) * 3 + (CHIP, QCOLS) if kind == WIDE else (SIDE, SIDE, PAIR, SIDE, C, 16, D)

    def source(self, k):
        return self.src.at[:, pl.ds(self.cols * k, self.cols)] if self.kind == WIDE else self.src.at[k]

    def piece(self, me, k, s, v, half=None):
        dims = COLOUR_DIMS[k]
        at = {**me.at, **{d: ALL for d in dims[:s]}, dims[s]: v}
        off, width = 0, self.cols
        if half is not None and s == FIRST:
            off, width = self.cut * half, (self.cut, self.cols - self.cut)[half]
        elif half is not None:
            at[dims[0]] = duo(half)
        if self.kind == WIDE:
            cols = pl.ds(pl.multiple_of(at["c"] * HALF + self.cols * k + off, 128), width)
            return self.dst.at[at["x"], at["z"], at["y"], :, cols]
        return self.dst.at[at["z"], at["y"], at["c"], at["x"], k, :, pl.ds(off, width)]

    def hop(self, k, s, m):
        me = Torus()
        dim = COLOUR_DIMS[k][s]
        by = toward(m)
        if m < FAR:
            ref = self.piece(me, k, s, me.at[dim])
        else:
            ref = self.piece(me, k, s, me.shift(dim, -by), m - FAR)
        src = self.source(k) if s == FIRST and m < FAR else ref
        return remote(src, ref, self.hops, (k, s, m), me.neighbour(dim, by))

    def push(self, k, n):
        me = Torus()
        dim = COLOUR_DIMS[k][THIRD]
        if n < FAR:
            ref = self.piece(me, k, THIRD, me.shift(dim, -toward(n)))
        elif n < ADDED:
            ref = self.piece(me, k, THIRD, me.shift(dim, FAR), n - FAR)
        else:
            ref = self.piece(me, k, THIRD, me.at[dim])
        return remote(ref, ref, self.pushes, (k, n), me.partner())

    def own(self, k):
        me = Torus()
        return pltpu.make_async_copy(self.source(k), self.piece(me, k, FIRST, me.at[COLOUR_DIMS[k][FIRST]]), self.local.at[k])

    def launch(self, s):
        for k in COLOURS:
            for m in WAYS:
                self.hop(k, s, m).start()
            if s == THIRD:
                self.push(k, ADDED).start()

    def relay(self, k, s):
        for m in WAYS:
            self.hop(k, s, m).wait_recv()
            self.hop(k, s, FAR + m).start()
            if s == THIRD:
                self.push(k, m).start()

    def settle(self, s):
        for k in COLOURS:
            for m in WAYS:
                self.hop(k, s, FAR + m).wait_recv()
                if s == THIRD:
                    self.push(k, FAR + m).start()
            if s == FIRST:
                self.own(k).wait()
        if s < THIRD:
            self.launch(s + 1)

    def begin(self):
        for k in COLOURS:
            self.own(k).start()
        self.launch(FIRST)

    def finish(self):
        for k in COLOURS:
            for s in COLOURS:
                for m in range(ADDED):
                    self.hop(k, s, m).wait_send()
            for n in range(ADDED + 1):
                self.push(k, n).wait()

    def steps(self):
        out = [self.begin]
        for s in COLOURS:
            out += [functools.partial(self.relay, k, s) for k in COLOURS] + [functools.partial(self.settle, s)]
        return out + [self.finish]


def add_into(total, *others):
    lead = total.shape[:-2]

    def body(i, carry):
        idx = []
        for n in reversed(lead):
            idx.insert(0, lax.rem(i, n))
            i = lax.div(i, n)
        value = total[tuple(idx)]
        for other in others:
            value = value + other[tuple(idx)]
        total[tuple(idx)] = value
        return carry

    lax.fori_loop(0, math.prod(lead), body, 0)


class Ring:
    def __init__(self, s, terms, passed, relay, landing, send, recv, rows=None):
        self.s, self.terms, self.passed, self.relay, self.landing = s, terms, passed, relay, landing
        self.sems, self.rows = (send, recv), rows

    def zone(self, k, way, half):
        return self.landing.at[k, way, self.rows[half] if self.rows else duo(half)]

    def carried(self, ref, k, way):
        return ref.at[k, way, pl.ds(0, self.rows[way].size)] if self.rows else ref.at[k, way]

    def hop(self, k, m):
        me = Torus()
        dim = COLOUR_DIMS[k][self.s]
        way, by = m % PAIR, toward(m)
        if m < FAR:
            src, dst = self.terms(k, me.shift(dim, FAR), way), self.carried(self.relay, k, way)
        elif m < ADDED:
            src, dst = self.terms(k, me.shift(dim, by), 1 - way), self.zone(k, way, 1 - way)
        else:
            src, dst = self.carried(self.passed, k, way), self.zone(k, way, way)
        return remote(src, dst, self.sems, (k, m), me.neighbour(dim, by))

    def start(self, k, base):
        for m in WAYS:
            self.hop(k, base + m).start()

    def arrived(self, k, base):
        for m in WAYS:
            self.hop(k, base + m).wait_recv()

    def finish(self):
        for k in COLOURS:
            for m in range(ADDED + PAIR):
                self.hop(k, m).wait_send()

    @staticmethod
    def semaphores():
        return [pltpu.SemaphoreType.DMA((C, ADDED + PAIR))] * PAIR


UNITS = {WIDE: (CHIP, LANES), DOWN: (FF // 192, HALF // PAIR)}


def unit_array(kind, *lead):
    return lead + UNITS[kind]


class First:
    def __init__(self, kind, half, part, acc, own, passed, relay, landing, send, recv, load, store):
        self.kind, self.half, self.part, self.acc, self.own, self.passed = kind, half, part, acc, own, passed
        self.relay_in, self.landing, self.load_sem, self.store_sem = relay, landing, load, store
        self.ring = Ring(FIRST, self.terms, passed, relay, landing, send, recv)

    @staticmethod
    def scratch(kind):
        vm = lambda *lead: pltpu.VMEM(unit_array(kind, *lead), F32)
        dma = pltpu.SemaphoreType.DMA
        relays = [vm(C, PAIR, PAIR, SIDE)] * PAIR
        return [vm(C, SIDE, SIDE), *relays, vm(C, PAIR, SIDE, SIDE), *Ring.semaphores(), dma((C, C)), dma((C,))]

    @staticmethod
    def sums(kind):
        return sds(F32, *unit_array(kind, C, SIDE, SIDE))

    def terms(self, k, v, half=None):
        order = ORDERS[self.kind]
        at = {d: ALL for d in order}
        at[COLOUR_DIMS[k][FIRST]] = v
        if half is not None:
            at[rest_dims(self.kind, k)[0]] = duo(half)
        lead = tuple(at[d] for d in order)
        width = UNITS[self.kind][1]
        if self.kind == WIDE:
            return self.part.at[lead + (ALL, pl.ds(width * (PAIR * k + self.half), width))]
        return self.part.at[lead + (k, ALL, pl.ds(width * self.half, width))]

    def load(self, k, m):
        me = Torus()
        dim = COLOUR_DIMS[k][FIRST]
        if m in WAYS:
            src, dst = self.terms(k, me.shift(dim, toward(m)), m), self.passed.at[k, m]
        else:
            src, dst = self.terms(k, me.at[dim]), self.own.at[k]
        return pltpu.make_async_copy(src, dst, self.load_sem.at[k, m])

    def store(self, k):
        return pltpu.make_async_copy(self.own.at[k], self.acc.at[k], self.store_sem.at[k])

    def near(self):
        for k in COLOURS:
            self.ring.start(k, NEAR)

    def far(self):
        for k in COLOURS:
            self.ring.start(k, FAR)
        for m in COLOURS:
            for k in COLOURS:
                self.load(k, m).start()

    def relay(self):
        for k in COLOURS:
            self.ring.arrived(k, NEAR)
            for m in WAYS:
                self.load(k, m).wait()
                add_into(self.passed.at[k, m], self.relay_in.at[k, m])
            self.ring.start(k, ADDED)

    def settle(self, then=None):
        for k in COLOURS:
            self.load(k, FAR).wait()
            for base in (FAR, ADDED):
                self.ring.arrived(k, base)
            add_into(self.own.at[k], *(self.landing.at[k, m] for m in WAYS))
            if then is None:
                self.store(k).start()
            else:
                then(k)

    def finish(self):
        self.ring.finish()
        if self.acc is not None:
            for k in COLOURS:
                self.store(k).wait()


ORDERS = {WIDE: "xzy", DOWN: "zyx"}


def rest_dims(kind, k):
    return [d for d in ORDERS[kind] if d != COLOUR_DIMS[k][FIRST]]


class Rest:
    def __init__(self, kind, acc, result, own, relay2, in2, relay3, in3, *sems):
        self.kind, self.acc, self.own, self.result = kind, acc, own, result
        self.in2, self.in3, self.relay2, self.relay3, self.load_sem, self.store_sem = in2, in3, relay2, relay3, *sems[-2:]
        rows, cut = UNITS[kind][0], relay3.shape[2]
        cuts = pl.ds(0, cut), pl.ds(cut, rows - cut)
        self.second = Ring(SECOND, functools.partial(self.terms, acc), relay2, relay2, in2, *sems[:PAIR])
        third = lambda k, v, half=None: in2.at[(k, 0, v) + (() if half is None else (cuts[half],))]
        self.third = Ring(THIRD, third, relay3, relay3, in3, *sems[PAIR:2 * PAIR], rows=cuts)

    @staticmethod
    def scratch(kind):
        vm = lambda *lead: pltpu.VMEM(unit_array(kind, *lead), F32)
        rows, cols = UNITS[kind]
        dma = pltpu.SemaphoreType.DMA
        cut = (rows // TAIL + 1) // PAIR * TAIL
        return [vm(C, SIDE, SIDE), vm(C, PAIR, PAIR), vm(C, PAIR, SIDE), pltpu.VMEM((C, PAIR, cut, cols), F32), vm(C, PAIR),
                *Ring.semaphores(), *Ring.semaphores(), dma((C,)), dma((C,))]

    @staticmethod
    def sums(kind):
        return sds(F32, *unit_array(kind, C))

    def terms(self, ref, k, v, half=None):
        other = ALL if half is None else duo(half)
        return ref.at[(k, v, other) if rest_dims(self.kind, k)[0] == COLOUR_DIMS[k][SECOND] else (k, other, v)]

    def load(self, k):
        return pltpu.make_async_copy(self.acc.at[k], self.own.at[k], self.load_sem.at[k])

    def store(self, k):
        return pltpu.make_async_copy(self.in3.at[k, 0], self.result.at[k], self.store_sem.at[k])

    def send(self, k):
        for base in (NEAR, FAR):
            self.second.start(k, base)

    def begin(self):
        for k in COLOURS:
            self.send(k)
        for k in COLOURS:
            self.load(k).start()

    def loaded(self):
        for k in COLOURS:
            self.load(k).wait()

    def relay(self):
        me = Torus()
        for k in COLOURS:
            self.second.arrived(k, NEAR)
            for m in WAYS:
                add_into(self.relay2.at[k, m], self.terms(self.own, k, me.shift(COLOUR_DIMS[k][SECOND], toward(m)), m))
            self.second.start(k, ADDED)

    def settle(self):
        me = Torus()
        for k in COLOURS:
            for base in (FAR, ADDED):
                self.second.arrived(k, base)
            add_into(self.in2.at[k, 0], self.in2.at[k, 1], self.terms(self.own, k, me.at[COLOUR_DIMS[k][SECOND]]))
            for base in (NEAR, FAR):
                self.third.start(k, base)

    def relay_third(self):
        me = Torus()
        for k in COLOURS:
            self.third.arrived(k, NEAR)
            for m in WAYS:
                mine = self.third.carried(self.relay3, k, m)
                mine[...] += self.third.terms(k, me.shift(COLOUR_DIMS[k][THIRD], toward(m)), m)[...]
            self.third.start(k, ADDED)

    def settle_third(self):
        me = Torus()
        for k in COLOURS:
            for base in (FAR, ADDED):
                self.third.arrived(k, base)
            self.in3[k, 0] += self.in3[k, 1] + self.third.terms(k, me.at[COLOUR_DIMS[k][THIRD]])[...]
            if self.result is not None:
                self.store(k).start()

    def finish(self):
        self.second.finish()
        self.third.finish()
        if self.result is not None:
            for k in COLOURS:
                self.store(k).wait()


class Spread:
    def __init__(self, kind, result, total, send, recv, local):
        rows = UNITS[kind][0]
        cut = rows // TAIL // PAIR * TAIL
        self.result, self.total, self.sems, self.local = result, total, (send, recv), local
        self.cuts = pl.ds(0, cut), pl.ds(cut, rows - cut)

    @staticmethod
    def scratch():
        return [pltpu.SemaphoreType.DMA((C, ADDED))] * PAIR + [pltpu.SemaphoreType.DMA((C,))]

    @staticmethod
    def sums(kind):
        return sds(F32, *unit_array(kind, SIDE, C))

    def hop(self, k, m):
        me = Torus()
        by = toward(m)
        if m < FAR:
            src, dst = self.result.at[k], self.total.at[me.at["x"], k]
        else:
            dst = src = self.total.at[me.shift("x", -by), k, self.cuts[m - FAR]]
        return remote(src, dst, self.sems, (k, m), me.neighbour("x", by))

    def own(self, k):
        return pltpu.make_async_copy(self.result.at[k], self.total.at[Torus().at["x"], k], self.local.at[k])

    def begin(self):
        for k in COLOURS:
            self.own(k).start()
            for m in WAYS:
                self.hop(k, m).start()

    def forward(self):
        for k in COLOURS:
            for m in WAYS:
                self.hop(k, m).wait_recv()
                self.hop(k, FAR + m).start()

    def finish(self):
        for k in COLOURS:
            for m in WAYS:
                self.hop(k, FAR + m).wait_recv()
            self.own(k).wait()
            for m in range(ADDED):
                self.hop(k, m).wait_send()


def comm_params(collective_id):
    return pltpu.CompilerParams(collective_id=collective_id, has_side_effects=True, vmem_limit_bytes=VMEM_LIMIT)


def torus_gather(kind, piece, collective_id):
    def kernel(*refs):
        enter()
        for step in Gather(kind, *refs).steps():
            step()

    return pl.pallas_call(
        kernel, out_shape=sds(BF16, *Gather.shape(kind)), in_specs=[ANY], out_specs=ANY,
        scratch_shapes=Gather.semaphores(), compiler_params=comm_params(collective_id), name="gather_" + kind)(piece)


def last_scatter_kernel(part, acc_up, result_up, *refs):
    outs, refs = refs[:SIDE], list(refs[SIDE:])
    take = lambda like: [refs.pop(0) for _ in like]
    a, b = (First(WIDE, h, part, None, *take(First.scratch(WIDE))) for h in WAYS)
    rest_a, rest_b = (Rest(WIDE, f.own, None, f.own, *take(Rest.scratch(WIDE)[1:])) for f in (a, b))
    late = Rest(WIDE, acc_up, None, *take(Rest.scratch(WIDE)))
    results = [rest.in3.at[:, 0] for rest in (rest_a, rest_b, late)]
    spread_a, spread_b, spread_late, early = (
        Spread(WIDE, *pair, *take(Spread.scratch())) for pair in zip([*results, result_up], outs))
    enter()
    for step in (late.begin, early.begin, a.near, late.loaded, late.relay, a.far, early.forward, late.settle, a.relay, b.near,
                 late.relay_third, late.settle_third, b.far, late.finish, spread_late.begin,
                 functools.partial(a.settle, rest_a.send), b.relay, rest_a.relay, spread_late.forward, rest_a.settle,
                 rest_a.relay_third, functools.partial(b.settle, rest_b.send), rest_a.settle_third, rest_b.relay,
                 rest_a.finish, spread_a.begin, rest_b.settle, spread_a.forward, rest_b.relay_third, rest_b.settle_third,
                 rest_b.finish, spread_b.begin, spread_b.forward, early.finish, spread_late.finish, spread_a.finish,
                 spread_b.finish, a.finish, b.finish):
        step()


def last_scatter(part, acc_up, result_up, collective_id):
    return pl.pallas_call(
        last_scatter_kernel, out_shape=(Spread.sums(WIDE),) * SIDE, in_specs=[ANY] * O, out_specs=(ANY,) * SIDE,
        scratch_shapes=First.scratch(WIDE) * PAIR + Rest.scratch(WIDE)[1:] * PAIR + Rest.scratch(WIDE) +
        Spread.scratch() * SIDE,
        compiler_params=comm_params(collective_id), name="last_scatter")(part, acc_up, result_up)


class Background:
    def __init__(self, steps, plan):
        self.steps, self.plan = steps, plan

    def visit(self, place):
        for j, first, end in self.plan.get(place, ()):
            @at_step(j)
            def _():
                for step in self.steps[first:end]:
                    step()


class Pipeline:
    def __init__(self, places, first, rest=None, spread=None):
        rest_steps = (rest.loaded, rest.relay) if rest else ()
        groups = [[*((rest.begin,) if rest else ()), *((spread.begin,) if spread else ()), first.near],
                  [*rest_steps, first.far, *((spread.forward,) if spread else ())],
                  [*((rest.settle,) if rest else ()), first.relay],
                  [rest.relay_third] if rest else [],
                  [first.settle, *((rest.settle_third,) if rest else ()), first.finish, *((rest.finish,) if rest else ()),
                   *((spread.finish,) if spread else ())]]
        self.groups = list(zip([("start", 0), *places], groups))

    def visit(self, place):
        for (where, j), group in self.groups:
            if where == place:
                @at_step(j)
                def _():
                    for step in group:
                        step()


class Push:
    def __init__(self, src, tail, rows, sems, slot):
        body = BODY * len(SEQ_PAIR)
        tails = TAIL * len(SEQ_PAIR)
        self.copies = [
            remote(src.at[pl.ds(start, size)], rows.at[pl.ds(to, size)], sems, (slot, i), Torus().partner())
            for i, (start, to, size) in enumerate(((0, body, body), (tail, PAIR * body + tails, tails)))]

    @staticmethod
    def semaphores(n):
        return [pltpu.SemaphoreType.DMA((n, PAIR))] * PAIR

    def start(self):
        for copy in self.copies:
            copy.start()

    def wait(self):
        for copy in self.copies:
            copy.wait_recv()

    def finish(self):
        for copy in self.copies:
            copy.wait_send()


class Exchange:
    def __init__(self, mine, theirs, rows, sems, slot):
        self.moves = []
        for s in SEQ_PAIR:
            for i, (start, size) in enumerate(((0, BODY), (BODY, TAIL))):
                place = lambda n: rows.at[pl.ds(start * len(SEQ_PAIR) * PAIR + size * n, size)]
                n = len(SEQ_PAIR) + s
                at = slot + (PAIR * s + i,)
                local = pltpu.make_async_copy(mine.at[s, pl.ds(start, size)], place(s), sems[2].at[at])
                far = remote(theirs.at[s, pl.ds(start, size)], place(n), sems, at, Torus().partner())
                self.moves.append((local, far))

    @staticmethod
    def semaphores(*lead):
        return [pltpu.SemaphoreType.DMA(lead + (2 * PAIR,))] * 3

    def start(self):
        for local, far in self.moves:
            far.start()
            local.start()

    def wait(self):
        for local, far in self.moves:
            local.wait()
            far.wait_recv()

    def finish(self):
        for _, far in self.moves:
            far.wait_send()


NT = (((1,), (1,)), ((), ()))
TN = (((0,), (0,)), ((), ()))


def dot(a, b):
    return jnp.dot(a, b, preferred_element_type=F32)


def dot_nt(a, b):
    return lax.dot_general(a, b, NT, preferred_element_type=F32)


def dot_tn(a, b):
    return lax.dot_general(a, b, TN, preferred_element_type=F32)


def zeros_but(n, axis, value):
    return tuple(value if i == axis else 0 for i in range(n))


def whole(*shape):
    return pl.BlockSpec(shape, lambda *_: (0,) * len(shape))


def along(axis, *block, index=lambda j: j):
    return pl.BlockSpec(block, lambda j: zeros_but(len(block), axis, index(j)))


def row(vec, i):
    return vec[i:i + 1]


def row_mean(t):
    return jnp.mean(t, axis=-1, keepdims=True)


def norm_stats(t):
    centered = t - row_mean(t)
    rstd = lax.rsqrt(row_mean(centered * centered) + LN_EPS)
    return centered * rstd, rstd


def norm_back(xhat, rstd, g):
    return rstd * (g - row_mean(g) - xhat * row_mean(g * xhat))


def col_sum(t):
    return jnp.sum(t, axis=0, keepdims=True)


def at_step(j):
    return pl.when(pl.program_id(0) == j)


def accumulate(ref, value):
    @at_step(0)
    def _():
        ref[...] = value

    @pl.when(pl.program_id(0) > 0)
    def _():
        ref[...] += value


def pad(t):
    return jnp.concatenate([t.astype(F32), jnp.zeros((TOK - SEQ, t.shape[1]), F32)], axis=0).astype(BF16)


def window(h):
    start = h * HEAD // LANES * LANES
    stop = min(D, -(-(h + 1) * HEAD // LANES) * LANES)
    lane = lax.broadcasted_iota(jnp.int32, (1, stop - start), 1) + (start - h * HEAD)
    return slice(start, stop), (lane >= 0) & (lane < HEAD)


def only(mask, t):
    return jnp.where(mask, t, jnp.zeros_like(t))


def softmax(scores):
    e = jnp.exp(scores - jnp.max(scores, axis=-1, keepdims=True))
    return e * (1.0 / jnp.sum(e, axis=-1, keepdims=True))


def attention(s, rows, x, w_out, vec, o, att, h2, acc, visit):
    acc[...] = jnp.zeros_like(acc)
    for h in range(HEADS):
        lanes, mask = window(h)
        k = only(mask, rows[K, s, :, lanes])
        v = only(mask, rows[V, s, :, lanes])
        probs = softmax(dot_nt(rows[Q, s, :, lanes], k) * SCALE).astype(BF16)
        acc[:, lanes] += dot(probs, v)
        visit(h)
    heads = acc[...]
    o[0] = pad(heads)
    a = dot(heads.astype(BF16), w_out[0]) + row(vec, BO)
    att[0] = a
    xhat, _ = norm_stats(x[s].astype(F32) + row(vec, S1) * a)
    h2[0] = pad(xhat * row(vec, G2) + row(vec, C2))


FRONT_PLAN = {"qkv": ((0, 0, 1), (1, 1, 5), (2, 5, 8)), 2: ((O, 8, 9),), "end": ((O + 1, 9, None),)}


def front_kernel(x, w, b, vec, up_src, qkv, h1, o, att, h2, up, rows, acc, *sems):
    hosted = Background(Gather(WIDE, up_src, up, *sems).steps(), FRONT_PLAN)
    j = pl.program_id(0)
    at_step(0)(enter)
    hosted.visit("qkv")

    @at_step(0)
    def _():
        for s in SEQ_PAIR:
            xhat, _ = norm_stats(x[s].astype(F32))
            h1[s] = pad(xhat * row(vec, G1) + row(vec, C1))

    @pl.when(j < O)
    def _():
        for s in SEQ_PAIR:
            t = (dot(h1[s, :SEQ], w[0]) + b[0]).astype(BF16)
            qkv[0, s] = t
            rows[j, s] = t

    @pl.when(j >= O)
    def _():
        attention(j - O, rows, x, w, vec, o, att, h2, acc, hosted.visit)

    hosted.visit("end")


def front_call(x, w_attn, b_qkv, vec, up, collective_id):
    upto = lambda n: lambda j: jnp.minimum(j, n)
    seq = lambda tokens: along(0, 1, tokens, D, index=lambda j: jnp.maximum(j - O, 0))
    return pl.pallas_call(
        front_kernel, grid=(O + PAIR,),
        out_shape=(sds(BF16, O, *SEQS), sds(BF16, *TOKS), sds(BF16, *TOKS), sds(F32, *SEQS), sds(BF16, *TOKS),
                   sds(BF16, *Gather.shape(WIDE))),
        in_specs=[whole(*SEQS), along(0, 1, D, D, index=upto(O)), along(0, 1, 1, D, index=upto(V)), whole(8, D), ANY],
        out_specs=(along(0, 1, *SEQS, index=upto(V)), whole(*TOKS), seq(TOK), seq(SEQ), seq(TOK), ANY),
        scratch_shapes=[pltpu.VMEM((O, *SEQS), BF16), pltpu.VMEM((SEQ, D), F32)] + Gather.semaphores(),
        compiler_params=comm_params(collective_id), name="front",
    )(x, w_attn, b_qkv, vec, up)


def w_out_block():
    return along(0, 1, D, D, index=lambda j: O)


TILES = FF // HALF
OWN_BODY = BODY * len(SEQ_PAIR)
TAILS = ROWS - TAIL * PAIR * len(SEQ_PAIR)


def put_rows(ref, tail, s, t):
    ref[pl.ds(BODY * s, BODY)] = t[:BODY]
    ref[pl.ds(tail + TAIL * s, TAIL)] = t[BODY:]


DOWN_PLAN = {"start": ((0, 0, 1),), "end": ((1, 1, 5), (3, 5, 8), (5, 8, 9), (TILES + 4, 9, 12), (2 * TILES - 1, 12, None))}


def mlp_in_kernel(h2, gz, w_up, b_up, vec, src, act, slope, d_down, down, a_rows, b_rows, b_away, *sems):
    a_sems, b_sems, sems = sems[:PAIR], sems[PAIR:2 * PAIR], sems[2 * PAIR:]
    hosted = Background(Gather(DOWN, src, down, *sems).steps(), DOWN_PLAN)
    j = pl.program_id(0)
    away = Push(b_away, OWN_BODY, b_rows, b_sems, 0)
    tile = lambda n: Push(a_rows.at[n], TAILS, a_rows.at[n], a_sems, n)
    at_step(0)(enter)
    hosted.visit("start")

    @at_step(0)
    def _():
        first = Torus().at["c"] == 0
        for s in SEQ_PAIR:
            d = pad(gz[s].astype(F32) * row(vec, S2))
            left, right = d[:, :HALF], d[:, D - HALF:]
            put_rows(b_rows, TAILS, s, jnp.where(first, left, right))
            put_rows(b_away, OWN_BODY, s, jnp.where(first, right, left))

    at_step(1)(away.start)
    for n in range(TILES):
        at_step(n + 1)(tile(n).start)

    @pl.when(j < TILES)
    def _():
        for s in SEQ_PAIR:
            u = dot(h2[s, :SEQ], w_up[0]) + b_up[0]
            phi = 0.5 * (1.0 + lax.erf(u * math.sqrt(0.5)))
            slope[s] = phi + u * (jnp.exp(-0.5 * u * u) * math.sqrt(0.5 / math.pi))
            a = pad(u * phi)
            act[s] = a
            put_rows(a_rows.at[j], TAILS, s, a)

    at_step(TILES)(away.wait)
    for n in range(TILES):
        at_step(TILES + n)(tile(n).wait)

    @pl.when(j >= TILES)
    def _():
        d_down[...] = dot_tn(a_rows[j - TILES], b_rows[...])

    hosted.visit("end")

    @at_step(2 * TILES - 1)
    def _():
        away.finish()
        for n in range(TILES):
            tile(n).finish()


def mlp_in_call(h2, gz, w_up, b_up, vec, down, collective_id):
    low = lambda j: jnp.minimum(j, TILES - 1)
    high = lambda j: jnp.maximum(j - TILES, 0)
    return pl.pallas_call(
        mlp_in_kernel, grid=(2 * TILES,),
        out_shape=(sds(BF16, 2, TOK, FF), sds(F32, 2, SEQ, FF), sds(F32, FF, HALF), sds(BF16, *Gather.shape(DOWN))),
        in_specs=[whole(*TOKS), whole(*SEQS), up_tile(low), along(0, 1, 1, HALF, index=low), whole(8, D), ANY],
        out_specs=(along(2, 2, TOK, HALF, index=low), along(2, 2, SEQ, HALF, index=low),
                   along(0, HALF, HALF, index=high), ANY),
        scratch_shapes=[pltpu.VMEM((TILES, ROWS, HALF), BF16), pltpu.VMEM((ROWS, HALF), BF16),
                        pltpu.VMEM((PAIR * TOK, HALF), BF16)] + Push.semaphores(TILES) + Push.semaphores(1) +
        Gather.semaphores(),
        compiler_params=comm_params(collective_id), name="mlp_in",
    )(h2, gz, w_up, b_up.reshape(TILES, 1, HALF), vec, down)


def up_tile(index=lambda j: j):
    return pl.BlockSpec((1, D, HALF), lambda j: (index(j) // PAIR, 0, index(j) % PAIR))


MLP_PLACES = (("end", 0), ("end", 2), ("end", 3), ("end", TILES - 1))


def mlp_out_kernel(act, slope, gz, w_up, w_down, vec, part, d_pre, db_up, mlp, d_h2, sums, dm, *scratch):
    hosted = Pipeline(MLP_PLACES, First(DOWN, 0, part, sums, *scratch))
    at_step(0)(enter)
    hosted.visit("start")

    @at_step(0)
    def _():
        for s in SEQ_PAIR:
            dm[s] = (gz[s].astype(F32) * row(vec, S2)).astype(BF16)

    db = jnp.zeros((1, HALF), F32)
    for s in SEQ_PAIR:
        accumulate(mlp.at[s], dot(act[s, :SEQ], w_down[...]))
        d = dot_nt(dm[s], w_down[...]) * slope[s]
        db = db + col_sum(d)
        d_pre[0, 0, s] = pad(d)
        accumulate(d_h2.at[s], dot_nt(d.astype(BF16), w_up[0]))
    db_up[0] = db
    hosted.visit("end")


def mlp_out_call(act, slope, gz, w_up, w_down, vec, part, collective_id):
    return pl.pallas_call(
        mlp_out_kernel, grid=(TILES,),
        out_shape=(sds(BF16, 2, 4, 2, TOK, HALF), sds(F32, TILES, 1, HALF), sds(F32, *SEQS), sds(F32, *SEQS),
                   First.sums(DOWN)),
        in_specs=[along(2, 2, TOK, HALF), along(2, 2, SEQ, HALF), whole(*SEQS), up_tile(), along(0, HALF, D), whole(8, D),
                  ANY],
        out_specs=(pl.BlockSpec((1, 1, 2, TOK, HALF), lambda j: (j % PAIR, j // PAIR, 0, 0, 0)), along(0, 1, 1, HALF),
                   whole(*SEQS), whole(*SEQS), ANY),
        scratch_shapes=[pltpu.VMEM(SEQS, BF16)] + First.scratch(DOWN),
        compiler_params=comm_params(collective_id), name="mlp_out",
    )(act, slope, gz, w_up, w_down, vec, part)


def halves_of(t):
    t = pad(t)
    return t[:, :HALF], jnp.concatenate([t[:, HALF:], jnp.zeros((TOK, QCOLS - D), BF16)], axis=1)


def mid(mlp, d_h2, att, x, gz, vec, w_out, z, g_res, d_att, d_o, sums):
    a = att[0]
    y = x[0].astype(F32) + row(vec, S1) * a
    m = mlp[0] + row(vec, B2)
    g = gz[0].astype(F32)
    z[0] = (y + row(vec, S2) * m).astype(BF16)
    xhat, rstd = norm_stats(y)
    dh = d_h2[0]
    gr = g + norm_back(xhat, rstd, dh * row(vec, G2))
    g_res[0] = gr
    da = gr * row(vec, S1)
    terms = (da, gr * a, dh * xhat, dh, g * row(vec, S2), g * m)
    accumulate(sums, jnp.concatenate([jnp.zeros((BO, D), F32)] + [col_sum(t) for t in terms], axis=0))
    for i, t in enumerate(halves_of(da)):
        d_att[i, 0] = t
    d_o[0] = dot_nt(da.astype(BF16), w_out[0]).astype(BF16)


def attention_back(qkv, d_o, d_qkv, db, acc, visit):
    acc[...] = jnp.zeros_like(acc)
    for h in range(HEADS):
        lanes, mask = window(h)
        q, k, v = (only(mask, qkv[i, 0, :, lanes]) for i in (Q, K, V))
        do = only(mask, d_o[0, :, lanes])
        probs = softmax(dot_nt(q, k) * SCALE)
        acc[V, :, lanes] += dot_tn(probs.astype(BF16), do)
        dp = dot_nt(do, v)
        ds = probs * (dp - jnp.sum(dp * probs, axis=-1, keepdims=True))
        ds = (ds * SCALE).astype(BF16)
        acc[Q, :, lanes] += dot(ds, k)
        acc[K, :, lanes] += dot_tn(ds, q)
        visit(h)
    accumulate(db, jnp.concatenate([col_sum(acc[i]) for i in (Q, K, V)], axis=0))
    for n in (Q, K, V):
        for i, t in enumerate(halves_of(acc[n])):
            d_qkv[i, n, 0] = t


THIN = HALF // PAIR


class WideGrads:
    def __init__(self, a, a_of, b, out, base, a_rows, b_rows, *sems):
        self.a, self.a_of, self.b, self.out, self.base, self.a_rows, self.b_rows = a, a_of, b, out, base, a_rows, b_rows
        self.a_sems, self.b_sems = sems[:3], sems[3:]

    @staticmethod
    def scratch(inputs):
        return ([pltpu.VMEM((inputs, ROWS, D), BF16), pltpu.VMEM((SIDE, ROWS, HALF), BF16)] +
                Exchange.semaphores(inputs) + Exchange.semaphores(SIDE))

    def input(self, i):
        return Exchange(self.a[i], self.a[i], self.a_rows.at[i], self.a_sems, (i,))

    def cotangent(self, n):
        c = Torus().at["c"]
        b = self.b[n]
        return Exchange(b(c), b(1 - c), self.b_rows.at[n], self.b_sems, (n,))

    def begin(self):
        for n in range(SIDE):
            if n == 0 or self.a_of[n] != self.a_of[n - 1]:
                self.input(self.a_of[n]).start()
            self.cotangent(n).start()

    def step(self):
        j = pl.program_id(0)
        for n in range(SIDE):
            @at_step(self.base + PAIR * n)
            def _():
                if n == 0 or self.a_of[n] != self.a_of[n - 1]:
                    self.input(self.a_of[n]).wait()
                self.cotangent(n).wait()

        @pl.when(j >= self.base)
        def _():
            n = lax.div(j - self.base, PAIR)
            cols = pl.ds(pl.multiple_of(lax.rem(j - self.base, PAIR) * THIN, LANES), THIN)
            a = self.a_rows[0 if len(self.a) == 1 else lax.div(n, O)]
            self.out[0] = dot_tn(a, self.b_rows[n, :, cols])

    def finish(self):
        for i in range(len(self.a)):
            self.input(i).finish()
        for n in range(SIDE):
            self.cotangent(n).finish()


def grads_block(base):
    def index(j):
        n = jnp.maximum(j - base, 0)
        return n // PAIR, 0, n % PAIR

    return pl.BlockSpec((1, D, THIN), index)


LAST_SEQ = SEQS[0] - 1
GRAD_STEPS = PAIR * SIDE


def upto(n):
    return lambda j: jnp.minimum(j, n)


def seq_block(tokens=SEQ):
    return along(0, 1, tokens, D, index=upto(LAST_SEQ))


MID_PLACES = (("end", 0), ("end", 3), ("end", 7), ("end", LAST_SEQ + GRAD_STEPS))


def mid_kernel(*refs):
    refs = list(refs)
    take = lambda n: [refs.pop(0) for _ in range(n)]
    ins, (h2, d_pre, part, acc), outs, (d_up, sums, result) = take(7), take(4), take(5), take(3)
    grads = WideGrads((h2,), (0,) * SIDE, [lambda c, i=i: d_pre.at[c, i] for i in range(SIDE)], d_up, SEQS[0],
                      *take(len(WideGrads.scratch(1))))
    first = First(DOWN, 1, part, sums, *take(len(First.scratch(DOWN))))
    hosted = Pipeline(MID_PLACES, first, Rest(DOWN, acc, result, *refs))
    at_step(0)(enter)
    hosted.visit("start")
    at_step(0)(grads.begin)
    pl.when(pl.program_id(0) < SEQS[0])(lambda: mid(*ins, *outs))
    grads.step()
    hosted.visit("end")
    at_step(LAST_SEQ + GRAD_STEPS)(grads.finish)


def mid_call(mlp, d_h2, att, x, gz, vec, w_attn, h2, d_pre, part, acc, collective_id):
    return pl.pallas_call(
        mid_kernel, grid=(SEQS[0] + GRAD_STEPS,),
        out_shape=(sds(BF16, *SEQS), sds(F32, *SEQS), sds(BF16, 2, 2, TOK, HALF), sds(BF16, *SEQS), sds(F32, 8, D),
                   sds(F32, SIDE, D, HALF), First.sums(DOWN), Rest.sums(DOWN)),
        in_specs=[seq_block()] * len("mdaxg") + [whole(8, D), w_out_block()] + [ANY] * SIDE,
        out_specs=(seq_block(), seq_block(), along(1, 2, 1, TOK, HALF, index=upto(LAST_SEQ)), seq_block(), whole(8, D),
                   grads_block(SEQS[0]), ANY, ANY),
        scratch_shapes=WideGrads.scratch(1) + First.scratch(DOWN) + Rest.scratch(DOWN),
        compiler_params=comm_params(collective_id), name="mid",
    )(mlp, d_h2, att, x, gz, vec, w_attn, h2, d_pre, part, acc)


ATTN_PLACES = ((6, 0), (1, LAST_SEQ), (11, LAST_SEQ), ("end", LAST_SEQ))


def attn_back_kernel(qkv, d_o, part, acc_down, result_down, d_qkv, db, sums, result, total, acc, *scratch):
    n, m = len(First.scratch(WIDE)), len(Rest.scratch(DOWN))
    hosted = Pipeline(ATTN_PLACES, First(WIDE, 0, part, sums, *scratch[:n]),
                      Rest(DOWN, acc_down, result, *scratch[n:n + m]), Spread(DOWN, result_down, total, *scratch[n + m:]))
    at_step(0)(enter)
    hosted.visit("start")
    attention_back(qkv, d_o, d_qkv, db, acc, hosted.visit)
    hosted.visit("end")


def attn_back_call(qkv, d_o, part, acc_down, result_down, collective_id):
    return pl.pallas_call(
        attn_back_kernel, grid=SEQS[:1],
        out_shape=(sds(BF16, 2, O, 2, TOK, HALF), sds(F32, O, D), First.sums(WIDE), Rest.sums(DOWN), Spread.sums(DOWN)),
        in_specs=[along(1, O, 1, SEQ, D), seq_block()] + [ANY] * O,
        out_specs=(along(2, 2, O, 1, TOK, HALF), whole(O, D)) + (ANY,) * O,
        scratch_shapes=[pltpu.VMEM((O, SEQ, D), F32)] + First.scratch(WIDE) + Rest.scratch(DOWN) + Spread.scratch(),
        compiler_params=comm_params(collective_id), name="attn_back",
    )(qkv, d_o, part, acc_down, result_down)


IN_STEPS = PAIR * O
IN_PLACES = (("end", 1), ("end", IN_STEPS - 1), ("end", IN_STEPS + O), ("end", IN_STEPS + GRAD_STEPS - 1))


def in_back_kernel(*refs):
    refs = list(refs)
    take = lambda n: [refs.pop(0) for _ in range(n)]
    (d_half, w, x, g_res, vec), (h1, o, d_qkv, d_att, part, acc_up, result_down) = take(5), take(7)
    (dx, sums, d_attn), outs, acc = take(3), take(3), refs.pop(0)
    b = [lambda c, i=i: d_qkv.at[c, i] for i in range(O)] + [lambda c: d_att.at[c]]
    grads = WideGrads((h1, o), (0,) * O + (1,), b, d_attn, IN_STEPS, *take(len(WideGrads.scratch(2))))
    first = First(WIDE, 1, part, outs[0], *take(len(First.scratch(WIDE))))
    rest = Rest(WIDE, acc_up, outs[1], *take(len(Rest.scratch(WIDE))))
    hosted = Pipeline(IN_PLACES, first, rest, Spread(DOWN, result_down, outs[2], *refs))
    at_step(0)(enter)
    hosted.visit("start")
    at_step(0)(grads.begin)

    @pl.when(pl.program_id(0) < IN_STEPS)
    def _():
        for s in SEQ_PAIR:
            accumulate(acc.at[s], dot_nt(d_half[0, 0, s, :SEQ], w[0]))

    @at_step(IN_STEPS - 1)
    def _():
        rows = jnp.zeros((BO, D), F32)
        for s in SEQ_PAIR:
            xhat, rstd = norm_stats(x[s].astype(F32))
            dh = acc[s]
            rows = rows + jnp.concatenate([col_sum(dh * xhat), col_sum(dh)], axis=0)
            dx[s] = (g_res[s] + norm_back(xhat, rstd, dh * row(vec, G1))).astype(BF16)
        sums[...] = rows

    grads.step()
    hosted.visit("end")
    at_step(IN_STEPS + GRAD_STEPS - 1)(grads.finish)


def in_back_call(d_qkv, w_attn, x, g_res, vec, h1, o, d_att, part, acc_up, result_down, collective_id):
    low = upto(IN_STEPS - 1)
    return pl.pallas_call(
        in_back_kernel, grid=(IN_STEPS + GRAD_STEPS,),
        out_shape=(sds(BF16, *SEQS), sds(F32, BO, D), sds(F32, SIDE, D, HALF), First.sums(WIDE), Rest.sums(WIDE),
                   Spread.sums(DOWN)),
        in_specs=[pl.BlockSpec((1, 1, 2, TOK, HALF), lambda j: (low(j) % PAIR, low(j) // PAIR, 0, 0, 0)), up_tile(low),
                  whole(*SEQS), whole(*SEQS), whole(8, D)] + [ANY] * 7,
        out_specs=(whole(*SEQS), whole(BO, D), grads_block(IN_STEPS), ANY, ANY, ANY),
        scratch_shapes=[pltpu.VMEM(SEQS, F32)] + WideGrads.scratch(2) + First.scratch(WIDE) + Rest.scratch(WIDE) +
        Spread.scratch(),
        compiler_params=comm_params(collective_id), name="in_back",
    )(d_qkv, w_attn, x, g_res, vec, h1, o, d_qkv, d_att, part, acc_up, result_down)


BQ, BU, VEC = 3 * D // 32, 3 * D // 32 + FF // 32, 3 * D // 32 + FF // 32 + 8 * OWN
DEVICES = 32


def pair_swap(a):
    return lax.ppermute(a, "fsdp", [(i, i ^ 1) for i in range(DEVICES)])


def by_core(first, a, b):
    return jnp.where(first, a, b), jnp.where(first, b, a)


def my_pieces(shards, first):
    w_qkv, b_qkv, w_out, w_up, b_up, w_down, vec_params = shards
    x = lax.axis_index("rep")
    small = jnp.concatenate([b_qkv, b_up, vec_params.reshape(-1)])
    small = jnp.pad(small, (0, OWN * LANES - VEC)).reshape(OWN, LANES)
    attn = lax.dynamic_slice_in_dim(jnp.concatenate([w_qkv, w_out], axis=1), x * D, D, 1)
    attn = jnp.concatenate([attn, small], axis=1)
    up = lax.dynamic_slice_in_dim(w_up, x * QCOLS, QCOLS, 1)
    wide = jnp.stack([attn, up]).astype(BF16)
    mine, theirs = by_core(first, wide[..., :HALF], wide[..., HALF:])
    theirs = pair_swap(theirs)
    piece = jnp.concatenate(by_core(first, mine, theirs), axis=1)
    down = lax.dynamic_slice_in_dim(w_down, x * 48, 48, 0).astype(BF16).reshape(3, 16, D)
    return piece[0], piece[1], down


def small_params(w_attn):
    small = w_attn[0, :, D:].astype(F32).reshape(DEVICES, OWN * LANES)
    vec = small[:, BU:VEC].reshape(DEVICES, 8, OWN).transpose(1, 0, 2).reshape(8, D)
    return small[:, :BQ].reshape(O, 1, D), small[:, BQ:BU].reshape(FF), vec


def small_grads(db_qkv, db_up, sums, core):
    vec = sums.reshape(8, DEVICES, OWN).transpose(1, 0, 2).reshape(DEVICES, VEC - BU)
    small = jnp.concatenate([db_qkv.reshape(DEVICES, BQ), db_up.reshape(DEVICES, BU - BQ), vec], axis=1)
    small = (small + pair_swap(small)) * core.astype(F32)
    return jnp.pad(small, ((0, 0), (0, OWN * LANES - VEC))).reshape(D, LANES)


def final_rows(halves, first):
    total = jnp.stack(halves, axis=2)
    keep, give = by_core(first, total[..., :OWN, :], total[..., OWN:, :])
    pair = jnp.stack(by_core(first, keep, pair_swap(give)), axis=1)
    return pair.transpose(4, 0, 1, 2, 3, 5).reshape(OWN, SIDE, QCOLS)


def final_down(halves, first):
    down = jnp.concatenate(halves, axis=-1).reshape(FF // 16, HALF)
    keep, give = by_core(first, down[:FF // DEVICES], down[FF // DEVICES:])
    left, right = by_core(first, keep, pair_swap(give))
    return jnp.concatenate([left, right[:, 2 * HALF - D:]], axis=1)


def device_step(x, gz, *shards):
    core = lax.rem(lax.axis_index("fsdp"), PAIR)
    first = core == 0
    attn, up, down = my_pieces(shards, first)
    w_attn = torus_gather(WIDE, attn, 0).reshape(SIDE, D, QCOLS)
    b_qkv, b_up, vec = small_params(w_attn)
    qkv, h1, o, att, h2, w_up = front_call(x, w_attn, b_qkv, vec, up, 1)
    w_up = w_up.reshape(SIDE, D, QCOLS)
    act, slope, part, w_down = mlp_in_call(h2, gz, w_up, b_up, vec, down, 2)
    part = part.reshape((SIDE,) * 3 + (C, 32, HALF))
    d_pre, db_up, mlp, d_h2, acc0 = mlp_out_call(act, slope, gz, w_up, w_down.reshape(FF, D), vec, part, 3)
    z, g_res, d_att, d_o, sums, part, acc1, result0 = mid_call(mlp, d_h2, att, x, gz, vec, w_attn, h2, d_pre, part, acc0, 4)
    part = part.reshape((SIDE,) * 3 + (CHIP, HALF))
    d_qkv, db_qkv, acc0, result1, down0 = attn_back_call(qkv, d_o, part, acc1, result0, 5)
    dx, in_sums, part, acc1, result0, down1 = in_back_call(d_qkv, w_attn, x, g_res, vec, h1, o, d_att, part, acc0, result1, 6)
    small = small_grads(db_qkv, db_up, jnp.concatenate([in_sums, sums[BO:]], axis=0), core)
    part = part.at[0, :, HALF - LANES:].add(small).reshape((SIDE,) * 3 + (CHIP, HALF))
    attn0, attn1, up1, up0 = last_scatter(part, acc1, result0, 7)
    g_up = final_rows((up0, up1), first).reshape(OWN, FF)
    attn = final_rows((attn0, attn1), first)
    small = attn[:, 0, D:].reshape(OWN * LANES)
    return (z, dx, attn[:, :O, :D].reshape(OWN, O * D), small[:BQ], attn[:, O, :D], g_up, small[BQ:BU],
            final_down((down0, down1), first), small[BU:VEC].reshape(8, OWN))


def solution(mesh):
    batch = P(("rep", "fsdp"), None, None)
    rows, flat, cols = P("fsdp", None), P("fsdp"), P(None, "fsdp")
    shards = (rows, flat, rows, rows, flat, rows, cols)
    return jax.shard_map(device_step, mesh=mesh, in_specs=(batch, batch) + shards,
                         out_specs=(batch, batch) + shards, check_vma=False)
```

time: 556 us -> 546 us (0.982); the launches traced: 553 us -> 536 us
  Pallas kernels: 487 us -> 469 us
    pallas_call x1, Pallas kernels: 85.8 us -> 54.2 us  [front_call(): pl.pallas_call(front_kernel, grid=(O + PAIR,), out_shape=(sds(BF16, O, *S...]
    pallas_call x6, Pallas kernels: 350 us -> 363 us  [the longest x1 99.5 us: last_scatter(): pl.pallas_call(last_scatter_kernel, out_shape=(Spread.sums(WIDE),) * SIDE...]
    unnamed x29 -> x34, local copies, waits for them, and re-layouts: 10.1 us -> 11.4 us
  transfers between devices with their start and end apart: 5 -> 5, of which waited for: 0 -> 0; matrix products, arithmetic and copies ran while one was open for 6% -> 6% of each run, Pallas kernels for 30% -> 19%
where the time goes in v3:
time: 546 us; the launch traced here: 536 us
  Pallas kernels  469 us (86%)
  local copies, waits for them, and re-layouts  31.4 us (6%)
  other arithmetic  21 us (4%)
  starting transfers between devices  13.4 us (2%)
    pallas_call x1, Pallas kernels, last_scatter(): pl.pallas_call(last_scatter_kernel, out_shape=(Spread.sums(WIDE),) * SIDE...  99.5 us
    pallas_call x1, Pallas kernels, mlp_out_call(): pl.pallas_call(mlp_out_kernel, grid=(TILES,), out_shape=(sds(BF16, 2, 4,...  59.4 us
    pallas_call x1, Pallas kernels, mlp_in_call(): pl.pallas_call(mlp_in_kernel, grid=(2 * TILES,), out_shape=(sds(BF16, 2,...  55.4 us
    pallas_call x1, Pallas kernels, attn_back_call(): pl.pallas_call(attn_back_kernel, grid=SEQS[:1], out_shape=(sds(BF16, 2, O...  54.6 us
    pallas_call x1, Pallas kernels, front_call(): pl.pallas_call(front_kernel, grid=(O + PAIR,), out_shape=(sds(BF16, O, *S...  54.2 us
    pallas_call x1, Pallas kernels, torus_gather(): pl.pallas_call(kernel, out_shape=sds(BF16, *Gather.shape(kind)), in_specs...  51.8 us
    pallas_call x1, Pallas kernels, in_back_call(): pl.pallas_call(in_back_kernel, grid=(IN_STEPS + GRAD_STEPS,), out_shape=(...  47.8 us
    pallas_call x1, Pallas kernels, mid_call(): pl.pallas_call(mid_kernel, grid=(SEQS[0] + GRAD_STEPS,), out_shape=(sds(B...  46.5 us
  transfers between devices with their start and end apart: 5, of which 0 were waited for; matrix products, arithmetic and copies ran while one was open for 6% of the time, Pallas kernels for 19%

profile of v3, /device:TPU:1, one launch (start us, length us, event | category | flops | bytes accessed | tf_op | source)
XLA Modules:
  0.0 536.5 jit_solution(178023655171068053)
XLA Ops:
  5.0 1.4 collective-permute-start
  6.5 1.6 dynamic-slice_convert_fusion.1
  8.7 1.3 copy.40.x.refs_3_.refs_2_
  10.6 1.3 copy.41.gz.refs_4_
  11.9 2.0 and_reduce_fusion
  14.7 51.8 %gather_wide.1 = bf16[4,4,4,88,1536]{4,3,2,1,0:T(8,128)(2,1)} custom-call(bf16[88,768]{1,0:T(8,128)(2,1)} %get-tuple-element.133.refs_0_), custom_call_target="tpu_custom_call" | custom-call | tf_op jit(solution)/shard_map/gather_wide/pallas_call | solution.py:497
  70.1 54.2 %front.1 = (bf16[3,2,257,1408]{3,2,1,0:T(8,128)(2,1)}, bf16[2,264,1408]{2,1,0:T(8,128)(2,1)}, bf16[2,264,1408]{2,1,0:T(8,128)(2,1)}, f32[2,257,1408]{2,1,0:T(8,1...) custom-call(bf16[2,257,1408]{2,1,0:T(8,128)(2,1)} %copy.40.x.refs_3_.refs_2_, ...), custom_call_target="tpu_custom_call" | custom-call | tf_op jit(solution)/shard_map/front/pallas_call | solution.py:751
  124.3 55.4 %mlp_in.1 = (bf16[2,264,6144]{2,1,0:T(8,128)(2,1)}, f32[2,257,6144]{2,1,0:T(8,128)}, f32[6144,768]{1,0:T(8,128)}, bf16[4,4,2,4,3,16,1408]{6,5,4,3,2,1,0:T(8,128)(2,1)}) custom-call(bf16[2,264,1408]{2,1,0:T(8,128)(2,1)} %get-tuple-element.59.h2.refs_7_, bf16[2,257,1408]{2,1,0:T(8,128)(2,1)} %copy.41.gz.refs_4_, bf16[4,1408,1536]{2,1,0:T(8,128)(2,1)} %bitcast.55, ...), custom_call_target="tpu_custom_call" | custom-call | tf_op jit(solution)/shard_map/mlp_in/pallas_call | solution.py:831
  179.8 59.4 %mlp_out.1 = (bf16[2,4,2,264,768]{4,3,2,1,0:T(8,128)(2,1)}, f32[8,1,768]{2,1,0:T(1,128)}, f32[2,257,1408]{2,1,0:T(8,128)}, f32[2,257,1408]{2,1,0:T(8,128)}, f32[3,4,4,32,384]{4,3,2,1,0:T(8,128)}) custom-call(bf16[2,264,6144]{2,1,0:T(8,128)(2,1)} %get-tuple-element.61.act, f32[2,257,6144]{2,1,0:T(8,128)} %get-tuple-element.62.slope, ...), custom_call_target="tpu_custom_call" | custom-call | tf_op jit(solution)/shard_map/mlp_out/pallas_call | solution.py:873
  239.2 46.5 %mid.1 = (bf16[2,257,1408]{2,1,0:T(8,128)(2,1)}, f32[2,257,1408]{2,1,0:T(8,128)}, bf16[2,2,264,768]{3,2,1,0:T(8,128)(2,1)}, bf16[2,257,1408]{2,1,0:T(8,128)(2,1)...) custom-call(f32[2,257,1408]{2,1,0:T(8,128)} %get-tuple-element.65.refs_0_, ...), custom_call_target="tpu_custom_call" | custom-call | tf_op jit(solution)/shard_map/mid/pallas_call | solution.py:1020
  285.7 54.6 %attn_back.1 = (bf16[2,3,2,264,768]{4,3,2,1,0:T(8,128)(2,1)}, f32[3,1408]{1,0:T(4,128)}, f32[3,4,4,88,128]{4,3,2,1,0:T(8,128)}, f32[3,32,384]{2,1,0:T(8,128)}, f32[4,3,32,384]{3,2,1,0:T(8,128)}) custom-call(bf16[3,2,257,1408]{3,2,1,0:T(8,128)(2,1)} %get-tuple-element.71.qkv, bf16[2,257,1408]{2,1,0:T(8,128)(2,1)} %get-tuple-element.72.d_o, ...), custom_call_target="tpu_custom_call" | custom-call | tf_op jit(solution)/shard_map/attn_back/pallas_call | solution.py:1046
  340.3 1.9 constant_dynamic-update-slice_fusion.1
  342.3 47.8 %in_back.1 = (bf16[2,257,1408]{2,1,0:T(8,128)(2,1)}, f32[2,1408]{1,0:T(2,128)}, f32[4,1408,768]{2,1,0:T(8,128)}, f32[3,4,4,88,128]{4,3,2,1,0:T(8,128)}, f32[3,88...) custom-call(bf16[2,3,2,264,768]{4,3,2,1,0:T(8,128)(2,1)} %get-tuple-element.76.refs_0_.refs_7_, bf16[4,1408,1536]{2,1,0:T(8,128)(2,1)} %bitcast.50, ...), custom_call_target="tpu_custom_call" | custom-call | tf_op jit(solution)/shard_map/in_back/pallas_call | solution.py:1096
  391.6 4.6 collective-permute-start.1
  397.1 2.3 slice_select_fusion
  399.6 2.2 copy.56
  401.8 2.2 copy.55
  404.3 3.3 add_select_fusion
  407.6 5.3 scatter-add.4
  412.9 99.5 %last_scatter.1 = (f32[4,3,88,128]{3,2,1,0:T(8,128)}, f32[4,3,88,128]{3,2,1,0:T(8,128)}, f32[4,3,88,128]{3,2,1,0:T(8,128)}, f32[4,3,88,128]{3,2,1,0:T(8,128)}) custom-call(f32[4,4,4,88,768]{4,3,2,1,0:T(8,128)} %bitcast.57, f32[3,4,4,88,128]{4,3,2,1,0:T(8,128)} %get-tuple-element.89.acc_up, f32[3,88,128]{2,1,0:T(8,128)} %get-tuple-element.90.result_up), custom_call_target="tpu_custom_call" | custom-call | tf_op jit(solution)/shard_map/last_scatter/pallas_call | solution.py:523
  512.5 1.4 broadcast_select_fusion.1
  514.9 6.7 %collective-permute-start.3 = (f32[4,3,2,44,128]{4,0,3,2,1:T(4,128)}, f32[4,3,2,44,128]{4,0,3,2,1:T(4,128)}, u32[]{:S(2)}, u32[]{:S(2)}) collective-permute-start(f32[4,3,2,44,128]{4,0,3,2,1:T(4,128)} %copy.51), channel_id=1, source_target_pairs={{0,1},{1,0},{2,3},{3,2},{4,5},{5,4},{6,7},{7,6},{8,9},{9,8},{10,11... | collective-permute-start | bytes 1622024 | tf_op jit(solution)/shard_map/ppermute | solution.py:1114
  529.4 1.2 select_bitcast_fusion.1
  531.6 1.9 reshape_reshape.7
  (90 shorter events, 25.1 us)
Async XLA Ops:
  2.8 5.9 %copy-start.6 = (bf16[2,257,1408]{2,0,1:T(2,128)(2,1)S(1)}, bf16[2,257,1408]{2,0,1:T(2,128)(2,1)}, u32[]{:S(2)}) copy-start(bf16[2,257,1408]{2,0,1:T(2,128)(2,1)} %param.11) | copy-start | bytes 4342276
  5.0 8.8 %collective-permute-start = (bf16[2,44,768]{2,1,0:T(8,128)(2,1)S(1)}, bf16[2,44,768]{2,1,0:T(8,128)(2,1)S(1)}, u32[]{:S(2)}, u32[]{:S(2)}) collective-permute-start(bf16[2,44,768]{2,1,0:T(8,128)(2,1)S(1)} %broadcast_select_fusion.7), channel_id=1, source_target_pairs={{0,1},{1,0},{2,3},{3,2},{4,5},{5,4},{6,7},{7,6},{8,9},{9,8},{10,11... | collective-permute-start | bytes 405512 | tf_op jit(solution)/shard_map/ppermute | solution.py:1114
  8.7 1.9 copy-start.7
  10.6 1.3 copy-start.12
  340.3 1.9 copy-start.9
  342.3 49.0 %copy-start.11 = (f32[3,1408]{1,0:T(4,128)S(1)}, f32[3,1408]{1,0:T(4,128)}, u32[]{:S(2)}) copy-start(f32[3,1408]{1,0:T(4,128)} %get-tuple-element.85) | copy-start | bytes 50692
  342.3 49.1 %copy-start.10 = (f32[8,1,768]{2,1,0:T(1,128)S(1)}, f32[8,1,768]{2,1,0:T(1,128)}, u32[]{:S(2)}) copy-start(f32[8,1,768]{2,1,0:T(1,128)} %get-tuple-element.86) | copy-start | bytes 73732
  390.1 6.1 %copy-start.8 = (f32[4,3,32,384]{3,2,1,0:T(8,128)S(1)}, f32[4,3,32,384]{3,2,1,0:T(8,128)}, u32[]{:S(2)}) copy-start(f32[4,3,32,384]{3,2,1,0:T(8,128)} %get-tuple-element.96) | copy-start | bytes 1769476
  391.6 12.4 %collective-permute-start.1 = (f32[32,676]{1,0:T(8,128)S(1)}, f32[32,676]{1,0:T(8,128)S(1)}, u32[]{:S(2)}, u32[]{:S(2)}) collective-permute-start(f32[32,676]{1,0:T(8,128)S(1)} %pad_maximum_fusion.5), channel_id=1, source_target_pairs={{0,1},{1,0},{2,3},{3,2},{4,5},{5,4},{6,7},{7,6},{8,9},{9,8},{10,11... | collective-permute-start | bytes 259592 | tf_op jit(solution)/shard_map/ppermute | solution.py:1114
  397.1 2.5 copy-start.5
  399.3 122.9 %collective-permute-start.4 = (f32[192,768]{1,0:T(8,128)}, f32[192,768]{1,0:T(8,128)}, u32[]{:S(2)}, u32[]{:S(2)}) collective-permute-start(f32[192,768]{1,0:T(8,128)} %bitcast.27), channel_id=1, source_target_pairs={{0,1},{1,0},{2,3},{3,2},{4,5},{5,4},{6,7},{7,6},{8,9},{9,8},{10,11... | collective-permute-start | bytes 1769480 | tf_op jit(solution)/shard_map/ppermute | solution.py:1114
  399.6 2.2 copy-start.4
  512.4 9.2 %copy-start.2 = (f32[4,3,88,128]{3,2,1,0:T(8,128)S(1)}, f32[4,3,88,128]{3,2,1,0:T(8,128)}, u32[]{:S(2)}) copy-start(f32[4,3,88,128]{3,2,1,0:T(8,128)} %get-tuple-element.91) | copy-start | bytes 1622020
  512.4 9.1 %copy-start.3 = (f32[4,3,88,128]{3,2,1,0:T(8,128)S(1)}, f32[4,3,88,128]{3,2,1,0:T(8,128)}, u32[]{:S(2)}) copy-start(f32[4,3,88,128]{3,2,1,0:T(8,128)} %get-tuple-element.92) | copy-start | bytes 1622020
  514.9 14.6 %collective-permute-start.3 = (f32[4,3,2,44,128]{4,0,3,2,1:T(4,128)}, f32[4,3,2,44,128]{4,0,3,2,1:T(4,128)}, u32[]{:S(2)}, u32[]{:S(2)}) collective-permute-start(f32[4,3,2,44,128]{4,0,3,2,1:T(4,128)} %copy.51), channel_id=1, source_target_pairs={{0,1},{1,0},{2,3},{3,2},{4,5},{5,4},{6,7},{7,6},{8,9},{9,8},{10,11... | collective-permute-start | bytes 1622024 | tf_op jit(solution)/shard_map/ppermute | solution.py:1114
  521.9 3.7 collective-permute-start.2
  527.7 1.7 copy-start
  527.7 1.7 copy-start.1

commit v4 on v3

--- a/solution.py
+++ b/solution.py
@@ -26,12 +26,14 @@
 G1, C1, BO, S1, G2, C2, B2, S2 = range(8)
 Q, K, V, O = range(4)
 SEQS = (2, SEQ, D)
+LAST_SEQ = SEQS[0] - 1
 SEQ_PAIR = range(SEQS[0])
-TAIL = 8
+TAIL = 16
 BODY = SEQ - 1
 TOK = BODY + TAIL
-TOKS = (2, TOK, D)
+TT = 2 * TOK
 ROWS = 4 * TOK
+STEP = 256
 
 
 def sds(dtype, *shape):
@@ -40,6 +42,7 @@
 
 MESH_ID = pl.DeviceIdType.MESH
 SIDE = 4
+SUB = 8
 PAIR = 2
 C = 3
 COLOURS = range(C)
@@ -361,7 +364,7 @@
         vm = lambda *lead: pltpu.VMEM(unit_array(kind, *lead), F32)
         rows, cols = UNITS[kind]
         dma = pltpu.SemaphoreType.DMA
-        cut = (rows // TAIL + 1) // PAIR * TAIL
+        cut = (rows // SUB + 1) // PAIR * SUB
         return [vm(C, SIDE, SIDE), vm(C, PAIR, PAIR), vm(C, PAIR, SIDE), pltpu.VMEM((C, PAIR, cut, cols), F32), vm(C, PAIR),
                 *Ring.semaphores(), *Ring.semaphores(), dma((C,)), dma((C,))]
 
@@ -439,7 +442,7 @@
 class Spread:
     def __init__(self, kind, result, total, send, recv, local):
         rows = UNITS[kind][0]
-        cut = rows // TAIL // PAIR * TAIL
+        cut = rows // SUB // PAIR * SUB
         self.result, self.total, self.sems, self.local = result, total, (send, recv), local
         self.cuts = pl.ds(0, cut), pl.ds(cut, rows - cut)
 
@@ -590,10 +593,10 @@
         for s in SEQ_PAIR:
             for i, (start, size) in enumerate(((0, BODY), (BODY, TAIL))):
                 place = lambda n: rows.at[pl.ds(start * len(SEQ_PAIR) * PAIR + size * n, size)]
-                n = len(SEQ_PAIR) + s
+                part = pl.ds(TOK * s + start, size)
                 at = slot + (PAIR * s + i,)
-                local = pltpu.make_async_copy(mine.at[s, pl.ds(start, size)], place(s), sems[2].at[at])
-                far = remote(theirs.at[s, pl.ds(start, size)], place(n), sems, at, Torus().partner())
+                local = pltpu.make_async_copy(mine.at[part], place(s), sems[2].at[at])
+                far = remote(theirs.at[part], place(len(SEQ_PAIR) + s), sems, at, Torus().partner())
                 self.moves.append((local, far))
 
     @staticmethod
@@ -699,21 +702,26 @@
     return e * (1.0 / jnp.sum(e, axis=-1, keepdims=True))
 
 
-def attention(s, rows, x, w_out, vec, o, att, h2, acc, visit):
+def attention(s, rows, o, acc, visit):
     acc[...] = jnp.zeros_like(acc)
+    start = pl.multiple_of(s * TOK, TAIL)
+    tokens = pl.ds(start, SEQ)
     for h in range(HEADS):
         lanes, mask = window(h)
-        k = only(mask, rows[K, s, :, lanes])
-        v = only(mask, rows[V, s, :, lanes])
-        probs = softmax(dot_nt(rows[Q, s, :, lanes], k) * SCALE).astype(BF16)
+        k = only(mask, rows[K, tokens, lanes])
+        v = only(mask, rows[V, tokens, lanes])
+        probs = softmax(dot_nt(rows[Q, tokens, lanes], k) * SCALE).astype(BF16)
         acc[:, lanes] += dot(probs, v)
         visit(h)
-    heads = acc[...]
-    o[0] = pad(heads)
-    a = dot(heads.astype(BF16), w_out[0]) + row(vec, BO)
-    att[0] = a
-    xhat, _ = norm_stats(x[s].astype(F32) + row(vec, S1) * a)
-    h2[0] = pad(xhat * row(vec, G2) + row(vec, C2))
+    o[pl.ds(start, TOK)] = pad(acc[...])
+
+
+def seq_rows(t, s):
+    return t[TOK * s:TOK * s + SEQ]
+
+
+def seq_tile(s):
+    return pl.ds(TOK * s, TOK)
 
 
 FRONT_PLAN = {"qkv": ((0, 0, 1), (1, 1, 5), (2, 5, 8)), 2: ((O, 8, 9),), "end": ((O + 1, 9, None),)}
@@ -729,38 +737,45 @@
     def _():
         for s in SEQ_PAIR:
             xhat, _ = norm_stats(x[s].astype(F32))
-            h1[s] = pad(xhat * row(vec, G1) + row(vec, C1))
+            h1[seq_tile(s)] = pad(xhat * row(vec, G1) + row(vec, C1))
 
     @pl.when(j < O)
     def _():
+        t = (dot(h1[...], w[0]) + b[0]).astype(BF16)
+        qkv[0] = t
+        rows[j] = t
+
+    pl.when(j >= O)(lambda: attention(j - O, rows, o, acc, hosted.visit))
+
+    @at_step(O + LAST_SEQ)
+    def _():
+        a = dot(o[...], w[0]) + row(vec, BO)
+        att[...] = a
         for s in SEQ_PAIR:
-            t = (dot(h1[s, :SEQ], w[0]) + b[0]).astype(BF16)
-            qkv[0, s] = t
-            rows[j, s] = t
-
-    @pl.when(j >= O)
-    def _():
-        attention(j - O, rows, x, w, vec, o, att, h2, acc, hosted.visit)
+            xhat, _ = norm_stats(x[s].astype(F32) + row(vec, S1) * seq_rows(a, s))
+            h2[seq_tile(s)] = pad(xhat * row(vec, G2) + row(vec, C2))
 
     hosted.visit("end")
 
 
+def upto(n):
+    return lambda j: jnp.minimum(j, n)
+
+
 def front_call(x, w_attn, b_qkv, vec, up, collective_id):
-    upto = lambda n: lambda j: jnp.minimum(j, n)
-    seq = lambda tokens: along(0, 1, tokens, D, index=lambda j: jnp.maximum(j - O, 0))
     return pl.pallas_call(
         front_kernel, grid=(O + PAIR,),
-        out_shape=(sds(BF16, O, *SEQS), sds(BF16, *TOKS), sds(BF16, *TOKS), sds(F32, *SEQS), sds(BF16, *TOKS),
+        out_shape=(sds(BF16, O, TT, D), sds(BF16, TT, D), sds(BF16, TT, D), sds(F32, TT, D), sds(BF16, TT, D),
                    sds(BF16, *Gather.shape(WIDE))),
         in_specs=[whole(*SEQS), along(0, 1, D, D, index=upto(O)), along(0, 1, 1, D, index=upto(V)), whole(8, D), ANY],
-        out_specs=(along(0, 1, *SEQS, index=upto(V)), whole(*TOKS), seq(TOK), seq(SEQ), seq(TOK), ANY),
-        scratch_shapes=[pltpu.VMEM((O, *SEQS), BF16), pltpu.VMEM((SEQ, D), F32)] + Gather.semaphores(),
+        out_specs=(along(0, 1, TT, D, index=upto(V)),) + (whole(TT, D),) * SIDE + (ANY,),
+        scratch_shapes=[pltpu.VMEM((O, TT, D), BF16), pltpu.VMEM((SEQ, D), F32)] + Gather.semaphores(),
         compiler_params=comm_params(collective_id), name="front",
     )(x, w_attn, b_qkv, vec, up)
 
 
 def w_out_block():
-    return along(0, 1, D, D, index=lambda j: O)
+    return pl.BlockSpec((1, D, D), lambda j: (O, 0, 0), pipeline_mode=pl.Buffered(1))
 
 
 TILES = FF // HALF
@@ -800,13 +815,14 @@
 
     @pl.when(j < TILES)
     def _():
+        u = dot(h2[...], w_up[0]) + b_up[0]
+        phi = 0.5 * (1.0 + lax.erf(u * math.sqrt(0.5)))
+        slope[...] = phi + u * (jnp.exp(-0.5 * u * u) * math.sqrt(0.5 / math.pi))
+        place = lax.rem(lax.broadcasted_iota(jnp.int32, (TT, 1), 0), TOK)
+        a = only(place < SEQ, u * phi).astype(BF16)
+        act[...] = a
         for s in SEQ_PAIR:
-            u = dot(h2[s, :SEQ], w_up[0]) + b_up[0]
-            phi = 0.5 * (1.0 + lax.erf(u * math.sqrt(0.5)))
-            slope[s] = phi + u * (jnp.exp(-0.5 * u * u) * math.sqrt(0.5 / math.pi))
-            a = pad(u * phi)
-            act[s] = a
-            put_rows(a_rows.at[j], TAILS, s, a)
+            put_rows(a_rows.at[j], TAILS, s, a[TOK * s:TOK * s + TOK])
 
     at_step(TILES)(away.wait)
     for n in range(TILES):
@@ -830,9 +846,9 @@
     high = lambda j: jnp.maximum(j - TILES, 0)
     return pl.pallas_call(
         mlp_in_kernel, grid=(2 * TILES,),
-        out_shape=(sds(BF16, 2, TOK, FF), sds(F32, 2, SEQ, FF), sds(F32, FF, HALF), sds(BF16, *Gather.shape(DOWN))),
-        in_specs=[whole(*TOKS), whole(*SEQS), up_tile(low), along(0, 1, 1, HALF, index=low), whole(8, D), ANY],
-        out_specs=(along(2, 2, TOK, HALF, index=low), along(2, 2, SEQ, HALF, index=low),
+        out_shape=(sds(BF16, TT, FF), sds(F32, TT, FF), sds(F32, FF, HALF), sds(BF16, *Gather.shape(DOWN))),
+        in_specs=[whole(TT, D), whole(*SEQS), up_tile(low), along(0, 1, 1, HALF, index=low), whole(8, D), ANY],
+        out_specs=(along(1, TT, HALF, index=low), along(1, TT, HALF, index=low),
                    along(0, HALF, HALF, index=high), ANY),
         scratch_shapes=[pltpu.VMEM((TILES, ROWS, HALF), BF16), pltpu.VMEM((ROWS, HALF), BF16),
                         pltpu.VMEM((PAIR * TOK, HALF), BF16)] + Push.semaphores(TILES) + Push.semaphores(1) +
@@ -856,29 +872,26 @@
     @at_step(0)
     def _():
         for s in SEQ_PAIR:
-            dm[s] = (gz[s].astype(F32) * row(vec, S2)).astype(BF16)
-
-    db = jnp.zeros((1, HALF), F32)
-    for s in SEQ_PAIR:
-        accumulate(mlp.at[s], dot(act[s, :SEQ], w_down[...]))
-        d = dot_nt(dm[s], w_down[...]) * slope[s]
-        db = db + col_sum(d)
-        d_pre[0, 0, s] = pad(d)
-        accumulate(d_h2.at[s], dot_nt(d.astype(BF16), w_up[0]))
-    db_up[0] = db
+            dm[seq_tile(s)] = pad(gz[s].astype(F32) * row(vec, S2))
+
+    accumulate(mlp, dot(act[...], w_down[...]))
+    d = dot_nt(dm[...], w_down[...]) * slope[...]
+    db_up[0] = col_sum(d)
+    d = d.astype(BF16)
+    d_pre[0, 0] = d
+    accumulate(d_h2, dot_nt(d, w_up[0]))
     hosted.visit("end")
 
 
 def mlp_out_call(act, slope, gz, w_up, w_down, vec, part, collective_id):
     return pl.pallas_call(
         mlp_out_kernel, grid=(TILES,),
-        out_shape=(sds(BF16, 2, 4, 2, TOK, HALF), sds(F32, TILES, 1, HALF), sds(F32, *SEQS), sds(F32, *SEQS),
+        out_shape=(sds(BF16, PAIR, SIDE, TT, HALF), sds(F32, TILES, 1, HALF), sds(F32, TT, D), sds(F32, TT, D),
                    First.sums(DOWN)),
-        in_specs=[along(2, 2, TOK, HALF), along(2, 2, SEQ, HALF), whole(*SEQS), up_tile(), along(0, HALF, D), whole(8, D),
-                  ANY],
-        out_specs=(pl.BlockSpec((1, 1, 2, TOK, HALF), lambda j: (j % PAIR, j // PAIR, 0, 0, 0)), along(0, 1, 1, HALF),
-                   whole(*SEQS), whole(*SEQS), ANY),
-        scratch_shapes=[pltpu.VMEM(SEQS, BF16)] + First.scratch(DOWN),
+        in_specs=[along(1, TT, HALF), along(1, TT, HALF), whole(*SEQS), up_tile(), along(0, HALF, D), whole(8, D), ANY],
+        out_specs=(pl.BlockSpec((1, 1, TT, HALF), lambda j: (j % PAIR, j // PAIR, 0, 0)), along(0, 1, 1, HALF),
+                   whole(TT, D), whole(TT, D), ANY),
+        scratch_shapes=[pltpu.VMEM((TT, D), BF16)] + First.scratch(DOWN),
         compiler_params=comm_params(collective_id), name="mlp_out",
     )(act, slope, gz, w_up, w_down, vec, part)
 
@@ -888,56 +901,63 @@
     return t[:, :HALF], jnp.concatenate([t[:, HALF:], jnp.zeros((TOK, QCOLS - D), BF16)], axis=1)
 
 
-def mid(mlp, d_h2, att, x, gz, vec, w_out, z, g_res, d_att, d_o, sums):
-    a = att[0]
+def mid(mlp, d_h2, att, x, gz, vec, w_out, z, g_res, d_att, d_o, sums, da_rows):
+    a = att[:SEQ]
     y = x[0].astype(F32) + row(vec, S1) * a
-    m = mlp[0] + row(vec, B2)
+    m = mlp[:SEQ] + row(vec, B2)
     g = gz[0].astype(F32)
     z[0] = (y + row(vec, S2) * m).astype(BF16)
     xhat, rstd = norm_stats(y)
-    dh = d_h2[0]
+    dh = d_h2[:SEQ]
     gr = g + norm_back(xhat, rstd, dh * row(vec, G2))
-    g_res[0] = gr
+    g_res[:SEQ] = gr
     da = gr * row(vec, S1)
     terms = (da, gr * a, dh * xhat, dh, g * row(vec, S2), g * m)
     accumulate(sums, jnp.concatenate([jnp.zeros((BO, D), F32)] + [col_sum(t) for t in terms], axis=0))
     for i, t in enumerate(halves_of(da)):
-        d_att[i, 0] = t
-    d_o[0] = dot_nt(da.astype(BF16), w_out[0]).astype(BF16)
+        d_att[i] = t
+    da_rows[pl.ds(pl.multiple_of(pl.program_id(0) * TOK, TAIL), TOK)] = pad(da)
+
+    @at_step(LAST_SEQ)
+    def _():
+        d_o[...] = dot_nt(da_rows[...], w_out[0]).astype(BF16)
 
 
 def attention_back(qkv, d_o, d_qkv, db, acc, visit):
     acc[...] = jnp.zeros_like(acc)
     for h in range(HEADS):
         lanes, mask = window(h)
-        q, k, v = (only(mask, qkv[i, 0, :, lanes]) for i in (Q, K, V))
-        do = only(mask, d_o[0, :, lanes])
-        probs = softmax(dot_nt(q, k) * SCALE)
-        acc[V, :, lanes] += dot_tn(probs.astype(BF16), do)
-        dp = dot_nt(do, v)
-        ds = probs * (dp - jnp.sum(dp * probs, axis=-1, keepdims=True))
+        q, k, v = (only(mask, qkv[i, :SEQ, lanes]) for i in (Q, K, V))
+        do = only(mask, d_o[:SEQ, lanes])
+        scores = dot_nt(k, q) * SCALE
+        e = jnp.exp(scores - jnp.max(scores, axis=0, keepdims=True))
+        probs = e * (1.0 / col_sum(e))
+        acc[V, :, lanes] += dot(probs.astype(BF16), do)
+        dp = dot_nt(v, do)
+        ds = probs * (dp - col_sum(dp * probs))
         ds = (ds * SCALE).astype(BF16)
-        acc[Q, :, lanes] += dot(ds, k)
-        acc[K, :, lanes] += dot_tn(ds, q)
+        acc[K, :, lanes] += dot(ds, q)
+        acc[Q, :, lanes] += dot_tn(ds, k)
         visit(h)
     accumulate(db, jnp.concatenate([col_sum(acc[i]) for i in (Q, K, V)], axis=0))
     for n in (Q, K, V):
         for i, t in enumerate(halves_of(acc[n])):
-            d_qkv[i, n, 0] = t
-
-
-THIN = HALF // PAIR
+            d_qkv[i, n] = t
+
+
+PER = HALF // STEP
 
 
 class WideGrads:
-    def __init__(self, a, a_of, b, out, base, a_rows, b_rows, *sems):
-        self.a, self.a_of, self.b, self.out, self.base, self.a_rows, self.b_rows = a, a_of, b, out, base, a_rows, b_rows
-        self.a_sems, self.b_sems = sems[:3], sems[3:]
+    def __init__(self, a, a_of, b, out, base, a_rows, a_cols, b_rows, *sems):
+        self.a, self.a_of, self.b, self.out, self.base = a, a_of, b, out, base
+        self.a_rows, self.a_cols, self.b_rows = a_rows, a_cols, b_rows
+        self.a_sems, self.b_sems = sems[:C], sems[C:]
 
     @staticmethod
     def scratch(inputs):
-        return ([pltpu.VMEM((inputs, ROWS, D), BF16), pltpu.VMEM((SIDE, ROWS, HALF), BF16)] +
-                Exchange.semaphores(inputs) + Exchange.semaphores(SIDE))
+        return ([pltpu.VMEM((inputs, ROWS, D), BF16), pltpu.VMEM((inputs, D, ROWS), BF16),
+                 pltpu.VMEM((SIDE, ROWS, HALF), BF16)] + Exchange.semaphores(inputs) + Exchange.semaphores(SIDE))
 
     def input(self, i):
         return Exchange(self.a[i], self.a[i], self.a_rows.at[i], self.a_sems, (i,))
@@ -947,27 +967,32 @@
         b = self.b[n]
         return Exchange(b(c), b(1 - c), self.b_rows.at[n], self.b_sems, (n,))
 
+    def new_input(self, n):
+        return n == 0 or self.a_of[n] != self.a_of[n - 1]
+
     def begin(self):
         for n in range(SIDE):
-            if n == 0 or self.a_of[n] != self.a_of[n - 1]:
+            if self.new_input(n):
                 self.input(self.a_of[n]).start()
             self.cotangent(n).start()
 
     def step(self):
         j = pl.program_id(0)
         for n in range(SIDE):
-            @at_step(self.base + PAIR * n)
+            @at_step(self.base + PER * n)
             def _():
-                if n == 0 or self.a_of[n] != self.a_of[n - 1]:
-                    self.input(self.a_of[n]).wait()
+                if self.new_input(n):
+                    i = self.a_of[n]
+                    self.input(i).wait()
+                    self.a_cols[i] = self.a_rows[i].T
                 self.cotangent(n).wait()
 
         @pl.when(j >= self.base)
         def _():
-            n = lax.div(j - self.base, PAIR)
-            cols = pl.ds(pl.multiple_of(lax.rem(j - self.base, PAIR) * THIN, LANES), THIN)
-            a = self.a_rows[0 if len(self.a) == 1 else lax.div(n, O)]
-            self.out[0] = dot_tn(a, self.b_rows[n, :, cols])
+            n = lax.div(j - self.base, PER)
+            cols = pl.ds(pl.multiple_of(lax.rem(j - self.base, PER) * STEP, STEP), STEP)
+            i = 0 if len(self.a) == 1 else lax.div(n, O)
+            self.out[0] = dot(self.a_cols[i], self.b_rows[n, :, cols])
 
     def finish(self):
         for i in range(len(self.a)):
@@ -979,30 +1004,30 @@
 def grads_block(base):
     def index(j):
         n = jnp.maximum(j - base, 0)
-        return n // PAIR, 0, n % PAIR
-
-    return pl.BlockSpec((1, D, THIN), index)
-
-
-LAST_SEQ = SEQS[0] - 1
-GRAD_STEPS = PAIR * SIDE
-
-
-def upto(n):
-    return lambda j: jnp.minimum(j, n)
-
-
-def seq_block(tokens=SEQ):
-    return along(0, 1, tokens, D, index=upto(LAST_SEQ))
-
-
-MID_PLACES = (("end", 0), ("end", 3), ("end", 7), ("end", LAST_SEQ + GRAD_STEPS))
+        return n // PER, 0, n % PER
+
+    return pl.BlockSpec((1, D, STEP), index)
+
+
+GRAD_STEPS = PER * SIDE
+
+
+def tok_block():
+    return along(0, TOK, D, index=upto(LAST_SEQ))
+
+
+def seq_block():
+    return along(0, 1, SEQ, D, index=upto(LAST_SEQ))
+
+
+MID_PLACES = (("end", 0), ("end", 4), ("end", 10), ("end", LAST_SEQ + GRAD_STEPS))
 
 
 def mid_kernel(*refs):
     refs = list(refs)
     take = lambda n: [refs.pop(0) for _ in range(n)]
     ins, (h2, d_pre, part, acc), outs, (d_up, sums, result) = take(7), take(4), take(5), take(3)
+    outs.append(refs.pop(0))
     grads = WideGrads((h2,), (0,) * SIDE, [lambda c, i=i: d_pre.at[c, i] for i in range(SIDE)], d_up, SEQS[0],
                       *take(len(WideGrads.scratch(1))))
     first = First(DOWN, 1, part, sums, *take(len(First.scratch(DOWN))))
@@ -1019,12 +1044,12 @@
 def mid_call(mlp, d_h2, att, x, gz, vec, w_attn, h2, d_pre, part, acc, collective_id):
     return pl.pallas_call(
         mid_kernel, grid=(SEQS[0] + GRAD_STEPS,),
-        out_shape=(sds(BF16, *SEQS), sds(F32, *SEQS), sds(BF16, 2, 2, TOK, HALF), sds(BF16, *SEQS), sds(F32, 8, D),
+        out_shape=(sds(BF16, *SEQS), sds(F32, TT, D), sds(BF16, PAIR, TT, HALF), sds(BF16, TT, D), sds(F32, 8, D),
                    sds(F32, SIDE, D, HALF), First.sums(DOWN), Rest.sums(DOWN)),
-        in_specs=[seq_block()] * len("mdaxg") + [whole(8, D), w_out_block()] + [ANY] * SIDE,
-        out_specs=(seq_block(), seq_block(), along(1, 2, 1, TOK, HALF, index=upto(LAST_SEQ)), seq_block(), whole(8, D),
+        in_specs=[tok_block()] * O + [seq_block()] * PAIR + [whole(8, D), w_out_block()] + [ANY] * SIDE,
+        out_specs=(seq_block(), tok_block(), along(1, PAIR, TOK, HALF, index=upto(LAST_SEQ)), whole(TT, D), whole(8, D),
                    grads_block(SEQS[0]), ANY, ANY),
-        scratch_shapes=WideGrads.scratch(1) + First.scratch(DOWN) + Rest.scratch(DOWN),
+        scratch_shapes=[pltpu.VMEM((TT, D), BF16)] + WideGrads.scratch(1) + First.scratch(DOWN) + Rest.scratch(DOWN),
         compiler_params=comm_params(collective_id), name="mid",
     )(mlp, d_h2, att, x, gz, vec, w_attn, h2, d_pre, part, acc)
 
@@ -1045,16 +1070,16 @@
 def attn_back_call(qkv, d_o, part, acc_down, result_down, collective_id):
     return pl.pallas_call(
         attn_back_kernel, grid=SEQS[:1],
-        out_shape=(sds(BF16, 2, O, 2, TOK, HALF), sds(F32, O, D), First.sums(WIDE), Rest.sums(DOWN), Spread.sums(DOWN)),
-        in_specs=[along(1, O, 1, SEQ, D), seq_block()] + [ANY] * O,
-        out_specs=(along(2, 2, O, 1, TOK, HALF), whole(O, D)) + (ANY,) * O,
+        out_shape=(sds(BF16, PAIR, O, TT, HALF), sds(F32, O, D), First.sums(WIDE), Rest.sums(DOWN), Spread.sums(DOWN)),
+        in_specs=[along(1, O, TOK, D), tok_block()] + [ANY] * O,
+        out_specs=(along(2, PAIR, O, TOK, HALF), whole(O, D)) + (ANY,) * O,
         scratch_shapes=[pltpu.VMEM((O, SEQ, D), F32)] + First.scratch(WIDE) + Rest.scratch(DOWN) + Spread.scratch(),
         compiler_params=comm_params(collective_id), name="attn_back",
     )(qkv, d_o, part, acc_down, result_down)
 
 
 IN_STEPS = PAIR * O
-IN_PLACES = (("end", 1), ("end", IN_STEPS - 1), ("end", IN_STEPS + O), ("end", IN_STEPS + GRAD_STEPS - 1))
+IN_PLACES = (("end", 1), ("end", IN_STEPS - 1), ("end", IN_STEPS + SIDE), ("end", IN_STEPS + GRAD_STEPS - 1))
 
 
 def in_back_kernel(*refs):
@@ -1073,17 +1098,17 @@
 
     @pl.when(pl.program_id(0) < IN_STEPS)
     def _():
-        for s in SEQ_PAIR:
-            accumulate(acc.at[s], dot_nt(d_half[0, 0, s, :SEQ], w[0]))
+        accumulate(acc, dot_nt(d_half[0, 0], w[0]))
 
     @at_step(IN_STEPS - 1)
     def _():
         rows = jnp.zeros((BO, D), F32)
         for s in SEQ_PAIR:
             xhat, rstd = norm_stats(x[s].astype(F32))
-            dh = acc[s]
+            tokens = pl.ds(TOK * s, SEQ)
+            dh = acc[tokens]
             rows = rows + jnp.concatenate([col_sum(dh * xhat), col_sum(dh)], axis=0)
-            dx[s] = (g_res[s] + norm_back(xhat, rstd, dh * row(vec, G1))).astype(BF16)
+            dx[s] = (g_res[tokens] + norm_back(xhat, rstd, dh * row(vec, G1))).astype(BF16)
         sums[...] = rows
 
     grads.step()
@@ -1097,10 +1122,10 @@
         in_back_kernel, grid=(IN_STEPS + GRAD_STEPS,),
         out_shape=(sds(BF16, *SEQS), sds(F32, BO, D), sds(F32, SIDE, D, HALF), First.sums(WIDE), Rest.sums(WIDE),
                    Spread.sums(DOWN)),
-        in_specs=[pl.BlockSpec((1, 1, 2, TOK, HALF), lambda j: (low(j) % PAIR, low(j) // PAIR, 0, 0, 0)), up_tile(low),
-                  whole(*SEQS), whole(*SEQS), whole(8, D)] + [ANY] * 7,
+        in_specs=[pl.BlockSpec((1, 1, TT, HALF), lambda j: (low(j) % PAIR, low(j) // PAIR, 0, 0)), up_tile(low),
+                  whole(*SEQS), whole(TT, D), whole(8, D)] + [ANY] * 7,
         out_specs=(whole(*SEQS), whole(BO, D), grads_block(IN_STEPS), ANY, ANY, ANY),
-        scratch_shapes=[pltpu.VMEM(SEQS, F32)] + WideGrads.scratch(2) + First.scratch(WIDE) + Rest.scratch(WIDE) +
+        scratch_shapes=[pltpu.VMEM((TT, D), F32)] + WideGrads.scratch(2) + First.scratch(WIDE) + Rest.scratch(WIDE) +
         Spread.scratch(),
         compiler_params=comm_params(collective_id), name="in_back",
     )(d_qkv, w_attn, x, g_res, vec, h1, o, d_qkv, d_att, part, acc_up, result_down)

time: 546 us -> 529 us (0.969); the launches traced: 536 us -> 525 us
  Pallas kernels: 469 us -> 458 us
    pallas_call x4, Pallas kernels: 224 us -> 212 us  [the longest x1 55.9 us: mlp_in_call(): pl.pallas_call(mlp_in_kernel, grid=(2 * TILES,), out_shape=(sds(BF16, TT,...]
where the time goes in v4:
time: 529 us; the launch traced here: 525 us
  Pallas kernels  458 us (87%)
  local copies, waits for them, and re-layouts  31.6 us (6%)
  other arithmetic  21 us (4%)
  starting transfers between devices  12.9 us (2%)
    pallas_call x1, Pallas kernels, last_scatter(): pl.pallas_call(last_scatter_kernel, out_shape=(Spread.sums(WIDE),) * SIDE...  99.5 us
    pallas_call x1, Pallas kernels, mlp_in_call(): pl.pallas_call(mlp_in_kernel, grid=(2 * TILES,), out_shape=(sds(BF16, TT,...  55.9 us
    pallas_call x1, Pallas kernels, mlp_out_call(): pl.pallas_call(mlp_out_kernel, grid=(TILES,), out_shape=(sds(BF16, PAIR,...  55.4 us
    pallas_call x1, Pallas kernels, front_call(): pl.pallas_call(front_kernel, grid=(O + PAIR,), out_shape=(sds(BF16, O, TT...  55.2 us
    pallas_call x1, Pallas kernels, torus_gather(): pl.pallas_call(kernel, out_shape=sds(BF16, *Gather.shape(kind)), in_specs...  51.8 us
    pallas_call x1, Pallas kernels, in_back_call(): pl.pallas_call(in_back_kernel, grid=(IN_STEPS + GRAD_STEPS,), out_shape=(...  47.8 us
    pallas_call x1, Pallas kernels, mid_call(): pl.pallas_call(mid_kernel, grid=(SEQS[0] + GRAD_STEPS,), out_shape=(sds(B...  47 us
    pallas_call x1, Pallas kernels, attn_back_call(): pl.pallas_call(attn_back_kernel, grid=SEQS[:1], out_shape=(sds(BF16, PAIR...  45.5 us
  transfers between devices with their start and end apart: 5, of which 0 were waited for; matrix products, arithmetic and copies ran while one was open for 6% of the time, Pallas kernels for 19%

profile of v4, /device:TPU:1, one launch (start us, length us, event | category | flops | bytes accessed | tf_op | source)
XLA Modules:
  0.0 524.9 jit_solution(2664235937230498566)
XLA Ops:
  5.0 1.4 collective-permute-start
  6.5 1.6 dynamic-slice_convert_fusion.1
  8.7 1.3 copy.40.x.refs_3_.refs_2_
  10.6 1.3 copy.41.gz.refs_4_
  11.9 2.0 and_reduce_fusion
  14.7 51.8 %gather_wide.1 = bf16[4,4,4,88,1536]{4,3,2,1,0:T(8,128)(2,1)} custom-call(bf16[88,768]{1,0:T(8,128)(2,1)} %get-tuple-element.133.refs_0_), custom_call_target="tpu_custom_call" | custom-call | tf_op jit(solution)/shard_map/gather_wide/pallas_call | solution.py:500
  70.1 55.2 %front.1 = (bf16[3,544,1408]{2,1,0:T(8,128)(2,1)}, bf16[544,1408]{1,0:T(8,128)(2,1)}, bf16[544,1408]{1,0:T(8,128)(2,1)}, f32[544,1408]{1,0:T(8,128)}, bf16[544,1...) custom-call(bf16[2,257,1408]{2,1,0:T(8,128)(2,1)} %copy.40.x.refs_3_.refs_2_, bf16[4,1408,1536]{2,1,0:T(8,128)(2,1)} %bitcast.48, ...), custom_call_target="tpu_custom_call" | custom-call | tf_op jit(solution)/shard_map/front/pallas_call | solution.py:766
  125.3 55.9 %mlp_in.1 = (bf16[544,6144]{1,0:T(8,128)(2,1)}, f32[544,6144]{1,0:T(8,128)}, f32[6144,768]{1,0:T(8,128)}, bf16[4,4,2,4,3,16,1408]{6,5,4,3,2,1,0:T(8,128)(2,1)}) custom-call(bf16[544,1408]{1,0:T(8,128)(2,1)} %get-tuple-element.59.h2.refs_7_, bf16[2,257,1408]{2,1,0:T(8,128)(2,1)} %copy.41.gz.refs_4_, bf16[4,1408,1536]{2,1,0:T(8,128)(2,1)} %bitcast.55, ...), custom_call_target="tpu_custom_call" | custom-call | tf_op jit(solution)/shard_map/mlp_in/pallas_call | solution.py:847
  181.3 55.4 %mlp_out.1 = (bf16[2,4,544,768]{3,2,1,0:T(8,128)(2,1)}, f32[8,1,768]{2,1,0:T(1,128)}, f32[544,1408]{1,0:T(8,128)}, f32[544,1408]{1,0:T(8,128)}, f32[3,4,4,32,384]{4,3,2,1,0:T(8,128)}) custom-call(bf16[544,6144]{1,0:T(8,128)(2,1)} %get-tuple-element.61.act, f32[544,6144]{1,0:T(8,128)} %get-tuple-element.62.slope, bf16[2,257,1408]{2,1,0:T(8,128)(2,1)} %copy.41.gz.refs_4_, ...), custom_call_target="tpu_custom_call" | custom-call | tf_op jit(solution)/shard_map/mlp_out/pallas_call | solution.py:887
  236.7 47.0 %mid.1 = (bf16[2,257,1408]{2,1,0:T(8,128)(2,1)}, f32[544,1408]{1,0:T(8,128)}, bf16[2,544,768]{2,1,0:T(8,128)(2,1)}, bf16[544,1408]{1,0:T(8,128)(2,1)}, f32[8,140...) custom-call(f32[544,1408]{1,0:T(8,128)} %get-tuple-element.65.refs_0_, ...), custom_call_target="tpu_custom_call" | custom-call | tf_op jit(solution)/shard_map/mid/pallas_call | solution.py:1045
  283.7 45.5 %attn_back.1 = (bf16[2,3,544,768]{3,2,1,0:T(8,128)(2,1)}, f32[3,1408]{1,0:T(4,128)}, f32[3,4,4,88,128]{4,3,2,1,0:T(8,128)}, f32[3,32,384]{2,1,0:T(8,128)}, f32[4,3,32,384]{3,2,1,0:T(8,128)}) custom-call(bf16[3,544,1408]{2,1,0:T(8,128)(2,1)} %get-tuple-element.71.qkv, bf16[544,1408]{1,0:T(8,128)(2,1)} %get-tuple-element.72.d_o, ...), custom_call_target="tpu_custom_call" | custom-call | tf_op jit(solution)/shard_map/attn_back/pallas_call | solution.py:1071
  329.2 1.9 constant_dynamic-update-slice_fusion.1
  331.2 47.8 %in_back.1 = (bf16[2,257,1408]{2,1,0:T(8,128)(2,1)}, f32[2,1408]{1,0:T(2,128)}, f32[4,1408,768]{2,1,0:T(8,128)}, f32[3,4,4,88,128]{4,3,2,1,0:T(8,128)}, f32[3,88...) custom-call(bf16[2,3,544,768]{3,2,1,0:T(8,128)(2,1)} %get-tuple-element.76.refs_0_.refs_7_, bf16[4,1408,1536]{2,1,0:T(8,128)(2,1)} %bitcast.50, ...), custom_call_target="tpu_custom_call" | custom-call | tf_op jit(solution)/shard_map/in_back/pallas_call | solution.py:1121
  380.5 4.6 collective-permute-start.1
  385.9 2.3 slice_select_fusion
  388.2 2.2 copy.56
  390.4 2.2 copy.55
  392.9 3.3 add_select_fusion
  396.2 5.6 %scatter-add.4 = f32[4,1408,768]{2,1,0:T(8,128)} dynamic-update-slice(f32[4,1408,768]{2,1,0:T(8,128)} %get-tuple-element.84, f32[1,1408,128]{2,1,0:T(8,128)S(1)} %add_select_fusion, s32[]{:T(128)} %bitcast.12, s32[]{:T(128)} %constant.42.clone.1, s32[]{:T(128)} %bitcast.13) | dynamic-update-slice | bytes 1441796 | tf_op jit(solution)/shard_map/scatter-add | solution.py:1205
  401.8 99.5 %last_scatter.1 = (f32[4,3,88,128]{3,2,1,0:T(8,128)}, f32[4,3,88,128]{3,2,1,0:T(8,128)}, f32[4,3,88,128]{3,2,1,0:T(8,128)}, f32[4,3,88,128]{3,2,1,0:T(8,128)}) custom-call(f32[4,4,4,88,768]{4,3,2,1,0:T(8,128)} %bitcast.57, f32[3,4,4,88,128]{4,3,2,1,0:T(8,128)} %get-tuple-element.89.acc_up, f32[3,88,128]{2,1,0:T(8,128)} %get-tuple-element.90.result_up), custom_call_target="tpu_custom_call" | custom-call | tf_op jit(solution)/shard_map/last_scatter/pallas_call | solution.py:526
  501.3 1.4 broadcast_select_fusion.1
  503.7 6.7 %collective-permute-start.3 = (f32[4,3,2,44,128]{4,0,3,2,1:T(4,128)}, f32[4,3,2,44,128]{4,0,3,2,1:T(4,128)}, u32[]{:S(2)}, u32[]{:S(2)}) collective-permute-start(f32[4,3,2,44,128]{4,0,3,2,1:T(4,128)} %copy.51), channel_id=1, source_target_pairs={{0,1},{1,0},{2,3},{3,2},{4,5},{5,4},{6,7},{7,6},{8,9},{9,8},{10,11... | collective-permute-start | bytes 1622024 | tf_op jit(solution)/shard_map/ppermute | solution.py:1139
  518.0 1.2 select_bitcast_fusion.1
  520.1 1.9 reshape_reshape.7
  (90 shorter events, 24.6 us)
Async XLA Ops:
  2.8 5.9 %copy-start.6 = (bf16[2,257,1408]{2,0,1:T(2,128)(2,1)S(1)}, bf16[2,257,1408]{2,0,1:T(2,128)(2,1)}, u32[]{:S(2)}) copy-start(bf16[2,257,1408]{2,0,1:T(2,128)(2,1)} %param.11) | copy-start | bytes 4342276
  5.0 8.8 %collective-permute-start = (bf16[2,44,768]{2,1,0:T(8,128)(2,1)S(1)}, bf16[2,44,768]{2,1,0:T(8,128)(2,1)S(1)}, u32[]{:S(2)}, u32[]{:S(2)}) collective-permute-start(bf16[2,44,768]{2,1,0:T(8,128)(2,1)S(1)} %broadcast_select_fusion.7), channel_id=1, source_target_pairs={{0,1},{1,0},{2,3},{3,2},{4,5},{5,4},{6,7},{7,6},{8,9},{9,8},{10,11... | collective-permute-start | bytes 405512 | tf_op jit(solution)/shard_map/ppermute | solution.py:1139
  8.7 1.9 copy-start.7
  10.6 1.3 copy-start.12
  329.2 1.9 copy-start.9
  331.1 48.9 %copy-start.11 = (f32[3,1408]{1,0:T(4,128)S(1)}, f32[3,1408]{1,0:T(4,128)}, u32[]{:S(2)}) copy-start(f32[3,1408]{1,0:T(4,128)} %get-tuple-element.85) | copy-start | bytes 50692
  331.1 49.1 %copy-start.10 = (f32[8,1,768]{2,1,0:T(1,128)S(1)}, f32[8,1,768]{2,1,0:T(1,128)}, u32[]{:S(2)}) copy-start(f32[8,1,768]{2,1,0:T(1,128)} %get-tuple-element.86) | copy-start | bytes 73732
  378.9 6.2 %copy-start.8 = (f32[4,3,32,384]{3,2,1,0:T(8,128)S(1)}, f32[4,3,32,384]{3,2,1,0:T(8,128)}, u32[]{:S(2)}) copy-start(f32[4,3,32,384]{3,2,1,0:T(8,128)} %get-tuple-element.96) | copy-start | bytes 1769476
  380.5 12.2 %collective-permute-start.1 = (f32[32,676]{1,0:T(8,128)S(1)}, f32[32,676]{1,0:T(8,128)S(1)}, u32[]{:S(2)}, u32[]{:S(2)}) collective-permute-start(f32[32,676]{1,0:T(8,128)S(1)} %pad_maximum_fusion.5), channel_id=1, source_target_pairs={{0,1},{1,0},{2,3},{3,2},{4,5},{5,4},{6,7},{7,6},{8,9},{9,8},{10,11... | collective-permute-start | bytes 259592 | tf_op jit(solution)/shard_map/ppermute | solution.py:1139
  385.9 2.3 copy-start.5
  388.2 122.6 %collective-permute-start.4 = (f32[192,768]{1,0:T(8,128)}, f32[192,768]{1,0:T(8,128)}, u32[]{:S(2)}, u32[]{:S(2)}) collective-permute-start(f32[192,768]{1,0:T(8,128)} %bitcast.27), channel_id=1, source_target_pairs={{0,1},{1,0},{2,3},{3,2},{4,5},{5,4},{6,7},{7,6},{8,9},{9,8},{10,11... | collective-permute-start | bytes 1769480 | tf_op jit(solution)/shard_map/ppermute | solution.py:1139
  388.2 2.2 copy-start.4
  501.3 9.2 %copy-start.2 = (f32[4,3,88,128]{3,2,1,0:T(8,128)S(1)}, f32[4,3,88,128]{3,2,1,0:T(8,128)}, u32[]{:S(2)}) copy-start(f32[4,3,88,128]{3,2,1,0:T(8,128)} %get-tuple-element.91) | copy-start | bytes 1622020
  501.3 9.2 %copy-start.3 = (f32[4,3,88,128]{3,2,1,0:T(8,128)S(1)}, f32[4,3,88,128]{3,2,1,0:T(8,128)}, u32[]{:S(2)}) copy-start(f32[4,3,88,128]{3,2,1,0:T(8,128)} %get-tuple-element.92) | copy-start | bytes 1622020
  503.7 14.3 %collective-permute-start.3 = (f32[4,3,2,44,128]{4,0,3,2,1:T(4,128)}, f32[4,3,2,44,128]{4,0,3,2,1:T(4,128)}, u32[]{:S(2)}, u32[]{:S(2)}) collective-permute-start(f32[4,3,2,44,128]{4,0,3,2,1:T(4,128)} %copy.51), channel_id=1, source_target_pairs={{0,1},{1,0},{2,3},{3,2},{4,5},{5,4},{6,7},{7,6},{8,9},{9,8},{10,11... | collective-permute-start | bytes 1622024 | tf_op jit(solution)/shard_map/ppermute | solution.py:1139
  510.7 3.4 collective-permute-start.2
  516.3 1.7 copy-start
  516.3 1.7 copy-start.1

commit v5 on v4

--- a/solution.py
+++ b/solution.py
@@ -20,6 +20,7 @@
 OWN = 44
 CHIP = 2 * OWN
 LANES = 128
+DEVICES = 32
 F32 = jnp.float32
 BF16 = jnp.bfloat16
 VMEM_LIMIT = 66 * 1000 * 1000
@@ -217,15 +218,19 @@
 
 
 class Ring:
-    def __init__(self, s, terms, passed, relay, landing, send, recv, rows=None):
-        self.s, self.terms, self.passed, self.relay, self.landing = s, terms, passed, relay, landing
-        self.sems, self.rows = (send, recv), rows
+    def __init__(self, s, bands, terms, passed, relay, landing, send, recv):
+        self.s, self.bands, self.terms, self.passed, self.relay, self.landing = s, bands, terms, passed, relay, landing
+        self.sems = (send, recv)
 
     def zone(self, k, way, half):
-        return self.landing.at[k, way, self.rows[half] if self.rows else duo(half)]
+        if self.s == THIRD:
+            return self.landing.at[k, way, self.bands.cuts(k)[half]]
+        return self.bands.rows(self.landing.at[k, way, duo(half)], k)
 
     def carried(self, ref, k, way):
-        return ref.at[k, way, pl.ds(0, self.rows[way].size)] if self.rows else ref.at[k, way]
+        if self.s == THIRD:
+            return ref.at[k, way, pl.ds(0, self.bands.cuts(k)[way].size)]
+        return self.bands.rows(ref.at[k, way], k)
 
     def hop(self, k, m):
         me = Torus()
@@ -257,53 +262,86 @@
         return [pltpu.SemaphoreType.DMA((C, ADDED + PAIR))] * PAIR
 
 
-UNITS = {WIDE: (CHIP, LANES), DOWN: (FF // 192, HALF // PAIR)}
-
-
-def unit_array(kind, *lead):
-    return lead + UNITS[kind]
+UNIT = 32
+BANDS = {WIDE: ((0, 24), (24, UNIT), (56, UNIT)), DOWN: ((0, UNIT), (UNIT, UNIT), (2 * UNIT, UNIT))}
+ORDERS = {WIDE: "xzy", DOWN: "zyx"}
+
+
+class Bands:
+    def __init__(self, kind, half=None):
+        self.order, self.bands = ORDERS[kind], BANDS[kind]
+        self.width = HALF if half is None else HALF // PAIR
+        self.cols = pl.ds(self.width * (half or 0), self.width)
+
+    def band(self, k):
+        return pl.ds(*self.bands[k])
+
+    def rows(self, ref, k):
+        return ref.at[(ALL,) * (len(ref.shape) - PAIR) + (pl.ds(0, self.bands[k][1]),)]
+
+    def cuts(self, k):
+        rows = self.bands[k][1]
+        cut = (rows // SUB + 1) // PAIR * SUB
+        return pl.ds(0, cut), pl.ds(cut, rows - cut)
+
+    def rest(self, k):
+        return [d for d in self.order if d != COLOUR_DIMS[k][FIRST]]
+
+    def units(self, *lead):
+        return lead + (UNIT, self.width)
+
+    def vmem(self, *lead):
+        return pltpu.VMEM(self.units(*lead), F32)
+
+    def sums(self):
+        return sds(F32, *self.units(C, SIDE, SIDE))
+
+    def result(self):
+        return sds(F32, *self.units(C))
+
+    def total(self):
+        return sds(F32, *self.units(SIDE, C))
+
+    def first(self):
+        relays = [self.vmem(C, PAIR, PAIR, SIDE)] * PAIR
+        dma = pltpu.SemaphoreType.DMA
+        return [self.vmem(C, SIDE, SIDE), *relays, self.vmem(C, PAIR, SIDE, SIDE), *Ring.semaphores(), dma((C, C)), dma((C,))]
+
+    def later(self):
+        dma = pltpu.SemaphoreType.DMA
+        return [self.vmem(C, SIDE, SIDE), self.vmem(C, PAIR, PAIR), self.vmem(C, PAIR, SIDE),
+                pltpu.VMEM((C, PAIR, UNIT // PAIR, self.width), F32), self.vmem(C, PAIR),
+                *Ring.semaphores(), *Ring.semaphores(), dma((C,)), dma((C,))]
 
 
 class First:
-    def __init__(self, kind, half, part, acc, own, passed, relay, landing, send, recv, load, store):
-        self.kind, self.half, self.part, self.acc, self.own, self.passed = kind, half, part, acc, own, passed
+    def __init__(self, bands, part, acc, own, passed, relay, landing, send, recv, load, store):
+        self.bands, self.part, self.acc, self.own_all, self.passed = bands, part, acc, own, passed
         self.relay_in, self.landing, self.load_sem, self.store_sem = relay, landing, load, store
-        self.ring = Ring(FIRST, self.terms, passed, relay, landing, send, recv)
-
-    @staticmethod
-    def scratch(kind):
-        vm = lambda *lead: pltpu.VMEM(unit_array(kind, *lead), F32)
-        dma = pltpu.SemaphoreType.DMA
-        relays = [vm(C, PAIR, PAIR, SIDE)] * PAIR
-        return [vm(C, SIDE, SIDE), *relays, vm(C, PAIR, SIDE, SIDE), *Ring.semaphores(), dma((C, C)), dma((C,))]
-
-    @staticmethod
-    def sums(kind):
-        return sds(F32, *unit_array(kind, C, SIDE, SIDE))
+        self.ring = Ring(FIRST, bands, self.terms, passed, relay, landing, send, recv)
+
+    def own(self, k):
+        return self.bands.rows(self.own_all.at[k], k)
 
     def terms(self, k, v, half=None):
-        order = ORDERS[self.kind]
-        at = {d: ALL for d in order}
+        b = self.bands
+        at = {d: ALL for d in b.order}
         at[COLOUR_DIMS[k][FIRST]] = v
         if half is not None:
-            at[rest_dims(self.kind, k)[0]] = duo(half)
-        lead = tuple(at[d] for d in order)
-        width = UNITS[self.kind][1]
-        if self.kind == WIDE:
-            return self.part.at[lead + (ALL, pl.ds(width * (PAIR * k + self.half), width))]
-        return self.part.at[lead + (k, ALL, pl.ds(width * self.half, width))]
+            at[b.rest(k)[0]] = duo(half)
+        return self.part.at[tuple(at[d] for d in b.order) + (b.band(k), b.cols)]
 
     def load(self, k, m):
         me = Torus()
         dim = COLOUR_DIMS[k][FIRST]
         if m in WAYS:
-            src, dst = self.terms(k, me.shift(dim, toward(m)), m), self.passed.at[k, m]
+            src, dst = self.terms(k, me.shift(dim, toward(m)), m), self.ring.carried(self.passed, k, m)
         else:
-            src, dst = self.terms(k, me.at[dim]), self.own.at[k]
+            src, dst = self.terms(k, me.at[dim]), self.own(k)
         return pltpu.make_async_copy(src, dst, self.load_sem.at[k, m])
 
     def store(self, k):
-        return pltpu.make_async_copy(self.own.at[k], self.acc.at[k], self.store_sem.at[k])
+        return pltpu.make_async_copy(self.own(k), self.bands.rows(self.acc.at[k], k), self.store_sem.at[k])
 
     def near(self):
         for k in COLOURS:
@@ -321,7 +359,7 @@
             self.ring.arrived(k, NEAR)
             for m in WAYS:
                 self.load(k, m).wait()
-                add_into(self.passed.at[k, m], self.relay_in.at[k, m])
+                add_into(self.ring.carried(self.passed, k, m), self.ring.carried(self.relay_in, k, m))
             self.ring.start(k, ADDED)
 
     def settle(self, then=None):
@@ -329,7 +367,7 @@
             self.load(k, FAR).wait()
             for base in (FAR, ADDED):
                 self.ring.arrived(k, base)
-            add_into(self.own.at[k], *(self.landing.at[k, m] for m in WAYS))
+            add_into(self.own(k), *(self.bands.rows(self.landing.at[k, m], k) for m in WAYS))
             if then is None:
                 self.store(k).start()
             else:
@@ -342,45 +380,29 @@
                 self.store(k).wait()
 
 
-ORDERS = {WIDE: "xzy", DOWN: "zyx"}
-
-
-def rest_dims(kind, k):
-    return [d for d in ORDERS[kind] if d != COLOUR_DIMS[k][FIRST]]
-
-
 class Rest:
-    def __init__(self, kind, acc, result, own, relay2, in2, relay3, in3, *sems):
-        self.kind, self.acc, self.own, self.result = kind, acc, own, result
+    def __init__(self, bands, acc, result, own, relay2, in2, relay3, in3, *sems):
+        self.bands, self.acc, self.own, self.result = bands, acc, own, result
         self.in2, self.in3, self.relay2, self.relay3, self.load_sem, self.store_sem = in2, in3, relay2, relay3, *sems[-2:]
-        rows, cut = UNITS[kind][0], relay3.shape[2]
-        cuts = pl.ds(0, cut), pl.ds(cut, rows - cut)
-        self.second = Ring(SECOND, functools.partial(self.terms, acc), relay2, relay2, in2, *sems[:PAIR])
-        third = lambda k, v, half=None: in2.at[(k, 0, v) + (() if half is None else (cuts[half],))]
-        self.third = Ring(THIRD, third, relay3, relay3, in3, *sems[PAIR:2 * PAIR], rows=cuts)
-
-    @staticmethod
-    def scratch(kind):
-        vm = lambda *lead: pltpu.VMEM(unit_array(kind, *lead), F32)
-        rows, cols = UNITS[kind]
-        dma = pltpu.SemaphoreType.DMA
-        cut = (rows // SUB + 1) // PAIR * SUB
-        return [vm(C, SIDE, SIDE), vm(C, PAIR, PAIR), vm(C, PAIR, SIDE), pltpu.VMEM((C, PAIR, cut, cols), F32), vm(C, PAIR),
-                *Ring.semaphores(), *Ring.semaphores(), dma((C,)), dma((C,))]
-
-    @staticmethod
-    def sums(kind):
-        return sds(F32, *unit_array(kind, C))
+        self.second = Ring(SECOND, bands, functools.partial(self.terms, acc), relay2, relay2, in2, *sems[:PAIR])
+        self.third = Ring(THIRD, bands, self.final, relay3, relay3, in3, *sems[PAIR:2 * PAIR])
 
     def terms(self, ref, k, v, half=None):
         other = ALL if half is None else duo(half)
-        return ref.at[(k, v, other) if rest_dims(self.kind, k)[0] == COLOUR_DIMS[k][SECOND] else (k, other, v)]
+        first = self.bands.rest(k)[0] == COLOUR_DIMS[k][SECOND]
+        return self.bands.rows(ref.at[(k, v, other) if first else (k, other, v)], k)
+
+    def final(self, k, v, half=None):
+        if half is None:
+            return self.bands.rows(self.in2.at[k, 0, v], k)
+        return self.in2.at[k, 0, v, self.bands.cuts(k)[half]]
 
     def load(self, k):
-        return pltpu.make_async_copy(self.acc.at[k], self.own.at[k], self.load_sem.at[k])
+        return pltpu.make_async_copy(self.bands.rows(self.acc.at[k], k), self.bands.rows(self.own.at[k], k), self.load_sem.at[k])
 
     def store(self, k):
-        return pltpu.make_async_copy(self.in3.at[k, 0], self.result.at[k], self.store_sem.at[k])
+        rows = self.bands.rows
+        return pltpu.make_async_copy(rows(self.in3.at[k, 0], k), rows(self.result.at[k], k), self.store_sem.at[k])
 
     def send(self, k):
         for base in (NEAR, FAR):
@@ -401,7 +423,8 @@
         for k in COLOURS:
             self.second.arrived(k, NEAR)
             for m in WAYS:
-                add_into(self.relay2.at[k, m], self.terms(self.own, k, me.shift(COLOUR_DIMS[k][SECOND], toward(m)), m))
+                terms = self.terms(self.own, k, me.shift(COLOUR_DIMS[k][SECOND], toward(m)), m)
+                add_into(self.second.carried(self.relay2, k, m), terms)
             self.second.start(k, ADDED)
 
     def settle(self):
@@ -409,7 +432,8 @@
         for k in COLOURS:
             for base in (FAR, ADDED):
                 self.second.arrived(k, base)
-            add_into(self.in2.at[k, 0], self.in2.at[k, 1], self.terms(self.own, k, me.at[COLOUR_DIMS[k][SECOND]]))
+            plus, minus = (self.bands.rows(self.in2.at[k, m], k) for m in WAYS)
+            add_into(plus, minus, self.terms(self.own, k, me.at[COLOUR_DIMS[k][SECOND]]))
             for base in (NEAR, FAR):
                 self.third.start(k, base)
 
@@ -419,7 +443,7 @@
             self.third.arrived(k, NEAR)
             for m in WAYS:
                 mine = self.third.carried(self.relay3, k, m)
-                mine[...] += self.third.terms(k, me.shift(COLOUR_DIMS[k][THIRD], toward(m)), m)[...]
+                mine[...] += self.final(k, me.shift(COLOUR_DIMS[k][THIRD], toward(m)), m)[...]
             self.third.start(k, ADDED)
 
     def settle_third(self):
@@ -427,7 +451,8 @@
         for k in COLOURS:
             for base in (FAR, ADDED):
                 self.third.arrived(k, base)
-            self.in3[k, 0] += self.in3[k, 1] + self.third.terms(k, me.at[COLOUR_DIMS[k][THIRD]])[...]
+            plus, minus = (self.bands.rows(self.in3.at[k, m], k) for m in WAYS)
+            plus[...] += minus[...] + self.final(k, me.at[COLOUR_DIMS[k][THIRD]])[...]
             if self.result is not None:
                 self.store(k).start()
 
@@ -438,33 +463,35 @@
             for k in COLOURS:
                 self.store(k).wait()
 
+    def sums(self):
+        return self.in3.at[:, 0]
+
 
 class Spread:
-    def __init__(self, kind, result, total, send, recv, local):
-        rows = UNITS[kind][0]
-        cut = rows // SUB // PAIR * SUB
-        self.result, self.total, self.sems, self.local = result, total, (send, recv), local
-        self.cuts = pl.ds(0, cut), pl.ds(cut, rows - cut)
+    def __init__(self, bands, result, total, send, recv, local):
+        self.bands, self.result, self.total, self.sems, self.local = bands, result, total, (send, recv), local
 
     @staticmethod
     def scratch():
         return [pltpu.SemaphoreType.DMA((C, ADDED))] * PAIR + [pltpu.SemaphoreType.DMA((C,))]
 
-    @staticmethod
-    def sums(kind):
-        return sds(F32, *unit_array(kind, SIDE, C))
+    def mine(self, k):
+        return self.bands.rows(self.result.at[k], k)
+
+    def place(self, k):
+        return self.bands.rows(self.total.at[Torus().at["x"], k], k)
 
     def hop(self, k, m):
         me = Torus()
         by = toward(m)
         if m < FAR:
-            src, dst = self.result.at[k], self.total.at[me.at["x"], k]
+            src, dst = self.mine(k), self.place(k)
         else:
-            dst = src = self.total.at[me.shift("x", -by), k, self.cuts[m - FAR]]
+            dst = src = self.total.at[me.shift("x", -by), k, self.bands.cuts(k)[m - FAR]]
         return remote(src, dst, self.sems, (k, m), me.neighbour("x", by))
 
     def own(self, k):
-        return pltpu.make_async_copy(self.result.at[k], self.total.at[Torus().at["x"], k], self.local.at[k])
+        return pltpu.make_async_copy(self.mine(k), self.place(k), self.local.at[k])
 
     def begin(self):
         for k in COLOURS:
@@ -500,34 +527,6 @@
     return pl.pallas_call(
         kernel, out_shape=sds(BF16, *Gather.shape(kind)), in_specs=[ANY], out_specs=ANY,
         scratch_shapes=Gather.semaphores(), compiler_params=comm_params(collective_id), name="gather_" + kind)(piece)
-
-
-def last_scatter_kernel(part, acc_up, result_up, *refs):
-    outs, refs = refs[:SIDE], list(refs[SIDE:])
-    take = lambda like: [refs.pop(0) for _ in like]
-    a, b = (First(WIDE, h, part, None, *take(First.scratch(WIDE))) for h in WAYS)
-    rest_a, rest_b = (Rest(WIDE, f.own, None, f.own, *take(Rest.scratch(WIDE)[1:])) for f in (a, b))
-    late = Rest(WIDE, acc_up, None, *take(Rest.scratch(WIDE)))
-    results = [rest.in3.at[:, 0] for rest in (rest_a, rest_b, late)]
-    spread_a, spread_b, spread_late, early = (
-        Spread(WIDE, *pair, *take(Spread.scratch())) for pair in zip([*results, result_up], outs))
-    enter()
-    for step in (late.begin, early.begin, a.near, late.loaded, late.relay, a.far, early.forward, late.settle, a.relay, b.near,
-                 late.relay_third, late.settle_third, b.far, late.finish, spread_late.begin,
-                 functools.partial(a.settle, rest_a.send), b.relay, rest_a.relay, spread_late.forward, rest_a.settle,
-                 rest_a.relay_third, functools.partial(b.settle, rest_b.send), rest_a.settle_third, rest_b.relay,
-                 rest_a.finish, spread_a.begin, rest_b.settle, spread_a.forward, rest_b.relay_third, rest_b.settle_third,
-                 rest_b.finish, spread_b.begin, spread_b.forward, early.finish, spread_late.finish, spread_a.finish,
-                 spread_b.finish, a.finish, b.finish):
-        step()
-
-
-def last_scatter(part, acc_up, result_up, collective_id):
-    return pl.pallas_call(
-        last_scatter_kernel, out_shape=(Spread.sums(WIDE),) * SIDE, in_specs=[ANY] * O, out_specs=(ANY,) * SIDE,
-        scratch_shapes=First.scratch(WIDE) * PAIR + Rest.scratch(WIDE)[1:] * PAIR + Rest.scratch(WIDE) +
-        Spread.scratch() * SIDE,
-        compiler_params=comm_params(collective_id), name="last_scatter")(part, acc_up, result_up)
 
 
 class Background:
@@ -542,28 +541,8 @@
                     step()
 
 
-class Pipeline:
-    def __init__(self, places, first, rest=None, spread=None):
-        rest_steps = (rest.loaded, rest.relay) if rest else ()
-        groups = [[*((rest.begin,) if rest else ()), *((spread.begin,) if spread else ()), first.near],
-                  [*rest_steps, first.far, *((spread.forward,) if spread else ())],
-                  [*((rest.settle,) if rest else ()), first.relay],
-                  [rest.relay_third] if rest else [],
-                  [first.settle, *((rest.settle_third,) if rest else ()), first.finish, *((rest.finish,) if rest else ()),
-                   *((spread.finish,) if spread else ())]]
-        self.groups = list(zip([("start", 0), *places], groups))
-
-    def visit(self, place):
-        for (where, j), group in self.groups:
-            if where == place:
-                @at_step(j)
-                def _():
-                    for step in group:
-                        step()
-
-
 class Push:
-    def __init__(self, src, tail, rows, sems, slot):
+    def __init__(self, src, tail, rows, sems, slot=0):
         body = BODY * len(SEQ_PAIR)
         tails = TAIL * len(SEQ_PAIR)
         self.copies = [
@@ -784,8 +763,8 @@
 
 
 def put_rows(ref, tail, s, t):
-    ref[pl.ds(BODY * s, BODY)] = t[:BODY]
-    ref[pl.ds(tail + TAIL * s, TAIL)] = t[BODY:]
+    ref[pl.ds(pl.multiple_of(BODY * s, BODY), BODY)] = t[:BODY]
+    ref[pl.ds(pl.multiple_of(tail + TAIL * s, TAIL), TAIL)] = t[BODY:]
 
 
 DOWN_PLAN = {"start": ((0, 0, 1),), "end": ((1, 1, 5), (3, 5, 8), (5, 8, 9), (TILES + 4, 9, 12), (2 * TILES - 1, 12, None))}
@@ -861,11 +840,12 @@
     return pl.BlockSpec((1, D, HALF), lambda j: (index(j) // PAIR, 0, index(j) % PAIR))
 
 
-MLP_PLACES = (("end", 0), ("end", 2), ("end", 3), ("end", TILES - 1))
+MLP_PLAN = {"start": ((0, 0, 2),), "end": ((3, 2, 3), (TILES - 1, 3, None))}
 
 
 def mlp_out_kernel(act, slope, gz, w_up, w_down, vec, part, d_pre, db_up, mlp, d_h2, sums, dm, *scratch):
-    hosted = Pipeline(MLP_PLACES, First(DOWN, 0, part, sums, *scratch))
+    first = First(Bands(DOWN), part, sums, *scratch)
+    hosted = Background([first.near, first.far, first.relay, first.settle, first.finish], MLP_PLAN)
     at_step(0)(enter)
     hosted.visit("start")
 
@@ -887,11 +867,11 @@
     return pl.pallas_call(
         mlp_out_kernel, grid=(TILES,),
         out_shape=(sds(BF16, PAIR, SIDE, TT, HALF), sds(F32, TILES, 1, HALF), sds(F32, TT, D), sds(F32, TT, D),
-                   First.sums(DOWN)),
+                   Bands(DOWN).sums()),
         in_specs=[along(1, TT, HALF), along(1, TT, HALF), whole(*SEQS), up_tile(), along(0, HALF, D), whole(8, D), ANY],
         out_specs=(pl.BlockSpec((1, 1, TT, HALF), lambda j: (j % PAIR, j // PAIR, 0, 0)), along(0, 1, 1, HALF),
                    whole(TT, D), whole(TT, D), ANY),
-        scratch_shapes=[pltpu.VMEM((TT, D), BF16)] + First.scratch(DOWN),
+        scratch_shapes=[pltpu.VMEM((TT, D), BF16)] + Bands(DOWN).first(),
         compiler_params=comm_params(collective_id), name="mlp_out",
     )(act, slope, gz, w_up, w_down, vec, part)
 
@@ -923,7 +903,7 @@
         d_o[...] = dot_nt(da_rows[...], w_out[0]).astype(BF16)
 
 
-def attention_back(qkv, d_o, d_qkv, db, acc, visit):
+def attention_back(s, qkv, d_o, d_qkv, db, acc, b_rows, away, first, visit):
     acc[...] = jnp.zeros_like(acc)
     for h in range(HEADS):
         lanes, mask = window(h)
@@ -941,70 +921,56 @@
         visit(h)
     accumulate(db, jnp.concatenate([col_sum(acc[i]) for i in (Q, K, V)], axis=0))
     for n in (Q, K, V):
-        for i, t in enumerate(halves_of(acc[n])):
-            d_qkv[i, n] = t
+        left, right = halves_of(acc[n])
+        d_qkv[0, n] = left
+        d_qkv[1, n] = right
+        put_rows(b_rows.at[n], TAILS, s, jnp.where(first, left, right))
+        put_rows(away.at[n], OWN_BODY, s, jnp.where(first, right, left))
 
 
 PER = HALF // STEP
 
 
 class WideGrads:
-    def __init__(self, a, a_of, b, out, base, a_rows, a_cols, b_rows, *sems):
-        self.a, self.a_of, self.b, self.out, self.base = a, a_of, b, out, base
+    def __init__(self, inputs, a_of, cotangents, out, base, lead, a_rows, a_cols, b_rows):
+        self.inputs, self.a_of, self.cotangents, self.out, self.base, self.lead = inputs, a_of, cotangents, out, base, lead
         self.a_rows, self.a_cols, self.b_rows = a_rows, a_cols, b_rows
-        self.a_sems, self.b_sems = sems[:C], sems[C:]
 
     @staticmethod
     def scratch(inputs):
-        return ([pltpu.VMEM((inputs, ROWS, D), BF16), pltpu.VMEM((inputs, D, ROWS), BF16),
-                 pltpu.VMEM((SIDE, ROWS, HALF), BF16)] + Exchange.semaphores(inputs) + Exchange.semaphores(SIDE))
-
-    def input(self, i):
-        return Exchange(self.a[i], self.a[i], self.a_rows.at[i], self.a_sems, (i,))
-
-    def cotangent(self, n):
-        c = Torus().at["c"]
-        b = self.b[n]
-        return Exchange(b(c), b(1 - c), self.b_rows.at[n], self.b_sems, (n,))
-
-    def new_input(self, n):
-        return n == 0 or self.a_of[n] != self.a_of[n - 1]
-
-    def begin(self):
-        for n in range(SIDE):
-            if self.new_input(n):
-                self.input(self.a_of[n]).start()
-            self.cotangent(n).start()
+        return [pltpu.VMEM((inputs, ROWS, D), BF16), pltpu.VMEM((inputs, D, ROWS), BF16), pltpu.VMEM((SIDE, ROWS, HALF), BF16)]
 
     def step(self):
         j = pl.program_id(0)
-        for n in range(SIDE):
-            @at_step(self.base + PER * n)
+        done = []
+        for t in range(SIDE):
+            n = (t + self.lead) % SIDE
+
+            @at_step(self.base + PER * t)
             def _():
-                if self.new_input(n):
-                    i = self.a_of[n]
-                    self.input(i).wait()
+                i = self.a_of[n]
+                if i not in done:
+                    self.inputs[i].wait()
                     self.a_cols[i] = self.a_rows[i].T
-                self.cotangent(n).wait()
+                    done.append(i)
+                self.cotangents[n].wait()
 
         @pl.when(j >= self.base)
         def _():
-            n = lax.div(j - self.base, PER)
+            n = lax.rem(lax.div(j - self.base, PER) + self.lead, SIDE)
             cols = pl.ds(pl.multiple_of(lax.rem(j - self.base, PER) * STEP, STEP), STEP)
-            i = 0 if len(self.a) == 1 else lax.div(n, O)
+            i = 0 if len(self.inputs) == 1 else lax.div(n, O)
             self.out[0] = dot(self.a_cols[i], self.b_rows[n, :, cols])
 
     def finish(self):
-        for i in range(len(self.a)):
-            self.input(i).finish()
-        for n in range(SIDE):
-            self.cotangent(n).finish()
-
-
-def grads_block(base):
+        for move in (*self.inputs, *self.cotangents):
+            move.finish()
+
+
+def grads_block(base, lead):
     def index(j):
         n = jnp.maximum(j - base, 0)
-        return n // PER, 0, n % PER
+        return (n // PER + lead) % SIDE, 0, n % PER
 
     return pl.BlockSpec((1, D, STEP), index)
 
@@ -1020,81 +986,124 @@
     return along(0, 1, SEQ, D, index=upto(LAST_SEQ))
 
 
-MID_PLACES = (("end", 0), ("end", 4), ("end", 10), ("end", LAST_SEQ + GRAD_STEPS))
+MID_PLAN = {"start": ((0, 0, 1),), "end": ((1, 1, 3), (8, 3, 4), (11, 4, 5), (LAST_SEQ + GRAD_STEPS, 5, None))}
 
 
 def mid_kernel(*refs):
     refs = list(refs)
     take = lambda n: [refs.pop(0) for _ in range(n)]
-    ins, (h2, d_pre, part, acc), outs, (d_up, sums, result) = take(7), take(4), take(5), take(3)
-    outs.append(refs.pop(0))
-    grads = WideGrads((h2,), (0,) * SIDE, [lambda c, i=i: d_pre.at[c, i] for i in range(SIDE)], d_up, SEQS[0],
-                      *take(len(WideGrads.scratch(1))))
-    first = First(DOWN, 1, part, sums, *take(len(First.scratch(DOWN))))
-    hosted = Pipeline(MID_PLACES, first, Rest(DOWN, acc, result, *refs))
+    ins, (h2, d_pre, acc), outs, (d_up, result), da_rows = take(7), take(3), take(5), take(2), refs.pop(0)
+    rows, a_sems, b_sems = take(3), take(C), take(C)
+    rest = Rest(Bands(DOWN), acc, result, *refs)
+    hosted = Background([rest.begin, rest.loaded, rest.relay, rest.settle, rest.relay_third, rest.settle_third, rest.finish],
+                        MID_PLAN)
+    c = Torus().at["c"]
+    grads = WideGrads(
+        [Exchange(h2, h2, rows[0].at[0], a_sems, ())], (0,) * SIDE,
+        [Exchange(d_pre.at[c, n], d_pre.at[1 - c, n], rows[2].at[n], b_sems, (n,)) for n in range(SIDE)], d_up, SEQS[0], 0, *rows)
     at_step(0)(enter)
     hosted.visit("start")
-    at_step(0)(grads.begin)
-    pl.when(pl.program_id(0) < SEQS[0])(lambda: mid(*ins, *outs))
+
+    @at_step(0)
+    def _():
+        for move in (*grads.inputs, *grads.cotangents):
+            move.start()
+
+    pl.when(pl.program_id(0) < SEQS[0])(lambda: mid(*ins, *outs, da_rows))
     grads.step()
     hosted.visit("end")
     at_step(LAST_SEQ + GRAD_STEPS)(grads.finish)
 
 
-def mid_call(mlp, d_h2, att, x, gz, vec, w_attn, h2, d_pre, part, acc, collective_id):
+def mid_call(mlp, d_h2, att, x, gz, vec, w_attn, h2, d_pre, acc, collective_id):
     return pl.pallas_call(
         mid_kernel, grid=(SEQS[0] + GRAD_STEPS,),
         out_shape=(sds(BF16, *SEQS), sds(F32, TT, D), sds(BF16, PAIR, TT, HALF), sds(BF16, TT, D), sds(F32, 8, D),
-                   sds(F32, SIDE, D, HALF), First.sums(DOWN), Rest.sums(DOWN)),
-        in_specs=[tok_block()] * O + [seq_block()] * PAIR + [whole(8, D), w_out_block()] + [ANY] * SIDE,
+                   sds(F32, SIDE, D, HALF), Bands(DOWN).result()),
+        in_specs=[tok_block()] * O + [seq_block()] * PAIR + [whole(8, D), w_out_block()] + [ANY] * O,
         out_specs=(seq_block(), tok_block(), along(1, PAIR, TOK, HALF, index=upto(LAST_SEQ)), whole(TT, D), whole(8, D),
-                   grads_block(SEQS[0]), ANY, ANY),
-        scratch_shapes=[pltpu.VMEM((TT, D), BF16)] + WideGrads.scratch(1) + First.scratch(DOWN) + Rest.scratch(DOWN),
+                   grads_block(SEQS[0], 0), ANY),
+        scratch_shapes=[pltpu.VMEM((TT, D), BF16)] + WideGrads.scratch(1) + Exchange.semaphores() + Exchange.semaphores(SIDE) +
+        Bands(DOWN).later(),
         compiler_params=comm_params(collective_id), name="mid",
-    )(mlp, d_h2, att, x, gz, vec, w_attn, h2, d_pre, part, acc)
-
-
-ATTN_PLACES = ((6, 0), (1, LAST_SEQ), (11, LAST_SEQ), ("end", LAST_SEQ))
-
-
-def attn_back_kernel(qkv, d_o, part, acc_down, result_down, d_qkv, db, sums, result, total, acc, *scratch):
-    n, m = len(First.scratch(WIDE)), len(Rest.scratch(DOWN))
-    hosted = Pipeline(ATTN_PLACES, First(WIDE, 0, part, sums, *scratch[:n]),
-                      Rest(DOWN, acc_down, result, *scratch[n:n + m]), Spread(DOWN, result_down, total, *scratch[n + m:]))
+    )(mlp, d_h2, att, x, gz, vec, w_attn, h2, d_pre, acc)
+
+
+ATTN_PLAN = {"start": ((0, 0, 3),), 6: ((0, 3, 4),), "end": ((LAST_SEQ, 4, 5), (LAST_SEQ + GRAD_STEPS, 5, None))}
+
+
+def attn_back_kernel(*refs):
+    refs = list(refs)
+    take = lambda n: [refs.pop(0) for _ in range(n)]
+    (qkv, d_o), (h1, o, d_att, part, result), (d_qkv, db, d_attn, sums, total) = take(2), take(5), take(5)
+    acc, away, rows = refs.pop(0), refs.pop(0), take(3)
+    a_sems, b_sems, away_sems = take(C), take(C), take(PAIR)
+    first = First(Bands(WIDE), part, sums, *take(len(Bands(WIDE).first())))
+    spread = Spread(Bands(DOWN), result, total, *refs)
+    hosted = Background([spread.begin, first.near, first.far, spread.forward, first.relay, first.settle, first.finish,
+                         spread.finish], ATTN_PLAN)
+    c = Torus().at["c"]
+    pushes = [Push(away.at[n], OWN_BODY, rows[2].at[n], away_sems, n) for n in range(O)]
+    grads = WideGrads(
+        [Exchange(a, a, rows[0].at[i], a_sems, (i,)) for i, a in enumerate((h1, o))], (0,) * O + (1,),
+        pushes + [Exchange(d_att.at[c], d_att.at[1 - c], rows[2].at[O], b_sems, ())], d_attn, SEQS[0], O, *rows)
     at_step(0)(enter)
     hosted.visit("start")
-    attention_back(qkv, d_o, d_qkv, db, acc, hosted.visit)
+
+    @at_step(0)
+    def _():
+        for move in (*grads.inputs, grads.cotangents[O]):
+            move.start()
+
+    @at_step(SEQS[0])
+    def _():
+        for push in pushes:
+            push.start()
+
+    j = pl.program_id(0)
+    pl.when(j < SEQS[0])(lambda: attention_back(j, qkv, d_o, d_qkv, db, acc, rows[2], away, c == 0, hosted.visit))
+
+    grads.step()
     hosted.visit("end")
-
-
-def attn_back_call(qkv, d_o, part, acc_down, result_down, collective_id):
+    at_step(LAST_SEQ + GRAD_STEPS)(grads.finish)
+
+
+def attn_back_call(qkv, d_o, h1, o, d_att, part, result, collective_id):
     return pl.pallas_call(
-        attn_back_kernel, grid=SEQS[:1],
-        out_shape=(sds(BF16, PAIR, O, TT, HALF), sds(F32, O, D), First.sums(WIDE), Rest.sums(DOWN), Spread.sums(DOWN)),
-        in_specs=[along(1, O, TOK, D), tok_block()] + [ANY] * O,
-        out_specs=(along(2, PAIR, O, TOK, HALF), whole(O, D)) + (ANY,) * O,
-        scratch_shapes=[pltpu.VMEM((O, SEQ, D), F32)] + First.scratch(WIDE) + Rest.scratch(DOWN) + Spread.scratch(),
+        attn_back_kernel, grid=(SEQS[0] + GRAD_STEPS,),
+        out_shape=(sds(BF16, PAIR, O, TT, HALF), sds(F32, O, D), sds(F32, SIDE, D, HALF), Bands(WIDE).sums(),
+                   Bands(DOWN).total()),
+        in_specs=[along(1, O, TOK, D, index=upto(LAST_SEQ)), tok_block()] + [ANY] * 5,
+        out_specs=(along(2, PAIR, O, TOK, HALF, index=upto(LAST_SEQ)), whole(O, D), grads_block(SEQS[0], O), ANY, ANY),
+        scratch_shapes=[pltpu.VMEM((O, SEQ, D), F32), pltpu.VMEM((O, PAIR * TOK, HALF), BF16)] + WideGrads.scratch(2) +
+        Exchange.semaphores(PAIR) + Exchange.semaphores() + Push.semaphores(O) + Bands(WIDE).first() + Spread.scratch(),
         compiler_params=comm_params(collective_id), name="attn_back",
-    )(qkv, d_o, part, acc_down, result_down)
+    )(qkv, d_o, h1, o, d_att, part, result)
 
 
 IN_STEPS = PAIR * O
-IN_PLACES = (("end", 1), ("end", IN_STEPS - 1), ("end", IN_STEPS + SIDE), ("end", IN_STEPS + GRAD_STEPS - 1))
-
-
-def in_back_kernel(*refs):
+SLOT = 40
+LAST_PLAN = {"start": ((0, 0, 2),), "end": ((O, 2, 5),)}
+
+
+def last_kernel(*refs):
     refs = list(refs)
     take = lambda n: [refs.pop(0) for _ in range(n)]
-    (d_half, w, x, g_res, vec), (h1, o, d_qkv, d_att, part, acc_up, result_down) = take(5), take(7)
-    (dx, sums, d_attn), outs, acc = take(3), take(3), refs.pop(0)
-    b = [lambda c, i=i: d_qkv.at[c, i] for i in range(O)] + [lambda c: d_att.at[c]]
-    grads = WideGrads((h1, o), (0,) * O + (1,), b, d_attn, IN_STEPS, *take(len(WideGrads.scratch(2))))
-    first = First(WIDE, 1, part, outs[0], *take(len(First.scratch(WIDE))))
-    rest = Rest(WIDE, acc_up, outs[1], *take(len(Rest.scratch(WIDE))))
-    hosted = Pipeline(IN_PLACES, first, rest, Spread(DOWN, result_down, outs[2], *refs))
+    (d_half, w, x, g_res, vec), (small, acc_up, _), (dx, part, *totals) = take(5), take(3), take(5)
+    acc, sums, pair_sums, block, block_sem, swap_sems = refs.pop(0), refs.pop(0), refs.pop(0), refs.pop(0), refs.pop(0), take(PAIR)
+    halves = [Bands(WIDE, h) for h in WAYS]
+    a, b = (First(bands, part, None, *take(len(bands.first()))) for bands in halves)
+    rest_a, rest_b = (Rest(f.bands, f.own_all, None, f.own_all, *take(len(f.bands.later()) - 1)) for f in (a, b))
+    rest_up = Rest(Bands(WIDE), acc_up, None, *take(len(Bands(WIDE).later())))
+    spread_up, spread_a, spread_b = (
+        Spread(r.bands, r.sums(), total, *take(len(Spread.scratch()))) for r, total in zip((rest_up, rest_a, rest_b), totals))
+    hosted = Background([rest_up.begin, a.near, rest_up.loaded, rest_up.relay, a.far], LAST_PLAN)
+    me = Torus()
+    swap = remote(sums, pair_sums, swap_sems, (), me.partner())
+    fetch = pltpu.make_async_copy(small, block, block_sem)
     at_step(0)(enter)
     hosted.visit("start")
-    at_step(0)(grads.begin)
+    at_step(0)(fetch.start)
 
     @pl.when(pl.program_id(0) < IN_STEPS)
     def _():
@@ -1102,37 +1111,66 @@
 
     @at_step(IN_STEPS - 1)
     def _():
-        rows = jnp.zeros((BO, D), F32)
+        rows = jnp.zeros((SUB, D), F32)
         for s in SEQ_PAIR:
             xhat, rstd = norm_stats(x[s].astype(F32))
             tokens = pl.ds(TOK * s, SEQ)
             dh = acc[tokens]
-            rows = rows + jnp.concatenate([col_sum(dh * xhat), col_sum(dh)], axis=0)
+            rows = rows + jnp.concatenate([col_sum(dh * xhat), col_sum(dh), jnp.zeros((SUB - BO, D), F32)], axis=0)
             dx[s] = (g_res[tokens] + norm_back(xhat, rstd, dh * row(vec, G1))).astype(BF16)
         sums[...] = rows
 
-    grads.step()
     hosted.visit("end")
-    at_step(IN_STEPS + GRAD_STEPS - 1)(grads.finish)
-
-
-def in_back_call(d_qkv, w_attn, x, g_res, vec, h1, o, d_att, part, acc_up, result_down, collective_id):
+
+    @at_step(IN_STEPS)
+    def _():
+        swap.start()
+        fetch.wait()
+        rest_up.settle()
+        a.relay()
+        swap.wait()
+        both = sums[...] + pair_sums[...]
+        for d in range(DEVICES):
+            at = CHIP * (d // PAIR) + SLOT + OWN * (d % PAIR)
+            block[at:at + BO, :OWN] = both[:BO, OWN * d:OWN * d + OWN]
+
+        @pl.when(me.at["c"] == 1)
+        def _():
+            for z in range(SIDE):
+                for y in range(SIDE):
+                    rows = block.at[pl.ds(CHIP * (SIDE * z + y), CHIP)]
+                    put = pltpu.make_async_copy(rows, part.at[0, z, y, :, pl.ds(HALF - LANES, LANES)], block_sem)
+                    put.start()
+            pltpu.make_async_copy(block, small, block_sem).wait()
+
+        for step in (b.near, rest_up.relay_third, b.far, functools.partial(a.settle, rest_a.send), rest_up.settle_third,
+                     spread_up.begin, b.relay, rest_a.relay, rest_a.settle, spread_up.forward, rest_a.relay_third,
+                     functools.partial(b.settle, rest_b.send), rest_a.settle_third, spread_a.begin, rest_b.relay, rest_b.settle,
+                     spread_a.forward, rest_b.relay_third, rest_b.settle_third, spread_b.begin, spread_b.forward,
+                     spread_up.finish, spread_a.finish, spread_b.finish, rest_up.finish, rest_a.finish, rest_b.finish,
+                     a.finish, b.finish):
+            step()
+
+
+def last_call(d_qkv, w_attn, x, g_res, vec, small, acc_up, part, collective_id):
     low = upto(IN_STEPS - 1)
+    halves = [Bands(WIDE, h) for h in WAYS]
+    dma = pltpu.SemaphoreType.DMA
     return pl.pallas_call(
-        in_back_kernel, grid=(IN_STEPS + GRAD_STEPS,),
-        out_shape=(sds(BF16, *SEQS), sds(F32, BO, D), sds(F32, SIDE, D, HALF), First.sums(WIDE), Rest.sums(WIDE),
-                   Spread.sums(DOWN)),
+        last_kernel, grid=(IN_STEPS + 1,),
+        out_shape=(sds(BF16, *SEQS), sds(F32, *part.shape), Bands(WIDE).total(), *(h.total() for h in halves)),
         in_specs=[pl.BlockSpec((1, 1, TT, HALF), lambda j: (low(j) % PAIR, low(j) // PAIR, 0, 0)), up_tile(low),
-                  whole(*SEQS), whole(TT, D), whole(8, D)] + [ANY] * 7,
-        out_specs=(whole(*SEQS), whole(BO, D), grads_block(IN_STEPS), ANY, ANY, ANY),
-        scratch_shapes=[pltpu.VMEM((TT, D), F32)] + WideGrads.scratch(2) + First.scratch(WIDE) + Rest.scratch(WIDE) +
-        Spread.scratch(),
-        compiler_params=comm_params(collective_id), name="in_back",
-    )(d_qkv, w_attn, x, g_res, vec, h1, o, d_qkv, d_att, part, acc_up, result_down)
+                  whole(*SEQS), whole(TT, D), whole(8, D)] + [ANY] * O,
+        out_specs=(whole(*SEQS),) + (ANY,) * SIDE,
+        scratch_shapes=[pltpu.VMEM((TT, D), F32), pltpu.VMEM((SUB, D), F32), pltpu.VMEM((SUB, D), F32),
+                        pltpu.VMEM((D, LANES), F32), dma, dma, dma] + halves[0].first() * PAIR + halves[0].later()[1:] * PAIR +
+        Bands(WIDE).later() + Spread.scratch() * O,
+        input_output_aliases={7: 1},
+        compiler_params=comm_params(collective_id), name="last",
+    )(d_qkv, w_attn, x, g_res, vec, small, acc_up, part)
 
 
 BQ, BU, VEC = 3 * D // 32, 3 * D // 32 + FF // 32, 3 * D // 32 + FF // 32 + 8 * OWN
-DEVICES = 32
 
 
 def pair_swap(a):
@@ -1165,50 +1203,56 @@
     return small[:, :BQ].reshape(O, 1, D), small[:, BQ:BU].reshape(FF), vec
 
 
-def small_grads(db_qkv, db_up, sums, core):
-    vec = sums.reshape(8, DEVICES, OWN).transpose(1, 0, 2).reshape(DEVICES, VEC - BU)
+ROOM = 5 * LANES
+
+
+def small_grads(db_qkv, db_up, sums):
+    vec = sums[BO:].reshape(8 - BO, DEVICES, OWN).transpose(1, 0, 2).reshape(DEVICES, VEC - BU - BO * OWN)
     small = jnp.concatenate([db_qkv.reshape(DEVICES, BQ), db_up.reshape(DEVICES, BU - BQ), vec], axis=1)
-    small = (small + pair_swap(small)) * core.astype(F32)
-    return jnp.pad(small, ((0, 0), (0, OWN * LANES - VEC))).reshape(D, LANES)
-
-
-def final_rows(halves, first):
-    total = jnp.stack(halves, axis=2)
-    keep, give = by_core(first, total[..., :OWN, :], total[..., OWN:, :])
+    small = small + pair_swap(small)
+    small = jnp.pad(small, ((0, 0), (0, ROOM - small.shape[1]))).reshape(DEVICES, ROOM // LANES, LANES)
+    return jnp.pad(small, ((0, 0), (0, OWN - ROOM // LANES), (0, 0))).reshape(D, LANES)
+
+
+def rows_of(total):
+    return jnp.concatenate([total[:, k, :n] for k, (_, n) in enumerate(BANDS[WIDE])], axis=1)
+
+
+def final_rows(total, first):
+    keep, give = by_core(first, total[:, :OWN], total[:, OWN:])
     pair = jnp.stack(by_core(first, keep, pair_swap(give)), axis=1)
-    return pair.transpose(4, 0, 1, 2, 3, 5).reshape(OWN, SIDE, QCOLS)
-
-
-def final_down(halves, first):
-    down = jnp.concatenate(halves, axis=-1).reshape(FF // 16, HALF)
+    return pair.transpose(2, 0, 1, 3).reshape(OWN, SIDE, QCOLS)
+
+
+def final_down(total, first):
+    down = total.reshape(FF // 16, HALF)
     keep, give = by_core(first, down[:FF // DEVICES], down[FF // DEVICES:])
     left, right = by_core(first, keep, pair_swap(give))
     return jnp.concatenate([left, right[:, 2 * HALF - D:]], axis=1)
 
 
 def device_step(x, gz, *shards):
-    core = lax.rem(lax.axis_index("fsdp"), PAIR)
-    first = core == 0
+    first = lax.rem(lax.axis_index("fsdp"), PAIR) == 0
     attn, up, down = my_pieces(shards, first)
     w_attn = torus_gather(WIDE, attn, 0).reshape(SIDE, D, QCOLS)
     b_qkv, b_up, vec = small_params(w_attn)
     qkv, h1, o, att, h2, w_up = front_call(x, w_attn, b_qkv, vec, up, 1)
     w_up = w_up.reshape(SIDE, D, QCOLS)
     act, slope, part, w_down = mlp_in_call(h2, gz, w_up, b_up, vec, down, 2)
-    part = part.reshape((SIDE,) * 3 + (C, 32, HALF))
-    d_pre, db_up, mlp, d_h2, acc0 = mlp_out_call(act, slope, gz, w_up, w_down.reshape(FF, D), vec, part, 3)
-    z, g_res, d_att, d_o, sums, part, acc1, result0 = mid_call(mlp, d_h2, att, x, gz, vec, w_attn, h2, d_pre, part, acc0, 4)
+    part = part.reshape((SIDE,) * 3 + (C * UNIT, HALF))
+    d_pre, db_up, mlp, d_h2, acc = mlp_out_call(act, slope, gz, w_up, w_down.reshape(FF, D), vec, part, 3)
+    z, g_res, d_att, d_o, sums, part, result = mid_call(mlp, d_h2, att, x, gz, vec, w_attn, h2, d_pre, acc, 4)
     part = part.reshape((SIDE,) * 3 + (CHIP, HALF))
-    d_qkv, db_qkv, acc0, result1, down0 = attn_back_call(qkv, d_o, part, acc1, result0, 5)
-    dx, in_sums, part, acc1, result0, down1 = in_back_call(d_qkv, w_attn, x, g_res, vec, h1, o, d_att, part, acc0, result1, 6)
-    small = small_grads(db_qkv, db_up, jnp.concatenate([in_sums, sums[BO:]], axis=0), core)
-    part = part.at[0, :, HALF - LANES:].add(small).reshape((SIDE,) * 3 + (CHIP, HALF))
-    attn0, attn1, up1, up0 = last_scatter(part, acc1, result0, 7)
-    g_up = final_rows((up0, up1), first).reshape(OWN, FF)
-    attn = final_rows((attn0, attn1), first)
-    small = attn[:, 0, D:].reshape(OWN * LANES)
+    d_qkv, db_qkv, part, acc, down = attn_back_call(qkv, d_o, h1, o, d_att, part, result, 5)
+    small = small_grads(db_qkv, db_up, sums)
+    part = part.reshape((SIDE,) * 3 + (CHIP, HALF))
+    dx, _, up, attn0, attn1 = last_call(d_qkv, w_attn, x, g_res, vec, small, acc, part, 6)
+    g_up = final_rows(rows_of(up), first).reshape(OWN, FF)
+    attn = final_rows(jnp.concatenate([rows_of(attn0), rows_of(attn1)], axis=-1), first)
+    small = attn[:ROOM // LANES, 0, D:].reshape(ROOM)
+    vec = jnp.concatenate([attn[SLOT:SLOT + BO, 0, D:D + OWN], small[BU:VEC - BO * OWN].reshape(8 - BO, OWN)], axis=0)
     return (z, dx, attn[:, :O, :D].reshape(OWN, O * D), small[:BQ], attn[:, O, :D], g_up, small[BQ:BU],
-            final_down((down0, down1), first), small[BU:VEC].reshape(8, OWN))
+            final_down(down, first), vec)
 
 
 def solution(mesh):

time: 529 us -> 495 us (0.936)
  Pallas kernels: 458 us -> 434 us
  other arithmetic: 21 us -> 15 us
    pallas_call x3 -> x2, Pallas kernels: 193 us -> 172 us  [the longest x1 111 us: last_call(): pl.pallas_call(last_kernel, grid=(IN_STEPS + 1,), out_shape=(sds(BF16, *S...]
    pallas_call x1, Pallas kernels: 47 us -> 36 us  [mid_call(): pl.pallas_call(mid_kernel, grid=(SEQS[0] + GRAD_STEPS,), out_shape=(sds(B...]
    pallas_call x1, Pallas kernels: 55.4 us -> 63.7 us  [mlp_out_call(): pl.pallas_call(mlp_out_kernel, grid=(TILES,), out_shape=(sds(BF16, PAIR,...]
    scatter-add x1 -> x0, local copies, waits for them, and re-layouts: 5.6 us -> none  [device_step(): part.at[0, :, HALF - LANES:].add(small).reshape((SIDE,) * 3 + (CHIP, HALF))]
    another operation x7 -> x4, other arithmetic: 8.48 us -> 3.17 us
    unnamed x34 -> x25, local copies, waits for them, and re-layouts: 11.4 us -> 11.7 us
  transfers between devices with their start and end apart: 5 -> 5, of which waited for: 0 -> 0; matrix products, arithmetic and copies ran while one was open for 6% -> 5% of each run, Pallas kernels for 19% -> 23%
where the time goes in v5:
time: 495 us; the launch traced here: 491 us
  Pallas kernels  434 us (88%)
  local copies, waits for them, and re-layouts  31.8 us (6%)
  other arithmetic  15 us (3%)
  starting transfers between devices  8.99 us (2%)
    pallas_call x1, Pallas kernels, last_call(): pl.pallas_call(last_kernel, grid=(IN_STEPS + 1,), out_shape=(sds(BF16, *S...  111 us
    pallas_call x1, Pallas kernels, mlp_out_call(): pl.pallas_call(mlp_out_kernel, grid=(TILES,), out_shape=(sds(BF16, PAIR,...  63.7 us
    pallas_call x1, Pallas kernels, attn_back_call(): pl.pallas_call(attn_back_kernel, grid=(SEQS[0] + GRAD_STEPS,), out_shape=...  60.8 us
    pallas_call x1, Pallas kernels, mlp_in_call(): pl.pallas_call(mlp_in_kernel, grid=(2 * TILES,), out_shape=(sds(BF16, TT,...  55.8 us
    pallas_call x1, Pallas kernels, front_call(): pl.pallas_call(front_kernel, grid=(O + PAIR,), out_shape=(sds(BF16, O, TT...  54.8 us
    pallas_call x1, Pallas kernels, torus_gather(): pl.pallas_call(kernel, out_shape=sds(BF16, *Gather.shape(kind)), in_specs...  51.8 us
    pallas_call x1, Pallas kernels, mid_call(): pl.pallas_call(mid_kernel, grid=(SEQS[0] + GRAD_STEPS,), out_shape=(sds(B...  36 us
    unnamed x25, local copies, waits for them, and re-layouts  11.7 us
  transfers between devices with their start and end apart: 5, of which 0 were waited for; matrix products, arithmetic and copies ran while one was open for 5% of the time, Pallas kernels for 23%

profile of v5, /device:TPU:1, one launch (start us, length us, event | category | flops | bytes accessed | tf_op | source)
XLA Modules:
  0.0 491.0 jit_solution(7123766369031816563)
XLA Ops:
  5.1 1.4 collective-permute-start
  6.5 1.3 copy.56.x.refs_3_.refs_2_
  8.4 1.3 copy.57.gz.refs_4_
  9.7 1.6 dynamic-slice_convert_fusion.1
  12.1 51.8 %gather_wide.1 = bf16[4,4,4,88,1536]{4,3,2,1,0:T(8,128)(2,1)} custom-call(bf16[88,768]{1,0:T(8,128)(2,1)} %get-tuple-element.111.refs_0_), custom_call_target="tpu_custom_call" | custom-call | tf_op jit(solution)/shard_map/gather_wide/pallas_call | solution.py:527
  67.6 54.8 %front.1 = (bf16[3,544,1408]{2,1,0:T(8,128)(2,1)}, bf16[544,1408]{1,0:T(8,128)(2,1)}, bf16[544,1408]{1,0:T(8,128)(2,1)}, f32[544,1408]{1,0:T(8,128)}, bf16[544,1...) custom-call(bf16[2,257,1408]{2,1,0:T(8,128)(2,1)} %copy.56.x.refs_3_.refs_2_, bf16[4,1408,1536]{2,1,0:T(8,128)(2,1)} %bitcast.63, ...), custom_call_target="tpu_custom_call" | custom-call | tf_op jit(solution)/shard_map/front/pallas_call | solution.py:745
  122.4 55.8 %mlp_in.1 = (bf16[544,6144]{1,0:T(8,128)(2,1)}, f32[544,6144]{1,0:T(8,128)}, f32[6144,768]{1,0:T(8,128)}, bf16[4,4,2,4,3,16,1408]{6,5,4,3,2,1,0:T(8,128)(2,1)}) custom-call(bf16[544,1408]{1,0:T(8,128)(2,1)} %get-tuple-element.40.h2.refs_7_, bf16[2,257,1408]{2,1,0:T(8,128)(2,1)} %copy.57.gz.refs_4_, bf16[4,1408,1536]{2,1,0:T(8,128)(2,1)} %bitcast.66, ...), custom_call_target="tpu_custom_call" | custom-call | tf_op jit(solution)/shard_map/mlp_in/pallas_call | solution.py:826
  178.2 63.7 %mlp_out.1 = (bf16[2,4,544,768]{3,2,1,0:T(8,128)(2,1)}, f32[8,1,768]{2,1,0:T(1,128)}, f32[544,1408]{1,0:T(8,128)}, f32[544,1408]{1,0:T(8,128)}, f32[3,4,4,32,768]{4,3,2,1,0:T(8,128)}) custom-call(bf16[544,6144]{1,0:T(8,128)(2,1)} %get-tuple-element.42.act, f32[544,6144]{1,0:T(8,128)} %get-tuple-element.43.slope, bf16[2,257,1408]{2,1,0:T(8,128)(2,1)} %copy.57.gz.refs_4_, ...), custom_call_target="tpu_custom_call" | custom-call | tf_op jit(solution)/shard_map/mlp_out/pallas_call | solution.py:867
  242.8 36.0 %mid.1 = (bf16[2,257,1408]{2,1,0:T(8,128)(2,1)}, f32[544,1408]{1,0:T(8,128)}, bf16[2,544,768]{2,1,0:T(8,128)(2,1)}, bf16[544,1408]{1,0:T(8,128)(2,1)}, f32[8,140...) custom-call(f32[544,1408]{1,0:T(8,128)} %get-tuple-element.46.refs_0_, ...), custom_call_target="tpu_custom_call" | custom-call | tf_op jit(solution)/shard_map/mid/pallas_call | solution.py:1019
  279.9 60.8 %attn_back.1 = (bf16[2,3,544,768]{3,2,1,0:T(8,128)(2,1)}, f32[3,1408]{1,0:T(4,128)}, f32[4,1408,768]{2,1,0:T(8,128)}, f32[3,4,4,32,768]{4,3,2,1,0:T(8,128)}, f32[4,3,32,768]{3,2,1,0:T(8,128)}) custom-call(bf16[3,544,1408]{2,1,0:T(8,128)(2,1)} %get-tuple-element.52.refs_0_, bf16[544,1408]{1,0:T(8,128)(2,1)} %get-tuple-element.53.refs_1_, ...), custom_call_target="tpu_custom_call" | custom-call | tf_op jit(solution)/shard_map/attn_back/pallas_call | solution.py:1072
  341.7 2.4 collective-permute-start.1
  344.1 2.3 slice_select_fusion.2
  346.4 2.2 copy.79
  349.7 111.0 %last.1 = (bf16[2,257,1408]{2,1,0:T(8,128)(2,1)}, f32[4,4,4,88,768]{4,3,2,1,0:T(8,128)}, f32[4,3,32,768]{3,2,1,0:T(8,128)}, f32[4,3,32,384]{3,2,1,0:T(8,128)}, f32[4,3,32,384]{3,2,1,0:T(8,128)}) custom-call(bf16[2,3,544,768]{3,2,1,0:T(8,128)(2,1)} %get-tuple-element.59.refs_0_, bf16[4,1408,1536]{2,1,0:T(8,128)(2,1)} %bitcast.65, ...), custom_call_target="tpu_custom_call", output_to_operand_aliasing={{1}: (7, {})} | custom-call | tf_op jit(solution)/shard_map/last/pallas_call | solution.py:1159
  461.7 1.1 slice_bitcast_fusion.5
  464.8 1.5 copy-done.5
  466.3 2.2 copy.80
  468.6 1.1 copy.75
  469.7 5.0 %collective-permute-start.3 = (f32[4,44,768]{2,0,1:T(4,128)}, f32[4,44,768]{2,0,1:T(4,128)}, u32[]{:S(2)}, u32[]{:S(2)}) collective-permute-start(f32[4,44,768]{2,0,1:T(4,128)} %copy.75), channel_id=1, source_target_pairs={{0,1},{1,0},{2,3},{3,2},{4,5},{5,4},{6,7},{7,6},{8,9},{9,8},{10,11... | collective-permute-start | bytes 1622024 | tf_op jit(solution)/shard_map/ppermute | solution.py:1177
  476.3 1.1 slice_select_fusion.4
  477.4 1.1 broadcast_select_fusion
  478.6 1.1 pad_maximum_fusion
  484.2 1.2 select_bitcast_fusion.1
  486.3 1.9 reshape_reshape.7
  (85 shorter events, 26.0 us)
Async XLA Ops:
  0.6 5.9 %copy-start.6 = (bf16[2,257,1408]{2,0,1:T(2,128)(2,1)S(1)}, bf16[2,257,1408]{2,0,1:T(2,128)(2,1)}, u32[]{:S(2)}) copy-start(bf16[2,257,1408]{2,0,1:T(2,128)(2,1)} %param.9) | copy-start | bytes 4342276
  5.1 6.3 %collective-permute-start = (bf16[2,44,768]{2,1,0:T(8,128)(2,1)S(1)}, bf16[2,44,768]{2,1,0:T(8,128)(2,1)S(1)}, u32[]{:S(2)}, u32[]{:S(2)}) collective-permute-start(bf16[2,44,768]{2,1,0:T(8,128)(2,1)S(1)} %broadcast_select_fusion.3), channel_id=1, source_target_pairs={{0,1},{1,0},{2,3},{3,2},{4,5},{5,4},{6,7},{7,6},{8,9},{9,8},{10,11... | collective-permute-start | bytes 405512 | tf_op jit(solution)/shard_map/ppermute | solution.py:1177
  6.5 1.9 copy-start.7
  341.7 6.9 %collective-permute-start.1 = (f32[32,588]{1,0:T(8,128)S(1)}, f32[32,588]{1,0:T(8,128)S(1)}, u32[]{:S(2)}, u32[]{:S(2)}) collective-permute-start(f32[32,588]{1,0:T(8,128)S(1)} %pad_maximum_fusion.5), channel_id=1, source_target_pairs={{0,1},{1,0},{2,3},{3,2},{4,5},{5,4},{6,7},{7,6},{8,9},{9,8},{10,11... | collective-permute-start | bytes 225800 | tf_op jit(solution)/shard_map/ppermute | solution.py:1177
  344.1 2.3 copy-start.4
  348.6 127.8 %collective-permute-start.4 = (f32[192,768]{1,0:T(8,128)}, f32[192,768]{1,0:T(8,128)}, u32[]{:S(2)}, u32[]{:S(2)}) collective-permute-start(f32[192,768]{1,0:T(8,128)} %bitcast.30), channel_id=1, source_target_pairs={{0,1},{1,0},{2,3},{3,2},{4,5},{5,4},{6,7},{7,6},{8,9},{9,8},{10,11... | collective-permute-start | bytes 1769480 | tf_op jit(solution)/shard_map/ppermute | solution.py:1177
  460.7 4.0 copy-start.8
  464.7 1.6 copy-start.5
  464.7 3.8 copy-start.2
  464.8 3.7 copy-start
  469.7 13.7 %collective-permute-start.3 = (f32[4,44,768]{2,0,1:T(4,128)}, f32[4,44,768]{2,0,1:T(4,128)}, u32[]{:S(2)}, u32[]{:S(2)}) collective-permute-start(f32[4,44,768]{2,0,1:T(4,128)} %copy.75), channel_id=1, source_target_pairs={{0,1},{1,0},{2,3},{3,2},{4,5},{5,4},{6,7},{7,6},{8,9},{9,8},{10,11... | collective-permute-start | bytes 1622024 | tf_op jit(solution)/shard_map/ppermute | solution.py:1177
  476.2 3.4 collective-permute-start.2
  483.1 1.0 copy-start.1
  483.1 1.1 copy-start.3

commit v6 on v5

--- a/solution.py
+++ b/solution.py
@@ -162,12 +162,13 @@
             if s == THIRD:
                 self.push(k, ADDED).start()
 
-    def relay(self, k, s):
-        for m in WAYS:
-            self.hop(k, s, m).wait_recv()
-            self.hop(k, s, FAR + m).start()
-            if s == THIRD:
-                self.push(k, m).start()
+    def relay(self, s):
+        for k in COLOURS:
+            for m in WAYS:
+                self.hop(k, s, m).wait_recv()
+                self.hop(k, s, FAR + m).start()
+                if s == THIRD:
+                    self.push(k, m).start()
 
     def settle(self, s):
         for k in COLOURS:
@@ -177,27 +178,23 @@
                     self.push(k, FAR + m).start()
             if s == FIRST:
                 self.own(k).wait()
-        if s < THIRD:
-            self.launch(s + 1)
 
     def begin(self):
         for k in COLOURS:
             self.own(k).start()
         self.launch(FIRST)
 
-    def finish(self):
-        for k in COLOURS:
-            for s in COLOURS:
+    def sent(self, *rings):
+        for k in COLOURS:
+            for s in rings:
                 for m in range(ADDED):
                     self.hop(k, s, m).wait_send()
-            for n in range(ADDED + 1):
-                self.push(k, n).wait()
-
-    def steps(self):
-        out = [self.begin]
-        for s in COLOURS:
-            out += [functools.partial(self.relay, k, s) for k in COLOURS] + [functools.partial(self.settle, s)]
-        return out + [self.finish]
+            if THIRD in rings:
+                for n in range(ADDED + 1):
+                    self.push(k, n).wait()
+
+    def last_ring(self):
+        return [functools.partial(f, THIRD) for f in (self.launch, self.relay, self.settle, self.sent)]
 
 
 def add_into(total, *others):
@@ -518,15 +515,25 @@
     return pltpu.CompilerParams(collective_id=collective_id, has_side_effects=True, vmem_limit_bytes=VMEM_LIMIT)
 
 
-def torus_gather(kind, piece, collective_id):
-    def kernel(*refs):
-        enter()
-        for step in Gather(kind, *refs).steps():
-            step()
-
+def gather_kernel(*refs):
+    n = len(Gather.semaphores())
+    a, u, d = (Gather(kind, *refs[i::C][:PAIR], *refs[PAIR * C + n * i:][:n]) for i, kind in enumerate((WIDE, WIDE, DOWN)))
+    enter()
+    for gather in (a, u, d):
+        gather.begin()
+    for step, *ring in ((a.relay, FIRST), (u.relay, FIRST), (d.relay, FIRST), (a.settle, FIRST), (a.launch, SECOND),
+                        (u.settle, FIRST), (u.launch, SECOND), (a.relay, SECOND), (d.settle, FIRST), (d.launch, SECOND),
+                        (u.relay, SECOND), (a.settle, SECOND), (a.launch, THIRD), (d.relay, SECOND), (u.settle, SECOND),
+                        (a.relay, THIRD), (d.settle, SECOND), (a.settle, THIRD), (u.sent, FIRST, SECOND),
+                        (d.sent, FIRST, SECOND), (a.sent, FIRST, SECOND, THIRD)):
+        step(*ring)
+
+
+def gather_call(attn, up, down, collective_id):
     return pl.pallas_call(
-        kernel, out_shape=sds(BF16, *Gather.shape(kind)), in_specs=[ANY], out_specs=ANY,
-        scratch_shapes=Gather.semaphores(), compiler_params=comm_params(collective_id), name="gather_" + kind)(piece)
+        gather_kernel, out_shape=[sds(BF16, *Gather.shape(kind)) for kind in (WIDE, WIDE, DOWN)], in_specs=[ANY] * C,
+        out_specs=[ANY] * C, scratch_shapes=Gather.semaphores() * C, compiler_params=comm_params(collective_id),
+        name="gather")(attn, up, down)
 
 
 class Background:
@@ -703,14 +710,14 @@
     return pl.ds(TOK * s, TOK)
 
 
-FRONT_PLAN = {"qkv": ((0, 0, 1), (1, 1, 5), (2, 5, 8)), 2: ((O, 8, 9),), "end": ((O + 1, 9, None),)}
-
-
-def front_kernel(x, w, b, vec, up_src, qkv, h1, o, att, h2, up, rows, acc, *sems):
-    hosted = Background(Gather(WIDE, up_src, up, *sems).steps(), FRONT_PLAN)
+FRONT_PLAN = {"start": ((0, 0, 1),), "wo": ((O + 1, 1, 2),), "end": ((O + 1, 2, None),)}
+
+
+def front_kernel(x, w, b, vec, _, qkv, h1, o, att, h2, up, rows, acc, *sems):
+    hosted = Background(Gather(WIDE, None, up, *sems).last_ring(), FRONT_PLAN)
     j = pl.program_id(0)
     at_step(0)(enter)
-    hosted.visit("qkv")
+    hosted.visit("start")
 
     @at_step(0)
     def _():
@@ -725,6 +732,8 @@
         rows[j] = t
 
     pl.when(j >= O)(lambda: attention(j - O, rows, o, acc, hosted.visit))
+
+    hosted.visit("wo")
 
     @at_step(O + LAST_SEQ)
     def _():
@@ -749,6 +758,7 @@
         in_specs=[whole(*SEQS), along(0, 1, D, D, index=upto(O)), along(0, 1, 1, D, index=upto(V)), whole(8, D), ANY],
         out_specs=(along(0, 1, TT, D, index=upto(V)),) + (whole(TT, D),) * SIDE + (ANY,),
         scratch_shapes=[pltpu.VMEM((O, TT, D), BF16), pltpu.VMEM((SEQ, D), F32)] + Gather.semaphores(),
+        input_output_aliases={SIDE: SIDE + 1},
         compiler_params=comm_params(collective_id), name="front",
     )(x, w_attn, b_qkv, vec, up)
 
@@ -767,12 +777,12 @@
     ref[pl.ds(pl.multiple_of(tail + TAIL * s, TAIL), TAIL)] = t[BODY:]
 
 
-DOWN_PLAN = {"start": ((0, 0, 1),), "end": ((1, 1, 5), (3, 5, 8), (5, 8, 9), (TILES + 4, 9, 12), (2 * TILES - 1, 12, None))}
-
-
-def mlp_in_kernel(h2, gz, w_up, b_up, vec, src, act, slope, d_down, down, a_rows, b_rows, b_away, *sems):
+DOWN_PLAN = {"start": ((0, 0, 1),), "end": ((TILES + 2, 1, 2), (2 * TILES - 1, 2, None))}
+
+
+def mlp_in_kernel(h2, gz, w_up, b_up, vec, _, act, slope, d_down, down, a_rows, b_rows, b_away, *sems):
     a_sems, b_sems, sems = sems[:PAIR], sems[PAIR:2 * PAIR], sems[2 * PAIR:]
-    hosted = Background(Gather(DOWN, src, down, *sems).steps(), DOWN_PLAN)
+    hosted = Background(Gather(DOWN, None, down, *sems).last_ring(), DOWN_PLAN)
     j = pl.program_id(0)
     away = Push(b_away, OWN_BODY, b_rows, b_sems, 0)
     tile = lambda n: Push(a_rows.at[n], TAILS, a_rows.at[n], a_sems, n)
@@ -832,6 +842,7 @@
         scratch_shapes=[pltpu.VMEM((TILES, ROWS, HALF), BF16), pltpu.VMEM((ROWS, HALF), BF16),
                         pltpu.VMEM((PAIR * TOK, HALF), BF16)] + Push.semaphores(TILES) + Push.semaphores(1) +
         Gather.semaphores(),
+        input_output_aliases={SIDE + 1: O},
         compiler_params=comm_params(collective_id), name="mlp_in",
     )(h2, gz, w_up, b_up.reshape(TILES, 1, HALF), vec, down)
 
@@ -1083,7 +1094,7 @@
 
 IN_STEPS = PAIR * O
 SLOT = 40
-LAST_PLAN = {"start": ((0, 0, 2),), "end": ((O, 2, 5),)}
+LAST_PLAN = {"start": ((0, 0, 2),), "end": ((O, 2, None),)}
 
 
 def last_kernel(*refs):
@@ -1097,7 +1108,7 @@
     rest_up = Rest(Bands(WIDE), acc_up, None, *take(len(Bands(WIDE).later())))
     spread_up, spread_a, spread_b = (
         Spread(r.bands, r.sums(), total, *take(len(Spread.scratch()))) for r, total in zip((rest_up, rest_a, rest_b), totals))
-    hosted = Background([rest_up.begin, a.near, rest_up.loaded, rest_up.relay, a.far], LAST_PLAN)
+    hosted = Background([rest_up.begin, a.near, rest_up.loaded, rest_up.relay], LAST_PLAN)
     me = Torus()
     swap = remote(sums, pair_sums, swap_sems, (), me.partner())
     fetch = pltpu.make_async_copy(small, block, block_sem)
@@ -1126,8 +1137,6 @@
     def _():
         swap.start()
         fetch.wait()
-        rest_up.settle()
-        a.relay()
         swap.wait()
         both = sums[...] + pair_sums[...]
         for d in range(DEVICES):
@@ -1143,12 +1152,12 @@
                     put.start()
             pltpu.make_async_copy(block, small, block_sem).wait()
 
-        for step in (b.near, rest_up.relay_third, b.far, functools.partial(a.settle, rest_a.send), rest_up.settle_third,
-                     spread_up.begin, b.relay, rest_a.relay, rest_a.settle, spread_up.forward, rest_a.relay_third,
-                     functools.partial(b.settle, rest_b.send), rest_a.settle_third, spread_a.begin, rest_b.relay, rest_b.settle,
-                     spread_a.forward, rest_b.relay_third, rest_b.settle_third, spread_b.begin, spread_b.forward,
-                     spread_up.finish, spread_a.finish, spread_b.finish, rest_up.finish, rest_a.finish, rest_b.finish,
-                     a.finish, b.finish):
+        for step in (b.near, rest_up.settle, a.far, rest_up.relay_third, b.far, a.relay, rest_up.settle_third, spread_up.begin,
+                     b.relay, spread_up.forward, functools.partial(a.settle, rest_a.send),
+                     functools.partial(b.settle, rest_b.send), rest_a.relay, rest_b.relay, rest_a.settle, rest_b.settle,
+                     rest_a.relay_third, rest_b.relay_third, rest_a.settle_third, spread_a.begin, rest_b.settle_third,
+                     spread_b.begin, spread_a.forward, spread_b.forward, spread_up.finish, spread_a.finish, spread_b.finish,
+                     rest_up.finish, rest_a.finish, rest_b.finish, a.finish, b.finish):
             step()
 
 
@@ -1234,7 +1243,8 @@
 def device_step(x, gz, *shards):
     first = lax.rem(lax.axis_index("fsdp"), PAIR) == 0
     attn, up, down = my_pieces(shards, first)
-    w_attn = torus_gather(WIDE, attn, 0).reshape(SIDE, D, QCOLS)
+    w_attn, up, down = gather_call(attn, up, down, 0)
+    w_attn = w_attn.reshape(SIDE, D, QCOLS)
     b_qkv, b_up, vec = small_params(w_attn)
     qkv, h1, o, att, h2, w_up = front_call(x, w_attn, b_qkv, vec, up, 1)
     w_up = w_up.reshape(SIDE, D, QCOLS)

time: 495 us -> 475 us (0.960)
  Pallas kernels: 434 us -> 414 us
    pallas_call x1, Pallas kernels: 54.8 us -> 41.4 us  [front_call(): pl.pallas_call(front_kernel, grid=(O + PAIR,), out_shape=(sds(BF16, O, TT...]
    pallas_call x1, Pallas kernels: 51.8 us -> 62.6 us  [gather_call(): pl.pallas_call(gather_kernel, out_shape=[sds(BF16, *Gather.shape(kind)) f...]
    pallas_call x1, Pallas kernels: 55.8 us -> 47 us  [mlp_in_call(): pl.pallas_call(mlp_in_kernel, grid=(2 * TILES,), out_shape=(sds(BF16, TT,...]
    pallas_call x1, Pallas kernels: 111 us -> 103 us  [last_call(): pl.pallas_call(last_kernel, grid=(IN_STEPS + 1,), out_shape=(sds(BF16, *S...]
  transfers between devices with their start and end apart: 5 -> 5, of which waited for: 0 -> 0; matrix products, arithmetic and copies ran while one was open for 5% -> 5% of each run, Pallas kernels for 23% -> 22%
where the time goes in v6:
time: 475 us; the launch traced here: 471 us
  Pallas kernels  414 us (87%)
  local copies, waits for them, and re-layouts  31.8 us (7%)
  other arithmetic  15 us (3%)
  starting transfers between devices  8.62 us (2%)
    pallas_call x1, Pallas kernels, last_call(): pl.pallas_call(last_kernel, grid=(IN_STEPS + 1,), out_shape=(sds(BF16, *S...  103 us
    pallas_call x1, Pallas kernels, mlp_out_call(): pl.pallas_call(mlp_out_kernel, grid=(TILES,), out_shape=(sds(BF16, PAIR,...  63.7 us
    pallas_call x1, Pallas kernels, gather_call(): pl.pallas_call(gather_kernel, out_shape=[sds(BF16, *Gather.shape(kind)) f...  62.6 us
    pallas_call x1, Pallas kernels, attn_back_call(): pl.pallas_call(attn_back_kernel, grid=(SEQS[0] + GRAD_STEPS,), out_shape=...  61 us
    pallas_call x1, Pallas kernels, mlp_in_call(): pl.pallas_call(mlp_in_kernel, grid=(2 * TILES,), out_shape=(sds(BF16, TT,...  47 us
    pallas_call x1, Pallas kernels, front_call(): pl.pallas_call(front_kernel, grid=(O + PAIR,), out_shape=(sds(BF16, O, TT...  41.4 us
    pallas_call x1, Pallas kernels, mid_call(): pl.pallas_call(mid_kernel, grid=(SEQS[0] + GRAD_STEPS,), out_shape=(sds(B...  36 us
    unnamed x25, local copies, waits for them, and re-layouts  11.7 us
  transfers between devices with their start and end apart: 5, of which 0 were waited for; matrix products, arithmetic and copies ran while one was open for 5% of the time, Pallas kernels for 22%

profile of v6, /device:TPU:1, one launch (start us, length us, event | category | flops | bytes accessed | tf_op | source)
XLA Modules:
  0.0 471.0 jit_solution(15226858520219192449)
XLA Ops:
  5.1 1.4 collective-permute-start
  6.5 1.3 copy.58.x.refs_3_.refs_2_
  8.4 1.3 copy.59.gz.refs_4_
  9.7 1.6 dynamic-slice_convert_fusion.1
  12.1 62.6 %gather.1 = (bf16[4,4,4,88,1536]{4,3,2,1,0:T(8,128)(2,1)}, bf16[4,4,4,88,1536]{4,3,2,1,0:T(8,128)(2,1)}, bf16[4,4,2,4,3,16,1408]{6,5,4,3,2,1,0:T(8,128)(2,1)}) custom-call(bf16[88,768]{1,0:T(8,128)(2,1)} %get-tuple-element.117.refs_0_, bf16[88,768]{1,0:T(8,128)(2,1)} %get-tuple-element.116.refs_1_, bf16[3,16,1408]{2,1,0:T(8,128)(2,1)} %bitcast.75), custom_call_target="tpu_custom_call" | custom-call | tf_op jit(solution)/shard_map/gather/pallas_call | solution.py:533
  78.4 41.4 %front.1 = (bf16[3,544,1408]{2,1,0:T(8,128)(2,1)}, bf16[544,1408]{1,0:T(8,128)(2,1)}, bf16[544,1408]{1,0:T(8,128)(2,1)}, f32[544,1408]{1,0:T(8,128)}, bf16[544,1...) custom-call(bf16[2,257,1408]{2,1,0:T(8,128)(2,1)} %copy.58.x.refs_3_.refs_2_, ...), custom_call_target="tpu_custom_call", output_to_operand_aliasing={{5}: (4, {})} | custom-call | tf_op jit(solution)/shard_map/front/pallas_call | solution.py:754
  119.8 47.0 %mlp_in.1 = (bf16[544,6144]{1,0:T(8,128)(2,1)}, f32[544,6144]{1,0:T(8,128)}, f32[6144,768]{1,0:T(8,128)}, bf16[4,4,2,4,3,16,1408]{6,5,4,3,2,1,0:T(8,128)(2,1)}) custom-call(bf16[544,1408]{1,0:T(8,128)(2,1)} %get-tuple-element.45.h2.refs_7_, bf16[2,257,1408]{2,1,0:T(8,128)(2,1)} %copy.59.gz.refs_4_, ...), custom_call_target="tpu_custom_call", output_to_operand_aliasing={{3}: (5, {})} | custom-call | tf_op jit(solution)/shard_map/mlp_in/pallas_call | solution.py:836
  166.8 63.7 %mlp_out.1 = (bf16[2,4,544,768]{3,2,1,0:T(8,128)(2,1)}, f32[8,1,768]{2,1,0:T(1,128)}, f32[544,1408]{1,0:T(8,128)}, f32[544,1408]{1,0:T(8,128)}, f32[3,4,4,32,768]{4,3,2,1,0:T(8,128)}) custom-call(bf16[544,6144]{1,0:T(8,128)(2,1)} %get-tuple-element.48.act, f32[544,6144]{1,0:T(8,128)} %get-tuple-element.49.slope, bf16[2,257,1408]{2,1,0:T(8,128)(2,1)} %copy.59.gz.refs_4_, ...), custom_call_target="tpu_custom_call" | custom-call | tf_op jit(solution)/shard_map/mlp_out/pallas_call | solution.py:878
  231.3 36.0 %mid.1 = (bf16[2,257,1408]{2,1,0:T(8,128)(2,1)}, f32[544,1408]{1,0:T(8,128)}, bf16[2,544,768]{2,1,0:T(8,128)(2,1)}, bf16[544,1408]{1,0:T(8,128)(2,1)}, f32[8,140...) custom-call(f32[544,1408]{1,0:T(8,128)} %get-tuple-element.52.refs_0_, ...), custom_call_target="tpu_custom_call" | custom-call | tf_op jit(solution)/shard_map/mid/pallas_call | solution.py:1030
  268.4 61.0 %attn_back.1 = (bf16[2,3,544,768]{3,2,1,0:T(8,128)(2,1)}, f32[3,1408]{1,0:T(4,128)}, f32[4,1408,768]{2,1,0:T(8,128)}, f32[3,4,4,32,768]{4,3,2,1,0:T(8,128)}, f32[4,3,32,768]{3,2,1,0:T(8,128)}) custom-call(bf16[3,544,1408]{2,1,0:T(8,128)(2,1)} %get-tuple-element.58.refs_0_, bf16[544,1408]{1,0:T(8,128)(2,1)} %get-tuple-element.59.refs_1_, ...), custom_call_target="tpu_custom_call" | custom-call | tf_op jit(solution)/shard_map/attn_back/pallas_call | solution.py:1083
  330.4 2.3 collective-permute-start.1
  332.6 2.3 slice_select_fusion.2
  334.9 2.2 copy.81
  338.3 102.7 %last.1 = (bf16[2,257,1408]{2,1,0:T(8,128)(2,1)}, f32[4,4,4,88,768]{4,3,2,1,0:T(8,128)}, f32[4,3,32,768]{3,2,1,0:T(8,128)}, f32[4,3,32,384]{3,2,1,0:T(8,128)}, f32[4,3,32,384]{3,2,1,0:T(8,128)}) custom-call(bf16[2,3,544,768]{3,2,1,0:T(8,128)(2,1)} %get-tuple-element.65.refs_0_, bf16[4,1408,1536]{2,1,0:T(8,128)(2,1)} %bitcast.65, ...), custom_call_target="tpu_custom_call", output_to_operand_aliasing={{1}: (7, {})} | custom-call | tf_op jit(solution)/shard_map/last/pallas_call | solution.py:1168
  442.0 1.1 slice_bitcast_fusion.5
  445.1 1.5 copy-done.5
  446.6 2.2 copy.82
  448.9 1.1 copy.77
  450.0 4.8 %collective-permute-start.3 = (f32[4,44,768]{2,0,1:T(4,128)}, f32[4,44,768]{2,0,1:T(4,128)}, u32[]{:S(2)}, u32[]{:S(2)}) collective-permute-start(f32[4,44,768]{2,0,1:T(4,128)} %copy.77), channel_id=1, source_target_pairs={{0,1},{1,0},{2,3},{3,2},{4,5},{5,4},{6,7},{7,6},{8,9},{9,8},{10,11... | collective-permute-start | bytes 1622024 | tf_op jit(solution)/shard_map/ppermute | solution.py:1186
  456.3 1.1 slice_select_fusion.4
  457.4 1.1 broadcast_select_fusion
  458.6 1.1 pad_maximum_fusion
  464.2 1.2 select_bitcast_fusion.1
  466.3 1.9 reshape_reshape.7
  (85 shorter events, 26.0 us)
Async XLA Ops:
  0.6 5.9 %copy-start.6 = (bf16[2,257,1408]{2,0,1:T(2,128)(2,1)S(1)}, bf16[2,257,1408]{2,0,1:T(2,128)(2,1)}, u32[]{:S(2)}) copy-start(bf16[2,257,1408]{2,0,1:T(2,128)(2,1)} %param.9) | copy-start | bytes 4342276
  5.1 6.2 %collective-permute-start = (bf16[2,44,768]{2,1,0:T(8,128)(2,1)S(1)}, bf16[2,44,768]{2,1,0:T(8,128)(2,1)S(1)}, u32[]{:S(2)}, u32[]{:S(2)}) collective-permute-start(bf16[2,44,768]{2,1,0:T(8,128)(2,1)S(1)} %broadcast_select_fusion.3), channel_id=1, source_target_pairs={{0,1},{1,0},{2,3},{3,2},{4,5},{5,4},{6,7},{7,6},{8,9},{9,8},{10,11... | collective-permute-start | bytes 405512 | tf_op jit(solution)/shard_map/ppermute | solution.py:1186
  6.5 1.9 copy-start.7
  330.4 6.8 %collective-permute-start.1 = (f32[32,588]{1,0:T(8,128)S(1)}, f32[32,588]{1,0:T(8,128)S(1)}, u32[]{:S(2)}, u32[]{:S(2)}) collective-permute-start(f32[32,588]{1,0:T(8,128)S(1)} %pad_maximum_fusion.5), channel_id=1, source_target_pairs={{0,1},{1,0},{2,3},{3,2},{4,5},{5,4},{6,7},{7,6},{8,9},{9,8},{10,11... | collective-permute-start | bytes 225800 | tf_op jit(solution)/shard_map/ppermute | solution.py:1186
  332.6 2.3 copy-start.4
  337.1 119.2 %collective-permute-start.4 = (f32[192,768]{1,0:T(8,128)}, f32[192,768]{1,0:T(8,128)}, u32[]{:S(2)}, u32[]{:S(2)}) collective-permute-start(f32[192,768]{1,0:T(8,128)} %bitcast.30), channel_id=1, source_target_pairs={{0,1},{1,0},{2,3},{3,2},{4,5},{5,4},{6,7},{7,6},{8,9},{9,8},{10,11... | collective-permute-start | bytes 1769480 | tf_op jit(solution)/shard_map/ppermute | solution.py:1186
  440.9 4.0 copy-start.8
  444.9 1.6 copy-start.5
  445.0 3.8 copy-start.2
  445.1 3.7 copy-start
  450.0 13.4 %collective-permute-start.3 = (f32[4,44,768]{2,0,1:T(4,128)}, f32[4,44,768]{2,0,1:T(4,128)}, u32[]{:S(2)}, u32[]{:S(2)}) collective-permute-start(f32[4,44,768]{2,0,1:T(4,128)} %copy.77), channel_id=1, source_target_pairs={{0,1},{1,0},{2,3},{3,2},{4,5},{5,4},{6,7},{7,6},{8,9},{9,8},{10,11... | collective-permute-start | bytes 1622024 | tf_op jit(solution)/shard_map/ppermute | solution.py:1186
  456.2 3.4 collective-permute-start.2
  463.1 1.0 copy-start.1
  463.1 1.1 copy-start.3

commit v7 on v6

--- a/solution.py
+++ b/solution.py
@@ -492,7 +492,10 @@
 
     def begin(self):
         for k in COLOURS:
-            self.own(k).start()
+            if self.local is None:
+                self.place(k)[...] = self.mine(k)[...]
+            else:
+                self.own(k).start()
             for m in WAYS:
                 self.hop(k, m).start()
 
@@ -506,7 +509,8 @@
         for k in COLOURS:
             for m in WAYS:
                 self.hop(k, FAR + m).wait_recv()
-            self.own(k).wait()
+            if self.local is not None:
+                self.own(k).wait()
             for m in range(ADDED):
                 self.hop(k, m).wait_send()
 
@@ -546,6 +550,24 @@
             def _():
                 for step in self.steps[first:end]:
                     step()
+
+
+class Share:
+    def __init__(self, mine, theirs, place, sems, slot):
+        self.local = pltpu.make_async_copy(mine, place, sems[PAIR].at[slot])
+        self.far = remote(theirs, place, sems, slot, Torus().partner())
+
+    def start(self):
+        self.far.start()
+        self.local.start()
+
+    def sent(self):
+        self.local.wait()
+        self.far.wait_send()
+
+    def wait(self):
+        self.sent()
+        self.far.wait_recv()
 
 
 class Push:
@@ -1097,24 +1119,96 @@
 LAST_PLAN = {"start": ((0, 0, 2),), "end": ((O, 2, None),)}
 
 
+CORE_COLS = D - HALF
+KEPT = 48
+GRADS = ((KEPT, O * D), (KEPT, D), (KEPT, FF), (PAIR, C, UNIT, D), (SIDE, KEPT, LANES))
+SHARES = PAIR * SIDE + SIDE + PAIR
+
+
+def split_rows(totals, first, keep, give):
+    for x in range(SIDE):
+        for total, bands in totals:
+            rows = jnp.concatenate([total[x, k, :n] for k, (_, n) in enumerate(BANDS[WIDE])], axis=0)
+            low, high = rows[:KEPT], jnp.concatenate([rows[OWN:], rows[:KEPT - OWN]], axis=0)
+            keep[x, :, bands.cols] = jnp.where(first, low, high)
+            give[x, :, bands.cols] = jnp.where(first, high, low)
+
+
+class Finals:
+    def __init__(self, down, up, attn, outs, sems):
+        self.c = Torus().at["c"]
+        self.down, self.up, self.attn, self.sems = down, up, attn, sems
+        self.qkv, self.out, self.up_out, self.down_out, self.pad = outs
+        self.edge = pl.ds(CORE_COLS, LANES)
+
+    def cols(self, base, width):
+        return pl.ds(pl.multiple_of(base + self.c * HALF, LANES), width)
+
+    def up_share(self, x):
+        place = self.up_out.at[:, self.cols(QCOLS * x, HALF)]
+        return Share(*(ref.at[x] for ref in self.up), place, self.sems, x)
+
+    def block(self, x):
+        return (self.out, 0) if x == O else (self.qkv, D * x)
+
+    def attn_share(self, x):
+        out, base = self.block(x)
+        sides = (ref.at[x, :, pl.ds(0, CORE_COLS)] for ref in self.attn)
+        return Share(*sides, out.at[:, self.cols(base, CORE_COLS)], self.sems, SIDE + x)
+
+    def edge_share(self, x, padding):
+        out, base = self.block(x)
+        place = self.pad.at[x] if padding else out.at[:, pl.ds(base + CORE_COLS, LANES)]
+        return Share(*(ref.at[x, :, self.edge] for ref in self.attn), place, self.sems, PAIR * SIDE + x)
+
+    def down_share(self, edge):
+        src = self.edge if edge else pl.ds(pl.multiple_of(self.c * LANES, LANES), CORE_COLS)
+        sides = (self.down.at[pl.ds(PAIR * c, PAIR), :, :, src] for c in (self.c, 1 - self.c))
+        place = self.down_out.at[:, :, :, self.edge if edge else self.cols(0, CORE_COLS)]
+        return Share(*sides, place, self.sems, SHARES - PAIR + edge)
+
+    def start_down(self):
+        self.down_share(0).start()
+        pl.when(self.c == 0)(lambda: self.down_share(1).start())
+
+    def start(self):
+        for x in range(SIDE):
+            self.attn_share(x).start()
+            pl.when(self.c == 0)(lambda: self.edge_share(x, False).start())
+            pl.when(self.c == 1)(lambda: self.edge_share(x, True).start())
+
+    def finish(self):
+        for x in range(SIDE):
+            for share in (self.up_share(x), self.attn_share(x), self.edge_share(x, True)):
+                share.wait()
+        self.down_share(0).wait()
+        pl.when(self.c == 0)(lambda: self.down_share(1).sent())
+        pl.when(self.c == 1)(lambda: self.down_share(1).far.wait_recv())
+
+
 def last_kernel(*refs):
     refs = list(refs)
     take = lambda n: [refs.pop(0) for _ in range(n)]
-    (d_half, w, x, g_res, vec), (small, acc_up, _), (dx, part, *totals) = take(5), take(3), take(5)
-    acc, sums, pair_sums, block, block_sem, swap_sems = refs.pop(0), refs.pop(0), refs.pop(0), refs.pop(0), refs.pop(0), take(PAIR)
+    (d_half, w, x, g_res, vec), (small, acc_up, down, _), (dx, part), outs = take(5), take(SIDE), take(PAIR), take(len(GRADS))
+    (acc, sums, pair_sums, block), (totals, sides), block_sem, swap_sems = take(4), (take(C), take(SIDE)), refs.pop(0), take(PAIR)
+    finals = Finals(down, sides[:PAIR], sides[PAIR:], outs, take(C))
     halves = [Bands(WIDE, h) for h in WAYS]
     a, b = (First(bands, part, None, *take(len(bands.first()))) for bands in halves)
     rest_a, rest_b = (Rest(f.bands, f.own_all, None, f.own_all, *take(len(f.bands.later()) - 1)) for f in (a, b))
     rest_up = Rest(Bands(WIDE), acc_up, None, *take(len(Bands(WIDE).later())))
     spread_up, spread_a, spread_b = (
-        Spread(r.bands, r.sums(), total, *take(len(Spread.scratch()))) for r, total in zip((rest_up, rest_a, rest_b), totals))
+        Spread(r.bands, r.sums(), total, *take(PAIR), None) for r, total in zip((rest_up, rest_a, rest_b), totals))
     hosted = Background([rest_up.begin, a.near, rest_up.loaded, rest_up.relay], LAST_PLAN)
-    me = Torus()
-    swap = remote(sums, pair_sums, swap_sems, (), me.partner())
+    first = finals.c == 0
+    swap = remote(sums, pair_sums, swap_sems, (), Torus().partner())
     fetch = pltpu.make_async_copy(small, block, block_sem)
     at_step(0)(enter)
     hosted.visit("start")
-    at_step(0)(fetch.start)
+
+    @at_step(0)
+    def _():
+        fetch.start()
+        finals.start_down()
 
     @pl.when(pl.program_id(0) < IN_STEPS)
     def _():
@@ -1143,40 +1237,51 @@
             at = CHIP * (d // PAIR) + SLOT + OWN * (d % PAIR)
             block[at:at + BO, :OWN] = both[:BO, OWN * d:OWN * d + OWN]
 
-        @pl.when(me.at["c"] == 1)
+        @pl.when(finals.c == 1)
         def _():
             for z in range(SIDE):
                 for y in range(SIDE):
                     rows = block.at[pl.ds(CHIP * (SIDE * z + y), CHIP)]
-                    put = pltpu.make_async_copy(rows, part.at[0, z, y, :, pl.ds(HALF - LANES, LANES)], block_sem)
+                    put = pltpu.make_async_copy(rows, part.at[0, z, y, :, pl.ds(CORE_COLS, LANES)], block_sem)
                     put.start()
             pltpu.make_async_copy(block, small, block_sem).wait()
+
+        def share_up():
+            spread_up.finish()
+            split_rows([(totals[0], Bands(WIDE))], first, *sides[:PAIR])
+            for x in range(SIDE):
+                finals.up_share(x).start()
 
         for step in (b.near, rest_up.settle, a.far, rest_up.relay_third, b.far, a.relay, rest_up.settle_third, spread_up.begin,
                      b.relay, spread_up.forward, functools.partial(a.settle, rest_a.send),
                      functools.partial(b.settle, rest_b.send), rest_a.relay, rest_b.relay, rest_a.settle, rest_b.settle,
-                     rest_a.relay_third, rest_b.relay_third, rest_a.settle_third, spread_a.begin, rest_b.settle_third,
-                     spread_b.begin, spread_a.forward, spread_b.forward, spread_up.finish, spread_a.finish, spread_b.finish,
-                     rest_up.finish, rest_a.finish, rest_b.finish, a.finish, b.finish):
+                     share_up, rest_a.relay_third, rest_b.relay_third, rest_a.settle_third, spread_a.begin,
+                     rest_b.settle_third, spread_b.begin, spread_a.forward, spread_b.forward, spread_a.finish, spread_b.finish):
             step()
-
-
-def last_call(d_qkv, w_attn, x, g_res, vec, small, acc_up, part, collective_id):
+        split_rows(list(zip(totals[1:], halves)), first, *sides[PAIR:])
+        finals.start()
+        for user in (rest_up, rest_a, rest_b, a, b, finals):
+            user.finish()
+
+
+def last_call(d_qkv, w_attn, x, g_res, vec, small, acc_up, down, part, collective_id):
     low = upto(IN_STEPS - 1)
     halves = [Bands(WIDE, h) for h in WAYS]
     dma = pltpu.SemaphoreType.DMA
+    rings = [Bands(WIDE), *halves]
     return pl.pallas_call(
         last_kernel, grid=(IN_STEPS + 1,),
-        out_shape=(sds(BF16, *SEQS), sds(F32, *part.shape), Bands(WIDE).total(), *(h.total() for h in halves)),
+        out_shape=(sds(BF16, *SEQS), sds(F32, *part.shape), *(sds(F32, *shape) for shape in GRADS)),
         in_specs=[pl.BlockSpec((1, 1, TT, HALF), lambda j: (low(j) % PAIR, low(j) // PAIR, 0, 0)), up_tile(low),
-                  whole(*SEQS), whole(TT, D), whole(8, D)] + [ANY] * O,
-        out_specs=(whole(*SEQS),) + (ANY,) * SIDE,
+                  whole(*SEQS), whole(TT, D), whole(8, D)] + [ANY] * SIDE,
+        out_specs=(whole(*SEQS),) + (ANY,) * (len(GRADS) + 1),
         scratch_shapes=[pltpu.VMEM((TT, D), F32), pltpu.VMEM((SUB, D), F32), pltpu.VMEM((SUB, D), F32),
-                        pltpu.VMEM((D, LANES), F32), dma, dma, dma] + halves[0].first() * PAIR + halves[0].later()[1:] * PAIR +
-        Bands(WIDE).later() + Spread.scratch() * O,
-        input_output_aliases={7: 1},
+                        pltpu.VMEM((D, LANES), F32)] + [r.vmem(SIDE, C) for r in rings] +
+        [pltpu.VMEM((SIDE, KEPT, HALF), F32)] * SIDE + [dma, dma, dma] + [dma((SHARES,))] * C + halves[0].first() * PAIR +
+        halves[0].later()[1:] * PAIR + Bands(WIDE).later() + Spread.scratch()[:PAIR] * C,
+        input_output_aliases={8: 1},
         compiler_params=comm_params(collective_id), name="last",
-    )(d_qkv, w_attn, x, g_res, vec, small, acc_up, part)
+    )(d_qkv, w_attn, x, g_res, vec, small, acc_up, down, part)
 
 
 BQ, BU, VEC = 3 * D // 32, 3 * D // 32 + FF // 32, 3 * D // 32 + FF // 32 + 8 * OWN
@@ -1221,23 +1326,6 @@
     small = small + pair_swap(small)
     small = jnp.pad(small, ((0, 0), (0, ROOM - small.shape[1]))).reshape(DEVICES, ROOM // LANES, LANES)
     return jnp.pad(small, ((0, 0), (0, OWN - ROOM // LANES), (0, 0))).reshape(D, LANES)
-
-
-def rows_of(total):
-    return jnp.concatenate([total[:, k, :n] for k, (_, n) in enumerate(BANDS[WIDE])], axis=1)
-
-
-def final_rows(total, first):
-    keep, give = by_core(first, total[:, :OWN], total[:, OWN:])
-    pair = jnp.stack(by_core(first, keep, pair_swap(give)), axis=1)
-    return pair.transpose(2, 0, 1, 3).reshape(OWN, SIDE, QCOLS)
-
-
-def final_down(total, first):
-    down = total.reshape(FF // 16, HALF)
-    keep, give = by_core(first, down[:FF // DEVICES], down[FF // DEVICES:])
-    left, right = by_core(first, keep, pair_swap(give))
-    return jnp.concatenate([left, right[:, 2 * HALF - D:]], axis=1)
 
 
 def device_step(x, gz, *shards):
@@ -1256,13 +1344,11 @@
     d_qkv, db_qkv, part, acc, down = attn_back_call(qkv, d_o, h1, o, d_att, part, result, 5)
     small = small_grads(db_qkv, db_up, sums)
     part = part.reshape((SIDE,) * 3 + (CHIP, HALF))
-    dx, _, up, attn0, attn1 = last_call(d_qkv, w_attn, x, g_res, vec, small, acc, part, 6)
-    g_up = final_rows(rows_of(up), first).reshape(OWN, FF)
-    attn = final_rows(jnp.concatenate([rows_of(attn0), rows_of(attn1)], axis=-1), first)
-    small = attn[:ROOM // LANES, 0, D:].reshape(ROOM)
-    vec = jnp.concatenate([attn[SLOT:SLOT + BO, 0, D:D + OWN], small[BU:VEC - BO * OWN].reshape(8 - BO, OWN)], axis=0)
-    return (z, dx, attn[:, :O, :D].reshape(OWN, O * D), small[:BQ], attn[:, O, :D], g_up, small[BQ:BU],
-            final_down(down, first), vec)
+    dx, _, g_qkv, g_out, g_up, g_down, edge = last_call(d_qkv, w_attn, x, g_res, vec, small, acc, down, part, 6)
+    small = edge[0, :ROOM // LANES].reshape(ROOM)
+    vec = jnp.concatenate([edge[0, SLOT:SLOT + BO, :OWN], small[BU:VEC - BO * OWN].reshape(8 - BO, OWN)], axis=0)
+    g_qkv, g_out, g_up = (g[:OWN] for g in (g_qkv, g_out, g_up))
+    return z, dx, g_qkv, small[:BQ], g_out, g_up, small[BQ:BU], g_down.reshape(FF // DEVICES, D), vec
 
 
 def solution(mesh):

time: 475 us -> 461 us (0.971)
  local copies, waits for them, and re-layouts: 31.8 us -> 23.6 us
  other arithmetic: 15 us -> 7.73 us
  Pallas kernels: 414 us -> 421 us
  starting transfers between devices: 8.62 us -> 3.62 us
    pallas_call x1, Pallas kernels: 103 us -> 109 us  [last_call(): pl.pallas_call(last_kernel, grid=(IN_STEPS + 1,), out_shape=(sds(BF16, *S...]
    ppermute x5 -> x2, starting transfers between devices: 8.62 us -> 3.62 us  [pair_swap(): return lax.ppermute(a, 'fsdp', [(i, i ^ 1) for i in range(DEVICES)])]
    unnamed x25 -> x20, local copies, waits for them, and re-layouts: 11.7 us -> 13.5 us
  transfers between devices with their start and end apart: 5 -> 2, of which waited for: 0 -> 0; matrix products, arithmetic and copies ran while one was open for 5% -> 2% of each run, Pallas kernels for 22% -> 0%
where the time goes in v7:
time: 461 us; the launch traced here: 457 us
  Pallas kernels  421 us (91%)
  local copies, waits for them, and re-layouts  23.6 us (5%)
  other arithmetic  7.73 us (2%)
    pallas_call x1, Pallas kernels, last_call(): pl.pallas_call(last_kernel, grid=(IN_STEPS + 1,), out_shape=(sds(BF16, *S...  109 us
    pallas_call x1, Pallas kernels, mlp_out_call(): pl.pallas_call(mlp_out_kernel, grid=(TILES,), out_shape=(sds(BF16, PAIR,...  63.8 us
    pallas_call x1, Pallas kernels, gather_call(): pl.pallas_call(gather_kernel, out_shape=[sds(BF16, *Gather.shape(kind)) f...  62.5 us
    pallas_call x1, Pallas kernels, attn_back_call(): pl.pallas_call(attn_back_kernel, grid=(SEQS[0] + GRAD_STEPS,), out_shape=...  61.1 us
    pallas_call x1, Pallas kernels, mlp_in_call(): pl.pallas_call(mlp_in_kernel, grid=(2 * TILES,), out_shape=(sds(BF16, TT,...  47.1 us
    pallas_call x1, Pallas kernels, front_call(): pl.pallas_call(front_kernel, grid=(O + PAIR,), out_shape=(sds(BF16, O, TT...  41.4 us
    pallas_call x1, Pallas kernels, mid_call(): pl.pallas_call(mid_kernel, grid=(SEQS[0] + GRAD_STEPS,), out_shape=(sds(B...  35.9 us
    unnamed x20, local copies, waits for them, and re-layouts  13.5 us
  transfers between devices with their start and end apart: 2, of which 0 were waited for; matrix products, arithmetic and copies ran while one was open for 2% of the time, Pallas kernels for 0%

profile of v7, /device:TPU:1, one launch (start us, length us, event | category | flops | bytes accessed | tf_op | source)
XLA Modules:
  0.0 456.8 jit_solution(1143431060284683652)
XLA Ops:
  3.0 1.0 fusion.1
  4.0 1.0 fusion.2
  5.1 1.4 collective-permute-start
  6.5 1.3 copy.30.x.refs_3_.refs_2_
  7.8 1.3 copy.31.gz.refs_4_
  9.1 1.6 dynamic-slice_convert_fusion.1
  11.6 62.5 %gather.1 = (bf16[4,4,4,88,1536]{4,3,2,1,0:T(8,128)(2,1)}, bf16[4,4,4,88,1536]{4,3,2,1,0:T(8,128)(2,1)}, bf16[4,4,2,4,3,16,1408]{6,5,4,3,2,1,0:T(8,128)(2,1)}) custom-call(bf16[88,768]{1,0:T(8,128)(2,1)} %get-tuple-element.102.refs_0_, bf16[88,768]{1,0:T(8,128)(2,1)} %get-tuple-element.101.refs_1_, bf16[3,16,1408]{2,1,0:T(8,128)(2,1)} %bitcast.42), custom_call_target="tpu_custom_call" | custom-call | tf_op jit(solution)/shard_map/gather/pallas_call | solution.py:537
  74.1 1.0 slice_convert_fusion
  77.8 41.4 %front.1 = (bf16[3,544,1408]{2,1,0:T(8,128)(2,1)}, bf16[544,1408]{1,0:T(8,128)(2,1)}, bf16[544,1408]{1,0:T(8,128)(2,1)}, f32[544,1408]{1,0:T(8,128)}, bf16[544,1...) custom-call(bf16[2,257,1408]{2,1,0:T(8,128)(2,1)} %copy.30.x.refs_3_.refs_2_, ...), custom_call_target="tpu_custom_call", output_to_operand_aliasing={{5}: (4, {})} | custom-call | tf_op jit(solution)/shard_map/front/pallas_call | solution.py:776
  119.2 47.1 %mlp_in.1 = (bf16[544,6144]{1,0:T(8,128)(2,1)}, f32[544,6144]{1,0:T(8,128)}, f32[6144,768]{1,0:T(8,128)}, bf16[4,4,2,4,3,16,1408]{6,5,4,3,2,1,0:T(8,128)(2,1)}) custom-call(bf16[544,1408]{1,0:T(8,128)(2,1)} %get-tuple-element.47.h2.refs_7_, bf16[2,257,1408]{2,1,0:T(8,128)(2,1)} %copy.31.gz.refs_4_, ...), custom_call_target="tpu_custom_call", output_to_operand_aliasing={{3}: (5, {})} | custom-call | tf_op jit(solution)/shard_map/mlp_in/pallas_call | solution.py:858
  166.3 63.8 %mlp_out.1 = (bf16[2,4,544,768]{3,2,1,0:T(8,128)(2,1)}, f32[8,1,768]{2,1,0:T(1,128)}, f32[544,1408]{1,0:T(8,128)}, f32[544,1408]{1,0:T(8,128)}, f32[3,4,4,32,768]{4,3,2,1,0:T(8,128)}) custom-call(bf16[544,6144]{1,0:T(8,128)(2,1)} %get-tuple-element.50.act, f32[544,6144]{1,0:T(8,128)} %get-tuple-element.51.slope, bf16[2,257,1408]{2,1,0:T(8,128)(2,1)} %copy.31.gz.refs_4_, ...), custom_call_target="tpu_custom_call" | custom-call | tf_op jit(solution)/shard_map/mlp_out/pallas_call | solution.py:900
  230.1 0.8 reduce
  230.9 35.9 %mid.1 = (bf16[2,257,1408]{2,1,0:T(8,128)(2,1)}, f32[544,1408]{1,0:T(8,128)}, bf16[2,544,768]{2,1,0:T(8,128)(2,1)}, bf16[544,1408]{1,0:T(8,128)(2,1)}, f32[8,140...) custom-call(f32[544,1408]{1,0:T(8,128)} %get-tuple-element.54.refs_0_, ...), custom_call_target="tpu_custom_call" | custom-call | tf_op jit(solution)/shard_map/mid/pallas_call | solution.py:1052
  266.9 0.8 slice.59
  268.0 61.1 %attn_back.1 = (bf16[2,3,544,768]{3,2,1,0:T(8,128)(2,1)}, f32[3,1408]{1,0:T(4,128)}, f32[4,1408,768]{2,1,0:T(8,128)}, f32[3,4,4,32,768]{4,3,2,1,0:T(8,128)}, f32[4,3,32,768]{3,2,1,0:T(8,128)}) custom-call(bf16[3,544,1408]{2,1,0:T(8,128)(2,1)} %get-tuple-element.60.refs_0_, bf16[544,1408]{1,0:T(8,128)(2,1)} %get-tuple-element.61.refs_1_, ...), custom_call_target="tpu_custom_call" | custom-call | tf_op jit(solution)/shard_map/attn_back/pallas_call | solution.py:1105
  329.1 0.9 reshape.95
  330.1 2.2 collective-permute-start.1
  332.3 3.6 copy.37
  336.1 0.9 reshape.100.refs_5_
  337.0 108.9 %last.1 = (bf16[2,257,1408]{2,1,0:T(8,128)(2,1)}, f32[4,4,4,88,768]{4,3,2,1,0:T(8,128)}, f32[48,4224]{1,0:T(8,128)}, f32[48,1408]{1,0:T(8,128)}, f32[48,6144]{1,...) custom-call(bf16[2,3,544,768]{3,2,1,0:T(8,128)(2,1)} %get-tuple-element.67.refs_0_,, ...), custom_call_target="tpu_custom_call", output_to_operand_aliasing={{1}: (8, {})} | custom-call | tf_op jit(solution)/shard_map/last/pallas_call | solution.py:1272
  448.6 3.6 copy.38
  452.9 0.9 copy.48
  454.5 1.0 copy.50
  455.6 1.0 copy.51
  (48 shorter events, 10.6 us)
Async XLA Ops:
  0.6 5.9 %copy-start = (bf16[2,257,1408]{2,0,1:T(2,128)(2,1)S(1)}, bf16[2,257,1408]{2,0,1:T(2,128)(2,1)}, u32[]{:S(2)}) copy-start(bf16[2,257,1408]{2,0,1:T(2,128)(2,1)} %param.9) | copy-start | bytes 4342276
  5.0 2.8 copy-start.1
  5.1 5.7 %collective-permute-start = (bf16[2,44,768]{2,1,0:T(8,128)(2,1)S(1)}, bf16[2,44,768]{2,1,0:T(8,128)(2,1)S(1)}, u32[]{:S(2)}, u32[]{:S(2)}) collective-permute-start(bf16[2,44,768]{2,1,0:T(8,128)(2,1)S(1)} %broadcast_select_fusion.2), channel_id=1, source_target_pairs={{0,1},{1,0},{2,3},{3,2},{4,5},{5,4},{6,7},{7,6},{8,9},{9,8},{10,11... | collective-permute-start | bytes 405512 | tf_op jit(solution)/shard_map/ppermute | solution.py:1291
  330.1 5.8 %collective-permute-start.1 = (f32[32,588]{1,0:T(8,128)S(1)}, f32[32,588]{1,0:T(8,128)S(1)}, u32[]{:S(2)}, u32[]{:S(2)}) collective-permute-start(f32[32,588]{1,0:T(8,128)S(1)} %pad_maximum_fusion.2), channel_id=1, source_target_pairs={{0,1},{1,0},{2,3},{3,2},{4,5},{5,4},{6,7},{7,6},{8,9},{9,8},{10,11... | collective-permute-start | bytes 225800 | tf_op jit(solution)/shard_map/ppermute | solution.py:1291
  445.9 7.0 %copy-start.4 = (f32[48,4224]{1,0:T(8,128)S(1)}, f32[48,4224]{1,0:T(8,128)}, u32[]{:S(2)}) copy-start(f32[48,4224]{1,0:T(8,128)} %get-tuple-element.76) | copy-start | bytes 2433028
  448.6 5.2 %copy-start.5 = (f32[48,1408]{1,0:T(8,128)S(1)}, f32[48,1408]{1,0:T(8,128)}, u32[]{:S(2)}) copy-start(f32[48,1408]{1,0:T(8,128)} %get-tuple-element.78) | copy-start | bytes 811012
  452.3 2.3 copy-start.2
  453.8 1.7 copy-start.3

commit v8 on v7

--- a/solution.py
+++ b/solution.py
@@ -103,25 +103,30 @@
         self.kind, self.src, self.dst, self.local = kind, src, dst, local
         self.hops, self.pushes = (hop_send, hop_recv), (push_send, push_recv)
         self.cols, self.cut = (256, 128) if kind == WIDE else (D, HALF)
+        self.parts = ((0, self.cut), (self.cut, self.cols - self.cut))
 
     @staticmethod
     def semaphores():
         dma = pltpu.SemaphoreType.DMA
-        return [dma((C, C, ADDED))] * PAIR + [dma((C, ADDED + 1))] * PAIR + [dma((C,))]
+        return [dma((C, SIDE, ADDED))] * PAIR + [dma((C, PAIR, ADDED + 1))] * PAIR + [dma((C,))]
 
     @staticmethod
     def shape(kind):
         return (SIDE,) * 3 + (CHIP, QCOLS) if kind == WIDE else (SIDE, SIDE, PAIR, SIDE, C, 16, D)
 
+    @staticmethod
+    def dim(k, s):
+        return COLOUR_DIMS[k][min(s, THIRD)]
+
     def source(self, k):
         return self.src.at[:, pl.ds(self.cols * k, self.cols)] if self.kind == WIDE else self.src.at[k]
 
     def piece(self, me, k, s, v, half=None):
         dims = COLOUR_DIMS[k]
-        at = {**me.at, **{d: ALL for d in dims[:s]}, dims[s]: v}
-        off, width = 0, self.cols
+        at = {**me.at, **{d: ALL for d in dims[:min(s, THIRD)]}, self.dim(k, s): v}
+        off, width = self.parts[s - THIRD] if s >= THIRD else (0, self.cols)
         if half is not None and s == FIRST:
-            off, width = self.cut * half, (self.cut, self.cols - self.cut)[half]
+            off, width = self.parts[half]
         elif half is not None:
             at[dims[0]] = duo(half)
         if self.kind == WIDE:
@@ -131,7 +136,7 @@
 
     def hop(self, k, s, m):
         me = Torus()
-        dim = COLOUR_DIMS[k][s]
+        dim = self.dim(k, s)
         by = toward(m)
         if m < FAR:
             ref = self.piece(me, k, s, me.at[dim])
@@ -140,16 +145,16 @@
         src = self.source(k) if s == FIRST and m < FAR else ref
         return remote(src, ref, self.hops, (k, s, m), me.neighbour(dim, by))
 
-    def push(self, k, n):
+    def push(self, k, s, n):
         me = Torus()
-        dim = COLOUR_DIMS[k][THIRD]
+        dim = self.dim(k, s)
         if n < FAR:
-            ref = self.piece(me, k, THIRD, me.shift(dim, -toward(n)))
+            ref = self.piece(me, k, s, me.shift(dim, -toward(n)))
         elif n < ADDED:
-            ref = self.piece(me, k, THIRD, me.shift(dim, FAR), n - FAR)
+            ref = self.piece(me, k, s, me.shift(dim, FAR), n - FAR)
         else:
-            ref = self.piece(me, k, THIRD, me.at[dim])
-        return remote(ref, ref, self.pushes, (k, n), me.partner())
+            ref = self.piece(me, k, s, me.at[dim])
+        return remote(ref, ref, self.pushes, (k, s - THIRD, n), me.partner())
 
     def own(self, k):
         me = Torus()
@@ -159,23 +164,23 @@
         for k in COLOURS:
             for m in WAYS:
                 self.hop(k, s, m).start()
-            if s == THIRD:
-                self.push(k, ADDED).start()
+            if s >= THIRD:
+                self.push(k, s, ADDED).start()
 
     def relay(self, s):
         for k in COLOURS:
             for m in WAYS:
                 self.hop(k, s, m).wait_recv()
                 self.hop(k, s, FAR + m).start()
-                if s == THIRD:
-                    self.push(k, m).start()
+                if s >= THIRD:
+                    self.push(k, s, m).start()
 
     def settle(self, s):
         for k in COLOURS:
             for m in WAYS:
                 self.hop(k, s, FAR + m).wait_recv()
-                if s == THIRD:
-                    self.push(k, FAR + m).start()
+                if s >= THIRD:
+                    self.push(k, s, FAR + m).start()
             if s == FIRST:
                 self.own(k).wait()
 
@@ -189,12 +194,14 @@
             for s in rings:
                 for m in range(ADDED):
                     self.hop(k, s, m).wait_send()
-            if THIRD in rings:
-                for n in range(ADDED + 1):
-                    self.push(k, n).wait()
+                if s >= THIRD:
+                    for n in range(ADDED + 1):
+                        self.push(k, s, n).wait()
 
     def last_ring(self):
-        return [functools.partial(f, THIRD) for f in (self.launch, self.relay, self.settle, self.sent)]
+        parts = THIRD, LAST
+        steps = [functools.partial(f, s) for f in (self.launch, self.relay, self.settle) for s in parts]
+        return steps + [functools.partial(self.sent, *parts)]
 
 
 def add_into(total, *others):
@@ -527,9 +534,9 @@
         gather.begin()
     for step, *ring in ((a.relay, FIRST), (u.relay, FIRST), (d.relay, FIRST), (a.settle, FIRST), (a.launch, SECOND),
                         (u.settle, FIRST), (u.launch, SECOND), (a.relay, SECOND), (d.settle, FIRST), (d.launch, SECOND),
-                        (u.relay, SECOND), (a.settle, SECOND), (a.launch, THIRD), (d.relay, SECOND), (u.settle, SECOND),
-                        (a.relay, THIRD), (d.settle, SECOND), (a.settle, THIRD), (u.sent, FIRST, SECOND),
-                        (d.sent, FIRST, SECOND), (a.sent, FIRST, SECOND, THIRD)):
+                        (u.relay, SECOND), (a.settle, SECOND), (a.launch, THIRD), (a.launch, LAST), (d.relay, SECOND),
+                        (u.settle, SECOND), (a.relay, THIRD), (d.settle, SECOND), (a.relay, LAST), (a.settle, THIRD),
+                        (a.settle, LAST), (u.sent, FIRST, SECOND), (d.sent, FIRST, SECOND), (a.sent, *range(SIDE))):
         step(*ring)
 
 
@@ -694,11 +701,23 @@
     return jnp.concatenate([t.astype(F32), jnp.zeros((TOK - SEQ, t.shape[1]), F32)], axis=0).astype(BF16)
 
 
+WINDOW = 2 * LANES
+
+
 def window(h):
-    start = h * HEAD // LANES * LANES
-    stop = min(D, -(-(h + 1) * HEAD // LANES) * LANES)
-    lane = lax.broadcasted_iota(jnp.int32, (1, stop - start), 1) + (start - h * HEAD)
-    return slice(start, stop), (lane >= 0) & (lane < HEAD)
+    first = h * HEAD
+    start = jnp.minimum(lax.div(first, LANES) * LANES, D - WINDOW)
+    lane = lax.broadcasted_iota(jnp.int32, (1, WINDOW), 1) + (start - first)
+    return pl.ds(pl.multiple_of(start, LANES), WINDOW), (lane >= 0) & (lane < HEAD)
+
+
+def each_head(body):
+    def trip(i, carry):
+        for n in range(PAIR):
+            body(i * PAIR + n)
+        return carry
+
+    lax.fori_loop(0, HEADS // PAIR, trip, 0)
 
 
 def only(mask, t):
@@ -714,13 +733,16 @@
     acc[...] = jnp.zeros_like(acc)
     start = pl.multiple_of(s * TOK, TAIL)
     tokens = pl.ds(start, SEQ)
-    for h in range(HEADS):
+
+    def head(h):
         lanes, mask = window(h)
         k = only(mask, rows[K, tokens, lanes])
         v = only(mask, rows[V, tokens, lanes])
         probs = softmax(dot_nt(rows[Q, tokens, lanes], k) * SCALE).astype(BF16)
         acc[:, lanes] += dot(probs, v)
-        visit(h)
+
+    each_head(head)
+    visit("half")
     o[pl.ds(start, TOK)] = pad(acc[...])
 
 
@@ -732,7 +754,7 @@
     return pl.ds(TOK * s, TOK)
 
 
-FRONT_PLAN = {"start": ((0, 0, 1),), "wo": ((O + 1, 1, 2),), "end": ((O + 1, 2, None),)}
+FRONT_PLAN = {"start": ((0, 0, 2),), "half": ((O, 2, 3),), "wo": ((O + 1, 3, 4),), "end": ((O + 1, 4, None),)}
 
 
 def front_kernel(x, w, b, vec, _, qkv, h1, o, att, h2, up, rows, acc, *sems):
@@ -799,7 +821,7 @@
     ref[pl.ds(pl.multiple_of(tail + TAIL * s, TAIL), TAIL)] = t[BODY:]
 
 
-DOWN_PLAN = {"start": ((0, 0, 1),), "end": ((TILES + 2, 1, 2), (2 * TILES - 1, 2, None))}
+DOWN_PLAN = {"start": ((0, 0, 2),), "end": ((TILES - PAIR, 2, 3), (TILES + 2, 3, 4), (2 * TILES - 1, 4, None))}
 
 
 def mlp_in_kernel(h2, gz, w_up, b_up, vec, _, act, slope, d_down, down, a_rows, b_rows, b_away, *sems):
@@ -938,7 +960,8 @@
 
 def attention_back(s, qkv, d_o, d_qkv, db, acc, b_rows, away, first, visit):
     acc[...] = jnp.zeros_like(acc)
-    for h in range(HEADS):
+
+    def head(h):
         lanes, mask = window(h)
         q, k, v = (only(mask, qkv[i, :SEQ, lanes]) for i in (Q, K, V))
         do = only(mask, d_o[:SEQ, lanes])
@@ -951,7 +974,9 @@
         ds = (ds * SCALE).astype(BF16)
         acc[K, :, lanes] += dot(ds, q)
         acc[Q, :, lanes] += dot_tn(ds, k)
-        visit(h)
+
+    each_head(head)
+    visit("half")
     accumulate(db, jnp.concatenate([col_sum(acc[i]) for i in (Q, K, V)], axis=0))
     for n in (Q, K, V):
         left, right = halves_of(acc[n])
@@ -1062,7 +1087,7 @@
     )(mlp, d_h2, att, x, gz, vec, w_attn, h2, d_pre, acc)
 
 
-ATTN_PLAN = {"start": ((0, 0, 3),), 6: ((0, 3, 4),), "end": ((LAST_SEQ, 4, 5), (LAST_SEQ + GRAD_STEPS, 5, None))}
+ATTN_PLAN = {"start": ((0, 0, 3),), "half": ((0, 3, 4),), "end": ((LAST_SEQ, 4, 5), (LAST_SEQ + GRAD_STEPS, 5, None))}
 
 
 def attn_back_kernel(*refs):

time: 461 us -> 462 us (level)
  no operation moved by 1% of the time
where the time goes in v8:
time: 462 us; the launch traced here: 457 us
  Pallas kernels  421 us (91%)
  local copies, waits for them, and re-layouts  23.6 us (5%)
  other arithmetic  7.73 us (2%)
    pallas_call x1, Pallas kernels, last_call(): pl.pallas_call(last_kernel, grid=(IN_STEPS + 1,), out_shape=(sds(BF16, *S...  109 us
    pallas_call x1, Pallas kernels, mlp_out_call(): pl.pallas_call(mlp_out_kernel, grid=(TILES,), out_shape=(sds(BF16, PAIR,...  63.8 us
    pallas_call x1, Pallas kernels, gather_call(): pl.pallas_call(gather_kernel, out_shape=[sds(BF16, *Gather.shape(kind)) f...  62.4 us
    pallas_call x1, Pallas kernels, attn_back_call(): pl.pallas_call(attn_back_kernel, grid=(SEQS[0] + GRAD_STEPS,), out_shape=...  60.1 us
    pallas_call x1, Pallas kernels, mlp_in_call(): pl.pallas_call(mlp_in_kernel, grid=(2 * TILES,), out_shape=(sds(BF16, TT,...  47.5 us
    pallas_call x1, Pallas kernels, front_call(): pl.pallas_call(front_kernel, grid=(O + PAIR,), out_shape=(sds(BF16, O, TT...  41.7 us
    pallas_call x1, Pallas kernels, mid_call(): pl.pallas_call(mid_kernel, grid=(SEQS[0] + GRAD_STEPS,), out_shape=(sds(B...  36.3 us
    unnamed x20, local copies, waits for them, and re-layouts  13.5 us
  transfers between devices with their start and end apart: 2, of which 0 were waited for; matrix products, arithmetic and copies ran while one was open for 2% of the time, Pallas kernels for 0%

profile of v8, /device:TPU:1, one launch (start us, length us, event | category | flops | bytes accessed | tf_op | source)
XLA Modules:
  0.0 457.0 jit_solution(2879860453250573674)
XLA Ops:
  3.0 1.0 fusion.1
  4.0 1.0 fusion.2
  5.1 1.4 collective-permute-start
  6.5 1.3 copy.30.x.refs_3_.refs_2_
  7.8 1.3 copy.31.gz.refs_4_
  9.1 1.6 dynamic-slice_convert_fusion.1
  11.6 62.4 %gather.1 = (bf16[4,4,4,88,1536]{4,3,2,1,0:T(8,128)(2,1)}, bf16[4,4,4,88,1536]{4,3,2,1,0:T(8,128)(2,1)}, bf16[4,4,2,4,3,16,1408]{6,5,4,3,2,1,0:T(8,128)(2,1)}) custom-call(bf16[88,768]{1,0:T(8,128)(2,1)} %get-tuple-element.102.refs_0_, bf16[88,768]{1,0:T(8,128)(2,1)} %get-tuple-element.101.refs_1_, bf16[3,16,1408]{2,1,0:T(8,128)(2,1)} %bitcast.42), custom_call_target="tpu_custom_call" | custom-call | tf_op jit(solution)/shard_map/gather/pallas_call | solution.py:544
  74.0 1.0 slice_convert_fusion
  77.7 41.7 %front.1 = (bf16[3,544,1408]{2,1,0:T(8,128)(2,1)}, bf16[544,1408]{1,0:T(8,128)(2,1)}, bf16[544,1408]{1,0:T(8,128)(2,1)}, f32[544,1408]{1,0:T(8,128)}, bf16[544,1...) custom-call(bf16[2,257,1408]{2,1,0:T(8,128)(2,1)} %copy.30.x.refs_3_.refs_2_, ...), custom_call_target="tpu_custom_call", output_to_operand_aliasing={{5}: (4, {})} | custom-call | tf_op jit(solution)/shard_map/front/pallas_call | solution.py:798
  119.4 47.5 %mlp_in.1 = (bf16[544,6144]{1,0:T(8,128)(2,1)}, f32[544,6144]{1,0:T(8,128)}, f32[6144,768]{1,0:T(8,128)}, bf16[4,4,2,4,3,16,1408]{6,5,4,3,2,1,0:T(8,128)(2,1)}) custom-call(bf16[544,1408]{1,0:T(8,128)(2,1)} %get-tuple-element.47.h2.refs_7_, bf16[2,257,1408]{2,1,0:T(8,128)(2,1)} %copy.31.gz.refs_4_, ...), custom_call_target="tpu_custom_call", output_to_operand_aliasing={{3}: (5, {})} | custom-call | tf_op jit(solution)/shard_map/mlp_in/pallas_call | solution.py:880
  166.9 63.8 %mlp_out.1 = (bf16[2,4,544,768]{3,2,1,0:T(8,128)(2,1)}, f32[8,1,768]{2,1,0:T(1,128)}, f32[544,1408]{1,0:T(8,128)}, f32[544,1408]{1,0:T(8,128)}, f32[3,4,4,32,768]{4,3,2,1,0:T(8,128)}) custom-call(bf16[544,6144]{1,0:T(8,128)(2,1)} %get-tuple-element.50.act, f32[544,6144]{1,0:T(8,128)} %get-tuple-element.51.slope, bf16[2,257,1408]{2,1,0:T(8,128)(2,1)} %copy.31.gz.refs_4_, ...), custom_call_target="tpu_custom_call" | custom-call | tf_op jit(solution)/shard_map/mlp_out/pallas_call | solution.py:922
  230.7 0.8 reduce
  231.6 36.3 %mid.1 = (bf16[2,257,1408]{2,1,0:T(8,128)(2,1)}, f32[544,1408]{1,0:T(8,128)}, bf16[2,544,768]{2,1,0:T(8,128)(2,1)}, bf16[544,1408]{1,0:T(8,128)(2,1)}, f32[8,140...) custom-call(f32[544,1408]{1,0:T(8,128)} %get-tuple-element.54.refs_0_, ...), custom_call_target="tpu_custom_call" | custom-call | tf_op jit(solution)/shard_map/mid/pallas_call | solution.py:1077
  267.9 0.8 slice.59
  269.0 60.1 %attn_back.1 = (bf16[2,3,544,768]{3,2,1,0:T(8,128)(2,1)}, f32[3,1408]{1,0:T(4,128)}, f32[4,1408,768]{2,1,0:T(8,128)}, f32[3,4,4,32,768]{4,3,2,1,0:T(8,128)}, f32[4,3,32,768]{3,2,1,0:T(8,128)}) custom-call(bf16[3,544,1408]{2,1,0:T(8,128)(2,1)} %get-tuple-element.60.refs_0_, bf16[544,1408]{1,0:T(8,128)(2,1)} %get-tuple-element.61.refs_1_, ...), custom_call_target="tpu_custom_call" | custom-call | tf_op jit(solution)/shard_map/attn_back/pallas_call | solution.py:1130
  329.2 0.9 reshape.95
  330.1 2.5 collective-permute-start.1
  332.6 3.6 copy.37
  336.4 0.9 reshape.100.refs_5_
  337.3 108.8 %last.1 = (bf16[2,257,1408]{2,1,0:T(8,128)(2,1)}, f32[4,4,4,88,768]{4,3,2,1,0:T(8,128)}, f32[48,4224]{1,0:T(8,128)}, f32[48,1408]{1,0:T(8,128)}, f32[48,6144]{1,...) custom-call(bf16[2,3,544,768]{3,2,1,0:T(8,128)(2,1)} %get-tuple-element.67.refs_0_,, ...), custom_call_target="tpu_custom_call", output_to_operand_aliasing={{1}: (8, {})} | custom-call | tf_op jit(solution)/shard_map/last/pallas_call | solution.py:1297
  448.9 3.6 copy.38
  453.2 0.9 copy.48
  454.8 1.0 copy.50
  455.8 1.0 copy.51
  (48 shorter events, 10.6 us)
Async XLA Ops:
  0.6 5.9 %copy-start = (bf16[2,257,1408]{2,0,1:T(2,128)(2,1)S(1)}, bf16[2,257,1408]{2,0,1:T(2,128)(2,1)}, u32[]{:S(2)}) copy-start(bf16[2,257,1408]{2,0,1:T(2,128)(2,1)} %param.9) | copy-start | bytes 4342276
  5.0 2.8 copy-start.1
  5.1 5.7 %collective-permute-start = (bf16[2,44,768]{2,1,0:T(8,128)(2,1)S(1)}, bf16[2,44,768]{2,1,0:T(8,128)(2,1)S(1)}, u32[]{:S(2)}, u32[]{:S(2)}) collective-permute-start(bf16[2,44,768]{2,1,0:T(8,128)(2,1)S(1)} %broadcast_select_fusion.2), channel_id=1, source_target_pairs={{0,1},{1,0},{2,3},{3,2},{4,5},{5,4},{6,7},{7,6},{8,9},{9,8},{10,11... | collective-permute-start | bytes 405512 | tf_op jit(solution)/shard_map/ppermute | solution.py:1316
  330.1 6.1 %collective-permute-start.1 = (f32[32,588]{1,0:T(8,128)S(1)}, f32[32,588]{1,0:T(8,128)S(1)}, u32[]{:S(2)}, u32[]{:S(2)}) collective-permute-start(f32[32,588]{1,0:T(8,128)S(1)} %pad_maximum_fusion.2), channel_id=1, source_target_pairs={{0,1},{1,0},{2,3},{3,2},{4,5},{5,4},{6,7},{7,6},{8,9},{9,8},{10,11... | collective-permute-start | bytes 225800 | tf_op jit(solution)/shard_map/ppermute | solution.py:1316
  446.2 7.0 %copy-start.4 = (f32[48,4224]{1,0:T(8,128)S(1)}, f32[48,4224]{1,0:T(8,128)}, u32[]{:S(2)}) copy-start(f32[48,4224]{1,0:T(8,128)} %get-tuple-element.76) | copy-start | bytes 2433028
  448.9 5.2 %copy-start.5 = (f32[48,1408]{1,0:T(8,128)S(1)}, f32[48,1408]{1,0:T(8,128)}, u32[]{:S(2)}) copy-start(f32[48,1408]{1,0:T(8,128)} %get-tuple-element.78) | copy-start | bytes 811012
  452.5 2.3 copy-start.2
  454.1 1.7 copy-start.3

commit v9 on v7

--- a/solution.py
+++ b/solution.py
@@ -694,11 +694,27 @@
     return jnp.concatenate([t.astype(F32), jnp.zeros((TOK - SEQ, t.shape[1]), F32)], axis=0).astype(BF16)
 
 
+WINDOW = 2 * LANES
+
+
 def window(h):
-    start = h * HEAD // LANES * LANES
-    stop = min(D, -(-(h + 1) * HEAD // LANES) * LANES)
-    lane = lax.broadcasted_iota(jnp.int32, (1, stop - start), 1) + (start - h * HEAD)
-    return slice(start, stop), (lane >= 0) & (lane < HEAD)
+    first = h * HEAD
+    start = jnp.minimum(lax.div(first, LANES) * LANES, D - WINDOW)
+    lane = lax.broadcasted_iota(jnp.int32, (1, WINDOW), 1) + (start - first)
+    return pl.ds(pl.multiple_of(start, LANES), WINDOW), (lane >= 0) & (lane < HEAD)
+
+
+def each_head(body):
+    lax.fori_loop(0, HEADS, lambda h, carry: (body(h), carry)[1], 0)
+
+
+def each_seq(body):
+    def trip(s, carry):
+        start = pl.multiple_of(s * TOK, TAIL)
+        body(s, pl.ds(start, TOK), pl.ds(start, SEQ))
+        return carry
+
+    lax.fori_loop(0, len(SEQ_PAIR), trip, 0)
 
 
 def only(mask, t):
@@ -714,28 +730,23 @@
     acc[...] = jnp.zeros_like(acc)
     start = pl.multiple_of(s * TOK, TAIL)
     tokens = pl.ds(start, SEQ)
-    for h in range(HEADS):
+
+    def head(h):
         lanes, mask = window(h)
         k = only(mask, rows[K, tokens, lanes])
         v = only(mask, rows[V, tokens, lanes])
         probs = softmax(dot_nt(rows[Q, tokens, lanes], k) * SCALE).astype(BF16)
         acc[:, lanes] += dot(probs, v)
-        visit(h)
+
+    each_head(head)
+    visit("half")
     o[pl.ds(start, TOK)] = pad(acc[...])
 
 
-def seq_rows(t, s):
-    return t[TOK * s:TOK * s + SEQ]
-
-
-def seq_tile(s):
-    return pl.ds(TOK * s, TOK)
-
-
-FRONT_PLAN = {"start": ((0, 0, 1),), "wo": ((O + 1, 1, 2),), "end": ((O + 1, 2, None),)}
-
-
-def front_kernel(x, w, b, vec, _, qkv, h1, o, att, h2, up, rows, acc, *sems):
+FRONT_PLAN = {"start": ((0, 0, 1),), "half": ((O + 1, 1, 2),), "end": ((O + 1, 2, None),)}
+
+
+def front_kernel(x, w, b, vec, _, qkv, h1, o, att, h2, up, rows, lhs, acc, *sems):
     hosted = Background(Gather(WIDE, None, up, *sems).last_ring(), FRONT_PLAN)
     j = pl.program_id(0)
     at_step(0)(enter)
@@ -743,27 +754,40 @@
 
     @at_step(0)
     def _():
-        for s in SEQ_PAIR:
+        def norm(s, tile, tokens):
             xhat, _ = norm_stats(x[s].astype(F32))
-            h1[seq_tile(s)] = pad(xhat * row(vec, G1) + row(vec, C1))
+            h1[tile] = pad(xhat * row(vec, G1) + row(vec, C1))
+
+        each_seq(norm)
+        lhs[...] = h1[...]
+
+    @pl.when(j >= O)
+    def _():
+        attention(j - O, rows, o, acc, hosted.visit)
+        lhs[...] = o[...]
+
+    @pl.when((j < O) | (j == O + LAST_SEQ))
+    def _():
+        bias = jnp.where(j < O, b[0], row(vec, BO))
+
+        def product(s, tile, tokens):
+            att[tile] = dot(lhs[tile], w[0]) + bias
+
+        each_seq(product)
 
     @pl.when(j < O)
     def _():
-        t = (dot(h1[...], w[0]) + b[0]).astype(BF16)
+        t = att[...].astype(BF16)
         qkv[0] = t
         rows[j] = t
 
-    pl.when(j >= O)(lambda: attention(j - O, rows, o, acc, hosted.visit))
-
-    hosted.visit("wo")
-
     @at_step(O + LAST_SEQ)
     def _():
-        a = dot(o[...], w[0]) + row(vec, BO)
-        att[...] = a
-        for s in SEQ_PAIR:
-            xhat, _ = norm_stats(x[s].astype(F32) + row(vec, S1) * seq_rows(a, s))
-            h2[seq_tile(s)] = pad(xhat * row(vec, G2) + row(vec, C2))
+        def norm(s, tile, tokens):
+            xhat, _ = norm_stats(x[s].astype(F32) + row(vec, S1) * att[tokens])
+            h2[tile] = pad(xhat * row(vec, G2) + row(vec, C2))
+
+        each_seq(norm)
 
     hosted.visit("end")
 
@@ -779,7 +803,7 @@
                    sds(BF16, *Gather.shape(WIDE))),
         in_specs=[whole(*SEQS), along(0, 1, D, D, index=upto(O)), along(0, 1, 1, D, index=upto(V)), whole(8, D), ANY],
         out_specs=(along(0, 1, TT, D, index=upto(V)),) + (whole(TT, D),) * SIDE + (ANY,),
-        scratch_shapes=[pltpu.VMEM((O, TT, D), BF16), pltpu.VMEM((SEQ, D), F32)] + Gather.semaphores(),
+        scratch_shapes=[pltpu.VMEM((O, TT, D), BF16), pltpu.VMEM((TT, D), BF16), pltpu.VMEM((SEQ, D), F32)] + Gather.semaphores(),
         input_output_aliases={SIDE: SIDE + 1},
         compiler_params=comm_params(collective_id), name="front",
     )(x, w_attn, b_qkv, vec, up)
@@ -814,11 +838,13 @@
     @at_step(0)
     def _():
         first = Torus().at["c"] == 0
-        for s in SEQ_PAIR:
+        def scale(s, tile, tokens):
             d = pad(gz[s].astype(F32) * row(vec, S2))
             left, right = d[:, :HALF], d[:, D - HALF:]
             put_rows(b_rows, TAILS, s, jnp.where(first, left, right))
             put_rows(b_away, OWN_BODY, s, jnp.where(first, right, left))
+
+        each_seq(scale)
 
     at_step(1)(away.start)
     for n in range(TILES):
@@ -873,7 +899,7 @@
     return pl.BlockSpec((1, D, HALF), lambda j: (index(j) // PAIR, 0, index(j) % PAIR))
 
 
-MLP_PLAN = {"start": ((0, 0, 2),), "end": ((3, 2, 3), (TILES - 1, 3, None))}
+MLP_PLAN = {"start": ((0, 0, 1),), "end": ((1, 1, 2), (3, 2, 3), (TILES - 1, 3, None))}
 
 
 def mlp_out_kernel(act, slope, gz, w_up, w_down, vec, part, d_pre, db_up, mlp, d_h2, sums, dm, *scratch):
@@ -884,8 +910,10 @@
 
     @at_step(0)
     def _():
-        for s in SEQ_PAIR:
-            dm[seq_tile(s)] = pad(gz[s].astype(F32) * row(vec, S2))
+        def scale(s, tile, tokens):
+            dm[tile] = pad(gz[s].astype(F32) * row(vec, S2))
+
+        each_seq(scale)
 
     accumulate(mlp, dot(act[...], w_down[...]))
     d = dot_nt(dm[...], w_down[...]) * slope[...]
@@ -914,7 +942,7 @@
     return t[:, :HALF], jnp.concatenate([t[:, HALF:], jnp.zeros((TOK, QCOLS - D), BF16)], axis=1)
 
 
-def mid(mlp, d_h2, att, x, gz, vec, w_out, z, g_res, d_att, d_o, sums, da_rows):
+def mid(mlp, d_h2, att, x, gz, vec, w_out, z, g_res, d_att, d_o, sums):
     a = att[:SEQ]
     y = x[0].astype(F32) + row(vec, S1) * a
     m = mlp[:SEQ] + row(vec, B2)
@@ -929,16 +957,13 @@
     accumulate(sums, jnp.concatenate([jnp.zeros((BO, D), F32)] + [col_sum(t) for t in terms], axis=0))
     for i, t in enumerate(halves_of(da)):
         d_att[i] = t
-    da_rows[pl.ds(pl.multiple_of(pl.program_id(0) * TOK, TAIL), TOK)] = pad(da)
-
-    @at_step(LAST_SEQ)
-    def _():
-        d_o[...] = dot_nt(da_rows[...], w_out[0]).astype(BF16)
+    d_o[...] = dot_nt(pad(da), w_out[0]).astype(BF16)
 
 
 def attention_back(s, qkv, d_o, d_qkv, db, acc, b_rows, away, first, visit):
     acc[...] = jnp.zeros_like(acc)
-    for h in range(HEADS):
+
+    def head(h):
         lanes, mask = window(h)
         q, k, v = (only(mask, qkv[i, :SEQ, lanes]) for i in (Q, K, V))
         do = only(mask, d_o[:SEQ, lanes])
@@ -951,7 +976,9 @@
         ds = (ds * SCALE).astype(BF16)
         acc[K, :, lanes] += dot(ds, q)
         acc[Q, :, lanes] += dot_tn(ds, k)
-        visit(h)
+
+    each_head(head)
+    visit("half")
     accumulate(db, jnp.concatenate([col_sum(acc[i]) for i in (Q, K, V)], axis=0))
     for n in (Q, K, V):
         left, right = halves_of(acc[n])
@@ -973,6 +1000,14 @@
     def scratch(inputs):
         return [pltpu.VMEM((inputs, ROWS, D), BF16), pltpu.VMEM((inputs, D, ROWS), BF16), pltpu.VMEM((SIDE, ROWS, HALF), BF16)]
 
+    def turn(self, i):
+        def trip(n, carry):
+            lanes = pl.ds(pl.multiple_of(n * LANES, LANES), LANES)
+            self.a_cols[i, lanes] = self.a_rows[i, :, lanes].T
+            return carry
+
+        lax.fori_loop(0, D // LANES, trip, 0)
+
     def step(self):
         j = pl.program_id(0)
         done = []
@@ -984,7 +1019,7 @@
                 i = self.a_of[n]
                 if i not in done:
                     self.inputs[i].wait()
-                    self.a_cols[i] = self.a_rows[i].T
+                    self.turn(i)
                     done.append(i)
                 self.cotangents[n].wait()
 
@@ -1025,7 +1060,7 @@
 def mid_kernel(*refs):
     refs = list(refs)
     take = lambda n: [refs.pop(0) for _ in range(n)]
-    ins, (h2, d_pre, acc), outs, (d_up, result), da_rows = take(7), take(3), take(5), take(2), refs.pop(0)
+    ins, (h2, d_pre, acc), outs, (d_up, result) = take(7), take(3), take(5), take(2)
     rows, a_sems, b_sems = take(3), take(C), take(C)
     rest = Rest(Bands(DOWN), acc, result, *refs)
     hosted = Background([rest.begin, rest.loaded, rest.relay, rest.settle, rest.relay_third, rest.settle_third, rest.finish],
@@ -1042,7 +1077,7 @@
         for move in (*grads.inputs, *grads.cotangents):
             move.start()
 
-    pl.when(pl.program_id(0) < SEQS[0])(lambda: mid(*ins, *outs, da_rows))
+    pl.when(pl.program_id(0) < SEQS[0])(lambda: mid(*ins, *outs))
     grads.step()
     hosted.visit("end")
     at_step(LAST_SEQ + GRAD_STEPS)(grads.finish)
@@ -1054,15 +1089,15 @@
         out_shape=(sds(BF16, *SEQS), sds(F32, TT, D), sds(BF16, PAIR, TT, HALF), sds(BF16, TT, D), sds(F32, 8, D),
                    sds(F32, SIDE, D, HALF), Bands(DOWN).result()),
         in_specs=[tok_block()] * O + [seq_block()] * PAIR + [whole(8, D), w_out_block()] + [ANY] * O,
-        out_specs=(seq_block(), tok_block(), along(1, PAIR, TOK, HALF, index=upto(LAST_SEQ)), whole(TT, D), whole(8, D),
+        out_specs=(seq_block(), tok_block(), along(1, PAIR, TOK, HALF, index=upto(LAST_SEQ)), tok_block(), whole(8, D),
                    grads_block(SEQS[0], 0), ANY),
-        scratch_shapes=[pltpu.VMEM((TT, D), BF16)] + WideGrads.scratch(1) + Exchange.semaphores() + Exchange.semaphores(SIDE) +
+        scratch_shapes=WideGrads.scratch(1) + Exchange.semaphores() + Exchange.semaphores(SIDE) +
         Bands(DOWN).later(),
         compiler_params=comm_params(collective_id), name="mid",
     )(mlp, d_h2, att, x, gz, vec, w_attn, h2, d_pre, acc)
 
 
-ATTN_PLAN = {"start": ((0, 0, 3),), 6: ((0, 3, 4),), "end": ((LAST_SEQ, 4, 5), (LAST_SEQ + GRAD_STEPS, 5, None))}
+ATTN_PLAN = {"start": ((0, 0, 2),), "half": ((0, 2, 4),), "end": ((SIDE, 4, 5), (LAST_SEQ + GRAD_STEPS, 5, None))}
 
 
 def attn_back_kernel(*refs):
@@ -1212,18 +1247,19 @@
 
     @pl.when(pl.program_id(0) < IN_STEPS)
     def _():
-        accumulate(acc, dot_nt(d_half[0, 0], w[0]))
+        each_seq(lambda s, tile, tokens: accumulate(acc.at[tile], dot_nt(d_half[0, 0, tile], w[0])))
 
     @at_step(IN_STEPS - 1)
     def _():
-        rows = jnp.zeros((SUB, D), F32)
-        for s in SEQ_PAIR:
+        sums[...] = jnp.zeros_like(sums)
+
+        def back(s, tile, tokens):
             xhat, rstd = norm_stats(x[s].astype(F32))
-            tokens = pl.ds(TOK * s, SEQ)
             dh = acc[tokens]
-            rows = rows + jnp.concatenate([col_sum(dh * xhat), col_sum(dh), jnp.zeros((SUB - BO, D), F32)], axis=0)
+            sums[:BO] += jnp.concatenate([col_sum(dh * xhat), col_sum(dh)], axis=0)
             dx[s] = (g_res[tokens] + norm_back(xhat, rstd, dh * row(vec, G1))).astype(BF16)
-        sums[...] = rows
+
+        each_seq(back)
 
     hosted.visit("end")
 

time: 461 us -> 475 us (1.030)
  Pallas kernels: 421 us -> 438 us
    pallas_call x1, Pallas kernels: 41.4 us -> 57.8 us  [front_call(): pl.pallas_call(front_kernel, grid=(O + PAIR,), out_shape=(sds(BF16, O, TT...]
where the time goes in v9:
time: 475 us; the launch traced here: 474 us
  Pallas kernels  438 us (92%)
  local copies, waits for them, and re-layouts  23.6 us (5%)
  other arithmetic  7.73 us (2%)
    pallas_call x1, Pallas kernels, last_call(): pl.pallas_call(last_kernel, grid=(IN_STEPS + 1,), out_shape=(sds(BF16, *S...  109 us
    pallas_call x1, Pallas kernels, mlp_out_call(): pl.pallas_call(mlp_out_kernel, grid=(TILES,), out_shape=(sds(BF16, PAIR,...  64 us
    pallas_call x1, Pallas kernels, gather_call(): pl.pallas_call(gather_kernel, out_shape=[sds(BF16, *Gather.shape(kind)) f...  62.5 us
    pallas_call x1, Pallas kernels, attn_back_call(): pl.pallas_call(attn_back_kernel, grid=(SEQS[0] + GRAD_STEPS,), out_shape=...  62.2 us
    pallas_call x1, Pallas kernels, front_call(): pl.pallas_call(front_kernel, grid=(O + PAIR,), out_shape=(sds(BF16, O, TT...  57.8 us
    pallas_call x1, Pallas kernels, mlp_in_call(): pl.pallas_call(mlp_in_kernel, grid=(2 * TILES,), out_shape=(sds(BF16, TT,...  46.7 us
    pallas_call x1, Pallas kernels, mid_call(): pl.pallas_call(mid_kernel, grid=(SEQS[0] + GRAD_STEPS,), out_shape=(sds(B...  36.4 us
    unnamed x20, local copies, waits for them, and re-layouts  13.5 us
  transfers between devices with their start and end apart: 2, of which 0 were waited for; matrix products, arithmetic and copies ran while one was open for 2% of the time, Pallas kernels for 0%

profile of v9, /device:TPU:1, one launch (start us, length us, event | category | flops | bytes accessed | tf_op | source)
XLA Modules:
  0.0 474.3 jit_solution(1123330546726402411)
XLA Ops:
  3.0 1.0 fusion.1
  4.0 1.0 fusion.2
  5.1 1.4 collective-permute-start
  6.5 1.3 copy.30.x.refs_3_.refs_2_
  7.8 1.3 copy.31.gz.refs_4_
  9.1 1.6 dynamic-slice_convert_fusion.1
  11.6 62.5 %gather.1 = (bf16[4,4,4,88,1536]{4,3,2,1,0:T(8,128)(2,1)}, bf16[4,4,4,88,1536]{4,3,2,1,0:T(8,128)(2,1)}, bf16[4,4,2,4,3,16,1408]{6,5,4,3,2,1,0:T(8,128)(2,1)}) custom-call(bf16[88,768]{1,0:T(8,128)(2,1)} %get-tuple-element.102.refs_0_, bf16[88,768]{1,0:T(8,128)(2,1)} %get-tuple-element.101.refs_1_, bf16[3,16,1408]{2,1,0:T(8,128)(2,1)} %bitcast.42), custom_call_target="tpu_custom_call" | custom-call | tf_op jit(solution)/shard_map/gather/pallas_call | solution.py:537
  74.1 1.0 slice_convert_fusion
  77.8 57.8 %front.1 = (bf16[3,544,1408]{2,1,0:T(8,128)(2,1)}, bf16[544,1408]{1,0:T(8,128)(2,1)}, bf16[544,1408]{1,0:T(8,128)(2,1)}, f32[544,1408]{1,0:T(8,128)}, bf16[544,1...) custom-call(bf16[2,257,1408]{2,1,0:T(8,128)(2,1)} %copy.30.x.refs_3_.refs_2_, ...), custom_call_target="tpu_custom_call", output_to_operand_aliasing={{5}: (4, {})} | custom-call | tf_op jit(solution)/shard_map/front/pallas_call | solution.py:800
  135.6 46.7 %mlp_in.1 = (bf16[544,6144]{1,0:T(8,128)(2,1)}, f32[544,6144]{1,0:T(8,128)}, f32[6144,768]{1,0:T(8,128)}, bf16[4,4,2,4,3,16,1408]{6,5,4,3,2,1,0:T(8,128)(2,1)}) custom-call(bf16[544,1408]{1,0:T(8,128)(2,1)} %get-tuple-element.47.h2.refs_7_, bf16[2,257,1408]{2,1,0:T(8,128)(2,1)} %copy.31.gz.refs_4_, ...), custom_call_target="tpu_custom_call", output_to_operand_aliasing={{3}: (5, {})} | custom-call | tf_op jit(solution)/shard_map/mlp_in/pallas_call | solution.py:884
  182.3 64.0 %mlp_out.1 = (bf16[2,4,544,768]{3,2,1,0:T(8,128)(2,1)}, f32[8,1,768]{2,1,0:T(1,128)}, f32[544,1408]{1,0:T(8,128)}, f32[544,1408]{1,0:T(8,128)}, f32[3,4,4,32,768]{4,3,2,1,0:T(8,128)}) custom-call(bf16[544,6144]{1,0:T(8,128)(2,1)} %get-tuple-element.50.act, f32[544,6144]{1,0:T(8,128)} %get-tuple-element.51.slope, bf16[2,257,1408]{2,1,0:T(8,128)(2,1)} %copy.31.gz.refs_4_, ...), custom_call_target="tpu_custom_call" | custom-call | tf_op jit(solution)/shard_map/mlp_out/pallas_call | solution.py:928
  246.3 0.8 reduce
  247.2 36.4 %mid.1 = (bf16[2,257,1408]{2,1,0:T(8,128)(2,1)}, f32[544,1408]{1,0:T(8,128)}, bf16[2,544,768]{2,1,0:T(8,128)(2,1)}, bf16[544,1408]{1,0:T(8,128)(2,1)}, f32[8,140...) custom-call(f32[544,1408]{1,0:T(8,128)} %get-tuple-element.54.refs_0_, ...), custom_call_target="tpu_custom_call" | custom-call | tf_op jit(solution)/shard_map/mid/pallas_call | solution.py:1087
  283.6 0.8 slice.59
  284.7 62.2 %attn_back.1 = (bf16[2,3,544,768]{3,2,1,0:T(8,128)(2,1)}, f32[3,1408]{1,0:T(4,128)}, f32[4,1408,768]{2,1,0:T(8,128)}, f32[3,4,4,32,768]{4,3,2,1,0:T(8,128)}, f32[4,3,32,768]{3,2,1,0:T(8,128)}) custom-call(bf16[3,544,1408]{2,1,0:T(8,128)(2,1)} %get-tuple-element.60.refs_0_, bf16[544,1408]{1,0:T(8,128)(2,1)} %get-tuple-element.61.refs_1_, ...), custom_call_target="tpu_custom_call" | custom-call | tf_op jit(solution)/shard_map/attn_back/pallas_call | solution.py:1140
  346.9 0.9 reshape.95
  347.8 2.2 collective-permute-start.1
  350.0 3.6 copy.37
  353.8 0.9 reshape.100.refs_5_
  354.7 108.9 %last.1 = (bf16[2,257,1408]{2,1,0:T(8,128)(2,1)}, f32[4,4,4,88,768]{4,3,2,1,0:T(8,128)}, f32[48,4224]{1,0:T(8,128)}, f32[48,1408]{1,0:T(8,128)}, f32[48,6144]{1,...) custom-call(bf16[2,3,544,768]{3,2,1,0:T(8,128)(2,1)} %get-tuple-element.67.refs_0_,, ...), custom_call_target="tpu_custom_call", output_to_operand_aliasing={{1}: (8, {})} | custom-call | tf_op jit(solution)/shard_map/last/pallas_call | solution.py:1308
  466.4 3.6 copy.38
  470.7 0.9 copy.48
  472.3 1.0 copy.50
  473.3 1.0 copy.51
  (48 shorter events, 10.6 us)
Async XLA Ops:
  0.6 5.9 %copy-start = (bf16[2,257,1408]{2,0,1:T(2,128)(2,1)S(1)}, bf16[2,257,1408]{2,0,1:T(2,128)(2,1)}, u32[]{:S(2)}) copy-start(bf16[2,257,1408]{2,0,1:T(2,128)(2,1)} %param.9) | copy-start | bytes 4342276
  5.0 2.8 copy-start.1
  5.1 5.7 %collective-permute-start = (bf16[2,44,768]{2,1,0:T(8,128)(2,1)S(1)}, bf16[2,44,768]{2,1,0:T(8,128)(2,1)S(1)}, u32[]{:S(2)}, u32[]{:S(2)}) collective-permute-start(bf16[2,44,768]{2,1,0:T(8,128)(2,1)S(1)} %broadcast_select_fusion.2), channel_id=1, source_target_pairs={{0,1},{1,0},{2,3},{3,2},{4,5},{5,4},{6,7},{7,6},{8,9},{9,8},{10,11... | collective-permute-start | bytes 405512 | tf_op jit(solution)/shard_map/ppermute | solution.py:1327
  347.8 5.8 %collective-permute-start.1 = (f32[32,588]{1,0:T(8,128)S(1)}, f32[32,588]{1,0:T(8,128)S(1)}, u32[]{:S(2)}, u32[]{:S(2)}) collective-permute-start(f32[32,588]{1,0:T(8,128)S(1)} %pad_maximum_fusion.2), channel_id=1, source_target_pairs={{0,1},{1,0},{2,3},{3,2},{4,5},{5,4},{6,7},{7,6},{8,9},{9,8},{10,11... | collective-permute-start | bytes 225800 | tf_op jit(solution)/shard_map/ppermute | solution.py:1327
  463.7 7.0 %copy-start.4 = (f32[48,4224]{1,0:T(8,128)S(1)}, f32[48,4224]{1,0:T(8,128)}, u32[]{:S(2)}) copy-start(f32[48,4224]{1,0:T(8,128)} %get-tuple-element.76) | copy-start | bytes 2433028
  466.4 5.2 %copy-start.5 = (f32[48,1408]{1,0:T(8,128)S(1)}, f32[48,1408]{1,0:T(8,128)}, u32[]{:S(2)}) copy-start(f32[48,1408]{1,0:T(8,128)} %get-tuple-element.78) | copy-start | bytes 811012
  470.0 2.3 copy-start.2
  471.6 1.7 copy-start.3

commit v10 on v9

--- a/solution.py
+++ b/solution.py
@@ -552,6 +552,31 @@
                     step()
 
 
+class Feed:
+    def __init__(self, block, steps, buffers, sems):
+        self.block, self.steps, self.buffers, self.sems = block, steps, buffers, sems
+
+    @staticmethod
+    def scratch(dtype, *shape):
+        return [pltpu.VMEM((PAIR,) + shape, dtype), pltpu.SemaphoreType.DMA((PAIR,))]
+
+    def copy(self, j):
+        slot = lax.rem(j, PAIR)
+        return pltpu.make_async_copy(self.block(j), self.buffers.at[slot], self.sems.at[slot])
+
+    def get(self, j):
+        pl.when(j + 1 < self.steps)(lambda: self.copy(j + 1).start())
+        self.copy(j).wait()
+        return self.buffers.at[lax.rem(j, PAIR)]
+
+
+def first_feeds(*feeds):
+    @at_step(0)
+    def _():
+        for feed in feeds:
+            feed.copy(0).start()
+
+
 class Share:
     def __init__(self, mine, theirs, place, sems, slot):
         self.local = pltpu.make_async_copy(mine, place, sems[PAIR].at[slot])
@@ -705,7 +730,12 @@
 
 
 def each_head(body):
-    lax.fori_loop(0, HEADS, lambda h, carry: (body(h), carry)[1], 0)
+    def trip(i, carry):
+        for n in range(PAIR):
+            body(i * PAIR + n)
+        return carry
+
+    lax.fori_loop(0, HEADS // PAIR, trip, 0)
 
 
 def each_seq(body):
@@ -746,14 +776,20 @@
 FRONT_PLAN = {"start": ((0, 0, 1),), "half": ((O + 1, 1, 2),), "end": ((O + 1, 2, None),)}
 
 
-def front_kernel(x, w, b, vec, _, qkv, h1, o, att, h2, up, rows, lhs, acc, *sems):
+def front_kernel(x_in, w_in, b, vec, _, qkv, h1, o, att, h2, up, rows, lhs, acc, x, x_sem, w_rows, w_sems, *sems):
     hosted = Background(Gather(WIDE, None, up, *sems).last_ring(), FRONT_PLAN)
     j = pl.program_id(0)
+    weights = Feed(lambda n: w_in.at[n, :, pl.ds(0, D)], SIDE, w_rows, w_sems)
+    fetch = pltpu.make_async_copy(x_in, x, x_sem)
+    at_step(0)(fetch.start)
+    first_feeds(weights)
     at_step(0)(enter)
     hosted.visit("start")
 
     @at_step(0)
     def _():
+        fetch.wait()
+
         def norm(s, tile, tokens):
             xhat, _ = norm_stats(x[s].astype(F32))
             h1[tile] = pad(xhat * row(vec, G1) + row(vec, C1))
@@ -769,9 +805,10 @@
     @pl.when((j < O) | (j == O + LAST_SEQ))
     def _():
         bias = jnp.where(j < O, b[0], row(vec, BO))
+        w = weights.get(jnp.minimum(j, O))
 
         def product(s, tile, tokens):
-            att[tile] = dot(lhs[tile], w[0]) + bias
+            att[tile] = dot(lhs[tile], w[...]) + bias
 
         each_seq(product)
 
@@ -801,9 +838,10 @@
         front_kernel, grid=(O + PAIR,),
         out_shape=(sds(BF16, O, TT, D), sds(BF16, TT, D), sds(BF16, TT, D), sds(F32, TT, D), sds(BF16, TT, D),
                    sds(BF16, *Gather.shape(WIDE))),
-        in_specs=[whole(*SEQS), along(0, 1, D, D, index=upto(O)), along(0, 1, 1, D, index=upto(V)), whole(8, D), ANY],
+        in_specs=[ANY, ANY, along(0, 1, 1, D, index=upto(V)), whole(8, D), ANY],
         out_specs=(along(0, 1, TT, D, index=upto(V)),) + (whole(TT, D),) * SIDE + (ANY,),
-        scratch_shapes=[pltpu.VMEM((O, TT, D), BF16), pltpu.VMEM((TT, D), BF16), pltpu.VMEM((SEQ, D), F32)] + Gather.semaphores(),
+        scratch_shapes=[pltpu.VMEM((O, TT, D), BF16), pltpu.VMEM((TT, D), BF16), pltpu.VMEM((SEQ, D), F32),
+                        pltpu.VMEM(SEQS, BF16), pltpu.SemaphoreType.DMA] + Feed.scratch(BF16, D, D) + Gather.semaphores(),
         input_output_aliases={SIDE: SIDE + 1},
         compiler_params=comm_params(collective_id), name="front",
     )(x, w_attn, b_qkv, vec, up)
@@ -902,9 +940,16 @@
 MLP_PLAN = {"start": ((0, 0, 1),), "end": ((1, 1, 2), (3, 2, 3), (TILES - 1, 3, None))}
 
 
-def mlp_out_kernel(act, slope, gz, w_up, w_down, vec, part, d_pre, db_up, mlp, d_h2, sums, dm, *scratch):
+def mlp_out_kernel(act_in, slope_in, gz, up_in, down_in, vec, part, d_pre, db_up, mlp, d_h2, sums, dm, *scratch):
+    scratch, tiles = scratch[:-8], scratch[-8:]
     first = First(Bands(DOWN), part, sums, *scratch)
     hosted = Background([first.near, first.far, first.relay, first.settle, first.finish], MLP_PLAN)
+    j = pl.program_id(0)
+    cols = lambda n: pl.ds(pl.multiple_of(n * HALF, HALF), HALF)
+    blocks = (lambda n: act_in.at[:, cols(n)], lambda n: slope_in.at[:, cols(n)],
+              lambda n: up_in.at[lax.div(n, PAIR), :, cols(lax.rem(n, PAIR))], lambda n: down_in.at[cols(n)])
+    feeds = [Feed(block, TILES, *tiles[PAIR * i:][:PAIR]) for i, block in enumerate(blocks)]
+    first_feeds(*feeds)
     at_step(0)(enter)
     hosted.visit("start")
 
@@ -915,12 +960,18 @@
 
         each_seq(scale)
 
-    accumulate(mlp, dot(act[...], w_down[...]))
-    d = dot_nt(dm[...], w_down[...]) * slope[...]
-    db_up[0] = col_sum(d)
-    d = d.astype(BF16)
-    d_pre[0, 0] = d
-    accumulate(d_h2, dot_nt(d, w_up[0]))
+    act, slope, w_up, w_down = (feed.get(j) for feed in feeds)
+    db_up[0] = jnp.zeros((1, HALF), F32)
+
+    def back(s, tile, tokens):
+        accumulate(mlp.at[tile], dot(act[tile], w_down[...]))
+        d = dot_nt(dm[tile], w_down[...]) * slope[tile]
+        db_up[0] += col_sum(d)
+        d = d.astype(BF16)
+        d_pre[0, 0, tile] = d
+        accumulate(d_h2.at[tile], dot_nt(d, w_up[...]))
+
+    each_seq(back)
     hosted.visit("end")
 
 
@@ -929,10 +980,11 @@
         mlp_out_kernel, grid=(TILES,),
         out_shape=(sds(BF16, PAIR, SIDE, TT, HALF), sds(F32, TILES, 1, HALF), sds(F32, TT, D), sds(F32, TT, D),
                    Bands(DOWN).sums()),
-        in_specs=[along(1, TT, HALF), along(1, TT, HALF), whole(*SEQS), up_tile(), along(0, HALF, D), whole(8, D), ANY],
+        in_specs=[ANY, ANY, whole(*SEQS), ANY, ANY, whole(8, D), ANY],
         out_specs=(pl.BlockSpec((1, 1, TT, HALF), lambda j: (j % PAIR, j // PAIR, 0, 0)), along(0, 1, 1, HALF),
                    whole(TT, D), whole(TT, D), ANY),
-        scratch_shapes=[pltpu.VMEM((TT, D), BF16)] + Bands(DOWN).first(),
+        scratch_shapes=[pltpu.VMEM((TT, D), BF16)] + Bands(DOWN).first() + Feed.scratch(BF16, TT, HALF) +
+        Feed.scratch(F32, TT, HALF) + Feed.scratch(BF16, D, HALF) + Feed.scratch(BF16, HALF, D),
         compiler_params=comm_params(collective_id), name="mlp_out",
     )(act, slope, gz, w_up, w_down, vec, part)
 
@@ -1103,8 +1155,12 @@
 def attn_back_kernel(*refs):
     refs = list(refs)
     take = lambda n: [refs.pop(0) for _ in range(n)]
-    (qkv, d_o), (h1, o, d_att, part, result), (d_qkv, db, d_attn, sums, total) = take(2), take(5), take(5)
-    acc, away, rows = refs.pop(0), refs.pop(0), take(3)
+    (qkv_in, do_in), (h1, o, d_att, part, result), (d_qkv, db, d_attn, sums, total) = take(2), take(5), take(5)
+    acc, away, rows, tiles = refs.pop(0), refs.pop(0), take(3), take(SIDE)
+    tokens = lambda n: pl.ds(pl.multiple_of(n * TOK, TAIL), TOK)
+    feeds = [Feed(lambda n: qkv_in.at[:, tokens(n)], SEQS[0], *tiles[:PAIR]),
+             Feed(lambda n: do_in.at[tokens(n)], SEQS[0], *tiles[PAIR:])]
+    first_feeds(*feeds)
     a_sems, b_sems, away_sems = take(C), take(C), take(PAIR)
     first = First(Bands(WIDE), part, sums, *take(len(Bands(WIDE).first())))
     spread = Spread(Bands(DOWN), result, total, *refs)
@@ -1129,7 +1185,12 @@
             push.start()
 
     j = pl.program_id(0)
-    pl.when(j < SEQS[0])(lambda: attention_back(j, qkv, d_o, d_qkv, db, acc, rows[2], away, c == 0, hosted.visit))
+
+    @pl.when(j < SEQS[0])
+    def _():
+        qkv, d_o = (feed.get(j) for feed in feeds)
+        attention_back(j, qkv, d_o, d_qkv, db, acc, rows[2], away, c == 0, hosted.visit)
+
 
     grads.step()
     hosted.visit("end")
@@ -1141,10 +1202,10 @@
         attn_back_kernel, grid=(SEQS[0] + GRAD_STEPS,),
         out_shape=(sds(BF16, PAIR, O, TT, HALF), sds(F32, O, D), sds(F32, SIDE, D, HALF), Bands(WIDE).sums(),
                    Bands(DOWN).total()),
-        in_specs=[along(1, O, TOK, D, index=upto(LAST_SEQ)), tok_block()] + [ANY] * 5,
+        in_specs=[ANY] * 7,
         out_specs=(along(2, PAIR, O, TOK, HALF, index=upto(LAST_SEQ)), whole(O, D), grads_block(SEQS[0], O), ANY, ANY),
         scratch_shapes=[pltpu.VMEM((O, SEQ, D), F32), pltpu.VMEM((O, PAIR * TOK, HALF), BF16)] + WideGrads.scratch(2) +
-        Exchange.semaphores(PAIR) + Exchange.semaphores() + Push.semaphores(O) + Bands(WIDE).first() + Spread.scratch(),
+        Feed.scratch(BF16, O, TOK, D) + Feed.scratch(BF16, TOK, D) + Exchange.semaphores(PAIR) + Exchange.semaphores() + Push.semaphores(O) + Bands(WIDE).first() + Spread.scratch(),
         compiler_params=comm_params(collective_id), name="attn_back",
     )(qkv, d_o, h1, o, d_att, part, result)
 
@@ -1224,7 +1285,14 @@
 def last_kernel(*refs):
     refs = list(refs)
     take = lambda n: [refs.pop(0) for _ in range(n)]
-    (d_half, w, x, g_res, vec), (small, acc_up, down, _), (dx, part), outs = take(5), take(SIDE), take(PAIR), take(len(GRADS))
+    (d_qkv, w_attn, x_in, g_in, vec), (small, acc_up, down, _), (dx, part) = take(5), take(SIDE), take(PAIR)
+    outs, (x, g_res, x_sem, g_sem), tiles = take(len(GRADS)), take(SIDE), take(SIDE)
+    j = pl.program_id(0)
+    fetches = [pltpu.make_async_copy(*move) for move in ((x_in, x, x_sem), (g_in, g_res, g_sem))]
+    feeds = [Feed(lambda n: d_qkv.at[lax.rem(n, PAIR), lax.div(n, PAIR)], IN_STEPS, *tiles[:PAIR]),
+             Feed(lambda n: w_attn.at[lax.div(n, PAIR), :, pl.ds(pl.multiple_of(lax.rem(n, PAIR) * HALF, HALF), HALF)],
+                  IN_STEPS, *tiles[PAIR:])]
+    first_feeds(*feeds)
     (acc, sums, pair_sums, block), (totals, sides), block_sem, swap_sems = take(4), (take(C), take(SIDE)), refs.pop(0), take(PAIR)
     finals = Finals(down, sides[:PAIR], sides[PAIR:], outs, take(C))
     halves = [Bands(WIDE, h) for h in WAYS]
@@ -1242,15 +1310,19 @@
 
     @at_step(0)
     def _():
-        fetch.start()
+        for move in (fetch, *fetches):
+            move.start()
         finals.start_down()
 
-    @pl.when(pl.program_id(0) < IN_STEPS)
-    def _():
-        each_seq(lambda s, tile, tokens: accumulate(acc.at[tile], dot_nt(d_half[0, 0, tile], w[0])))
+    @pl.when(j < IN_STEPS)
+    def _():
+        d_half, w = (feed.get(j) for feed in feeds)
+        each_seq(lambda s, tile, tokens: accumulate(acc.at[tile], dot_nt(d_half[tile], w[...])))
 
     @at_step(IN_STEPS - 1)
     def _():
+        for move in fetches:
+            move.wait()
         sums[...] = jnp.zeros_like(sums)
 
         def back(s, tile, tokens):
@@ -1301,17 +1373,16 @@
 
 
 def last_call(d_qkv, w_attn, x, g_res, vec, small, acc_up, down, part, collective_id):
-    low = upto(IN_STEPS - 1)
     halves = [Bands(WIDE, h) for h in WAYS]
     dma = pltpu.SemaphoreType.DMA
     rings = [Bands(WIDE), *halves]
     return pl.pallas_call(
         last_kernel, grid=(IN_STEPS + 1,),
         out_shape=(sds(BF16, *SEQS), sds(F32, *part.shape), *(sds(F32, *shape) for shape in GRADS)),
-        in_specs=[pl.BlockSpec((1, 1, TT, HALF), lambda j: (low(j) % PAIR, low(j) // PAIR, 0, 0)), up_tile(low),
-                  whole(*SEQS), whole(TT, D), whole(8, D)] + [ANY] * SIDE,
+        in_specs=[ANY] * SIDE + [whole(8, D)] + [ANY] * SIDE,
         out_specs=(whole(*SEQS),) + (ANY,) * (len(GRADS) + 1),
-        scratch_shapes=[pltpu.VMEM((TT, D), F32), pltpu.VMEM((SUB, D), F32), pltpu.VMEM((SUB, D), F32),
+        scratch_shapes=[pltpu.VMEM(SEQS, BF16), pltpu.VMEM((TT, D), F32), dma, dma] + Feed.scratch(BF16, TT, HALF) +
+        Feed.scratch(BF16, D, HALF) + [pltpu.VMEM((TT, D), F32), pltpu.VMEM((SUB, D), F32), pltpu.VMEM((SUB, D), F32),
                         pltpu.VMEM((D, LANES), F32)] + [r.vmem(SIDE, C) for r in rings] +
         [pltpu.VMEM((SIDE, KEPT, HALF), F32)] * SIDE + [dma, dma, dma] + [dma((SHARES,))] * C + halves[0].first() * PAIR +
         halves[0].later()[1:] * PAIR + Bands(WIDE).later() + Spread.scratch()[:PAIR] * C,

time: 475 us -> 456 us (0.960)
  Pallas kernels: 438 us -> 419 us
    pallas_call x1, Pallas kernels: 57.8 us -> 46.1 us  [front_call(): pl.pallas_call(front_kernel, grid=(O + PAIR,), out_shape=(sds(BF16, O, TT...]
where the time goes in v10:
time: 456 us; the launch traced here: 455 us
  Pallas kernels  419 us (92%)
  local copies, waits for them, and re-layouts  23.6 us (5%)
  other arithmetic  7.73 us (2%)
    pallas_call x1, Pallas kernels, last_call(): pl.pallas_call(last_kernel, grid=(IN_STEPS + 1,), out_shape=(sds(BF16, *S...  107 us
    pallas_call x1, Pallas kernels, gather_call(): pl.pallas_call(gather_kernel, out_shape=[sds(BF16, *Gather.shape(kind)) f...  62.5 us
    pallas_call x1, Pallas kernels, mlp_out_call(): pl.pallas_call(mlp_out_kernel, grid=(TILES,), out_shape=(sds(BF16, PAIR,...  61.3 us
    pallas_call x1, Pallas kernels, attn_back_call(): pl.pallas_call(attn_back_kernel, grid=(SEQS[0] + GRAD_STEPS,), out_shape=...  59.1 us
    pallas_call x1, Pallas kernels, mlp_in_call(): pl.pallas_call(mlp_in_kernel, grid=(2 * TILES,), out_shape=(sds(BF16, TT,...  46.7 us
    pallas_call x1, Pallas kernels, front_call(): pl.pallas_call(front_kernel, grid=(O + PAIR,), out_shape=(sds(BF16, O, TT...  46.1 us
    pallas_call x1, Pallas kernels, mid_call(): pl.pallas_call(mid_kernel, grid=(SEQS[0] + GRAD_STEPS,), out_shape=(sds(B...  36.6 us
    unnamed x20, local copies, waits for them, and re-layouts  13.5 us
  transfers between devices with their start and end apart: 2, of which 0 were waited for; matrix products, arithmetic and copies ran while one was open for 2% of the time, Pallas kernels for 0%

profile of v10, /device:TPU:1, one launch (start us, length us, event | category | flops | bytes accessed | tf_op | source)
XLA Modules:
  0.0 454.9 jit_solution(11868455632909022495)
XLA Ops:
  3.0 1.0 fusion.1
  4.0 1.0 fusion.2
  5.1 1.4 collective-permute-start
  6.5 1.3 copy.30.x_in.refs_3_.refs_2_
  7.8 1.3 copy.31.gz.refs_4_
  9.1 1.6 dynamic-slice_convert_fusion.1
  11.6 62.5 %gather.1 = (bf16[4,4,4,88,1536]{4,3,2,1,0:T(8,128)(2,1)}, bf16[4,4,4,88,1536]{4,3,2,1,0:T(8,128)(2,1)}, bf16[4,4,2,4,3,16,1408]{6,5,4,3,2,1,0:T(8,128)(2,1)}) custom-call(bf16[88,768]{1,0:T(8,128)(2,1)} %get-tuple-element.102.refs_0_, bf16[88,768]{1,0:T(8,128)(2,1)} %get-tuple-element.101.refs_1_, bf16[3,16,1408]{2,1,0:T(8,128)(2,1)} %bitcast.42), custom_call_target="tpu_custom_call" | custom-call | tf_op jit(solution)/shard_map/gather/pallas_call | solution.py:537
  74.1 1.0 slice_convert_fusion
  77.8 46.1 %front.1 = (bf16[3,544,1408]{2,1,0:T(8,128)(2,1)}, bf16[544,1408]{1,0:T(8,128)(2,1)}, bf16[544,1408]{1,0:T(8,128)(2,1)}, f32[544,1408]{1,0:T(8,128)}, bf16[544,1...) custom-call(bf16[2,257,1408]{2,1,0:T(8,128)(2,1)} %copy.30.x_in.refs_3_.refs_2_, ...), custom_call_target="tpu_custom_call", output_to_operand_aliasing={{5}: (4, {})} | custom-call | tf_op jit(solution)/shard_map/front/pallas_call | solution.py:837
  123.9 46.7 %mlp_in.1 = (bf16[544,6144]{1,0:T(8,128)(2,1)}, f32[544,6144]{1,0:T(8,128)}, f32[6144,768]{1,0:T(8,128)}, bf16[4,4,2,4,3,16,1408]{6,5,4,3,2,1,0:T(8,128)(2,1)}) custom-call(bf16[544,1408]{1,0:T(8,128)(2,1)} %get-tuple-element.47.h2.refs_7_, bf16[2,257,1408]{2,1,0:T(8,128)(2,1)} %copy.31.gz.refs_4_, ...), custom_call_target="tpu_custom_call", output_to_operand_aliasing={{3}: (5, {})} | custom-call | tf_op jit(solution)/shard_map/mlp_in/pallas_call | solution.py:922
  170.6 61.3 %mlp_out.1 = (bf16[2,4,544,768]{3,2,1,0:T(8,128)(2,1)}, f32[8,1,768]{2,1,0:T(1,128)}, f32[544,1408]{1,0:T(8,128)}, f32[544,1408]{1,0:T(8,128)}, f32[3,4,4,32,768]{4,3,2,1,0:T(8,128)}) custom-call(bf16[544,6144]{1,0:T(8,128)(2,1)} %get-tuple-element.50.act_in, f32[544,6144]{1,0:T(8,128)} %get-tuple-element.51.slope_in, ...), custom_call_target="tpu_custom_call" | custom-call | tf_op jit(solution)/shard_map/mlp_out/pallas_call | solution.py:979
  231.9 0.8 reduce
  232.7 36.6 %mid.1 = (bf16[2,257,1408]{2,1,0:T(8,128)(2,1)}, f32[544,1408]{1,0:T(8,128)}, bf16[2,544,768]{2,1,0:T(8,128)(2,1)}, bf16[544,1408]{1,0:T(8,128)(2,1)}, f32[8,140...) custom-call(f32[544,1408]{1,0:T(8,128)} %get-tuple-element.54.refs_0_, ...), custom_call_target="tpu_custom_call" | custom-call | tf_op jit(solution)/shard_map/mid/pallas_call | solution.py:1139
  269.4 0.8 slice.59
  270.5 59.1 %attn_back.1 = (bf16[2,3,544,768]{3,2,1,0:T(8,128)(2,1)}, f32[3,1408]{1,0:T(4,128)}, f32[4,1408,768]{2,1,0:T(8,128)}, f32[3,4,4,32,768]{4,3,2,1,0:T(8,128)}, f32[4,3,32,768]{3,2,1,0:T(8,128)}) custom-call(bf16[3,544,1408]{2,1,0:T(8,128)(2,1)} %get-tuple-element.60.refs_0_, bf16[544,1408]{1,0:T(8,128)(2,1)} %get-tuple-element.61.refs_1_, ...), custom_call_target="tpu_custom_call" | custom-call | tf_op jit(solution)/shard_map/attn_back/pallas_call | solution.py:1201
  329.6 0.9 reshape.95
  330.5 2.4 collective-permute-start.1
  333.0 3.6 copy.37
  336.8 0.9 reshape.100.refs_5_
  337.7 106.6 %last.1 = (bf16[2,257,1408]{2,1,0:T(8,128)(2,1)}, f32[4,4,4,88,768]{4,3,2,1,0:T(8,128)}, f32[48,4224]{1,0:T(8,128)}, f32[48,1408]{1,0:T(8,128)}, f32[48,6144]{1,...) custom-call(bf16[2,3,544,768]{3,2,1,0:T(8,128)(2,1)} %get-tuple-element.67.refs_0_,, ...), custom_call_target="tpu_custom_call", output_to_operand_aliasing={{1}: (8, {})} | custom-call | tf_op jit(solution)/shard_map/last/pallas_call | solution.py:1379
  446.9 3.6 copy.38
  451.3 0.9 copy.48
  452.9 1.0 copy.50
  453.9 1.0 copy.51
  (48 shorter events, 10.6 us)
Async XLA Ops:
  0.6 5.9 %copy-start = (bf16[2,257,1408]{2,0,1:T(2,128)(2,1)S(1)}, bf16[2,257,1408]{2,0,1:T(2,128)(2,1)}, u32[]{:S(2)}) copy-start(bf16[2,257,1408]{2,0,1:T(2,128)(2,1)} %param.9) | copy-start | bytes 4342276
  5.0 2.8 copy-start.1
  5.1 5.7 %collective-permute-start = (bf16[2,44,768]{2,1,0:T(8,128)(2,1)S(1)}, bf16[2,44,768]{2,1,0:T(8,128)(2,1)S(1)}, u32[]{:S(2)}, u32[]{:S(2)}) collective-permute-start(bf16[2,44,768]{2,1,0:T(8,128)(2,1)S(1)} %broadcast_select_fusion.2), channel_id=1, source_target_pairs={{0,1},{1,0},{2,3},{3,2},{4,5},{5,4},{6,7},{7,6},{8,9},{9,8},{10,11... | collective-permute-start | bytes 405512 | tf_op jit(solution)/shard_map/ppermute | solution.py:1398
  330.5 6.0 %collective-permute-start.1 = (f32[32,588]{1,0:T(8,128)S(1)}, f32[32,588]{1,0:T(8,128)S(1)}, u32[]{:S(2)}, u32[]{:S(2)}) collective-permute-start(f32[32,588]{1,0:T(8,128)S(1)} %pad_maximum_fusion.2), channel_id=1, source_target_pairs={{0,1},{1,0},{2,3},{3,2},{4,5},{5,4},{6,7},{7,6},{8,9},{9,8},{10,11... | collective-permute-start | bytes 225800 | tf_op jit(solution)/shard_map/ppermute | solution.py:1398
  444.2 7.0 %copy-start.4 = (f32[48,4224]{1,0:T(8,128)S(1)}, f32[48,4224]{1,0:T(8,128)}, u32[]{:S(2)}) copy-start(f32[48,4224]{1,0:T(8,128)} %get-tuple-element.76) | copy-start | bytes 2433028
  446.9 5.2 %copy-start.5 = (f32[48,1408]{1,0:T(8,128)S(1)}, f32[48,1408]{1,0:T(8,128)}, u32[]{:S(2)}) copy-start(f32[48,1408]{1,0:T(8,128)} %get-tuple-element.78) | copy-start | bytes 811012
  450.6 2.3 copy-start.2
  452.2 1.7 copy-start.3

commit v11 on v10

--- a/solution.py
+++ b/solution.py
@@ -729,13 +729,13 @@
     return pl.ds(pl.multiple_of(start, LANES), WINDOW), (lane >= 0) & (lane < HEAD)
 
 
-def each_head(body):
+def each_head(body, unroll):
     def trip(i, carry):
-        for n in range(PAIR):
-            body(i * PAIR + n)
+        for n in range(unroll):
+            body(i * unroll + n)
         return carry
 
-    lax.fori_loop(0, HEADS // PAIR, trip, 0)
+    lax.fori_loop(0, HEADS // unroll, trip, 0)
 
 
 def each_seq(body):
@@ -768,7 +768,7 @@
         probs = softmax(dot_nt(rows[Q, tokens, lanes], k) * SCALE).astype(BF16)
         acc[:, lanes] += dot(probs, v)
 
-    each_head(head)
+    each_head(head, PAIR)
     visit("half")
     o[pl.ds(start, TOK)] = pad(acc[...])
 
@@ -805,12 +805,7 @@
     @pl.when((j < O) | (j == O + LAST_SEQ))
     def _():
         bias = jnp.where(j < O, b[0], row(vec, BO))
-        w = weights.get(jnp.minimum(j, O))
-
-        def product(s, tile, tokens):
-            att[tile] = dot(lhs[tile], w[...]) + bias
-
-        each_seq(product)
+        att[...] = dot(lhs[...], weights.get(jnp.minimum(j, O))[...]) + bias
 
     @pl.when(j < O)
     def _():
@@ -847,10 +842,6 @@
     )(x, w_attn, b_qkv, vec, up)
 
 
-def w_out_block():
-    return pl.BlockSpec((1, D, D), lambda j: (O, 0, 0), pipeline_mode=pl.Buffered(1))
-
-
 TILES = FF // HALF
 OWN_BODY = BODY * len(SEQ_PAIR)
 TAILS = ROWS - TAIL * PAIR * len(SEQ_PAIR)
@@ -864,7 +855,13 @@
 DOWN_PLAN = {"start": ((0, 0, 1),), "end": ((TILES + 2, 1, 2), (2 * TILES - 1, 2, None))}
 
 
-def mlp_in_kernel(h2, gz, w_up, b_up, vec, _, act, slope, d_down, down, a_rows, b_rows, b_away, *sems):
+def mlp_in_kernel(h2_in, gz_in, up_in, b_up, vec, _, act, slope, d_down, down, a_rows, b_rows, b_away, *sems):
+    (h2, gz, h2_sem, gz_sem, *tiles), sems = sems[:SIDE + PAIR], sems[SIDE + PAIR:]
+    feed = Feed(lambda n: up_in.at[lax.div(n, PAIR), :, tile_cols(lax.rem(n, PAIR))], TILES, *tiles)
+    fetches = [pltpu.make_async_copy(*move) for move in ((gz_in, gz, gz_sem), (h2_in, h2, h2_sem))]
+    for move in fetches:
+        at_step(0)(move.start)
+    first_feeds(feed)
     a_sems, b_sems, sems = sems[:PAIR], sems[PAIR:2 * PAIR], sems[2 * PAIR:]
     hosted = Background(Gather(DOWN, None, down, *sems).last_ring(), DOWN_PLAN)
     j = pl.program_id(0)
@@ -875,6 +872,8 @@
 
     @at_step(0)
     def _():
+        for move in fetches:
+            move.wait()
         first = Torus().at["c"] == 0
         def scale(s, tile, tokens):
             d = pad(gz[s].astype(F32) * row(vec, S2))
@@ -890,7 +889,7 @@
 
     @pl.when(j < TILES)
     def _():
-        u = dot(h2[...], w_up[0]) + b_up[0]
+        u = dot(h2[...], feed.get(j)[...]) + b_up[0]
         phi = 0.5 * (1.0 + lax.erf(u * math.sqrt(0.5)))
         slope[...] = phi + u * (jnp.exp(-0.5 * u * u) * math.sqrt(0.5 / math.pi))
         place = lax.rem(lax.broadcasted_iota(jnp.int32, (TT, 1), 0), TOK)
@@ -922,32 +921,34 @@
     return pl.pallas_call(
         mlp_in_kernel, grid=(2 * TILES,),
         out_shape=(sds(BF16, TT, FF), sds(F32, TT, FF), sds(F32, FF, HALF), sds(BF16, *Gather.shape(DOWN))),
-        in_specs=[whole(TT, D), whole(*SEQS), up_tile(low), along(0, 1, 1, HALF, index=low), whole(8, D), ANY],
+        in_specs=[ANY] * O + [along(0, 1, 1, HALF, index=low), whole(8, D), ANY],
         out_specs=(along(1, TT, HALF, index=low), along(1, TT, HALF, index=low),
                    along(0, HALF, HALF, index=high), ANY),
         scratch_shapes=[pltpu.VMEM((TILES, ROWS, HALF), BF16), pltpu.VMEM((ROWS, HALF), BF16),
-                        pltpu.VMEM((PAIR * TOK, HALF), BF16)] + Push.semaphores(TILES) + Push.semaphores(1) +
+                        pltpu.VMEM((PAIR * TOK, HALF), BF16), pltpu.VMEM((TT, D), BF16), pltpu.VMEM(SEQS, BF16),
+                        pltpu.SemaphoreType.DMA, pltpu.SemaphoreType.DMA] + Feed.scratch(BF16, D, HALF) + Push.semaphores(TILES) + Push.semaphores(1) +
         Gather.semaphores(),
         input_output_aliases={SIDE + 1: O},
         compiler_params=comm_params(collective_id), name="mlp_in",
     )(h2, gz, w_up, b_up.reshape(TILES, 1, HALF), vec, down)
 
 
-def up_tile(index=lambda j: j):
-    return pl.BlockSpec((1, D, HALF), lambda j: (index(j) // PAIR, 0, index(j) % PAIR))
+def tile_cols(n):
+    return pl.ds(pl.multiple_of(n * HALF, HALF), HALF)
 
 
 MLP_PLAN = {"start": ((0, 0, 1),), "end": ((1, 1, 2), (3, 2, 3), (TILES - 1, 3, None))}
 
 
-def mlp_out_kernel(act_in, slope_in, gz, up_in, down_in, vec, part, d_pre, db_up, mlp, d_h2, sums, dm, *scratch):
+def mlp_out_kernel(act_in, slope_in, gz, up_in, down_in, vec, part, d_pre, db_up, mlp_out, d_out, sums, dm, mlp, d_h2, mlp_sem,
+                   d_sem, *scratch):
     scratch, tiles = scratch[:-8], scratch[-8:]
+    stores = [pltpu.make_async_copy(*move) for move in ((mlp, mlp_out, mlp_sem), (d_h2, d_out, d_sem))]
     first = First(Bands(DOWN), part, sums, *scratch)
     hosted = Background([first.near, first.far, first.relay, first.settle, first.finish], MLP_PLAN)
     j = pl.program_id(0)
-    cols = lambda n: pl.ds(pl.multiple_of(n * HALF, HALF), HALF)
-    blocks = (lambda n: act_in.at[:, cols(n)], lambda n: slope_in.at[:, cols(n)],
-              lambda n: up_in.at[lax.div(n, PAIR), :, cols(lax.rem(n, PAIR))], lambda n: down_in.at[cols(n)])
+    blocks = (lambda n: act_in.at[:, tile_cols(n)], lambda n: slope_in.at[:, tile_cols(n)],
+              lambda n: up_in.at[lax.div(n, PAIR), :, tile_cols(lax.rem(n, PAIR))], lambda n: down_in.at[tile_cols(n)])
     feeds = [Feed(block, TILES, *tiles[PAIR * i:][:PAIR]) for i, block in enumerate(blocks)]
     first_feeds(*feeds)
     at_step(0)(enter)
@@ -972,7 +973,11 @@
         accumulate(d_h2.at[tile], dot_nt(d, w_up[...]))
 
     each_seq(back)
+    for move in stores:
+        at_step(TILES - 1)(move.start)
     hosted.visit("end")
+    for move in stores:
+        at_step(TILES - 1)(move.wait)
 
 
 def mlp_out_call(act, slope, gz, w_up, w_down, vec, part, collective_id):
@@ -982,8 +987,9 @@
                    Bands(DOWN).sums()),
         in_specs=[ANY, ANY, whole(*SEQS), ANY, ANY, whole(8, D), ANY],
         out_specs=(pl.BlockSpec((1, 1, TT, HALF), lambda j: (j % PAIR, j // PAIR, 0, 0)), along(0, 1, 1, HALF),
-                   whole(TT, D), whole(TT, D), ANY),
-        scratch_shapes=[pltpu.VMEM((TT, D), BF16)] + Bands(DOWN).first() + Feed.scratch(BF16, TT, HALF) +
+                   ANY, ANY, ANY),
+        scratch_shapes=[pltpu.VMEM((TT, D), BF16), pltpu.VMEM((TT, D), F32), pltpu.VMEM((TT, D), F32),
+                        pltpu.SemaphoreType.DMA, pltpu.SemaphoreType.DMA] + Bands(DOWN).first() + Feed.scratch(BF16, TT, HALF) +
         Feed.scratch(F32, TT, HALF) + Feed.scratch(BF16, D, HALF) + Feed.scratch(BF16, HALF, D),
         compiler_params=comm_params(collective_id), name="mlp_out",
     )(act, slope, gz, w_up, w_down, vec, part)
@@ -994,11 +1000,11 @@
     return t[:, :HALF], jnp.concatenate([t[:, HALF:], jnp.zeros((TOK, QCOLS - D), BF16)], axis=1)
 
 
-def mid(mlp, d_h2, att, x, gz, vec, w_out, z, g_res, d_att, d_o, sums):
+def mid(mlp, d_h2, att, x, gz, w_out, vec, z, g_res, d_att, d_o, sums):
     a = att[:SEQ]
-    y = x[0].astype(F32) + row(vec, S1) * a
+    y = x[...].astype(F32) + row(vec, S1) * a
     m = mlp[:SEQ] + row(vec, B2)
-    g = gz[0].astype(F32)
+    g = gz[...].astype(F32)
     z[0] = (y + row(vec, S2) * m).astype(BF16)
     xhat, rstd = norm_stats(y)
     dh = d_h2[:SEQ]
@@ -1009,7 +1015,7 @@
     accumulate(sums, jnp.concatenate([jnp.zeros((BO, D), F32)] + [col_sum(t) for t in terms], axis=0))
     for i, t in enumerate(halves_of(da)):
         d_att[i] = t
-    d_o[...] = dot_nt(pad(da), w_out[0]).astype(BF16)
+    d_o[...] = dot_nt(pad(da), w_out[...]).astype(BF16)
 
 
 def attention_back(s, qkv, d_o, d_qkv, db, acc, b_rows, away, first, visit):
@@ -1029,7 +1035,7 @@
         acc[K, :, lanes] += dot(ds, q)
         acc[Q, :, lanes] += dot_tn(ds, k)
 
-    each_head(head)
+    each_head(head, PAIR)
     visit("half")
     accumulate(db, jnp.concatenate([col_sum(acc[i]) for i in (Q, K, V)], axis=0))
     for n in (Q, K, V):
@@ -1112,7 +1118,14 @@
 def mid_kernel(*refs):
     refs = list(refs)
     take = lambda n: [refs.pop(0) for _ in range(n)]
-    ins, (h2, d_pre, acc), outs, (d_up, result) = take(7), take(3), take(5), take(2)
+    ins, (w_attn, vec), (h2, d_pre, acc), outs, (d_up, result) = take(5), take(2), take(3), take(5), take(2)
+    tiles, (w_out, w_sem) = [take(PAIR) for _ in ins], take(PAIR)
+    tokens = lambda n: pl.ds(pl.multiple_of(n * TOK, TAIL), TOK)
+    feeds = [Feed(lambda n, ref=ref: ref.at[tokens(n) if len(ref.shape) == PAIR else n], SEQS[0], *tile)
+             for ref, tile in zip(ins, tiles)]
+    fetch = pltpu.make_async_copy(w_attn.at[O, :, pl.ds(0, D)], w_out, w_sem)
+    first_feeds(*feeds)
+    at_step(0)(fetch.start)
     rows, a_sems, b_sems = take(3), take(C), take(C)
     rest = Rest(Bands(DOWN), acc, result, *refs)
     hosted = Background([rest.begin, rest.loaded, rest.relay, rest.settle, rest.relay_third, rest.settle_third, rest.finish],
@@ -1129,7 +1142,14 @@
         for move in (*grads.inputs, *grads.cotangents):
             move.start()
 
-    pl.when(pl.program_id(0) < SEQS[0])(lambda: mid(*ins, *outs))
+    j = pl.program_id(0)
+
+    @pl.when(j < SEQS[0])
+    def _():
+        blocks = [feed.get(j) for feed in feeds]
+        at_step(0)(fetch.wait)
+        mid(*blocks, w_out, vec, *outs)
+
     grads.step()
     hosted.visit("end")
     at_step(LAST_SEQ + GRAD_STEPS)(grads.finish)
@@ -1140,13 +1160,14 @@
         mid_kernel, grid=(SEQS[0] + GRAD_STEPS,),
         out_shape=(sds(BF16, *SEQS), sds(F32, TT, D), sds(BF16, PAIR, TT, HALF), sds(BF16, TT, D), sds(F32, 8, D),
                    sds(F32, SIDE, D, HALF), Bands(DOWN).result()),
-        in_specs=[tok_block()] * O + [seq_block()] * PAIR + [whole(8, D), w_out_block()] + [ANY] * O,
+        in_specs=[ANY] * (O + O) + [whole(8, D)] + [ANY] * O,
         out_specs=(seq_block(), tok_block(), along(1, PAIR, TOK, HALF, index=upto(LAST_SEQ)), tok_block(), whole(8, D),
                    grads_block(SEQS[0], 0), ANY),
-        scratch_shapes=WideGrads.scratch(1) + Exchange.semaphores() + Exchange.semaphores(SIDE) +
+        scratch_shapes=Feed.scratch(F32, TOK, D) * O + Feed.scratch(BF16, SEQ, D) * PAIR +
+        [pltpu.VMEM((D, D), BF16), pltpu.SemaphoreType.DMA] + WideGrads.scratch(1) + Exchange.semaphores() + Exchange.semaphores(SIDE) +
         Bands(DOWN).later(),
         compiler_params=comm_params(collective_id), name="mid",
-    )(mlp, d_h2, att, x, gz, vec, w_attn, h2, d_pre, acc)
+    )(mlp, d_h2, att, x, gz, w_attn, vec, h2, d_pre, acc)
 
 
 ATTN_PLAN = {"start": ((0, 0, 2),), "half": ((0, 2, 4),), "end": ((SIDE, 4, 5), (LAST_SEQ + GRAD_STEPS, 5, None))}
@@ -1222,12 +1243,15 @@
 
 
 def split_rows(totals, first, keep, give):
-    for x in range(SIDE):
+    def trip(x, carry):
         for total, bands in totals:
             rows = jnp.concatenate([total[x, k, :n] for k, (_, n) in enumerate(BANDS[WIDE])], axis=0)
             low, high = rows[:KEPT], jnp.concatenate([rows[OWN:], rows[:KEPT - OWN]], axis=0)
             keep[x, :, bands.cols] = jnp.where(first, low, high)
             give[x, :, bands.cols] = jnp.where(first, high, low)
+        return carry
+
+    lax.fori_loop(0, SIDE, trip, 0)
 
 
 class Finals:
@@ -1285,10 +1309,11 @@
 def last_kernel(*refs):
     refs = list(refs)
     take = lambda n: [refs.pop(0) for _ in range(n)]
-    (d_qkv, w_attn, x_in, g_in, vec), (small, acc_up, down, _), (dx, part) = take(5), take(SIDE), take(PAIR)
-    outs, (x, g_res, x_sem, g_sem), tiles = take(len(GRADS)), take(SIDE), take(SIDE)
+    (d_qkv, w_attn, x_in, g_in, vec), (small, acc_up, down, _), (dx_out, part) = take(5), take(SIDE), take(PAIR)
+    outs, (x, g_res, dx, x_sem, g_sem, dx_sem), tiles = take(len(GRADS)), take(SIDE + PAIR), take(SIDE)
     j = pl.program_id(0)
     fetches = [pltpu.make_async_copy(*move) for move in ((x_in, x, x_sem), (g_in, g_res, g_sem))]
+    store = pltpu.make_async_copy(dx, dx_out, dx_sem)
     feeds = [Feed(lambda n: d_qkv.at[lax.rem(n, PAIR), lax.div(n, PAIR)], IN_STEPS, *tiles[:PAIR]),
              Feed(lambda n: w_attn.at[lax.div(n, PAIR), :, pl.ds(pl.multiple_of(lax.rem(n, PAIR) * HALF, HALF), HALF)],
                   IN_STEPS, *tiles[PAIR:])]
@@ -1332,6 +1357,7 @@
             dx[s] = (g_res[tokens] + norm_back(xhat, rstd, dh * row(vec, G1))).astype(BF16)
 
         each_seq(back)
+        store.start()
 
     hosted.visit("end")
 
@@ -1370,6 +1396,7 @@
         finals.start()
         for user in (rest_up, rest_a, rest_b, a, b, finals):
             user.finish()
+        store.wait()
 
 
 def last_call(d_qkv, w_attn, x, g_res, vec, small, acc_up, down, part, collective_id):
@@ -1380,8 +1407,8 @@
         last_kernel, grid=(IN_STEPS + 1,),
         out_shape=(sds(BF16, *SEQS), sds(F32, *part.shape), *(sds(F32, *shape) for shape in GRADS)),
         in_specs=[ANY] * SIDE + [whole(8, D)] + [ANY] * SIDE,
-        out_specs=(whole(*SEQS),) + (ANY,) * (len(GRADS) + 1),
-        scratch_shapes=[pltpu.VMEM(SEQS, BF16), pltpu.VMEM((TT, D), F32), dma, dma] + Feed.scratch(BF16, TT, HALF) +
+        out_specs=(ANY,) * (len(GRADS) + PAIR),
+        scratch_shapes=[pltpu.VMEM(SEQS, BF16), pltpu.VMEM((TT, D), F32), pltpu.VMEM(SEQS, BF16), dma, dma, dma] + Feed.scratch(BF16, TT, HALF) +
         Feed.scratch(BF16, D, HALF) + [pltpu.VMEM((TT, D), F32), pltpu.VMEM((SUB, D), F32), pltpu.VMEM((SUB, D), F32),
                         pltpu.VMEM((D, LANES), F32)] + [r.vmem(SIDE, C) for r in rings] +
         [pltpu.VMEM((SIDE, KEPT, HALF), F32)] * SIDE + [dma, dma, dma] + [dma((SHARES,))] * C + halves[0].first() * PAIR +

time: 456 us -> 450 us (0.987)
  Pallas kernels: 419 us -> 413 us
where the time goes in v11:
time: 450 us; the launch traced here: 449 us
  Pallas kernels  413 us (92%)
  local copies, waits for them, and re-layouts  23.6 us (5%)
  other arithmetic  7.73 us (2%)
    pallas_call x1, Pallas kernels, last_call(): pl.pallas_call(last_kernel, grid=(IN_STEPS + 1,), out_shape=(sds(BF16, *S...  106 us
    pallas_call x1, Pallas kernels, gather_call(): pl.pallas_call(gather_kernel, out_shape=[sds(BF16, *Gather.shape(kind)) f...  62.5 us
    pallas_call x1, Pallas kernels, mlp_out_call(): pl.pallas_call(mlp_out_kernel, grid=(TILES,), out_shape=(sds(BF16, PAIR,...  59.9 us
    pallas_call x1, Pallas kernels, attn_back_call(): pl.pallas_call(attn_back_kernel, grid=(SEQS[0] + GRAD_STEPS,), out_shape=...  58.2 us
    pallas_call x1, Pallas kernels, front_call(): pl.pallas_call(front_kernel, grid=(O + PAIR,), out_shape=(sds(BF16, O, TT...  45.6 us
    pallas_call x1, Pallas kernels, mlp_in_call(): pl.pallas_call(mlp_in_kernel, grid=(2 * TILES,), out_shape=(sds(BF16, TT,...  45.3 us
    pallas_call x1, Pallas kernels, mid_call(): pl.pallas_call(mid_kernel, grid=(SEQS[0] + GRAD_STEPS,), out_shape=(sds(B...  35.5 us
    unnamed x20, local copies, waits for them, and re-layouts  13.5 us
  transfers between devices with their start and end apart: 2, of which 0 were waited for; matrix products, arithmetic and copies ran while one was open for 2% of the time, Pallas kernels for 0%

profile of v11, /device:TPU:1, one launch (start us, length us, event | category | flops | bytes accessed | tf_op | source)
XLA Modules:
  0.0 448.9 jit_solution(8761789372107385917)
XLA Ops:
  3.0 1.0 fusion.1
  4.0 1.0 fusion.2
  5.1 1.4 collective-permute-start
  6.5 1.3 copy.30.x_in.refs_3_.refs_2_
  7.8 1.3 copy.31.gz_in.gz.refs_4_
  9.1 1.6 dynamic-slice_convert_fusion.1
  11.6 62.5 %gather.1 = (bf16[4,4,4,88,1536]{4,3,2,1,0:T(8,128)(2,1)}, bf16[4,4,4,88,1536]{4,3,2,1,0:T(8,128)(2,1)}, bf16[4,4,2,4,3,16,1408]{6,5,4,3,2,1,0:T(8,128)(2,1)}) custom-call(bf16[88,768]{1,0:T(8,128)(2,1)} %get-tuple-element.102.refs_0_, bf16[88,768]{1,0:T(8,128)(2,1)} %get-tuple-element.101.refs_1_, bf16[3,16,1408]{2,1,0:T(8,128)(2,1)} %bitcast.42), custom_call_target="tpu_custom_call" | custom-call | tf_op jit(solution)/shard_map/gather/pallas_call | solution.py:537
  74.1 1.0 slice_convert_fusion
  77.8 45.6 %front.1 = (bf16[3,544,1408]{2,1,0:T(8,128)(2,1)}, bf16[544,1408]{1,0:T(8,128)(2,1)}, bf16[544,1408]{1,0:T(8,128)(2,1)}, f32[544,1408]{1,0:T(8,128)}, bf16[544,1...) custom-call(bf16[2,257,1408]{2,1,0:T(8,128)(2,1)} %copy.30.x_in.refs_3_.refs_2_, ...), custom_call_target="tpu_custom_call", output_to_operand_aliasing={{5}: (4, {})} | custom-call | tf_op jit(solution)/shard_map/front/pallas_call | solution.py:832
  123.4 45.3 %mlp_in.1 = (bf16[544,6144]{1,0:T(8,128)(2,1)}, f32[544,6144]{1,0:T(8,128)}, f32[6144,768]{1,0:T(8,128)}, bf16[4,4,2,4,3,16,1408]{6,5,4,3,2,1,0:T(8,128)(2,1)}) custom-call(bf16[544,1408]{1,0:T(8,128)(2,1)} %get-tuple-element.47.h2_in.refs_7_, bf16[2,257,1408]{2,1,0:T(8,128)(2,1)} %copy.31.gz_in.gz.refs_4_, ...), custom_call_target="tpu_custom_call", output_to_operand_aliasing={{3}: (5, {})} | custom-call | tf_op jit(solution)/shard_map/mlp_in/pallas_call | solution.py:921
  168.7 59.9 %mlp_out.1 = (bf16[2,4,544,768]{3,2,1,0:T(8,128)(2,1)}, f32[8,1,768]{2,1,0:T(1,128)}, f32[544,1408]{1,0:T(8,128)}, f32[544,1408]{1,0:T(8,128)}, f32[3,4,4,32,768]{4,3,2,1,0:T(8,128)}) custom-call(bf16[544,6144]{1,0:T(8,128)(2,1)} %get-tuple-element.50.act_in, f32[544,6144]{1,0:T(8,128)} %get-tuple-element.51.slope_in, ...), custom_call_target="tpu_custom_call" | custom-call | tf_op jit(solution)/shard_map/mlp_out/pallas_call | solution.py:984
  228.7 0.8 reduce
  229.5 35.5 %mid.1 = (bf16[2,257,1408]{2,1,0:T(8,128)(2,1)}, f32[544,1408]{1,0:T(8,128)}, bf16[2,544,768]{2,1,0:T(8,128)(2,1)}, bf16[544,1408]{1,0:T(8,128)(2,1)}, f32[8,140...) custom-call(f32[544,1408]{1,0:T(8,128)} %get-tuple-element.54.refs_0_, ...), custom_call_target="tpu_custom_call" | custom-call | tf_op jit(solution)/shard_map/mid/pallas_call | solution.py:1159
  265.1 0.8 slice.59
  266.2 58.2 %attn_back.1 = (bf16[2,3,544,768]{3,2,1,0:T(8,128)(2,1)}, f32[3,1408]{1,0:T(4,128)}, f32[4,1408,768]{2,1,0:T(8,128)}, f32[3,4,4,32,768]{4,3,2,1,0:T(8,128)}, f32[4,3,32,768]{3,2,1,0:T(8,128)}) custom-call(bf16[3,544,1408]{2,1,0:T(8,128)(2,1)} %get-tuple-element.60.refs_0_, bf16[544,1408]{1,0:T(8,128)(2,1)} %get-tuple-element.61.refs_1_, ...), custom_call_target="tpu_custom_call" | custom-call | tf_op jit(solution)/shard_map/attn_back/pallas_call | solution.py:1222
  324.4 0.9 reshape.95
  325.3 2.5 collective-permute-start.1
  327.8 3.6 copy.37
  331.6 0.9 reshape.100.refs_5_
  332.5 105.8 %last.1 = (bf16[2,257,1408]{2,1,0:T(8,128)(2,1)}, f32[4,4,4,88,768]{4,3,2,1,0:T(8,128)}, f32[48,4224]{1,0:T(8,128)}, f32[48,1408]{1,0:T(8,128)}, f32[48,6144]{1,...) custom-call(bf16[2,3,544,768]{3,2,1,0:T(8,128)(2,1)} %get-tuple-element.67.refs_0_,, ...), custom_call_target="tpu_custom_call", output_to_operand_aliasing={{1}: (8, {})} | custom-call | tf_op jit(solution)/shard_map/last/pallas_call | solution.py:1406
  441.0 3.6 copy.38
  445.3 0.9 copy.48
  446.9 1.0 copy.50
  447.9 1.0 copy.51
  (48 shorter events, 10.6 us)
Async XLA Ops:
  0.6 5.9 %copy-start = (bf16[2,257,1408]{2,0,1:T(2,128)(2,1)S(1)}, bf16[2,257,1408]{2,0,1:T(2,128)(2,1)}, u32[]{:S(2)}) copy-start(bf16[2,257,1408]{2,0,1:T(2,128)(2,1)} %param.9) | copy-start | bytes 4342276
  5.0 2.8 copy-start.1
  5.1 5.7 %collective-permute-start = (bf16[2,44,768]{2,1,0:T(8,128)(2,1)S(1)}, bf16[2,44,768]{2,1,0:T(8,128)(2,1)S(1)}, u32[]{:S(2)}, u32[]{:S(2)}) collective-permute-start(bf16[2,44,768]{2,1,0:T(8,128)(2,1)S(1)} %broadcast_select_fusion.2), channel_id=1, source_target_pairs={{0,1},{1,0},{2,3},{3,2},{4,5},{5,4},{6,7},{7,6},{8,9},{9,8},{10,11... | collective-permute-start | bytes 405512 | tf_op jit(solution)/shard_map/ppermute | solution.py:1425
  325.3 6.1 %collective-permute-start.1 = (f32[32,588]{1,0:T(8,128)S(1)}, f32[32,588]{1,0:T(8,128)S(1)}, u32[]{:S(2)}, u32[]{:S(2)}) collective-permute-start(f32[32,588]{1,0:T(8,128)S(1)} %pad_maximum_fusion.2), channel_id=1, source_target_pairs={{0,1},{1,0},{2,3},{3,2},{4,5},{5,4},{6,7},{7,6},{8,9},{9,8},{10,11... | collective-permute-start | bytes 225800 | tf_op jit(solution)/shard_map/ppermute | solution.py:1425
  438.3 7.0 %copy-start.4 = (f32[48,4224]{1,0:T(8,128)S(1)}, f32[48,4224]{1,0:T(8,128)}, u32[]{:S(2)}) copy-start(f32[48,4224]{1,0:T(8,128)} %get-tuple-element.76) | copy-start | bytes 2433028
  441.0 5.2 %copy-start.5 = (f32[48,1408]{1,0:T(8,128)S(1)}, f32[48,1408]{1,0:T(8,128)}, u32[]{:S(2)}) copy-start(f32[48,1408]{1,0:T(8,128)} %get-tuple-element.78) | copy-start | bytes 811012
  444.6 2.3 copy-start.2
  446.2 1.7 copy-start.3

commit v12 on v11

--- a/solution.py
+++ b/solution.py
@@ -193,6 +193,11 @@
                 for n in range(ADDED + 1):
                     self.push(k, n).wait()
 
+    def first_rings(self):
+        ring = functools.partial
+        return [self.begin, ring(self.relay, FIRST), lambda: (self.settle(FIRST), self.launch(SECOND)),
+                ring(self.relay, SECOND), ring(self.settle, SECOND), ring(self.sent, FIRST, SECOND)]
+
     def last_ring(self):
         return [functools.partial(f, THIRD) for f in (self.launch, self.relay, self.settle, self.sent)]
 
@@ -521,23 +526,22 @@
 
 def gather_kernel(*refs):
     n = len(Gather.semaphores())
-    a, u, d = (Gather(kind, *refs[i::C][:PAIR], *refs[PAIR * C + n * i:][:n]) for i, kind in enumerate((WIDE, WIDE, DOWN)))
+    a, u = (Gather(WIDE, *refs[i::PAIR][:PAIR], *refs[SIDE + n * i:][:n]) for i in WAYS)
     enter()
-    for gather in (a, u, d):
+    for gather in (a, u):
         gather.begin()
-    for step, *ring in ((a.relay, FIRST), (u.relay, FIRST), (d.relay, FIRST), (a.settle, FIRST), (a.launch, SECOND),
-                        (u.settle, FIRST), (u.launch, SECOND), (a.relay, SECOND), (d.settle, FIRST), (d.launch, SECOND),
-                        (u.relay, SECOND), (a.settle, SECOND), (a.launch, THIRD), (d.relay, SECOND), (u.settle, SECOND),
-                        (a.relay, THIRD), (d.settle, SECOND), (a.settle, THIRD), (u.sent, FIRST, SECOND),
-                        (d.sent, FIRST, SECOND), (a.sent, FIRST, SECOND, THIRD)):
+    for step, *ring in ((a.relay, FIRST), (u.relay, FIRST), (a.settle, FIRST), (a.launch, SECOND), (u.settle, FIRST),
+                        (a.relay, SECOND), (u.launch, SECOND), (a.settle, SECOND), (a.launch, THIRD), (u.relay, SECOND),
+                        (u.settle, SECOND), (a.relay, THIRD), (a.settle, THIRD), (u.sent, FIRST, SECOND),
+                        (a.sent, FIRST, SECOND, THIRD)):
         step(*ring)
 
 
-def gather_call(attn, up, down, collective_id):
+def gather_call(attn, up, collective_id):
     return pl.pallas_call(
-        gather_kernel, out_shape=[sds(BF16, *Gather.shape(kind)) for kind in (WIDE, WIDE, DOWN)], in_specs=[ANY] * C,
-        out_specs=[ANY] * C, scratch_shapes=Gather.semaphores() * C, compiler_params=comm_params(collective_id),
-        name="gather")(attn, up, down)
+        gather_kernel, out_shape=[sds(BF16, *Gather.shape(WIDE))] * PAIR, in_specs=[ANY] * PAIR,
+        out_specs=[ANY] * PAIR, scratch_shapes=Gather.semaphores() * PAIR, compiler_params=comm_params(collective_id),
+        name="gather")(attn, up)
 
 
 class Background:
@@ -773,14 +777,21 @@
     o[pl.ds(start, TOK)] = pad(acc[...])
 
 
-FRONT_PLAN = {"start": ((0, 0, 1),), "half": ((O + 1, 1, 2),), "end": ((O + 1, 2, None),)}
-
-
-def front_kernel(x_in, w_in, b, vec, _, qkv, h1, o, att, h2, up, rows, lhs, acc, x, x_sem, w_rows, w_sems, *sems):
-    hosted = Background(Gather(WIDE, None, up, *sems).last_ring(), FRONT_PLAN)
+FRONT_PLAN = {"start": ((0, 0, 2),), "end": ((0, 2, 3), (1, 3, 4), (O, 4, 5), (O + 1, 6, None)), "half": ((O + 1, 5, 6),)}
+
+
+def front_kernel(x_in, w_in, b, vec, _, down_in, qkv_out, h1_out, o_out, att_out, h2_out, up, down, rows, lhs, att, h2, acc, x,
+                 x_sem, w_rows, w_sems, sems, *ring_sems):
+    n = len(ring_sems) // PAIR
+    early = Gather(DOWN, down_in, down, *ring_sems[n:]).first_rings()
+    late = Gather(WIDE, None, up, *ring_sems[:n]).last_ring()
+    hosted = Background([early[0], late[0], *early[1:SIDE], late[1], *early[SIDE:], *late[PAIR:]], FRONT_PLAN)
     j = pl.program_id(0)
     weights = Feed(lambda n: w_in.at[n, :, pl.ds(0, D)], SIDE, w_rows, w_sems)
     fetch = pltpu.make_async_copy(x_in, x, x_sem)
+    h1, o = (lhs.at[i] for i in WAYS)
+    stores = [pltpu.make_async_copy(*move, sems.at[i]) for i, move in enumerate(
+        ((h1, h1_out), (rows, qkv_out), (o, o_out), (att, att_out), (h2, h2_out)))]
     at_step(0)(fetch.start)
     first_feeds(weights)
     at_step(0)(enter)
@@ -795,23 +806,22 @@
             h1[tile] = pad(xhat * row(vec, G1) + row(vec, C1))
 
         each_seq(norm)
-        lhs[...] = h1[...]
+
+    for i in WAYS:
+        at_step(PAIR * i + 1)(stores[i].start)
 
     @pl.when(j >= O)
     def _():
         attention(j - O, rows, o, acc, hosted.visit)
-        lhs[...] = o[...]
 
     @pl.when((j < O) | (j == O + LAST_SEQ))
     def _():
         bias = jnp.where(j < O, b[0], row(vec, BO))
-        att[...] = dot(lhs[...], weights.get(jnp.minimum(j, O))[...]) + bias
+        att[...] = dot(lhs[lax.div(j, O)], weights.get(jnp.minimum(j, O))[...]) + bias
 
     @pl.when(j < O)
     def _():
-        t = att[...].astype(BF16)
-        qkv[0] = t
-        rows[j] = t
+        rows[j] = att[...].astype(BF16)
 
     @at_step(O + LAST_SEQ)
     def _():
@@ -820,26 +830,34 @@
             h2[tile] = pad(xhat * row(vec, G2) + row(vec, C2))
 
         each_seq(norm)
+        for store in stores[PAIR:]:
+            store.start()
 
     hosted.visit("end")
+
+    @at_step(O + LAST_SEQ)
+    def _():
+        for store in stores:
+            store.wait()
 
 
 def upto(n):
     return lambda j: jnp.minimum(j, n)
 
 
-def front_call(x, w_attn, b_qkv, vec, up, collective_id):
+def front_call(x, w_attn, b_qkv, vec, up, down, collective_id):
+    outs = ((BF16, O, TT, D), (BF16, TT, D), (BF16, TT, D), (F32, TT, D), (BF16, TT, D), (BF16, *Gather.shape(WIDE)),
+            (BF16, *Gather.shape(DOWN)))
+    dma = pltpu.SemaphoreType.DMA
     return pl.pallas_call(
-        front_kernel, grid=(O + PAIR,),
-        out_shape=(sds(BF16, O, TT, D), sds(BF16, TT, D), sds(BF16, TT, D), sds(F32, TT, D), sds(BF16, TT, D),
-                   sds(BF16, *Gather.shape(WIDE))),
-        in_specs=[ANY, ANY, along(0, 1, 1, D, index=upto(V)), whole(8, D), ANY],
-        out_specs=(along(0, 1, TT, D, index=upto(V)),) + (whole(TT, D),) * SIDE + (ANY,),
-        scratch_shapes=[pltpu.VMEM((O, TT, D), BF16), pltpu.VMEM((TT, D), BF16), pltpu.VMEM((SEQ, D), F32),
-                        pltpu.VMEM(SEQS, BF16), pltpu.SemaphoreType.DMA] + Feed.scratch(BF16, D, D) + Gather.semaphores(),
+        front_kernel, grid=(O + PAIR,), out_shape=[sds(*out) for out in outs],
+        in_specs=[ANY, ANY, along(0, 1, 1, D, index=upto(V)), whole(8, D), ANY, ANY], out_specs=[ANY] * len(outs),
+        scratch_shapes=[pltpu.VMEM((O, TT, D), BF16), pltpu.VMEM((PAIR, TT, D), BF16), pltpu.VMEM((TT, D), F32),
+                        pltpu.VMEM((TT, D), BF16), pltpu.VMEM((SEQ, D), F32), pltpu.VMEM(SEQS, BF16), dma] +
+        Feed.scratch(BF16, D, D) + [dma((SIDE + 1,))] + Gather.semaphores() * PAIR,
         input_output_aliases={SIDE: SIDE + 1},
         compiler_params=comm_params(collective_id), name="front",
-    )(x, w_attn, b_qkv, vec, up)
+    )(x, w_attn, b_qkv, vec, up, down)
 
 
 TILES = FF // HALF
@@ -1465,10 +1483,10 @@
 def device_step(x, gz, *shards):
     first = lax.rem(lax.axis_index("fsdp"), PAIR) == 0
     attn, up, down = my_pieces(shards, first)
-    w_attn, up, down = gather_call(attn, up, down, 0)
+    w_attn, up = gather_call(attn, up, 0)
     w_attn = w_attn.reshape(SIDE, D, QCOLS)
     b_qkv, b_up, vec = small_params(w_attn)
-    qkv, h1, o, att, h2, w_up = front_call(x, w_attn, b_qkv, vec, up, 1)
+    qkv, h1, o, att, h2, w_up, down = front_call(x, w_attn, b_qkv, vec, up, down, 1)
     w_up = w_up.reshape(SIDE, D, QCOLS)
     act, slope, part, w_down = mlp_in_call(h2, gz, w_up, b_up, vec, down, 2)
     part = part.reshape((SIDE,) * 3 + (C * UNIT, HALF))

time: 450 us -> 453 us (level)
  no operation moved by 1% of the time
where the time goes in v12:
time: 453 us; the launch traced here: 452 us
  Pallas kernels  416 us (92%)
  local copies, waits for them, and re-layouts  23.6 us (5%)
  other arithmetic  7.73 us (2%)
    pallas_call x1, Pallas kernels, last_call(): pl.pallas_call(last_kernel, grid=(IN_STEPS + 1,), out_shape=(sds(BF16, *S...  106 us
    pallas_call x1, Pallas kernels, mlp_out_call(): pl.pallas_call(mlp_out_kernel, grid=(TILES,), out_shape=(sds(BF16, PAIR,...  60.1 us
    pallas_call x1, Pallas kernels, attn_back_call(): pl.pallas_call(attn_back_kernel, grid=(SEQS[0] + GRAD_STEPS,), out_shape=...  58.3 us
    pallas_call x1, Pallas kernels, gather_call(): pl.pallas_call(gather_kernel, out_shape=[sds(BF16, *Gather.shape(WIDE))]...  56.3 us
    pallas_call x1, Pallas kernels, front_call(): pl.pallas_call(front_kernel, grid=(O + PAIR,), out_shape=[sds(*out) for o...  54.8 us
    pallas_call x1, Pallas kernels, mlp_in_call(): pl.pallas_call(mlp_in_kernel, grid=(2 * TILES,), out_shape=(sds(BF16, TT,...  45.1 us
    pallas_call x1, Pallas kernels, mid_call(): pl.pallas_call(mid_kernel, grid=(SEQS[0] + GRAD_STEPS,), out_shape=(sds(B...  35.5 us
    unnamed x20, local copies, waits for them, and re-layouts  13.5 us
  transfers between devices with their start and end apart: 2, of which 0 were waited for; matrix products, arithmetic and copies ran while one was open for 2% of the time, Pallas kernels for 0%

profile of v12, /device:TPU:1, one launch (start us, length us, event | category | flops | bytes accessed | tf_op | source)
XLA Modules:
  0.0 451.6 jit_solution(12052337658897289760)
XLA Ops:
  3.0 1.0 fusion.1
  4.0 1.0 fusion.2
  5.1 1.4 collective-permute-start
  6.5 1.3 copy.30.x_in.refs_3_.refs_2_
  7.8 1.3 copy.31.gz_in.gz.refs_4_
  9.1 1.6 dynamic-slice_convert_fusion.1
  11.6 56.3 %gather.1 = (bf16[4,4,4,88,1536]{4,3,2,1,0:T(8,128)(2,1)}, bf16[4,4,4,88,1536]{4,3,2,1,0:T(8,128)(2,1)}) custom-call(bf16[88,768]{1,0:T(8,128)(2,1)} %get-tuple-element.102.refs_0_, bf16[88,768]{1,0:T(8,128)(2,1)} %get-tuple-element.101.refs_1_), custom_call_target="tpu_custom_call" | custom-call | tf_op jit(solution)/shard_map/gather/pallas_call | solution.py:541
  67.9 1.0 slice_convert_fusion
  71.5 54.8 %front.1 = (bf16[3,544,1408]{2,1,0:T(8,128)(2,1)}, bf16[544,1408]{1,0:T(8,128)(2,1)}, bf16[544,1408]{1,0:T(8,128)(2,1)}, f32[544,1408]{1,0:T(8,128)}, bf16[544,1...) custom-call(bf16[2,257,1408]{2,1,0:T(8,128)(2,1)} %copy.30.x_in.refs, ...), custom_call_target="tpu_custom_call", output_to_operand_aliasing={{5}: (4, {})} | custom-call | tf_op jit(solution)/shard_map/front/pallas_call | solution.py:852
  126.4 45.1 %mlp_in.1 = (bf16[544,6144]{1,0:T(8,128)(2,1)}, f32[544,6144]{1,0:T(8,128)}, f32[6144,768]{1,0:T(8,128)}, bf16[4,4,2,4,3,16,1408]{6,5,4,3,2,1,0:T(8,128)(2,1)}) custom-call(bf16[544,1408]{1,0:T(8,128)(2,1)} %get-tuple-element.47.h2_in.refs_7_, bf16[2,257,1408]{2,1,0:T(8,128)(2,1)} %copy.31.gz_in.gz.refs_4_, ...), custom_call_target="tpu_custom_call", output_to_operand_aliasing={{3}: (5, {})} | custom-call | tf_op jit(solution)/shard_map/mlp_in/pallas_call | solution.py:939
  171.5 60.1 %mlp_out.1 = (bf16[2,4,544,768]{3,2,1,0:T(8,128)(2,1)}, f32[8,1,768]{2,1,0:T(1,128)}, f32[544,1408]{1,0:T(8,128)}, f32[544,1408]{1,0:T(8,128)}, f32[3,4,4,32,768]{4,3,2,1,0:T(8,128)}) custom-call(bf16[544,6144]{1,0:T(8,128)(2,1)} %get-tuple-element.50.act_in, f32[544,6144]{1,0:T(8,128)} %get-tuple-element.51.slope_in, ...), custom_call_target="tpu_custom_call" | custom-call | tf_op jit(solution)/shard_map/mlp_out/pallas_call | solution.py:1002
  231.6 0.8 reduce
  232.5 35.5 %mid.1 = (bf16[2,257,1408]{2,1,0:T(8,128)(2,1)}, f32[544,1408]{1,0:T(8,128)}, bf16[2,544,768]{2,1,0:T(8,128)(2,1)}, bf16[544,1408]{1,0:T(8,128)(2,1)}, f32[8,140...) custom-call(f32[544,1408]{1,0:T(8,128)} %get-tuple-element.54.refs_0_, ...), custom_call_target="tpu_custom_call" | custom-call | tf_op jit(solution)/shard_map/mid/pallas_call | solution.py:1177
  268.1 0.8 slice.59
  269.2 58.3 %attn_back.1 = (bf16[2,3,544,768]{3,2,1,0:T(8,128)(2,1)}, f32[3,1408]{1,0:T(4,128)}, f32[4,1408,768]{2,1,0:T(8,128)}, f32[3,4,4,32,768]{4,3,2,1,0:T(8,128)}, f32[4,3,32,768]{3,2,1,0:T(8,128)}) custom-call(bf16[3,544,1408]{2,1,0:T(8,128)(2,1)} %get-tuple-element.60.refs_0_, bf16[544,1408]{1,0:T(8,128)(2,1)} %get-tuple-element.61.refs_1_, ...), custom_call_target="tpu_custom_call" | custom-call | tf_op jit(solution)/shard_map/attn_back/pallas_call | solution.py:1240
  327.5 0.9 reshape.95
  328.5 2.3 collective-permute-start.1
  330.7 3.6 copy.37
  334.5 0.9 reshape.100.refs_5_
  335.4 105.5 %last.1 = (bf16[2,257,1408]{2,1,0:T(8,128)(2,1)}, f32[4,4,4,88,768]{4,3,2,1,0:T(8,128)}, f32[48,4224]{1,0:T(8,128)}, f32[48,1408]{1,0:T(8,128)}, f32[48,6144]{1,...) custom-call(bf16[2,3,544,768]{3,2,1,0:T(8,128)(2,1)} %get-tuple-element.67.refs_0_,, ...), custom_call_target="tpu_custom_call", output_to_operand_aliasing={{1}: (8, {})} | custom-call | tf_op jit(solution)/shard_map/last/pallas_call | solution.py:1424
  443.7 3.6 copy.38
  448.0 0.9 copy.48
  449.6 1.0 copy.50
  450.6 1.0 copy.51
  (48 shorter events, 10.6 us)
Async XLA Ops:
  0.6 5.9 %copy-start = (bf16[2,257,1408]{2,0,1:T(2,128)(2,1)S(1)}, bf16[2,257,1408]{2,0,1:T(2,128)(2,1)}, u32[]{:S(2)}) copy-start(bf16[2,257,1408]{2,0,1:T(2,128)(2,1)} %param.9) | copy-start | bytes 4342276
  5.0 2.8 copy-start.1
  5.1 5.7 %collective-permute-start = (bf16[2,44,768]{2,1,0:T(8,128)(2,1)S(1)}, bf16[2,44,768]{2,1,0:T(8,128)(2,1)S(1)}, u32[]{:S(2)}, u32[]{:S(2)}) collective-permute-start(bf16[2,44,768]{2,1,0:T(8,128)(2,1)S(1)} %broadcast_select_fusion.2), channel_id=1, source_target_pairs={{0,1},{1,0},{2,3},{3,2},{4,5},{5,4},{6,7},{7,6},{8,9},{9,8},{10,11... | collective-permute-start | bytes 405512 | tf_op jit(solution)/shard_map/ppermute | solution.py:1443
  328.5 5.9 %collective-permute-start.1 = (f32[32,588]{1,0:T(8,128)S(1)}, f32[32,588]{1,0:T(8,128)S(1)}, u32[]{:S(2)}, u32[]{:S(2)}) collective-permute-start(f32[32,588]{1,0:T(8,128)S(1)} %pad_maximum_fusion.2), channel_id=1, source_target_pairs={{0,1},{1,0},{2,3},{3,2},{4,5},{5,4},{6,7},{7,6},{8,9},{9,8},{10,11... | collective-permute-start | bytes 225800 | tf_op jit(solution)/shard_map/ppermute | solution.py:1443
  441.0 7.0 %copy-start.4 = (f32[48,4224]{1,0:T(8,128)S(1)}, f32[48,4224]{1,0:T(8,128)}, u32[]{:S(2)}) copy-start(f32[48,4224]{1,0:T(8,128)} %get-tuple-element.76) | copy-start | bytes 2433028
  443.7 5.2 %copy-start.5 = (f32[48,1408]{1,0:T(8,128)S(1)}, f32[48,1408]{1,0:T(8,128)}, u32[]{:S(2)}) copy-start(f32[48,1408]{1,0:T(8,128)} %get-tuple-element.78) | copy-start | bytes 811012
  447.3 2.3 copy-start.2
  448.9 1.7 copy-start.3

commit v13 on v11

--- a/solution.py
+++ b/solution.py
@@ -776,11 +776,15 @@
 FRONT_PLAN = {"start": ((0, 0, 1),), "half": ((O + 1, 1, 2),), "end": ((O + 1, 2, None),)}
 
 
-def front_kernel(x_in, w_in, b, vec, _, qkv, h1, o, att, h2, up, rows, lhs, acc, x, x_sem, w_rows, w_sems, *sems):
-    hosted = Background(Gather(WIDE, None, up, *sems).last_ring(), FRONT_PLAN)
+def front_kernel(x_in, w_in, b, vec, _, qkv_out, h1_out, o_out, att_out, h2_out, up, rows, lhs, att, h2, acc, x,
+                 x_sem, w_rows, w_sems, sems, *ring_sems):
+    hosted = Background(Gather(WIDE, None, up, *ring_sems).last_ring(), FRONT_PLAN)
     j = pl.program_id(0)
     weights = Feed(lambda n: w_in.at[n, :, pl.ds(0, D)], SIDE, w_rows, w_sems)
     fetch = pltpu.make_async_copy(x_in, x, x_sem)
+    h1, o = (lhs.at[i] for i in WAYS)
+    stores = [pltpu.make_async_copy(*move, sems.at[i]) for i, move in enumerate(
+        ((h1, h1_out), (rows, qkv_out), (o, o_out), (att, att_out), (h2, h2_out)))]
     at_step(0)(fetch.start)
     first_feeds(weights)
     at_step(0)(enter)
@@ -795,23 +799,22 @@
             h1[tile] = pad(xhat * row(vec, G1) + row(vec, C1))
 
         each_seq(norm)
-        lhs[...] = h1[...]
+
+    for i in WAYS:
+        at_step(PAIR * i + 1)(stores[i].start)
 
     @pl.when(j >= O)
     def _():
         attention(j - O, rows, o, acc, hosted.visit)
-        lhs[...] = o[...]
 
     @pl.when((j < O) | (j == O + LAST_SEQ))
     def _():
         bias = jnp.where(j < O, b[0], row(vec, BO))
-        att[...] = dot(lhs[...], weights.get(jnp.minimum(j, O))[...]) + bias
+        att[...] = dot(lhs[lax.div(j, O)], weights.get(jnp.minimum(j, O))[...]) + bias
 
     @pl.when(j < O)
     def _():
-        t = att[...].astype(BF16)
-        qkv[0] = t
-        rows[j] = t
+        rows[j] = att[...].astype(BF16)
 
     @at_step(O + LAST_SEQ)
     def _():
@@ -820,8 +823,15 @@
             h2[tile] = pad(xhat * row(vec, G2) + row(vec, C2))
 
         each_seq(norm)
+        for store in stores[PAIR:]:
+            store.start()
 
     hosted.visit("end")
+
+    @at_step(O + LAST_SEQ)
+    def _():
+        for store in stores:
+            store.wait()
 
 
 def upto(n):
@@ -829,14 +839,14 @@
 
 
 def front_call(x, w_attn, b_qkv, vec, up, collective_id):
+    outs = ((BF16, O, TT, D), (BF16, TT, D), (BF16, TT, D), (F32, TT, D), (BF16, TT, D), (BF16, *Gather.shape(WIDE)))
+    dma = pltpu.SemaphoreType.DMA
     return pl.pallas_call(
-        front_kernel, grid=(O + PAIR,),
-        out_shape=(sds(BF16, O, TT, D), sds(BF16, TT, D), sds(BF16, TT, D), sds(F32, TT, D), sds(BF16, TT, D),
-                   sds(BF16, *Gather.shape(WIDE))),
-        in_specs=[ANY, ANY, along(0, 1, 1, D, index=upto(V)), whole(8, D), ANY],
-        out_specs=(along(0, 1, TT, D, index=upto(V)),) + (whole(TT, D),) * SIDE + (ANY,),
-        scratch_shapes=[pltpu.VMEM((O, TT, D), BF16), pltpu.VMEM((TT, D), BF16), pltpu.VMEM((SEQ, D), F32),
-                        pltpu.VMEM(SEQS, BF16), pltpu.SemaphoreType.DMA] + Feed.scratch(BF16, D, D) + Gather.semaphores(),
+        front_kernel, grid=(O + PAIR,), out_shape=[sds(*out) for out in outs],
+        in_specs=[ANY, ANY, along(0, 1, 1, D, index=upto(V)), whole(8, D), ANY], out_specs=[ANY] * len(outs),
+        scratch_shapes=[pltpu.VMEM((O, TT, D), BF16), pltpu.VMEM((PAIR, TT, D), BF16), pltpu.VMEM((TT, D), F32),
+                        pltpu.VMEM((TT, D), BF16), pltpu.VMEM((SEQ, D), F32), pltpu.VMEM(SEQS, BF16), dma] +
+        Feed.scratch(BF16, D, D) + [dma((SIDE + 1,))] + Gather.semaphores(),
         input_output_aliases={SIDE: SIDE + 1},
         compiler_params=comm_params(collective_id), name="front",
     )(x, w_attn, b_qkv, vec, up)

time: 450 us -> 446 us (level)
  no operation moved by 1% of the time
where the time goes in v13:
time: 446 us; the launch traced here: 445 us
  Pallas kernels  409 us (92%)
  local copies, waits for them, and re-layouts  23.6 us (5%)
  other arithmetic  7.73 us (2%)
    pallas_call x1, Pallas kernels, last_call(): pl.pallas_call(last_kernel, grid=(IN_STEPS + 1,), out_shape=(sds(BF16, *S...  106 us
    pallas_call x1, Pallas kernels, gather_call(): pl.pallas_call(gather_kernel, out_shape=[sds(BF16, *Gather.shape(kind)) f...  62.5 us
    pallas_call x1, Pallas kernels, mlp_out_call(): pl.pallas_call(mlp_out_kernel, grid=(TILES,), out_shape=(sds(BF16, PAIR,...  59.9 us
    pallas_call x1, Pallas kernels, attn_back_call(): pl.pallas_call(attn_back_kernel, grid=(SEQS[0] + GRAD_STEPS,), out_shape=...  58.2 us
    pallas_call x1, Pallas kernels, mlp_in_call(): pl.pallas_call(mlp_in_kernel, grid=(2 * TILES,), out_shape=(sds(BF16, TT,...  45.3 us
    pallas_call x1, Pallas kernels, front_call(): pl.pallas_call(front_kernel, grid=(O + PAIR,), out_shape=[sds(*out) for o...  41.6 us
    pallas_call x1, Pallas kernels, mid_call(): pl.pallas_call(mid_kernel, grid=(SEQS[0] + GRAD_STEPS,), out_shape=(sds(B...  35.9 us
    unnamed x20, local copies, waits for them, and re-layouts  13.5 us
  transfers between devices with their start and end apart: 2, of which 0 were waited for; matrix products, arithmetic and copies ran while one was open for 2% of the time, Pallas kernels for 0%

profile of v13, /device:TPU:1, one launch (start us, length us, event | category | flops | bytes accessed | tf_op | source)
XLA Modules:
  0.0 445.2 jit_solution(5851041579169190222)
XLA Ops:
  3.0 1.0 fusion.1
  4.0 1.0 fusion.2
  5.1 1.4 collective-permute-start
  6.5 1.3 copy.30.x_in.refs_3_.refs_2_
  7.8 1.3 copy.31.gz_in.gz.refs_4_
  9.1 1.6 dynamic-slice_convert_fusion.1
  11.6 62.5 %gather.1 = (bf16[4,4,4,88,1536]{4,3,2,1,0:T(8,128)(2,1)}, bf16[4,4,4,88,1536]{4,3,2,1,0:T(8,128)(2,1)}, bf16[4,4,2,4,3,16,1408]{6,5,4,3,2,1,0:T(8,128)(2,1)}) custom-call(bf16[88,768]{1,0:T(8,128)(2,1)} %get-tuple-element.102.refs_0_, bf16[88,768]{1,0:T(8,128)(2,1)} %get-tuple-element.101.refs_1_, bf16[3,16,1408]{2,1,0:T(8,128)(2,1)} %bitcast.42), custom_call_target="tpu_custom_call" | custom-call | tf_op jit(solution)/shard_map/gather/pallas_call | solution.py:537
  74.1 1.0 slice_convert_fusion
  77.8 41.6 %front.1 = (bf16[3,544,1408]{2,1,0:T(8,128)(2,1)}, bf16[544,1408]{1,0:T(8,128)(2,1)}, bf16[544,1408]{1,0:T(8,128)(2,1)}, f32[544,1408]{1,0:T(8,128)}, bf16[544,1...) custom-call(bf16[2,257,1408]{2,1,0:T(8,128)(2,1)} %copy.30.x_in.refs_3_.refs_2_, ...), custom_call_target="tpu_custom_call", output_to_operand_aliasing={{5}: (4, {})} | custom-call | tf_op jit(solution)/shard_map/front/pallas_call | solution.py:844
  119.4 45.3 %mlp_in.1 = (bf16[544,6144]{1,0:T(8,128)(2,1)}, f32[544,6144]{1,0:T(8,128)}, f32[6144,768]{1,0:T(8,128)}, bf16[4,4,2,4,3,16,1408]{6,5,4,3,2,1,0:T(8,128)(2,1)}) custom-call(bf16[544,1408]{1,0:T(8,128)(2,1)} %get-tuple-element.47.h2_in.refs_7_, bf16[2,257,1408]{2,1,0:T(8,128)(2,1)} %copy.31.gz_in.gz.refs_4_, ...), custom_call_target="tpu_custom_call", output_to_operand_aliasing={{3}: (5, {})} | custom-call | tf_op jit(solution)/shard_map/mlp_in/pallas_call | solution.py:931
  164.7 59.9 %mlp_out.1 = (bf16[2,4,544,768]{3,2,1,0:T(8,128)(2,1)}, f32[8,1,768]{2,1,0:T(1,128)}, f32[544,1408]{1,0:T(8,128)}, f32[544,1408]{1,0:T(8,128)}, f32[3,4,4,32,768]{4,3,2,1,0:T(8,128)}) custom-call(bf16[544,6144]{1,0:T(8,128)(2,1)} %get-tuple-element.50.act_in, f32[544,6144]{1,0:T(8,128)} %get-tuple-element.51.slope_in, ...), custom_call_target="tpu_custom_call" | custom-call | tf_op jit(solution)/shard_map/mlp_out/pallas_call | solution.py:994
  224.7 0.8 reduce
  225.6 35.9 %mid.1 = (bf16[2,257,1408]{2,1,0:T(8,128)(2,1)}, f32[544,1408]{1,0:T(8,128)}, bf16[2,544,768]{2,1,0:T(8,128)(2,1)}, bf16[544,1408]{1,0:T(8,128)(2,1)}, f32[8,140...) custom-call(f32[544,1408]{1,0:T(8,128)} %get-tuple-element.54.refs_0_, ...), custom_call_target="tpu_custom_call" | custom-call | tf_op jit(solution)/shard_map/mid/pallas_call | solution.py:1169
  261.4 0.8 slice.59
  262.5 58.2 %attn_back.1 = (bf16[2,3,544,768]{3,2,1,0:T(8,128)(2,1)}, f32[3,1408]{1,0:T(4,128)}, f32[4,1408,768]{2,1,0:T(8,128)}, f32[3,4,4,32,768]{4,3,2,1,0:T(8,128)}, f32[4,3,32,768]{3,2,1,0:T(8,128)}) custom-call(bf16[3,544,1408]{2,1,0:T(8,128)(2,1)} %get-tuple-element.60.refs_0_, bf16[544,1408]{1,0:T(8,128)(2,1)} %get-tuple-element.61.refs_1_, ...), custom_call_target="tpu_custom_call" | custom-call | tf_op jit(solution)/shard_map/attn_back/pallas_call | solution.py:1232
  320.7 0.9 reshape.95
  321.7 2.4 collective-permute-start.1
  324.1 3.6 copy.37
  327.9 0.9 reshape.100.refs_5_
  328.9 105.7 %last.1 = (bf16[2,257,1408]{2,1,0:T(8,128)(2,1)}, f32[4,4,4,88,768]{4,3,2,1,0:T(8,128)}, f32[48,4224]{1,0:T(8,128)}, f32[48,1408]{1,0:T(8,128)}, f32[48,6144]{1,...) custom-call(bf16[2,3,544,768]{3,2,1,0:T(8,128)(2,1)} %get-tuple-element.67.refs_0_,, ...), custom_call_target="tpu_custom_call", output_to_operand_aliasing={{1}: (8, {})} | custom-call | tf_op jit(solution)/shard_map/last/pallas_call | solution.py:1416
  437.2 3.6 copy.38
  441.6 0.9 copy.48
  443.2 1.0 copy.50
  444.2 1.0 copy.51
  (48 shorter events, 10.6 us)
Async XLA Ops:
  0.6 5.9 %copy-start = (bf16[2,257,1408]{2,0,1:T(2,128)(2,1)S(1)}, bf16[2,257,1408]{2,0,1:T(2,128)(2,1)}, u32[]{:S(2)}) copy-start(bf16[2,257,1408]{2,0,1:T(2,128)(2,1)} %param.9) | copy-start | bytes 4342276
  5.0 2.8 copy-start.1
  5.1 5.7 %collective-permute-start = (bf16[2,44,768]{2,1,0:T(8,128)(2,1)S(1)}, bf16[2,44,768]{2,1,0:T(8,128)(2,1)S(1)}, u32[]{:S(2)}, u32[]{:S(2)}) collective-permute-start(bf16[2,44,768]{2,1,0:T(8,128)(2,1)S(1)} %broadcast_select_fusion.2), channel_id=1, source_target_pairs={{0,1},{1,0},{2,3},{3,2},{4,5},{5,4},{6,7},{7,6},{8,9},{9,8},{10,11... | collective-permute-start | bytes 405512 | tf_op jit(solution)/shard_map/ppermute | solution.py:1435
  321.7 6.0 %collective-permute-start.1 = (f32[32,588]{1,0:T(8,128)S(1)}, f32[32,588]{1,0:T(8,128)S(1)}, u32[]{:S(2)}, u32[]{:S(2)}) collective-permute-start(f32[32,588]{1,0:T(8,128)S(1)} %pad_maximum_fusion.2), channel_id=1, source_target_pairs={{0,1},{1,0},{2,3},{3,2},{4,5},{5,4},{6,7},{7,6},{8,9},{9,8},{10,11... | collective-permute-start | bytes 225800 | tf_op jit(solution)/shard_map/ppermute | solution.py:1435
  434.5 7.0 %copy-start.4 = (f32[48,4224]{1,0:T(8,128)S(1)}, f32[48,4224]{1,0:T(8,128)}, u32[]{:S(2)}) copy-start(f32[48,4224]{1,0:T(8,128)} %get-tuple-element.76) | copy-start | bytes 2433028
  437.2 5.2 %copy-start.5 = (f32[48,1408]{1,0:T(8,128)S(1)}, f32[48,1408]{1,0:T(8,128)}, u32[]{:S(2)}) copy-start(f32[48,1408]{1,0:T(8,128)} %get-tuple-element.78) | copy-start | bytes 811012
  440.9 2.3 copy-start.2
  442.5 1.7 copy-start.3

commit v14 on v13

--- a/solution.py
+++ b/solution.py
@@ -773,7 +773,7 @@
     o[pl.ds(start, TOK)] = pad(acc[...])
 
 
-FRONT_PLAN = {"start": ((0, 0, 1),), "half": ((O + 1, 1, 2),), "end": ((O + 1, 2, None),)}
+FRONT_PLAN = {"start": ((0, 0, 1),), "end": ((O, 1, 2), (O + 1, 2, None))}
 
 
 def front_kernel(x_in, w_in, b, vec, _, qkv_out, h1_out, o_out, att_out, h2_out, up, rows, lhs, att, h2, acc, x,
@@ -862,7 +862,7 @@
     ref[pl.ds(pl.multiple_of(tail + TAIL * s, TAIL), TAIL)] = t[BODY:]
 
 
-DOWN_PLAN = {"start": ((0, 0, 1),), "end": ((TILES + 2, 1, 2), (2 * TILES - 1, 2, None))}
+DOWN_PLAN = {"start": ((0, 0, 1),), "end": ((TILES - 1, 1, 2), (TILES + SIDE, 2, 3), (2 * TILES - 1, 3, None))}
 
 
 def mlp_in_kernel(h2_in, gz_in, up_in, b_up, vec, _, act, slope, d_down, down, a_rows, b_rows, b_away, *sems):

time: 446 us -> 438 us (0.982)
  Pallas kernels: 409 us -> 401 us
    pallas_call x1, Pallas kernels: 41.6 us -> 36.4 us  [front_call(): pl.pallas_call(front_kernel, grid=(O + PAIR,), out_shape=[sds(*out) for o...]
where the time goes in v14:
time: 438 us; the launch traced here: 437 us
  Pallas kernels  401 us (92%)
  local copies, waits for them, and re-layouts  23.6 us (5%)
  other arithmetic  7.73 us (2%)
    pallas_call x1, Pallas kernels, last_call(): pl.pallas_call(last_kernel, grid=(IN_STEPS + 1,), out_shape=(sds(BF16, *S...  106 us
    pallas_call x1, Pallas kernels, gather_call(): pl.pallas_call(gather_kernel, out_shape=[sds(BF16, *Gather.shape(kind)) f...  62.5 us
    pallas_call x1, Pallas kernels, mlp_out_call(): pl.pallas_call(mlp_out_kernel, grid=(TILES,), out_shape=(sds(BF16, PAIR,...  59.9 us
    pallas_call x1, Pallas kernels, attn_back_call(): pl.pallas_call(attn_back_kernel, grid=(SEQS[0] + GRAD_STEPS,), out_shape=...  58.2 us
    pallas_call x1, Pallas kernels, mlp_in_call(): pl.pallas_call(mlp_in_kernel, grid=(2 * TILES,), out_shape=(sds(BF16, TT,...  42.7 us
    pallas_call x1, Pallas kernels, front_call(): pl.pallas_call(front_kernel, grid=(O + PAIR,), out_shape=[sds(*out) for o...  36.4 us
    pallas_call x1, Pallas kernels, mid_call(): pl.pallas_call(mid_kernel, grid=(SEQS[0] + GRAD_STEPS,), out_shape=(sds(B...  36 us
    unnamed x20, local copies, waits for them, and re-layouts  13.5 us
  transfers between devices with their start and end apart: 2, of which 0 were waited for; matrix products, arithmetic and copies ran while one was open for 2% of the time, Pallas kernels for 0%

profile of v14, /device:TPU:1, one launch (start us, length us, event | category | flops | bytes accessed | tf_op | source)
XLA Modules:
  0.0 437.4 jit_solution(6695715061610691064)
XLA Ops:
  3.0 1.0 fusion.1
  4.0 1.0 fusion.2
  5.1 1.4 collective-permute-start
  6.5 1.3 copy.30.x_in.refs_3_.refs_2_
  7.8 1.3 copy.31.gz_in.gz.refs_4_
  9.1 1.6 dynamic-slice_convert_fusion.1
  11.6 62.5 %gather.1 = (bf16[4,4,4,88,1536]{4,3,2,1,0:T(8,128)(2,1)}, bf16[4,4,4,88,1536]{4,3,2,1,0:T(8,128)(2,1)}, bf16[4,4,2,4,3,16,1408]{6,5,4,3,2,1,0:T(8,128)(2,1)}) custom-call(bf16[88,768]{1,0:T(8,128)(2,1)} %get-tuple-element.102.refs_0_, bf16[88,768]{1,0:T(8,128)(2,1)} %get-tuple-element.101.refs_1_, bf16[3,16,1408]{2,1,0:T(8,128)(2,1)} %bitcast.42), custom_call_target="tpu_custom_call" | custom-call | tf_op jit(solution)/shard_map/gather/pallas_call | solution.py:537
  74.1 1.0 slice_convert_fusion
  77.8 36.4 %front.1 = (bf16[3,544,1408]{2,1,0:T(8,128)(2,1)}, bf16[544,1408]{1,0:T(8,128)(2,1)}, bf16[544,1408]{1,0:T(8,128)(2,1)}, f32[544,1408]{1,0:T(8,128)}, bf16[544,1...) custom-call(bf16[2,257,1408]{2,1,0:T(8,128)(2,1)} %copy.30.x_in.refs_3_.refs_2_, ...), custom_call_target="tpu_custom_call", output_to_operand_aliasing={{5}: (4, {})} | custom-call | tf_op jit(solution)/shard_map/front/pallas_call | solution.py:844
  114.2 42.7 %mlp_in.1 = (bf16[544,6144]{1,0:T(8,128)(2,1)}, f32[544,6144]{1,0:T(8,128)}, f32[6144,768]{1,0:T(8,128)}, bf16[4,4,2,4,3,16,1408]{6,5,4,3,2,1,0:T(8,128)(2,1)}) custom-call(bf16[544,1408]{1,0:T(8,128)(2,1)} %get-tuple-element.47.h2_in.refs_7_, bf16[2,257,1408]{2,1,0:T(8,128)(2,1)} %copy.31.gz_in.gz.refs_4_, ...), custom_call_target="tpu_custom_call", output_to_operand_aliasing={{3}: (5, {})} | custom-call | tf_op jit(solution)/shard_map/mlp_in/pallas_call | solution.py:931
  156.9 59.9 %mlp_out.1 = (bf16[2,4,544,768]{3,2,1,0:T(8,128)(2,1)}, f32[8,1,768]{2,1,0:T(1,128)}, f32[544,1408]{1,0:T(8,128)}, f32[544,1408]{1,0:T(8,128)}, f32[3,4,4,32,768]{4,3,2,1,0:T(8,128)}) custom-call(bf16[544,6144]{1,0:T(8,128)(2,1)} %get-tuple-element.50.act_in, f32[544,6144]{1,0:T(8,128)} %get-tuple-element.51.slope_in, ...), custom_call_target="tpu_custom_call" | custom-call | tf_op jit(solution)/shard_map/mlp_out/pallas_call | solution.py:994
  216.9 0.8 reduce
  217.8 36.0 %mid.1 = (bf16[2,257,1408]{2,1,0:T(8,128)(2,1)}, f32[544,1408]{1,0:T(8,128)}, bf16[2,544,768]{2,1,0:T(8,128)(2,1)}, bf16[544,1408]{1,0:T(8,128)(2,1)}, f32[8,140...) custom-call(f32[544,1408]{1,0:T(8,128)} %get-tuple-element.54.refs_0_, ...), custom_call_target="tpu_custom_call" | custom-call | tf_op jit(solution)/shard_map/mid/pallas_call | solution.py:1169
  253.7 0.8 slice.59
  254.8 58.2 %attn_back.1 = (bf16[2,3,544,768]{3,2,1,0:T(8,128)(2,1)}, f32[3,1408]{1,0:T(4,128)}, f32[4,1408,768]{2,1,0:T(8,128)}, f32[3,4,4,32,768]{4,3,2,1,0:T(8,128)}, f32[4,3,32,768]{3,2,1,0:T(8,128)}) custom-call(bf16[3,544,1408]{2,1,0:T(8,128)(2,1)} %get-tuple-element.60.refs_0_, bf16[544,1408]{1,0:T(8,128)(2,1)} %get-tuple-element.61.refs_1_, ...), custom_call_target="tpu_custom_call" | custom-call | tf_op jit(solution)/shard_map/attn_back/pallas_call | solution.py:1232
  313.0 0.9 reshape.95
  314.0 2.4 collective-permute-start.1
  316.4 3.6 copy.37
  320.2 0.9 reshape.100.refs_5_
  321.2 105.6 %last.1 = (bf16[2,257,1408]{2,1,0:T(8,128)(2,1)}, f32[4,4,4,88,768]{4,3,2,1,0:T(8,128)}, f32[48,4224]{1,0:T(8,128)}, f32[48,1408]{1,0:T(8,128)}, f32[48,6144]{1,...) custom-call(bf16[2,3,544,768]{3,2,1,0:T(8,128)(2,1)} %get-tuple-element.67.refs_0_,, ...), custom_call_target="tpu_custom_call", output_to_operand_aliasing={{1}: (8, {})} | custom-call | tf_op jit(solution)/shard_map/last/pallas_call | solution.py:1416
  429.5 3.6 copy.38
  433.8 0.9 copy.48
  435.4 1.0 copy.50
  436.4 1.0 copy.51
  (48 shorter events, 10.6 us)
Async XLA Ops:
  0.6 5.9 %copy-start = (bf16[2,257,1408]{2,0,1:T(2,128)(2,1)S(1)}, bf16[2,257,1408]{2,0,1:T(2,128)(2,1)}, u32[]{:S(2)}) copy-start(bf16[2,257,1408]{2,0,1:T(2,128)(2,1)} %param.9) | copy-start | bytes 4342276
  5.0 2.8 copy-start.1
  5.1 5.7 %collective-permute-start = (bf16[2,44,768]{2,1,0:T(8,128)(2,1)S(1)}, bf16[2,44,768]{2,1,0:T(8,128)(2,1)S(1)}, u32[]{:S(2)}, u32[]{:S(2)}) collective-permute-start(bf16[2,44,768]{2,1,0:T(8,128)(2,1)S(1)} %broadcast_select_fusion.2), channel_id=1, source_target_pairs={{0,1},{1,0},{2,3},{3,2},{4,5},{5,4},{6,7},{7,6},{8,9},{9,8},{10,11... | collective-permute-start | bytes 405512 | tf_op jit(solution)/shard_map/ppermute | solution.py:1435
  314.0 6.0 %collective-permute-start.1 = (f32[32,588]{1,0:T(8,128)S(1)}, f32[32,588]{1,0:T(8,128)S(1)}, u32[]{:S(2)}, u32[]{:S(2)}) collective-permute-start(f32[32,588]{1,0:T(8,128)S(1)} %pad_maximum_fusion.2), channel_id=1, source_target_pairs={{0,1},{1,0},{2,3},{3,2},{4,5},{5,4},{6,7},{7,6},{8,9},{9,8},{10,11... | collective-permute-start | bytes 225800 | tf_op jit(solution)/shard_map/ppermute | solution.py:1435
  426.8 7.0 %copy-start.4 = (f32[48,4224]{1,0:T(8,128)S(1)}, f32[48,4224]{1,0:T(8,128)}, u32[]{:S(2)}) copy-start(f32[48,4224]{1,0:T(8,128)} %get-tuple-element.76) | copy-start | bytes 2433028
  429.5 5.2 %copy-start.5 = (f32[48,1408]{1,0:T(8,128)S(1)}, f32[48,1408]{1,0:T(8,128)}, u32[]{:S(2)}) copy-start(f32[48,1408]{1,0:T(8,128)} %get-tuple-element.78) | copy-start | bytes 811012
  433.1 2.3 copy-start.2
  434.7 1.7 copy-start.3
